TPU v7x, 32 devices: a whole 2x2x4 slice. The times are simulated.
32 devices in a mesh: lat: 4 (over y, x), lon: 8 (over z, core).
Axes of the slice: x: 2, y: 2, z: 4, core: 2. Of those that a mesh axis runs over, the one named last changes fastest.
Arguments:
- pressure: float32 [4, 30, 5120], P('lat', None, 'lon'), may hold values from -6 to 6
- velocity: float32 [4, 30, 7680], P('lat', None, 'lon'), may hold values from -6 to 6
- edge_cells: int32 [4, 2, 7680], P('lat', None, 'lon'), may hold values from 0 to 1663
- cell_edges: int32 [4, 3, 5120], P('lat', None, 'lon'), may hold values from 0 to 1983
- send_cells: int32 [4, 8, 1024], P('lat', None, 'lon'), may hold values from 0 to 639
- send_edges: int32 [4, 8, 1024], P('lat', None, 'lon'), may hold values from 0 to 959
- inv_dual: float32 [4, 7680], P('lat', 'lon'), may hold values from 0.5 to 2
- edge_weight: float32 [4, 3, 5120], P('lat', None, 'lon'), may hold values from -3 to 3
- sound_speed: float32 [4, 5120], P('lat', 'lon'), may hold values from 0.1 to 0.6
- coupling: float32 [4, 30, 5120], P('lat', None, 'lon'), may hold values from 0.1 to 2
Outputs:
- pressure_out: float32 [4, 30, 5120], P('lat', None, 'lon')
- velocity_out: float32 [4, 30, 7680], P('lat', None, 'lon')
Inputs may be any that keep to these rules, and one draw needn't show every extreme that they name: `edge_cells`: positions below 640 are own cells; position 640 + r * 128 + j is slot j of the halo piece from the neighbour at offset number r. `cell_edges`: positions below 960 are own edges; position 960 + r * 128 + j is slot j of the edge halo piece from the neighbour at offset number r. `send_cells`: indices of own cells. `send_edges`: indices of own edges.
All inputs are finite; a program needn't handle non-finite values.
Results may differ from a plain program's by a relative error of at most 0.0001.
Values sent between devices are 32-bit elements; how exact they have to be, the bound alone decides.
No kernel may reach another device: no remote copies, remote signals or barrier semaphores. Data moves between devices by JAX's collectives and lax.ppermute only.
A program may use at most 64 MiB of HBM per device.

v0:
```python
import jax
import jax.numpy as jnp
from jax import lax
from jax.sharding import PartitionSpec as P

NSUB = 3


DIRECTIONS = ((-1, -1), (-1, 0), (-1, 1), (0, -1), (0, 1), (1, -1), (1, 0), (1, 1))
step_scale = 0.5


def from_behind(block, axis, distance):
    devices = range(lax.axis_size(axis))
    route = [((i - distance) % len(devices), i) for i in devices]
    return lax.ppermute(block, axis, route)


def passed_along(value, axis, steps):
    count = lax.axis_size(axis)
    first, last = (max(0, -steps), min(count, count - steps))
    return lax.ppermute(value, axis, [(source, source + steps) for source in range(first, last)])


def position(offset):
    return DIRECTIONS.index(offset)


def edge_update(normal, extended, edge_cells, inv_dual):
    gradient = (
        jnp.take(extended, edge_cells[1], axis=1) - jnp.take(extended, edge_cells[0], axis=1)
    ) * inv_dual[None, :]
    return normal - step_scale * gradient


def column_solve(right_side, coupling):
    levels = right_side.shape[0]
    ratios = []
    scaled = []
    for level_index in range(levels):
        if level_index < levels - 1:
            upper_term = -coupling[level_index]
        else:
            upper_term = 0.0 * coupling[0]
        if level_index == 0:
            divisor = 1.0 + coupling[0]
            current = right_side[0] / divisor
        else:
            lower_term = -coupling[level_index - 1]
            diagonal = 1.0 + coupling[level_index - 1] + coupling[level_index]
            divisor = diagonal - lower_term * ratios[-1]
            current = (right_side[level_index] - lower_term * scaled[-1]) / divisor
        ratios.append(upper_term / divisor)
        scaled.append(current)
    result = [scaled[-1]]
    for level_index in range(levels - 2, -1, -1):
        result.insert(0, scaled[level_index] - ratios[level_index] * result[0])
    return jnp.stack(result)


def cell_update(values, edges_ext, cell_edges, edge_weight, sound_speed, coupling):
    divergence = jnp.take(edges_ext, cell_edges[0], axis=1) * edge_weight[0][None, :]
    divergence = divergence + jnp.take(edges_ext, cell_edges[1], axis=1) * edge_weight[1][None, :]
    divergence = divergence + jnp.take(edges_ext, cell_edges[2], axis=1) * edge_weight[2][None, :]
    right_side = values - sound_speed[None, :] * divergence
    return column_solve(right_side, coupling)


def extend(source, send_list):
    buffers = [jnp.take(source, send_list[member], axis=1) for member in range(8)]
    received = {}
    passing = {}
    for lon_step in (1, -1):
        bundle = jnp.stack([buffers[position((lat_step, lon_step))] for lat_step in (-1, 0, 1)])
        arrived = from_behind(bundle, "lon", lon_step)
        received[0, -lon_step] = arrived[1]
        passing[-1, lon_step] = arrived[0]
        passing[1, lon_step] = arrived[2]
    for lat_step in (1, -1):
        bundle = jnp.stack(
            [passing[lat_step, -1], buffers[position((lat_step, 0))], passing[lat_step, 1]]
        )
        arrived = passed_along(bundle, "lat", lat_step)
        for member, lon_step in enumerate((-1, 0, 1)):
            received[-lat_step, -lon_step] = arrived[member]
    return jnp.concatenate([source] + [received[offset] for offset in DIRECTIONS], axis=1)


def on_device(
    pressure,
    velocity,
    edge_cells,
    cell_edges,
    send_cells,
    send_edges,
    inv_dual,
    edge_weight,
    sound_speed,
    coupling,
):
    values = pressure[0]
    normal = velocity[0]
    for substep in range(NSUB):
        extended = extend(values, send_cells[0])
        normal = edge_update(normal, extended, edge_cells[0], inv_dual[0])
        edges_ext = extend(normal, send_edges[0])
        values = cell_update(
            values, edges_ext, cell_edges[0], edge_weight[0], sound_speed[0], coupling[0]
        )
    return (values[None], normal[None])


def solution(mesh):
    return jax.shard_map(
        on_device,
        mesh=mesh,
        in_specs=(
            P("lat", None, "lon"),
            P("lat", None, "lon"),
            P("lat", None, "lon"),
            P("lat", None, "lon"),
            P("lat", None, "lon"),
            P("lat", None, "lon"),
            P("lat", "lon"),
            P("lat", None, "lon"),
            P("lat", "lon"),
            P("lat", None, "lon"),
        ),
        out_specs=(P("lat", None, "lon"), P("lat", None, "lon")),
        check_vma=False,
    )
```

profile of v0, /device:TPU:0, one launch (start us, length us, event | category | flops | bytes accessed | tf_op | source)
XLA Modules:
  0.0 204.8 jit_solution(5628865552744668317)
XLA Ops:
  0.6 1.1 copy.961
  7.0 4.1 %collective-permute-start = (f32[3,30,128]{2,1,0:T(8,128)S(1)}, f32[3,30,128]{2,1,0:T(8,128)S(1)}, u32[]{:S(2)}, u32[]{:S(2)}) collective-permute-start(f32[3,30,128]{2,1,0:T(8,128)S(1)} %pad_maximum_fusion.12), channel_id=1, source_target_pairs={{1,0},{2,1},{3,2},{4,3},{5,4},{6,5},{7,6},{0,7},{9,8},{10,9},{11,1... | collective-permute-start | bytes 138248 | tf_op jit(solution)/shard_map/ppermute | solution.py:16
  18.2 3.9 %collective-permute-start.2 = (f32[3,30,128]{2,1,0:T(8,128)S(1)}, f32[3,30,128]{2,1,0:T(8,128)S(1)}, u32[]{:S(2)}, u32[]{:S(2)}) collective-permute-start(f32[3,30,128]{2,1,0:T(8,128)S(1)} %pad_maximum_fusion.14), channel_id=1, source_target_pairs={{0,8},{8,16},{16,24},{1,9},{9,17},{17,25},{2,10},{10,18},{18,26},{... | collective-permute-start | bytes 138248 | tf_op jit(solution)/shard_map/ppermute | solution.py:22
  22.1 1.3 collective-permute-start.3
  23.8 4.2 %collective-permute-done.3 = f32[3,30,128]{2,1,0:T(8,128)S(1)} collective-permute-done((f32[3,30,128]{2,1,0:T(8,128)S(1)}, f32[3,30,128]{2,1,0:T(8,128)S(1)}, u32[]{:S(2)}, u32[]{:S(2)}) %collective-permute-start.3) | collective-permute-done | bytes 46112 | tf_op jit(solution)/shard_map/ppermute | solution.py:22
  28.4 2.9 %gather_fusion.9 = f32[960,30]{1,0:T(8,128)S(1)} fusion(f32[30,1664]{0,1:T(8,128)S(1)} %copy.911, s32[1024]{0:T(1024)S(1)} %pad_clamp_fusion.11), kind=kCustom, calls=%fused_computation.27.clone | custom fusion | bytes 234240 | tf_op jit(solution)/shard_map/jit(_take)/gather | solution.py:31
  31.3 2.9 %gather_fusion.8 = f32[960,30]{1,0:T(8,128)S(1)} fusion(f32[30,1664]{0,1:T(8,128)S(1)} %copy.911, s32[1024]{0:T(1024)S(1)} %pad_clamp_fusion.12), kind=kCustom, calls=%fused_computation.1.clone | custom fusion | bytes 234240 | tf_op jit(solution)/shard_map/jit(_take)/gather | solution.py:31
  40.4 3.6 %collective-permute-start.4 = (f32[3,30,128]{1,2,0:T(8,128)S(1)}, f32[3,30,128]{1,2,0:T(8,128)S(1)}, u32[]{:S(2)}, u32[]{:S(2)}) collective-permute-start(f32[3,30,128]{1,2,0:T(8,128)S(1)} %pad_maximum_fusion), channel_id=1, source_target_pairs={{1,0},{2,1},{3,2},{4,3},{5,4},{6,5},{7,6},{0,7},{9,8},{10,9},{11,1... | collective-permute-start | bytes 138248 | tf_op jit(solution)/shard_map/ppermute | solution.py:16
  44.8 2.3 %collective-permute-done.4 = f32[3,30,128]{1,2,0:T(8,128)S(1)} collective-permute-done((f32[3,30,128]{1,2,0:T(8,128)S(1)}, f32[3,30,128]{1,2,0:T(8,128)S(1)}, u32[]{:S(2)}, u32[]{:S(2)}) %collective-permute-start.4) | collective-permute-done | bytes 46112 | tf_op jit(solution)/shard_map/ppermute | solution.py:16
  47.2 4.3 %collective-permute-start.6 = (f32[3,30,128]{1,2,0:T(8,128)S(1)}, f32[3,30,128]{1,2,0:T(8,128)S(1)}, u32[]{:S(2)}, u32[]{:S(2)}) collective-permute-start(f32[3,30,128]{1,2,0:T(8,128)S(1)} %pad_maximum_fusion.2), channel_id=1, source_target_pairs={{0,8},{8,16},{16,24},{1,9},{9,17},{17,25},{2,10},{10,18},{18,26},{... | collective-permute-start | bytes 138248 | tf_op jit(solution)/shard_map/ppermute | solution.py:22
  51.5 1.3 collective-permute-start.7
  52.8 2.1 %collective-permute-done.6 = f32[3,30,128]{1,2,0:T(8,128)S(1)} collective-permute-done((f32[3,30,128]{1,2,0:T(8,128)S(1)}, f32[3,30,128]{1,2,0:T(8,128)S(1)}, u32[]{:S(2)}, u32[]{:S(2)}) %collective-permute-start.6) | collective-permute-done | bytes 46112 | tf_op jit(solution)/shard_map/ppermute | solution.py:22
  55.0 5.2 %collective-permute-done.7 = f32[3,30,128]{1,2,0:T(8,128)S(1)} collective-permute-done((f32[3,30,128]{1,2,0:T(8,128)S(1)}, f32[3,30,128]{1,2,0:T(8,128)S(1)}, u32[]{:S(2)}, u32[]{:S(2)}) %collective-permute-start.7) | collective-permute-done | bytes 46112 | tf_op jit(solution)/shard_map/ppermute | solution.py:22
  60.2 1.7 gather_fusion.20
  62.0 1.7 gather_fusion.19
  63.8 1.7 gather_fusion.18
  81.5 3.2 %collective-permute-start.8 = (f32[3,30,128]{2,1,0:T(8,128)S(1)}, f32[3,30,128]{2,1,0:T(8,128)S(1)}, u32[]{:S(2)}, u32[]{:S(2)}) collective-permute-start(f32[3,30,128]{2,1,0:T(8,128)S(1)} %pad_maximum_fusion.16), channel_id=1, source_target_pairs={{1,0},{2,1},{3,2},{4,3},{5,4},{6,5},{7,6},{0,7},{9,8},{10,9},{11,1... | collective-permute-start | bytes 138248 | tf_op jit(solution)/shard_map/ppermute | solution.py:16
  84.7 1.7 collective-permute-done.8
  86.4 2.3 %collective-permute-start.10 = (f32[3,30,128]{2,1,0:T(8,128)S(1)}, f32[3,30,128]{2,1,0:T(8,128)S(1)}, u32[]{:S(2)}, u32[]{:S(2)}) collective-permute-start(f32[3,30,128]{2,1,0:T(8,128)S(1)} %pad_maximum_fusion.18), channel_id=1, source_target_pairs={{0,8},{8,16},{16,24},{1,9},{9,17},{17,25},{2,10},{10,18},{18,26},{... | collective-permute-start | bytes 138248 | tf_op jit(solution)/shard_map/ppermute | solution.py:22
  88.8 1.3 collective-permute-start.11
  90.5 4.2 %collective-permute-done.11 = f32[3,30,128]{2,1,0:T(8,128)S(1)} collective-permute-done((f32[3,30,128]{2,1,0:T(8,128)S(1)}, f32[3,30,128]{2,1,0:T(8,128)S(1)}, u32[]{:S(2)}, u32[]{:S(2)}) %collective-permute-start.11) | collective-permute-done | bytes 46112 | tf_op jit(solution)/shard_map/ppermute | solution.py:22
  95.1 2.9 %gather_fusion.30 = f32[960,30]{1,0:T(8,128)S(1)} fusion(f32[30,1664]{0,1:T(8,128)S(1)} %copy.932, s32[1024]{0:T(1024)S(1)} %pad_clamp_fusion.11), kind=kCustom, calls=%fused_computation.29.clone | custom fusion | bytes 234240 | tf_op jit(solution)/shard_map/jit(_take)/gather | solution.py:31
  98.0 2.9 %gather_fusion.29 = f32[960,30]{1,0:T(8,128)S(1)} fusion(f32[30,1664]{0,1:T(8,128)S(1)} %copy.932, s32[1024]{0:T(1024)S(1)} %pad_clamp_fusion.12), kind=kCustom, calls=%fused_computation.28.clone | custom fusion | bytes 234240 | tf_op jit(solution)/shard_map/jit(_take)/gather | solution.py:31
  111.4 3.1 %collective-permute-start.12 = (f32[3,30,128]{1,2,0:T(8,128)S(1)}, f32[3,30,128]{1,2,0:T(8,128)S(1)}, u32[]{:S(2)}, u32[]{:S(2)}) collective-permute-start(f32[3,30,128]{1,2,0:T(8,128)S(1)} %pad_maximum_fusion.4), channel_id=1, source_target_pairs={{1,0},{2,1},{3,2},{4,3},{5,4},{6,5},{7,6},{0,7},{9,8},{10,9},{11,1... | collective-permute-start | bytes 138248 | tf_op jit(solution)/shard_map/ppermute | solution.py:16
  114.5 3.0 %collective-permute-done.13 = f32[3,30,128]{1,2,0:T(8,128)S(1)} collective-permute-done((f32[3,30,128]{1,2,0:T(8,128)S(1)}, f32[3,30,128]{1,2,0:T(8,128)S(1)}, u32[]{:S(2)}, u32[]{:S(2)}) %collective-permute-start.13) | collective-permute-done | bytes 46112 | tf_op jit(solution)/shard_map/ppermute | solution.py:16
  117.7 2.8 %collective-permute-start.14 = (f32[3,30,128]{1,2,0:T(8,128)S(1)}, f32[3,30,128]{1,2,0:T(8,128)S(1)}, u32[]{:S(2)}, u32[]{:S(2)}) collective-permute-start(f32[3,30,128]{1,2,0:T(8,128)S(1)} %pad_maximum_fusion.6), channel_id=1, source_target_pairs={{0,8},{8,16},{16,24},{1,9},{9,17},{17,25},{2,10},{10,18},{18,26},{... | collective-permute-start | bytes 138248 | tf_op jit(solution)/shard_map/ppermute | solution.py:22
  120.5 1.5 collective-permute-start.15
  122.0 2.6 %collective-permute-done.14 = f32[3,30,128]{1,2,0:T(8,128)S(1)} collective-permute-done((f32[3,30,128]{1,2,0:T(8,128)S(1)}, f32[3,30,128]{1,2,0:T(8,128)S(1)}, u32[]{:S(2)}, u32[]{:S(2)}) %collective-permute-start.14) | collective-permute-done | bytes 46112 | tf_op jit(solution)/shard_map/ppermute | solution.py:22
  124.7 4.9 %collective-permute-done.15 = f32[3,30,128]{1,2,0:T(8,128)S(1)} collective-permute-done((f32[3,30,128]{1,2,0:T(8,128)S(1)}, f32[3,30,128]{1,2,0:T(8,128)S(1)}, u32[]{:S(2)}, u32[]{:S(2)}) %collective-permute-start.15) | collective-permute-done | bytes 46112 | tf_op jit(solution)/shard_map/ppermute | solution.py:22
  129.6 1.7 gather_fusion.41
  131.3 1.7 gather_fusion.40
  133.0 1.7 gather_fusion.39
  146.6 3.6 %collective-permute-start.16 = (f32[3,30,128]{2,1,0:T(8,128)S(1)}, f32[3,30,128]{2,1,0:T(8,128)S(1)}, u32[]{:S(2)}, u32[]{:S(2)}) collective-permute-start(f32[3,30,128]{2,1,0:T(8,128)S(1)} %pad_maximum_fusion.20), channel_id=1, source_target_pairs={{1,0},{2,1},{3,2},{4,3},{5,4},{6,5},{7,6},{0,7},{9,8},{10,9},{11,1... | collective-permute-start | bytes 138248 | tf_op jit(solution)/shard_map/ppermute | solution.py:16
  150.2 1.7 collective-permute-done.17
  152.0 2.3 %collective-permute-start.18 = (f32[3,30,128]{2,1,0:T(8,128)S(1)}, f32[3,30,128]{2,1,0:T(8,128)S(1)}, u32[]{:S(2)}, u32[]{:S(2)}) collective-permute-start(f32[3,30,128]{2,1,0:T(8,128)S(1)} %pad_maximum_fusion.22), channel_id=1, source_target_pairs={{0,8},{8,16},{16,24},{1,9},{9,17},{17,25},{2,10},{10,18},{18,26},{... | collective-permute-start | bytes 138248 | tf_op jit(solution)/shard_map/ppermute | solution.py:22
  154.3 1.3 collective-permute-start.19
  156.0 4.2 %collective-permute-done.19 = f32[3,30,128]{2,1,0:T(8,128)S(1)} collective-permute-done((f32[3,30,128]{2,1,0:T(8,128)S(1)}, f32[3,30,128]{2,1,0:T(8,128)S(1)}, u32[]{:S(2)}, u32[]{:S(2)}) %collective-permute-start.19) | collective-permute-done | bytes 46112 | tf_op jit(solution)/shard_map/ppermute | solution.py:22
  160.6 2.9 %gather_fusion.51 = f32[960,30]{1,0:T(8,128)S(1)} fusion(f32[30,1664]{0,1:T(8,128)S(1)} %copy.953, s32[1024]{0:T(1024)S(1)} %pad_clamp_fusion.11), kind=kCustom, calls=%fused_computation.31.clone | custom fusion | bytes 234240 | tf_op jit(solution)/shard_map/jit(_take)/gather | solution.py:31
  163.5 2.9 %gather_fusion.50 = f32[960,30]{1,0:T(8,128)S(1)} fusion(f32[30,1664]{0,1:T(8,128)S(1)} %copy.953, s32[1024]{0:T(1024)S(1)} %copy-done.8), kind=kCustom, calls=%fused_computation.30.clone | custom fusion | bytes 234240 | tf_op jit(solution)/shard_map/jit(_take)/gather | solution.py:31
  176.9 3.1 %collective-permute-start.20 = (f32[3,30,128]{1,2,0:T(8,128)S(1)}, f32[3,30,128]{1,2,0:T(8,128)S(1)}, u32[]{:S(2)}, u32[]{:S(2)}) collective-permute-start(f32[3,30,128]{1,2,0:T(8,128)S(1)} %pad_maximum_fusion.8), channel_id=1, source_target_pairs={{1,0},{2,1},{3,2},{4,3},{5,4},{6,5},{7,6},{0,7},{9,8},{10,9},{11,1... | collective-permute-start | bytes 138248 | tf_op jit(solution)/shard_map/ppermute | solution.py:16
  180.9 2.1 %collective-permute-done.21 = f32[3,30,128]{1,2,0:T(8,128)S(1)} collective-permute-done((f32[3,30,128]{1,2,0:T(8,128)S(1)}, f32[3,30,128]{1,2,0:T(8,128)S(1)}, u32[]{:S(2)}, u32[]{:S(2)}) %collective-permute-start.21) | collective-permute-done | bytes 46112 | tf_op jit(solution)/shard_map/ppermute | solution.py:16
  183.2 2.8 %collective-permute-start.22 = (f32[3,30,128]{1,2,0:T(8,128)S(1)}, f32[3,30,128]{1,2,0:T(8,128)S(1)}, u32[]{:S(2)}, u32[]{:S(2)}) collective-permute-start(f32[3,30,128]{1,2,0:T(8,128)S(1)} %pad_maximum_fusion.10), channel_id=1, source_target_pairs={{0,8},{8,16},{16,24},{1,9},{9,17},{17,25},{2,10},{10,18},{18,26},{... | collective-permute-start | bytes 138248 | tf_op jit(solution)/shard_map/ppermute | solution.py:22
  186.0 1.3 collective-permute-start.23
  187.3 1.8 collective-permute-done.22
  189.2 4.8 %collective-permute-done.23 = f32[3,30,128]{1,2,0:T(8,128)S(1)} collective-permute-done((f32[3,30,128]{1,2,0:T(8,128)S(1)}, f32[3,30,128]{1,2,0:T(8,128)S(1)}, u32[]{:S(2)}, u32[]{:S(2)}) %collective-permute-start.23) | collective-permute-done | bytes 46112 | tf_op jit(solution)/shard_map/ppermute | solution.py:22
  194.1 1.7 gather_fusion.62
  195.8 1.7 gather_fusion.61
  197.5 1.7 gather_fusion.60
  (700 shorter events, 75.3 us)
Async XLA Ops:
  1.8 5.2 %copy-start.173 = (pred[128]{0:T(512)(128)(4,1)}, pred[128]{0:T(512)(128)(4,1)S(1)}, u32[]{:S(2)}) copy-start(pred[128]{0:T(512)(128)(4,1)S(1)} %get-tuple-element.349) | copy-start | bytes 388
  1.8 15.0 %copy-start.175 = (pred[128]{0:T(512)(128)(4,1)}, pred[128]{0:T(512)(128)(4,1)S(1)}, u32[]{:S(2)}) copy-start(pred[128]{0:T(512)(128)(4,1)S(1)} %get-tuple-element.343) | copy-start | bytes 388
  1.8 15.0 %copy-start.168 = (pred[128]{0:T(512)(128)(4,1)}, pred[128]{0:T(512)(128)(4,1)S(1)}, u32[]{:S(2)}) copy-start(pred[128]{0:T(512)(128)(4,1)S(1)} %get-tuple-element.283) | copy-start | bytes 388
  4.1 14.0 %collective-permute-start.1 = (f32[3,30,128]{2,1,0:T(8,128)S(1)}, f32[3,30,128]{2,1,0:T(8,128)S(1)}, u32[]{:S(2)}, u32[]{:S(2)}) collective-permute-start(f32[3,30,128]{2,1,0:T(8,128)S(1)} %pad_maximum_fusion.13), channel_id=1, source_target_pairs={{7,0},{0,1},{1,2},{2,3},{3,4},{4,5},{5,6},{6,7},{15,8},{8,9},{9,10... | collective-permute-start | bytes 138248 | tf_op jit(solution)/shard_map/ppermute | solution.py:16
  7.0 11.1 %collective-permute-start = (f32[3,30,128]{2,1,0:T(8,128)S(1)}, f32[3,30,128]{2,1,0:T(8,128)S(1)}, u32[]{:S(2)}, u32[]{:S(2)}) collective-permute-start(f32[3,30,128]{2,1,0:T(8,128)S(1)} %pad_maximum_fusion.12), channel_id=1, source_target_pairs={{1,0},{2,1},{3,2},{4,3},{5,4},{6,5},{7,6},{0,7},{9,8},{10,9},{11,1... | collective-permute-start | bytes 138248 | tf_op jit(solution)/shard_map/ppermute | solution.py:16
  11.2 23.0 %copy-start.137 = (pred[960]{0:T(1024)(128)(4,1)}, pred[960]{0:T(1024)(128)(4,1)S(1)}, u32[]{:S(2)}) copy-start(pred[960]{0:T(1024)(128)(4,1)S(1)} %compare_and_fusion.3) | copy-start | bytes 2884
  11.9 22.3 %copy-start.140 = (pred[960]{0:T(1024)(128)(4,1)}, pred[960]{0:T(1024)(128)(4,1)S(1)}, u32[]{:S(2)}) copy-start(pred[960]{0:T(1024)(128)(4,1)S(1)} %compare_and_fusion.4) | copy-start | bytes 2884
  15.2 82.8 %copy-start.7 = (s32[1024]{0:T(1024)}, s32[1024]{0:T(1024)S(1)}, u32[]{:S(2)}) copy-start(s32[1024]{0:T(1024)S(1)} %pad_clamp_fusion.12) | copy-start | bytes 12292
  15.2 21.8 %copy-start.170 = (pred[128]{0:T(512)(128)(4,1)}, pred[128]{0:T(512)(128)(4,1)S(1)}, u32[]{:S(2)}) copy-start(pred[128]{0:T(512)(128)(4,1)S(1)} %get-tuple-element.337) | copy-start | bytes 388
  15.2 21.9 %copy-start.165 = (pred[128]{0:T(512)(128)(4,1)}, pred[128]{0:T(512)(128)(4,1)S(1)}, u32[]{:S(2)}) copy-start(pred[128]{0:T(512)(128)(4,1)S(1)} %get-tuple-element.325) | copy-start | bytes 388
  15.2 22.0 %copy-start.162 = (pred[128]{0:T(512)(128)(4,1)}, pred[128]{0:T(512)(128)(4,1)S(1)}, u32[]{:S(2)}) copy-start(pred[128]{0:T(512)(128)(4,1)S(1)} %get-tuple-element.327) | copy-start | bytes 388
  15.3 24.8 %copy-start.152 = (pred[128]{0:T(512)(128)(4,1)}, pred[128]{0:T(512)(128)(4,1)S(1)}, u32[]{:S(2)}) copy-start(pred[128]{0:T(512)(128)(4,1)S(1)} %get-tuple-element.331) | copy-start | bytes 388
  15.3 24.9 %copy-start.149 = (pred[128]{0:T(512)(128)(4,1)}, pred[128]{0:T(512)(128)(4,1)S(1)}, u32[]{:S(2)}) copy-start(pred[128]{0:T(512)(128)(4,1)S(1)} %get-tuple-element.333) | copy-start | bytes 388
  15.3 25.0 %copy-start.146 = (pred[128]{0:T(512)(128)(4,1)}, pred[128]{0:T(512)(128)(4,1)S(1)}, u32[]{:S(2)}) copy-start(pred[128]{0:T(512)(128)(4,1)S(1)} %get-tuple-element.335) | copy-start | bytes 388
  15.3 29.3 %copy-start.155 = (pred[128]{0:T(512)(128)(4,1)}, pred[128]{0:T(512)(128)(4,1)S(1)}, u32[]{:S(2)}) copy-start(pred[128]{0:T(512)(128)(4,1)S(1)} %get-tuple-element.329) | copy-start | bytes 388
  15.3 29.4 %copy-start.143 = (pred[128]{0:T(512)(128)(4,1)}, pred[128]{0:T(512)(128)(4,1)S(1)}, u32[]{:S(2)}) copy-start(pred[128]{0:T(512)(128)(4,1)S(1)} %get-tuple-element.265) | copy-start | bytes 388
  15.3 19.8 %copy-start.184 = (s32[1024]{0:T(1024)}, s32[1024]{0:T(1024)S(1)}, u32[]{:S(2)}) copy-start(s32[1024]{0:T(1024)S(1)} %pad_clamp_fusion.4) | copy-start | bytes 12292
  15.3 20.4 %copy-start.185 = (s32[1024]{0:T(1024)}, s32[1024]{0:T(1024)S(1)}, u32[]{:S(2)}) copy-start(s32[1024]{0:T(1024)S(1)} %pad_clamp_fusion.5) | copy-start | bytes 12292
  15.4 21.0 %copy-start.186 = (s32[1024]{0:T(1024)}, s32[1024]{0:T(1024)S(1)}, u32[]{:S(2)}) copy-start(s32[1024]{0:T(1024)S(1)} %pad_clamp_fusion.6) | copy-start | bytes 12292
  15.4 22.1 %copy-start.187 = (s32[1024]{0:T(1024)}, s32[1024]{0:T(1024)S(1)}, u32[]{:S(2)}) copy-start(s32[1024]{0:T(1024)S(1)} %pad_clamp_fusion.7) | copy-start | bytes 12292
  15.4 22.7 %copy-start.188 = (s32[1024]{0:T(1024)}, s32[1024]{0:T(1024)S(1)}, u32[]{:S(2)}) copy-start(s32[1024]{0:T(1024)S(1)} %pad_clamp_fusion.8) | copy-start | bytes 12292
  15.4 23.3 %copy-start.189 = (s32[1024]{0:T(1024)}, s32[1024]{0:T(1024)S(1)}, u32[]{:S(2)}) copy-start(s32[1024]{0:T(1024)S(1)} %pad_clamp_fusion.9) | copy-start | bytes 12292
  15.5 23.9 %copy-start.190 = (s32[1024]{0:T(1024)}, s32[1024]{0:T(1024)S(1)}, u32[]{:S(2)}) copy-start(s32[1024]{0:T(1024)S(1)} %pad_clamp_fusion.10) | copy-start | bytes 12292
  15.5 28.5 %copy-start.191 = (s32[1024]{0:T(1024)}, s32[1024]{0:T(1024)S(1)}, u32[]{:S(2)}) copy-start(s32[1024]{0:T(1024)S(1)} %pad_clamp_fusion.3) | copy-start | bytes 12292
  16.2 115.1 %copy-start.3 = (s32[1024]{0:T(1024)}, s32[1024]{0:T(1024)S(1)}, u32[]{:S(2)}) copy-start(s32[1024]{0:T(1024)S(1)} %pad_clamp_fusion.1) | copy-start | bytes 12292
  16.9 116.1 %copy-start.5 = (s32[1024]{0:T(1024)}, s32[1024]{0:T(1024)S(1)}, u32[]{:S(2)}) copy-start(s32[1024]{0:T(1024)S(1)} %pad_clamp_fusion.2) | copy-start | bytes 12292
  18.2 5.6 %collective-permute-start.2 = (f32[3,30,128]{2,1,0:T(8,128)S(1)}, f32[3,30,128]{2,1,0:T(8,128)S(1)}, u32[]{:S(2)}, u32[]{:S(2)}) collective-permute-start(f32[3,30,128]{2,1,0:T(8,128)S(1)} %pad_maximum_fusion.14), channel_id=1, source_target_pairs={{0,8},{8,16},{16,24},{1,9},{9,17},{17,25},{2,10},{10,18},{18,26},{... | collective-permute-start | bytes 138248 | tf_op jit(solution)/shard_map/ppermute | solution.py:22
  22.1 6.0 %collective-permute-start.3 = (f32[3,30,128]{2,1,0:T(8,128)S(1)}, f32[3,30,128]{2,1,0:T(8,128)S(1)}, u32[]{:S(2)}, u32[]{:S(2)}) collective-permute-start(f32[3,30,128]{2,1,0:T(8,128)S(1)} %pad_maximum_fusion.15), channel_id=1, source_target_pairs={{8,0},{16,8},{24,16},{9,1},{17,9},{25,17},{10,2},{18,10},{26,18},{... | collective-permute-start | bytes 138248 | tf_op jit(solution)/shard_map/ppermute | solution.py:22
  37.4 7.4 %collective-permute-start.5 = (f32[3,30,128]{1,2,0:T(8,128)S(1)}, f32[3,30,128]{1,2,0:T(8,128)S(1)}, u32[]{:S(2)}, u32[]{:S(2)}) collective-permute-start(f32[3,30,128]{1,2,0:T(8,128)S(1)} %pad_maximum_fusion.1), channel_id=1, source_target_pairs={{7,0},{0,1},{1,2},{2,3},{3,4},{4,5},{5,6},{6,7},{15,8},{8,9},{9,10... | collective-permute-start | bytes 138248 | tf_op jit(solution)/shard_map/ppermute | solution.py:16
  40.4 6.8 %collective-permute-start.4 = (f32[3,30,128]{1,2,0:T(8,128)S(1)}, f32[3,30,128]{1,2,0:T(8,128)S(1)}, u32[]{:S(2)}, u32[]{:S(2)}) collective-permute-start(f32[3,30,128]{1,2,0:T(8,128)S(1)} %pad_maximum_fusion), channel_id=1, source_target_pairs={{1,0},{2,1},{3,2},{4,3},{5,4},{6,5},{7,6},{0,7},{9,8},{10,9},{11,1... | collective-permute-start | bytes 138248 | tf_op jit(solution)/shard_map/ppermute | solution.py:16
  47.2 7.7 %collective-permute-start.6 = (f32[3,30,128]{1,2,0:T(8,128)S(1)}, f32[3,30,128]{1,2,0:T(8,128)S(1)}, u32[]{:S(2)}, u32[]{:S(2)}) collective-permute-start(f32[3,30,128]{1,2,0:T(8,128)S(1)} %pad_maximum_fusion.2), channel_id=1, source_target_pairs={{0,8},{8,16},{16,24},{1,9},{9,17},{17,25},{2,10},{10,18},{18,26},{... | collective-permute-start | bytes 138248 | tf_op jit(solution)/shard_map/ppermute | solution.py:22
  51.5 8.6 %collective-permute-start.7 = (f32[3,30,128]{1,2,0:T(8,128)S(1)}, f32[3,30,128]{1,2,0:T(8,128)S(1)}, u32[]{:S(2)}, u32[]{:S(2)}) collective-permute-start(f32[3,30,128]{1,2,0:T(8,128)S(1)} %pad_maximum_fusion.3), channel_id=1, source_target_pairs={{8,0},{16,8},{24,16},{9,1},{17,9},{25,17},{10,2},{18,10},{26,18},{... | collective-permute-start | bytes 138248 | tf_op jit(solution)/shard_map/ppermute | solution.py:22
  78.3 6.4 %collective-permute-start.9 = (f32[3,30,128]{2,1,0:T(8,128)S(1)}, f32[3,30,128]{2,1,0:T(8,128)S(1)}, u32[]{:S(2)}, u32[]{:S(2)}) collective-permute-start(f32[3,30,128]{2,1,0:T(8,128)S(1)} %pad_maximum_fusion.17), channel_id=1, source_target_pairs={{7,0},{0,1},{1,2},{2,3},{3,4},{4,5},{5,6},{6,7},{15,8},{8,9},{9,10... | collective-permute-start | bytes 138248 | tf_op jit(solution)/shard_map/ppermute | solution.py:16
  81.5 4.9 %collective-permute-start.8 = (f32[3,30,128]{2,1,0:T(8,128)S(1)}, f32[3,30,128]{2,1,0:T(8,128)S(1)}, u32[]{:S(2)}, u32[]{:S(2)}) collective-permute-start(f32[3,30,128]{2,1,0:T(8,128)S(1)} %pad_maximum_fusion.16), channel_id=1, source_target_pairs={{1,0},{2,1},{3,2},{4,3},{5,4},{6,5},{7,6},{0,7},{9,8},{10,9},{11,1... | collective-permute-start | bytes 138248 | tf_op jit(solution)/shard_map/ppermute | solution.py:16
  86.4 4.0 %collective-permute-start.10 = (f32[3,30,128]{2,1,0:T(8,128)S(1)}, f32[3,30,128]{2,1,0:T(8,128)S(1)}, u32[]{:S(2)}, u32[]{:S(2)}) collective-permute-start(f32[3,30,128]{2,1,0:T(8,128)S(1)} %pad_maximum_fusion.18), channel_id=1, source_target_pairs={{0,8},{8,16},{16,24},{1,9},{9,17},{17,25},{2,10},{10,18},{18,26},{... | collective-permute-start | bytes 138248 | tf_op jit(solution)/shard_map/ppermute | solution.py:22
  88.8 6.0 %collective-permute-start.11 = (f32[3,30,128]{2,1,0:T(8,128)S(1)}, f32[3,30,128]{2,1,0:T(8,128)S(1)}, u32[]{:S(2)}, u32[]{:S(2)}) collective-permute-start(f32[3,30,128]{2,1,0:T(8,128)S(1)} %pad_maximum_fusion.19), channel_id=1, source_target_pairs={{8,0},{16,8},{24,16},{9,1},{17,9},{25,17},{10,2},{18,10},{26,18},{... | collective-permute-start | bytes 138248 | tf_op jit(solution)/shard_map/ppermute | solution.py:22
  109.3 8.2 %collective-permute-start.13 = (f32[3,30,128]{1,2,0:T(8,128)S(1)}, f32[3,30,128]{1,2,0:T(8,128)S(1)}, u32[]{:S(2)}, u32[]{:S(2)}) collective-permute-start(f32[3,30,128]{1,2,0:T(8,128)S(1)} %pad_maximum_fusion.5), channel_id=1, source_target_pairs={{7,0},{0,1},{1,2},{2,3},{3,4},{4,5},{5,6},{6,7},{15,8},{8,9},{9,10... | collective-permute-start | bytes 138248 | tf_op jit(solution)/shard_map/ppermute | solution.py:16
  111.4 6.3 %collective-permute-start.12 = (f32[3,30,128]{1,2,0:T(8,128)S(1)}, f32[3,30,128]{1,2,0:T(8,128)S(1)}, u32[]{:S(2)}, u32[]{:S(2)}) collective-permute-start(f32[3,30,128]{1,2,0:T(8,128)S(1)} %pad_maximum_fusion.4), channel_id=1, source_target_pairs={{1,0},{2,1},{3,2},{4,3},{5,4},{6,5},{7,6},{0,7},{9,8},{10,9},{11,1... | collective-permute-start | bytes 138248 | tf_op jit(solution)/shard_map/ppermute | solution.py:16
  117.7 6.9 %collective-permute-start.14 = (f32[3,30,128]{1,2,0:T(8,128)S(1)}, f32[3,30,128]{1,2,0:T(8,128)S(1)}, u32[]{:S(2)}, u32[]{:S(2)}) collective-permute-start(f32[3,30,128]{1,2,0:T(8,128)S(1)} %pad_maximum_fusion.6), channel_id=1, source_target_pairs={{0,8},{8,16},{16,24},{1,9},{9,17},{17,25},{2,10},{10,18},{18,26},{... | collective-permute-start | bytes 138248 | tf_op jit(solution)/shard_map/ppermute | solution.py:22
  120.5 9.0 %collective-permute-start.15 = (f32[3,30,128]{1,2,0:T(8,128)S(1)}, f32[3,30,128]{1,2,0:T(8,128)S(1)}, u32[]{:S(2)}, u32[]{:S(2)}) collective-permute-start(f32[3,30,128]{1,2,0:T(8,128)S(1)} %pad_maximum_fusion.7), channel_id=1, source_target_pairs={{8,0},{16,8},{24,16},{9,1},{17,9},{25,17},{10,2},{18,10},{26,18},{... | collective-permute-start | bytes 138248 | tf_op jit(solution)/shard_map/ppermute | solution.py:22
  146.1 5.8 %collective-permute-start.17 = (f32[3,30,128]{2,1,0:T(8,128)S(1)}, f32[3,30,128]{2,1,0:T(8,128)S(1)}, u32[]{:S(2)}, u32[]{:S(2)}) collective-permute-start(f32[3,30,128]{2,1,0:T(8,128)S(1)} %pad_maximum_fusion.21), channel_id=1, source_target_pairs={{7,0},{0,1},{1,2},{2,3},{3,4},{4,5},{5,6},{6,7},{15,8},{8,9},{9,10... | collective-permute-start | bytes 138248 | tf_op jit(solution)/shard_map/ppermute | solution.py:16
  146.6 5.3 %collective-permute-start.16 = (f32[3,30,128]{2,1,0:T(8,128)S(1)}, f32[3,30,128]{2,1,0:T(8,128)S(1)}, u32[]{:S(2)}, u32[]{:S(2)}) collective-permute-start(f32[3,30,128]{2,1,0:T(8,128)S(1)} %pad_maximum_fusion.20), channel_id=1, source_target_pairs={{1,0},{2,1},{3,2},{4,3},{5,4},{6,5},{7,6},{0,7},{9,8},{10,9},{11,1... | collective-permute-start | bytes 138248 | tf_op jit(solution)/shard_map/ppermute | solution.py:16
  152.0 4.0 %collective-permute-start.18 = (f32[3,30,128]{2,1,0:T(8,128)S(1)}, f32[3,30,128]{2,1,0:T(8,128)S(1)}, u32[]{:S(2)}, u32[]{:S(2)}) collective-permute-start(f32[3,30,128]{2,1,0:T(8,128)S(1)} %pad_maximum_fusion.22), channel_id=1, source_target_pairs={{0,8},{8,16},{16,24},{1,9},{9,17},{17,25},{2,10},{10,18},{18,26},{... | collective-permute-start | bytes 138248 | tf_op jit(solution)/shard_map/ppermute | solution.py:22
  154.3 6.0 %collective-permute-start.19 = (f32[3,30,128]{2,1,0:T(8,128)S(1)}, f32[3,30,128]{2,1,0:T(8,128)S(1)}, u32[]{:S(2)}, u32[]{:S(2)}) collective-permute-start(f32[3,30,128]{2,1,0:T(8,128)S(1)} %pad_maximum_fusion.23), channel_id=1, source_target_pairs={{8,0},{16,8},{24,16},{9,1},{17,9},{25,17},{10,2},{18,10},{26,18},{... | collective-permute-start | bytes 138248 | tf_op jit(solution)/shard_map/ppermute | solution.py:22
  174.8 8.2 %collective-permute-start.21 = (f32[3,30,128]{1,2,0:T(8,128)S(1)}, f32[3,30,128]{1,2,0:T(8,128)S(1)}, u32[]{:S(2)}, u32[]{:S(2)}) collective-permute-start(f32[3,30,128]{1,2,0:T(8,128)S(1)} %pad_maximum_fusion.9), channel_id=1, source_target_pairs={{7,0},{0,1},{1,2},{2,3},{3,4},{4,5},{5,6},{6,7},{15,8},{8,9},{9,10... | collective-permute-start | bytes 138248 | tf_op jit(solution)/shard_map/ppermute | solution.py:16
  176.9 6.3 %collective-permute-start.20 = (f32[3,30,128]{1,2,0:T(8,128)S(1)}, f32[3,30,128]{1,2,0:T(8,128)S(1)}, u32[]{:S(2)}, u32[]{:S(2)}) collective-permute-start(f32[3,30,128]{1,2,0:T(8,128)S(1)} %pad_maximum_fusion.8), channel_id=1, source_target_pairs={{1,0},{2,1},{3,2},{4,3},{5,4},{6,5},{7,6},{0,7},{9,8},{10,9},{11,1... | collective-permute-start | bytes 138248 | tf_op jit(solution)/shard_map/ppermute | solution.py:16
  183.2 6.0 %collective-permute-start.22 = (f32[3,30,128]{1,2,0:T(8,128)S(1)}, f32[3,30,128]{1,2,0:T(8,128)S(1)}, u32[]{:S(2)}, u32[]{:S(2)}) collective-permute-start(f32[3,30,128]{1,2,0:T(8,128)S(1)} %pad_maximum_fusion.10), channel_id=1, source_target_pairs={{0,8},{8,16},{16,24},{1,9},{9,17},{17,25},{2,10},{10,18},{18,26},{... | collective-permute-start | bytes 138248 | tf_op jit(solution)/shard_map/ppermute | solution.py:22
  186.0 8.0 %collective-permute-start.23 = (f32[3,30,128]{1,2,0:T(8,128)S(1)}, f32[3,30,128]{1,2,0:T(8,128)S(1)}, u32[]{:S(2)}, u32[]{:S(2)}) collective-permute-start(f32[3,30,128]{1,2,0:T(8,128)S(1)} %pad_maximum_fusion.11), channel_id=1, source_target_pairs={{8,0},{16,8},{24,16},{9,1},{17,9},{25,17},{10,2},{18,10},{26,18},{... | collective-permute-start | bytes 138248 | tf_op jit(solution)/shard_map/ppermute | solution.py:22
  (181 other events, 224.8 us)
where the time goes:
time: 206 us; the launch traced here: 205 us
  local copies, waits for them, and re-layouts  92.4 us (45%)
  starting transfers between devices  47.8 us (23%)
  waiting for transfers between devices  46.5 us (23%)
  other arithmetic  13.8 us (7%)
  between operations  4.19 us (2%)
    gather x72, local copies, waits for them, and re-layouts, extend(): jnp.take(source, send_list[member], axis=1)  36.5 us
    ppermute x12, waiting for transfers between devices, passed_along(): lax.ppermute(value, axis, [(source, source + steps) for source in range(f...  35.4 us
    ppermute x12, starting transfers between devices, passed_along(): lax.ppermute(value, axis, [(source, source + steps) for source in range(f...  26.3 us
    ppermute x12, starting transfers between devices, from_behind(): return lax.ppermute(block, axis, route)  21.5 us
    unnamed x459, local copies, waits for them, and re-layouts  19.8 us
    ppermute x12, waiting for transfers between devices, from_behind(): return lax.ppermute(block, axis, route)  11.1 us
    gather x3, local copies, waits for them, and re-layouts, edge_update(): jnp.take(extended, edge_cells[1], axis=1)  8.64 us
    gather x3, local copies, waits for them, and re-layouts, edge_update(): jnp.take(extended, edge_cells[0], axis=1)  8.64 us
  transfers between devices with their start and end apart: 24, of which 20 were waited for; matrix products, arithmetic and copies ran while one was open for 7% of the time, Pallas kernels for 0%

commit v1 on v0

v1 whole, which is shorter than its diff:
```python
import functools

import jax
import jax.numpy as jnp
from jax import lax
from jax.experimental import pallas as pl
from jax.experimental.pallas import tpu as pltpu
from jax.sharding import PartitionSpec as P

NSUB = 3
STEP_SCALE = 0.5
LANES = 128
PARTS = 3

f32 = jnp.float32
bf16 = jnp.bfloat16


def round_up(value, step):
    return -(-value // step) * step


def swap_routes(count):
    inner = [(i, i ^ 1) for i in range(count)]
    outer = [(i, (((i + 1) ^ 1) - 1) % count) for i in range(count)]
    return inner, outer


LOCAL = ((0, 1), (0, 2), (1, 1), (1, 2), (1, 0), (2, 1), (2, 2), (2, 0))
SENT = ((0, 1), (1, 1), (2, 1), (0, 2), (1, 2), (2, 2), (1, 0), (2, 0))


def link_signs(a, b):
    lat_inner = 1 - 2 * lax.rem(a, 2)
    lon_inner = 1 - 2 * lax.rem(b, 2)
    return lat_inner, lon_inner


def sent_row(member, lat_inner, lon_inner):
    lat_link, lon_link = member
    p = (0, lat_inner, -lat_inner)[lat_link]
    q = (0, lon_inner, -lon_inner)[lon_link]
    flat = (p + 1) * 3 + (q + 1)
    return flat - jnp.where(flat > 4, 1, 0)


def local_positions(index, own, own_padded, halo, a, b, lat_count):
    lat_inner, lon_inner = link_signs(a, b)
    beyond = index - own
    piece = lax.div(jnp.maximum(beyond, 0), halo)
    slot = beyond - piece * halo
    flat = piece + jnp.where(piece >= 4, 1, 0)
    p = jnp.where(flat >= 6, 1, jnp.where(flat >= 3, 0, -1))
    q = flat - 3 * (p + 1) - 1
    lat_is_inner = p == lat_inner
    lon_member = jnp.where(q == 0, 2, jnp.where(q == lon_inner, 0, 1))
    member = jnp.where(p == 0, lon_member, jnp.where(lat_is_inner, 2, 5) + lon_member)
    outside = (a + p < 0) | (a + p >= lat_count)
    row = own_padded + member * halo + slot
    return jnp.where(beyond < 0, index, jnp.where(outside, -1, row))


def split_parts(value):
    parts = []
    rest = value
    for part in range(PARTS):
        piece = rest.astype(bf16)
        parts.append(piece)
        if part < PARTS - 1:
            rest = rest - piece.astype(f32)
    return parts


def put_parts(stack_ref, value, start):
    rows, width = value.shape
    for part, piece in enumerate(split_parts(value)):
        stack_ref[part * rows : (part + 1) * rows, start : start + width] = piece


def sum_parts(product, rows):
    total = product[(PARTS - 1) * rows : PARTS * rows]
    for part in range(PARTS - 2, -1, -1):
        total = total + product[part * rows : (part + 1) * rows]
    return total


def matmul(left, right):
    return jnp.dot(left, right, preferred_element_type=f32)


def fill_sent(matrix_ref, list_ref, lat_inner, lon_inner):
    rows = matrix_ref.shape[0]
    halo = list_ref.shape[1]
    lanes = [list_ref[pl.ds(sent_row(member, lat_inner, lon_inner), 1), :] for member in SENT]
    block = 16

    def body(step, carry):
        first = pl.multiple_of(step * block, block)
        row = lax.broadcasted_iota(jnp.int32, (block, halo), 0) + first
        for member, index in enumerate(lanes):
            hit = jnp.where(row == index, 1.0, 0.0).astype(bf16)
            matrix_ref[pl.ds(first, block), member * halo : (member + 1) * halo] = hit
        return carry

    lax.fori_loop(0, rows // block, body, 0)


def store_sent(product, rows, halo, inner_ref, outer_ref, lat_inner_ref, lat_outer_ref):
    pieces = sum_parts(product, rows)
    for member in range(3):
        inner_ref[member] = pieces[:, member * halo : (member + 1) * halo]
        outer_ref[member] = pieces[:, (3 + member) * halo : (4 + member) * halo]
    lat_inner_ref[...] = pieces[:, 6 * halo : 7 * halo]
    lat_outer_ref[...] = pieces[:, 7 * halo : 8 * halo]


def put_extended(stack_ref, own, inner_ref, outer_ref, lat_inner_ref, lat_outer_ref):
    halo = inner_ref.shape[2]
    start = own.shape[1]
    put_parts(stack_ref, own, 0)
    pieces = [inner_ref[0], outer_ref[0]]
    pieces += [lat_inner_ref[i] for i in range(3)] + [lat_outer_ref[i] for i in range(3)]
    for member, piece in enumerate(pieces):
        put_parts(stack_ref, piece, start + member * halo)


def start_kernel(pressure_ref, list_ref, cells_ref, inner_ref, outer_ref, lat_inner_ref, lat_outer_ref, matrix_ref, stack_ref):
    a, b = lax.axis_index("lat"), lax.axis_index("lon")
    lat_inner, lon_inner = link_signs(a, b)
    levels = pressure_ref.shape[0]
    rows = cells_ref.shape[0]
    cells_ref[0:levels, :] = pressure_ref[:, 0, :]
    cells_ref[levels:rows, :] = jnp.zeros((rows - levels, cells_ref.shape[1]), f32)
    fill_sent(matrix_ref, list_ref, lat_inner, lon_inner)
    put_parts(stack_ref, cells_ref[...], 0)
    product = matmul(stack_ref[...], matrix_ref[...])
    store_sent(product, rows, list_ref.shape[1], inner_ref, outer_ref, lat_inner_ref, lat_outer_ref)


def build_kernel(
    velocity_ref,
    edge_cells_ref,
    cell_edges_ref,
    send_edges_ref,
    weight_ref,
    coupling_ref,
    edges_ref,
    gradient_ref,
    high_ref,
    low_ref,
    matrix_ref,
    inverse_ref,
    forward_ref,
    back_ref,
    coupling_scr,
    *,
    lat_count,
):
    a, b = lax.axis_index("lat"), lax.axis_index("lon")
    lat_inner, lon_inner = link_signs(a, b)
    levels = velocity_ref.shape[0]
    rows, edge_pad = edges_ref.shape
    edges = velocity_ref.shape[2]
    cells = cell_edges_ref.shape[1]
    halo = send_edges_ref.shape[1]

    edges_ref[...] = jnp.zeros((rows, edge_pad), f32)
    edges_ref[0:levels, 0:edges] = velocity_ref[:, 0, :]
    fill_sent(matrix_ref, send_edges_ref, lat_inner, lon_inner)

    ends = local_positions(edge_cells_ref[...], cells, cells, halo, a, b, lat_count)
    if edge_pad > edges:
        ends = jnp.concatenate([ends, jnp.full((2, edge_pad - edges), -1, jnp.int32)], axis=1)
    near = ends[0:1, :]
    far = ends[1:2, :]
    block = 16

    def gradient_body(step, carry):
        first = pl.multiple_of(step * block, block)
        row = lax.broadcasted_iota(jnp.int32, (block, edge_pad), 0) + first
        entry = jnp.where(row == far, 1.0, 0.0) - jnp.where(row == near, 1.0, 0.0)
        gradient_ref[pl.ds(first, block), :] = entry.astype(bf16)
        return carry

    lax.fori_loop(0, gradient_ref.shape[0] // block, gradient_body, 0)

    sides = local_positions(cell_edges_ref[...], edges, edge_pad, halo, a, b, lat_count)
    weight = weight_ref[...]

    def weight_body(step, carry):
        first = pl.multiple_of(step * block, block)
        row = lax.broadcasted_iota(jnp.int32, (block, cells), 0) + first
        entry = jnp.where(row == sides[0:1, :], weight[0:1, :], 0.0)
        entry = entry + jnp.where(row == sides[1:2, :], weight[1:2, :], 0.0)
        entry = entry + jnp.where(row == sides[2:3, :], weight[2:3, :], 0.0)
        high = entry.astype(bf16)
        high_ref[pl.ds(first, block), :] = high
        low_ref[pl.ds(first, block), :] = (entry - high.astype(f32)).astype(bf16)
        return carry

    lax.fori_loop(0, high_ref.shape[0] // block, weight_body, 0)

    for group in range(cells // LANES):
        coupling_scr[0:levels, group, :] = coupling_ref[:, 0, group * LANES : (group + 1) * LANES]
    above = coupling_scr[0]
    divisor = 1.0 + above
    inverse = 1.0 / divisor
    inverse_ref[0] = inverse
    ratio = above * inverse
    back_ref[0] = ratio
    for level in range(1, levels):
        below = above
        above = coupling_scr[level]
        divisor = 1.0 + below + above - below * ratio
        inverse = 1.0 / divisor
        inverse_ref[level] = inverse
        forward_ref[level] = below * inverse
        ratio = above * inverse
        back_ref[level] = ratio


def edge_kernel(
    cells_ref,
    inner_in,
    outer_in,
    lat_inner_in,
    lat_outer_in,
    edges_ref,
    dual_ref,
    gradient_ref,
    matrix_ref,
    new_edges_ref,
    inner_ref,
    outer_ref,
    lat_inner_ref,
    lat_outer_ref,
    stack_ref,
    own_stack_ref,
):
    rows = cells_ref.shape[0]
    edges = dual_ref.shape[1]
    edge_pad = edges_ref.shape[1]
    put_extended(stack_ref, cells_ref[...], inner_in, outer_in, lat_inner_in, lat_outer_in)
    difference = sum_parts(matmul(stack_ref[...], gradient_ref[...]), rows)
    scale = STEP_SCALE * dual_ref[...]
    if edge_pad > edges:
        scale = jnp.concatenate([scale, jnp.zeros((1, edge_pad - edges), f32)], axis=1)
    new_edges = edges_ref[...] - scale * difference
    new_edges_ref[...] = new_edges
    put_parts(own_stack_ref, new_edges, 0)
    product = matmul(own_stack_ref[...], matrix_ref[...])
    store_sent(product, rows, inner_in.shape[2], inner_ref, outer_ref, lat_inner_ref, lat_outer_ref)


def solve_columns(edges_ref, pieces, cells_ref, speed_ref, high_ref, low_ref, inverse_ref, forward_ref, back_ref, levels, stack_ref, column_scr):
    rows, cells = cells_ref.shape
    put_extended(stack_ref, edges_ref[...], *pieces)
    stack = stack_ref[...]
    divergence = sum_parts(matmul(stack, high_ref[...]) + matmul(stack, low_ref[...]), rows)
    right_side = cells_ref[...] - speed_ref[...] * divergence
    for group in range(cells // LANES):
        column_scr[:, group, :] = right_side[:, group * LANES : (group + 1) * LANES]
    current = column_scr[0] * inverse_ref[0]
    scaled = [current]
    for level in range(1, levels):
        current = column_scr[level] * inverse_ref[level] + forward_ref[level] * current
        scaled.append(current)
    column_scr[levels - 1] = current
    for level in range(levels - 2, -1, -1):
        current = scaled[level] + back_ref[level] * current
        column_scr[level] = current
    for level in range(levels, rows):
        column_scr[level] = jnp.zeros_like(current)


def cell_kernel(
    edges_ref,
    inner_in,
    outer_in,
    lat_inner_in,
    lat_outer_in,
    cells_ref,
    speed_ref,
    high_ref,
    low_ref,
    inverse_ref,
    forward_ref,
    back_ref,
    matrix_ref,
    new_cells_ref,
    inner_ref,
    outer_ref,
    lat_inner_ref,
    lat_outer_ref,
    stack_ref,
    own_stack_ref,
    column_scr,
    *,
    levels,
):
    rows, cells = cells_ref.shape
    pieces = (inner_in, outer_in, lat_inner_in, lat_outer_in)
    solve_columns(edges_ref, pieces, cells_ref, speed_ref, high_ref, low_ref, inverse_ref, forward_ref, back_ref, levels, stack_ref, column_scr)
    for group in range(cells // LANES):
        part = column_scr[:, group, :]
        new_cells_ref[:, group * LANES : (group + 1) * LANES] = part
        put_parts(own_stack_ref, part, group * LANES)
    product = matmul(own_stack_ref[...], matrix_ref[...])
    store_sent(product, rows, inner_in.shape[2], inner_ref, outer_ref, lat_inner_ref, lat_outer_ref)


def last_kernel(
    edges_ref,
    inner_in,
    outer_in,
    lat_inner_in,
    lat_outer_in,
    cells_ref,
    speed_ref,
    high_ref,
    low_ref,
    inverse_ref,
    forward_ref,
    back_ref,
    out_ref,
    stack_ref,
    column_scr,
    *,
    levels,
):
    cells = cells_ref.shape[1]
    pieces = (inner_in, outer_in, lat_inner_in, lat_outer_in)
    solve_columns(edges_ref, pieces, cells_ref, speed_ref, high_ref, low_ref, inverse_ref, forward_ref, back_ref, levels, stack_ref, column_scr)
    for group in range(cells // LANES):
        out_ref[:, 0, group * LANES : (group + 1) * LANES] = column_scr[0:levels, group, :]


def call(body, name, outs, scratch, limit_mib, *operands):
    return pl.pallas_call(
        body,
        out_shape=tuple(jax.ShapeDtypeStruct(shape, kind) for shape, kind in outs),
        scratch_shapes=[pltpu.VMEM(shape, kind) for shape, kind in scratch],
        compiler_params=pltpu.CompilerParams(vmem_limit_bytes=limit_mib * 1024 * 1024),
        name=name,
    )(*operands)


def on_device(lat_count, lon_count, pressure, velocity, edge_cells, cell_edges, send_cells, send_edges, inv_dual, edge_weight, sound_speed, coupling):
    _, levels, cells = pressure.shape
    edges = velocity.shape[2]
    halo = send_cells.shape[2]
    rows = round_up(levels, 16)
    edge_pad = round_up(edges, 2 * LANES)
    sent = [((3, rows, halo), f32)] * 2 + [((rows, halo), f32)] * 2
    lon_routes = swap_routes(lon_count)
    lat_routes = swap_routes(lat_count)

    def exchange(pieces):
        inner, outer, lat_inner, lat_outer = pieces
        outer_in = lax.ppermute(outer, "lon", lon_routes[1])
        inner_in = lax.ppermute(inner, "lon", lon_routes[0])
        first = jnp.stack([inner_in[1], outer_in[1], lat_inner])
        second = jnp.stack([inner_in[2], outer_in[2], lat_outer])
        second_in = lax.ppermute(second, "lat", lat_routes[1])
        first_in = lax.ppermute(first, "lat", lat_routes[0])
        return inner_in, outer_in, first_in, second_in

    by_level = lambda value: value.transpose(1, 0, 2)
    stack_cells = ((PARTS * rows, cells), bf16)
    stack_edges = ((PARTS * rows, edge_pad), bf16)
    column = ((rows, cells // LANES, LANES), f32)

    values, *pieces, cell_matrix = call(
        start_kernel,
        "start",
        [((rows, cells), f32)] + sent + [((cells, 8 * halo), bf16)],
        [stack_cells],
        16,
        by_level(pressure),
        send_cells[0],
    )
    normal, gradient, high, low, edge_matrix, inverse, forward, back = call(
        functools.partial(build_kernel, lat_count=lat_count),
        "build",
        [
            ((rows, edge_pad), f32),
            ((cells + 8 * halo, edge_pad), bf16),
            ((edge_pad + 8 * halo, cells), bf16),
            ((edge_pad + 8 * halo, cells), bf16),
            ((edge_pad, 8 * halo), bf16),
            column,
            column,
            column,
        ],
        [column],
        24,
        by_level(velocity),
        edge_cells[0],
        cell_edges[0],
        send_edges[0],
        edge_weight[0],
        by_level(coupling),
    )
    for substep in range(NSUB):
        arrived = exchange(pieces)
        normal, *pieces = call(
            edge_kernel,
            "edges",
            [((rows, edge_pad), f32)] + sent,
            [((PARTS * rows, cells + 8 * halo), bf16), stack_edges],
            24,
            values,
            *arrived,
            normal,
            inv_dual,
            gradient,
            edge_matrix,
        )
        arrived = exchange(pieces)
        operands = (normal, *arrived, values, sound_speed, high, low, inverse, forward, back)
        stack = ((PARTS * rows, edge_pad + 8 * halo), bf16)
        if substep < NSUB - 1:
            values, *pieces = call(
                functools.partial(cell_kernel, levels=levels),
                "cells",
                [((rows, cells), f32)] + sent,
                [stack, stack_cells, column],
                24,
                *operands,
                cell_matrix,
            )
        else:
            (values,) = call(
                functools.partial(last_kernel, levels=levels),
                "last",
                [((levels, 1, cells), f32)],
                [stack, column],
                24,
                *operands,
            )
    return by_level(values), normal[:levels, :edges][None]


def solution(mesh):
    return jax.shard_map(
        functools.partial(on_device, mesh.shape["lat"], mesh.shape["lon"]),
        mesh=mesh,
        in_specs=(
            P("lat", None, "lon"),
            P("lat", None, "lon"),
            P("lat", None, "lon"),
            P("lat", None, "lon"),
            P("lat", None, "lon"),
            P("lat", None, "lon"),
            P("lat", "lon"),
            P("lat", None, "lon"),
            P("lat", "lon"),
            P("lat", None, "lon"),
        ),
        out_specs=(P("lat", None, "lon"), P("lat", None, "lon")),
        check_vma=False,
    )
```

time: 206 us -> 92.2 us (0.45)
  local copies, waits for them, and re-layouts: 92.4 us -> 7.64 us
  starting transfers between devices: 47.8 us -> 22.7 us
  Pallas kernels: 0 us -> 15.8 us
  other arithmetic: 13.8 us -> 0.06 us
  between operations: 4.19 us -> 0.82 us
    gather x96 -> x0, local copies, waits for them, and re-layouts: 70.1 us -> none  [the longest x72 36.5 us: extend(): jnp.take(source, send_list[member], axis=1)]
    ppermute x24, starting transfers between devices: 47.8 us -> 22.7 us  [the longest x6 8.88 us: exchange(): outer_in = lax.ppermute(outer, 'lon', lon_routes[1])]
    pallas_call x0 -> x8, Pallas kernels: none -> 15.8 us  [call(): pl.pallas_call(body, out_shape=tuple((jax.ShapeDtypeStruct(shape, kind) f...]
    unnamed x459 -> x19, local copies, waits for them, and re-layouts: 19.8 us -> 7.59 us
    sub x6 -> x0, other arithmetic: 3.21 us -> none  [the longest x3 2.42 us: column_solve(): result.insert(0, scaled[level_index] - ratios[level_index] * result[0])]
    unnamed x4 -> x0, other arithmetic: 3.21 us -> none
    div x3 -> x0, other arithmetic: 3.01 us -> none  [column_solve(): current = (right_side[level_index] - lower_term * scaled[-1]) / divisor]
    another operation x70 -> x12, other arithmetic: 2.44 us -> 0.06 us  [the longest x6 0.04 us: exchange(): first = jnp.stack([inner_in[1], outer_in[1], lat_inner])]
  transfers between devices with their start and end apart: 24 -> 24, of which waited for: 20 -> 20; matrix products, arithmetic and copies ran while one was open for 7% -> 2% of each run, Pallas kernels for 0% -> 7%
where the time goes in v1:
time: 92.2 us; the launch traced here: 91.8 us
  waiting for transfers between devices  44.8 us (49%)
  starting transfers between devices  22.7 us (25%)
  Pallas kernels  15.8 us (17%)
  local copies, waits for them, and re-layouts  7.64 us (8%)
    ppermute x6, waiting for transfers between devices, exchange(): outer_in = lax.ppermute(outer, 'lon', lon_routes[1])  21.3 us
    pallas_call x8, Pallas kernels, call(): pl.pallas_call(body, out_shape=tuple((jax.ShapeDtypeStruct(shape, kind) f...  15.8 us
    ppermute x6, waiting for transfers between devices, exchange(): second_in = lax.ppermute(second, 'lat', lat_routes[1])  10.1 us
    ppermute x6, waiting for transfers between devices, exchange(): first_in = lax.ppermute(first, 'lat', lat_routes[0])  9.69 us
    ppermute x6, starting transfers between devices, exchange(): outer_in = lax.ppermute(outer, 'lon', lon_routes[1])  8.88 us
    unnamed x19, local copies, waits for them, and re-layouts  7.59 us
    ppermute x6, starting transfers between devices, exchange(): first_in = lax.ppermute(first, 'lat', lat_routes[0])  7.43 us
    ppermute x6, starting transfers between devices, exchange(): second_in = lax.ppermute(second, 'lat', lat_routes[1])  5.9 us
  transfers between devices with their start and end apart: 24, of which 20 were waited for; matrix products, arithmetic and copies ran while one was open for 2% of the time, Pallas kernels for 7%

profile of v1, /device:TPU:0, one launch (start us, length us, event | category | flops | bytes accessed | tf_op | source)
XLA Modules:
  0.0 91.8 jit_solution(11241696415933627186)
XLA Ops:
  0.6 0.9 copy-done.2
  1.5 0.7 copy-done.7
  2.2 0.8 start.1
  3.5 4.7 %collective-permute-start.1 = (f32[3,32,128]{2,1,0:T(8,128)S(1)}, f32[3,32,128]{2,1,0:T(8,128)S(1)}, u32[]{:S(2)}, u32[]{:S(2)}) collective-permute-start(f32[3,32,128]{2,1,0:T(8,128)S(1)} %get-tuple-element.43), channel_id=1, source_target_pairs={{0,7},{1,2},{2,1},{3,4},{4,3},{5,6},{6,5},{7,0},{8,15},{9,10},{10,... | collective-permute-start | bytes 147464 | tf_op jit(solution)/shard_map/ppermute | solution.py:360
  8.2 1.9 %collective-permute-done.1.outer_in = f32[3,32,128]{2,1,0:T(8,128)S(1)} collective-permute-done((f32[3,32,128]{2,1,0:T(8,128)S(1)}, f32[3,32,128]{2,1,0:T(8,128)S(1)}, u32[]{:S(2)}, u32[]{:S(2)}) %collective-permute-start.1) | collective-permute-done | bytes 49184 | tf_op jit(solution)/shard_map/ppermute | solution.py:360
  10.1 1.6 %collective-permute-start.2 = (f32[3,32,128]{2,1,0:T(8,128)S(1)}, f32[3,32,128]{2,1,0:T(8,128)S(1)}, u32[]{:S(2)}, u32[]{:S(2)}) collective-permute-start(f32[3,32,128]{2,1,0:T(8,128)S(1)} %pad_maximum_fusion), channel_id=1, source_target_pairs={{0,8},{8,0},{16,24},{24,16},{1,9},{9,1},{17,25},{25,17},{2,10},{10... | collective-permute-start | bytes 147464 | tf_op jit(solution)/shard_map/ppermute | solution.py:365
  11.7 1.5 %collective-permute-start.3 = (f32[3,32,128]{2,1,0:T(8,128)S(1)}, f32[3,32,128]{2,1,0:T(8,128)S(1)}, u32[]{:S(2)}, u32[]{:S(2)}) collective-permute-start(f32[3,32,128]{2,1,0:T(8,128)S(1)} %pad_maximum_fusion.1), channel_id=1, source_target_pairs={{0,24},{8,16},{16,8},{24,0},{1,25},{9,17},{17,9},{25,1},{2,26},{10... | collective-permute-start | bytes 147464 | tf_op jit(solution)/shard_map/ppermute | solution.py:364
  13.1 0.7 copy.18
  13.8 0.7 copy.17
  14.5 0.9 copy-done
  15.5 0.9 copy-done.1
  16.3 0.7 copy-done.5
  17.0 0.7 copy-done.6
  17.7 6.3 %build.1 = (f32[32,1024]{1,0:T(8,128)S(1)}, bf16[1664,1024]{1,0:T(8,128)(2,1)S(1)}, bf16[2048,640]{1,0:T(8,128)(2,1)S(1)}, bf16[2048,640]{1,0:T(8,128)(2,1)S(1)}...) custom-call(f32[30,1,960]{2,1,0:T(1,128)S(1)} %bitcast.27, ...), custom_call_target="tpu_custom_call" | custom-call | tf_op jit(solution)/shard_map/build/pallas_call | solution.py:339
  24.1 0.7 copy-done.3
  24.8 1.1 %edges.3 = (f32[32,1024]{1,0:T(8,128)S(1)}, f32[3,32,128]{2,1,0:T(8,128)S(1)}, f32[3,32,128]{2,1,0:T(8,128)S(1)}, f32[32,128]{1,0:T(8,128)S(1)}, f32[32,128]{1,0:T(8,128)S(1)}) custom-call(f32[32,640]{1,0:T(8,128)S(1)} %get-tuple-element.41.cells_ref, f32[3,32,128]{2,1,0:T(8,128)S(1)} %collective-permute-done.inner_in, ...), custom_call_target="tpu_custom_call" | custom-call | tf_op jit(solution)/shard_map/edges/pallas_call | solution.py:339
  25.8 2.9 %collective-permute-start.5 = (f32[3,32,128]{2,1,0:T(8,128)S(1)}, f32[3,32,128]{2,1,0:T(8,128)S(1)}, u32[]{:S(2)}, u32[]{:S(2)}) collective-permute-start(f32[3,32,128]{2,1,0:T(8,128)S(1)} %get-tuple-element.51), channel_id=1, source_target_pairs={{0,7},{1,2},{2,1},{3,4},{4,3},{5,6},{6,5},{7,0},{8,15},{9,10},{10,... | collective-permute-start | bytes 147464 | tf_op jit(solution)/shard_map/ppermute | solution.py:360
  28.8 2.9 %collective-permute-done.5.outer_in = f32[3,32,128]{2,1,0:T(8,128)S(1)} collective-permute-done((f32[3,32,128]{2,1,0:T(8,128)S(1)}, f32[3,32,128]{2,1,0:T(8,128)S(1)}, u32[]{:S(2)}, u32[]{:S(2)}) %collective-permute-start.5) | collective-permute-done | bytes 49184 | tf_op jit(solution)/shard_map/ppermute | solution.py:360
  31.7 1.6 %collective-permute-start.6 = (f32[3,32,128]{2,1,0:T(8,128)S(1)}, f32[3,32,128]{2,1,0:T(8,128)S(1)}, u32[]{:S(2)}, u32[]{:S(2)}) collective-permute-start(f32[3,32,128]{2,1,0:T(8,128)S(1)} %pad_maximum_fusion.2), channel_id=1, source_target_pairs={{0,8},{8,0},{16,24},{24,16},{1,9},{9,1},{17,25},{25,17},{2,10},{10... | collective-permute-start | bytes 147464 | tf_op jit(solution)/shard_map/ppermute | solution.py:365
  33.8 2.1 %collective-permute-done.6.lat_inner_in = f32[3,32,128]{2,1,0:T(8,128)S(1)} collective-permute-done((f32[3,32,128]{2,1,0:T(8,128)S(1)}, f32[3,32,128]{2,1,0:T(8,128)S(1)}, u32[]{:S(2)}, u32[]{:S(2)}) %collective-permute-start.6) | collective-permute-done | bytes 49184 | tf_op jit(solution)/shard_map/ppermute | solution.py:365
  35.9 2.4 %collective-permute-done.7.lat_outer_in = f32[3,32,128]{2,1,0:T(8,128)S(1)} collective-permute-done((f32[3,32,128]{2,1,0:T(8,128)S(1)}, f32[3,32,128]{2,1,0:T(8,128)S(1)}, u32[]{:S(2)}, u32[]{:S(2)}) %collective-permute-start.7) | collective-permute-done | bytes 49184 | tf_op jit(solution)/shard_map/ppermute | solution.py:364
  38.3 1.8 %cells.2 = (f32[32,640]{1,0:T(8,128)S(1)}, f32[3,32,128]{2,1,0:T(8,128)S(1)}, f32[3,32,128]{2,1,0:T(8,128)S(1)}, f32[32,128]{1,0:T(8,128)S(1)}, f32[32,128]{1,0:T(8,128)S(1)}) custom-call(f32[32,1024]{1,0:T(8,128)S(1)} %get-tuple-element.49.edges_ref, f32[3,32,128]{2,1,0:T(8,128)S(1)} %collective-permute-done.4.inner_in, ...), custom_call_target="tpu_custom_call" | custom-call | tf_op jit(solution)/shard_map/cells/pallas_call | solution.py:339
  40.1 1.0 %collective-permute-start.9 = (f32[3,32,128]{2,1,0:T(8,128)S(1)}, f32[3,32,128]{2,1,0:T(8,128)S(1)}, u32[]{:S(2)}, u32[]{:S(2)}) collective-permute-start(f32[3,32,128]{2,1,0:T(8,128)S(1)} %get-tuple-element.62), channel_id=1, source_target_pairs={{0,7},{1,2},{2,1},{3,4},{4,3},{5,6},{6,5},{7,0},{8,15},{9,10},{10,... | collective-permute-start | bytes 147464 | tf_op jit(solution)/shard_map/ppermute | solution.py:360
  41.4 4.1 %collective-permute-done.9.outer_in = f32[3,32,128]{2,1,0:T(8,128)S(1)} collective-permute-done((f32[3,32,128]{2,1,0:T(8,128)S(1)}, f32[3,32,128]{2,1,0:T(8,128)S(1)}, u32[]{:S(2)}, u32[]{:S(2)}) %collective-permute-start.9) | collective-permute-done | bytes 49184 | tf_op jit(solution)/shard_map/ppermute | solution.py:360
  45.5 0.6 collective-permute-start.10
  46.1 1.4 %collective-permute-start.11 = (f32[3,32,128]{2,1,0:T(8,128)S(1)}, f32[3,32,128]{2,1,0:T(8,128)S(1)}, u32[]{:S(2)}, u32[]{:S(2)}) collective-permute-start(f32[3,32,128]{2,1,0:T(8,128)S(1)} %pad_maximum_fusion.5), channel_id=1, source_target_pairs={{0,24},{8,16},{16,8},{24,0},{1,25},{9,17},{17,9},{25,1},{2,26},{10... | collective-permute-start | bytes 147464 | tf_op jit(solution)/shard_map/ppermute | solution.py:364
  47.5 2.1 %collective-permute-done.10.lat_inner_in = f32[3,32,128]{2,1,0:T(8,128)S(1)} collective-permute-done((f32[3,32,128]{2,1,0:T(8,128)S(1)}, f32[3,32,128]{2,1,0:T(8,128)S(1)}, u32[]{:S(2)}, u32[]{:S(2)}) %collective-permute-start.10) | collective-permute-done | bytes 49184 | tf_op jit(solution)/shard_map/ppermute | solution.py:365
  49.7 1.4 %collective-permute-done.11.lat_outer_in = f32[3,32,128]{2,1,0:T(8,128)S(1)} collective-permute-done((f32[3,32,128]{2,1,0:T(8,128)S(1)}, f32[3,32,128]{2,1,0:T(8,128)S(1)}, u32[]{:S(2)}, u32[]{:S(2)}) %collective-permute-start.11) | collective-permute-done | bytes 49184 | tf_op jit(solution)/shard_map/ppermute | solution.py:364
  51.1 1.0 %edges.4 = (f32[32,1024]{1,0:T(8,128)S(1)}, f32[3,32,128]{2,1,0:T(8,128)S(1)}, f32[3,32,128]{2,1,0:T(8,128)S(1)}, f32[32,128]{1,0:T(8,128)S(1)}, f32[32,128]{1,0:T(8,128)S(1)}) custom-call(f32[32,640]{1,0:T(8,128)S(1)} %get-tuple-element.60.cells_ref, f32[3,32,128]{2,1,0:T(8,128)S(1)} %collective-permute-done.8.inner_in, ...), custom_call_target="tpu_custom_call" | custom-call | tf_op jit(solution)/shard_map/edges/pallas_call | solution.py:339
  52.2 1.2 %collective-permute-done.12.inner_in = f32[3,32,128]{2,1,0:T(8,128)S(1)} collective-permute-done((f32[3,32,128]{2,1,0:T(8,128)S(1)}, f32[3,32,128]{2,1,0:T(8,128)S(1)}, u32[]{:S(2)}, u32[]{:S(2)}) %collective-permute-start.12) | collective-permute-done | bytes 49184 | tf_op jit(solution)/shard_map/ppermute | solution.py:361
  53.4 4.1 %collective-permute-done.13.outer_in = f32[3,32,128]{2,1,0:T(8,128)S(1)} collective-permute-done((f32[3,32,128]{2,1,0:T(8,128)S(1)}, f32[3,32,128]{2,1,0:T(8,128)S(1)}, u32[]{:S(2)}, u32[]{:S(2)}) %collective-permute-start.13) | collective-permute-done | bytes 49184 | tf_op jit(solution)/shard_map/ppermute | solution.py:360
  57.6 1.6 %collective-permute-start.14 = (f32[3,32,128]{2,1,0:T(8,128)S(1)}, f32[3,32,128]{2,1,0:T(8,128)S(1)}, u32[]{:S(2)}, u32[]{:S(2)}) collective-permute-start(f32[3,32,128]{2,1,0:T(8,128)S(1)} %pad_maximum_fusion.6), channel_id=1, source_target_pairs={{0,8},{8,0},{16,24},{24,16},{1,9},{9,1},{17,25},{25,17},{2,10},{10... | collective-permute-start | bytes 147464 | tf_op jit(solution)/shard_map/ppermute | solution.py:365
  59.6 2.1 %collective-permute-done.14.lat_inner_in = f32[3,32,128]{2,1,0:T(8,128)S(1)} collective-permute-done((f32[3,32,128]{2,1,0:T(8,128)S(1)}, f32[3,32,128]{2,1,0:T(8,128)S(1)}, u32[]{:S(2)}, u32[]{:S(2)}) %collective-permute-start.14) | collective-permute-done | bytes 49184 | tf_op jit(solution)/shard_map/ppermute | solution.py:365
  61.7 2.4 %collective-permute-done.15.lat_outer_in = f32[3,32,128]{2,1,0:T(8,128)S(1)} collective-permute-done((f32[3,32,128]{2,1,0:T(8,128)S(1)}, f32[3,32,128]{2,1,0:T(8,128)S(1)}, u32[]{:S(2)}, u32[]{:S(2)}) %collective-permute-start.15) | collective-permute-done | bytes 49184 | tf_op jit(solution)/shard_map/ppermute | solution.py:364
  64.1 1.8 %cells.3 = (f32[32,640]{1,0:T(8,128)S(1)}, f32[3,32,128]{2,1,0:T(8,128)S(1)}, f32[3,32,128]{2,1,0:T(8,128)S(1)}, f32[32,128]{1,0:T(8,128)S(1)}, f32[32,128]{1,0:T(8,128)S(1)}) custom-call(f32[32,1024]{1,0:T(8,128)S(1)} %get-tuple-element.65.edges_ref, f32[3,32,128]{2,1,0:T(8,128)S(1)} %collective-permute-done.12.inner_in, ...), custom_call_target="tpu_custom_call" | custom-call | tf_op jit(solution)/shard_map/cells/pallas_call | solution.py:339
  66.0 1.2 %collective-permute-done.16.inner_in = f32[3,32,128]{2,1,0:T(8,128)S(1)} collective-permute-done((f32[3,32,128]{2,1,0:T(8,128)S(1)}, f32[3,32,128]{2,1,0:T(8,128)S(1)}, u32[]{:S(2)}, u32[]{:S(2)}) %collective-permute-start.16) | collective-permute-done | bytes 49184 | tf_op jit(solution)/shard_map/ppermute | solution.py:361
  67.2 4.1 %collective-permute-done.17.outer_in = f32[3,32,128]{2,1,0:T(8,128)S(1)} collective-permute-done((f32[3,32,128]{2,1,0:T(8,128)S(1)}, f32[3,32,128]{2,1,0:T(8,128)S(1)}, u32[]{:S(2)}, u32[]{:S(2)}) %collective-permute-start.17) | collective-permute-done | bytes 49184 | tf_op jit(solution)/shard_map/ppermute | solution.py:360
  71.9 1.4 %collective-permute-start.19 = (f32[3,32,128]{2,1,0:T(8,128)S(1)}, f32[3,32,128]{2,1,0:T(8,128)S(1)}, u32[]{:S(2)}, u32[]{:S(2)}) collective-permute-start(f32[3,32,128]{2,1,0:T(8,128)S(1)} %pad_maximum_fusion.9), channel_id=1, source_target_pairs={{0,24},{8,16},{16,8},{24,0},{1,25},{9,17},{17,9},{25,1},{2,26},{10... | collective-permute-start | bytes 147464 | tf_op jit(solution)/shard_map/ppermute | solution.py:364
  73.4 2.1 %collective-permute-done.18.lat_inner_in = f32[3,32,128]{2,1,0:T(8,128)S(1)} collective-permute-done((f32[3,32,128]{2,1,0:T(8,128)S(1)}, f32[3,32,128]{2,1,0:T(8,128)S(1)}, u32[]{:S(2)}, u32[]{:S(2)}) %collective-permute-start.18) | collective-permute-done | bytes 49184 | tf_op jit(solution)/shard_map/ppermute | solution.py:365
  75.5 1.4 %collective-permute-done.19.lat_outer_in = f32[3,32,128]{2,1,0:T(8,128)S(1)} collective-permute-done((f32[3,32,128]{2,1,0:T(8,128)S(1)}, f32[3,32,128]{2,1,0:T(8,128)S(1)}, u32[]{:S(2)}, u32[]{:S(2)}) %collective-permute-start.19) | collective-permute-done | bytes 49184 | tf_op jit(solution)/shard_map/ppermute | solution.py:364
  76.9 1.0 %edges.5 = (f32[32,1024]{1,0:T(8,128)S(1)}, f32[3,32,128]{2,1,0:T(8,128)S(1)}, f32[3,32,128]{2,1,0:T(8,128)S(1)}, f32[32,128]{1,0:T(8,128)S(1)}, f32[32,128]{1,0:T(8,128)S(1)}) custom-call(f32[32,640]{1,0:T(8,128)S(1)} %get-tuple-element.70.cells_ref, f32[3,32,128]{2,1,0:T(8,128)S(1)} %collective-permute-done.16.inner_in, ...), custom_call_target="tpu_custom_call" | custom-call | tf_op jit(solution)/shard_map/edges/pallas_call | solution.py:339
  78.1 1.2 %collective-permute-done.20.inner_in = f32[3,32,128]{2,1,0:T(8,128)S(1)} collective-permute-done((f32[3,32,128]{2,1,0:T(8,128)S(1)}, f32[3,32,128]{2,1,0:T(8,128)S(1)}, u32[]{:S(2)}, u32[]{:S(2)}) %collective-permute-start.20) | collective-permute-done | bytes 49184 | tf_op jit(solution)/shard_map/ppermute | solution.py:361
  79.2 4.1 %collective-permute-done.21.outer_in = f32[3,32,128]{2,1,0:T(8,128)S(1)} collective-permute-done((f32[3,32,128]{2,1,0:T(8,128)S(1)}, f32[3,32,128]{2,1,0:T(8,128)S(1)}, u32[]{:S(2)}, u32[]{:S(2)}) %collective-permute-start.21) | collective-permute-done | bytes 49184 | tf_op jit(solution)/shard_map/ppermute | solution.py:360
  83.4 1.6 %collective-permute-start.22 = (f32[3,32,128]{2,1,0:T(8,128)S(1)}, f32[3,32,128]{2,1,0:T(8,128)S(1)}, u32[]{:S(2)}, u32[]{:S(2)}) collective-permute-start(f32[3,32,128]{2,1,0:T(8,128)S(1)} %pad_maximum_fusion.10), channel_id=1, source_target_pairs={{0,8},{8,0},{16,24},{24,16},{1,9},{9,1},{17,25},{25,17},{2,10},{10... | collective-permute-start | bytes 147464 | tf_op jit(solution)/shard_map/ppermute | solution.py:365
  85.5 0.8 copy.12
  86.3 1.3 %collective-permute-done.22.lat_inner_in = f32[3,32,128]{2,1,0:T(8,128)S(1)} collective-permute-done((f32[3,32,128]{2,1,0:T(8,128)S(1)}, f32[3,32,128]{2,1,0:T(8,128)S(1)}, u32[]{:S(2)}, u32[]{:S(2)}) %collective-permute-start.22) | collective-permute-done | bytes 49184 | tf_op jit(solution)/shard_map/ppermute | solution.py:365
  87.5 2.4 %collective-permute-done.23.lat_outer_in = f32[3,32,128]{2,1,0:T(8,128)S(1)} collective-permute-done((f32[3,32,128]{2,1,0:T(8,128)S(1)}, f32[3,32,128]{2,1,0:T(8,128)S(1)}, u32[]{:S(2)}, u32[]{:S(2)}) %collective-permute-start.23) | collective-permute-done | bytes 49184 | tf_op jit(solution)/shard_map/ppermute | solution.py:364
  89.9 1.8 %last.1 = f32[30,1,640]{2,1,0:T(1,128)} custom-call(f32[32,1024]{1,0:T(8,128)S(1)} %get-tuple-element.75.edges_ref, f32[3,32,128]{2,1,0:T(8,128)S(1)} %collective-permute-done.20.inner_in, f32[3,32,128]{2,1,0:T(8,128)S(1)} %collective-permute-done.21.outer_in, f32[3,32,128]{2,1,0:T(8,128)S(1)} %collective-permute-done.22.lat_inner_in, ...), custom_call_target="tpu_custom_call" | custom-call | tf_op jit(solution)/shard_map/last/pallas_call | solution.py:339
  (52 shorter events, 3.2 us)
Async XLA Ops:
  0.6 0.9 copy-start.2
  1.5 0.7 copy-start.7
  3.0 5.2 %collective-permute-start = (f32[3,32,128]{2,1,0:T(8,128)S(1)}, f32[3,32,128]{2,1,0:T(8,128)S(1)}, u32[]{:S(2)}, u32[]{:S(2)}) collective-permute-start(f32[3,32,128]{2,1,0:T(8,128)S(1)} %get-tuple-element.42), channel_id=1, source_target_pairs={{0,1},{1,0},{2,3},{3,2},{4,5},{5,4},{6,7},{7,6},{8,9},{9,8},{10,11... | collective-permute-start | bytes 147464 | tf_op jit(solution)/shard_map/ppermute | solution.py:361
  3.5 6.6 %collective-permute-start.1 = (f32[3,32,128]{2,1,0:T(8,128)S(1)}, f32[3,32,128]{2,1,0:T(8,128)S(1)}, u32[]{:S(2)}, u32[]{:S(2)}) collective-permute-start(f32[3,32,128]{2,1,0:T(8,128)S(1)} %get-tuple-element.43), channel_id=1, source_target_pairs={{0,7},{1,2},{2,1},{3,4},{4,3},{5,6},{6,5},{7,0},{8,15},{9,10},{10,... | collective-permute-start | bytes 147464 | tf_op jit(solution)/shard_map/ppermute | solution.py:360
  10.1 14.0 %collective-permute-start.2 = (f32[3,32,128]{2,1,0:T(8,128)S(1)}, f32[3,32,128]{2,1,0:T(8,128)S(1)}, u32[]{:S(2)}, u32[]{:S(2)}) collective-permute-start(f32[3,32,128]{2,1,0:T(8,128)S(1)} %pad_maximum_fusion), channel_id=1, source_target_pairs={{0,8},{8,0},{16,24},{24,16},{1,9},{9,1},{17,25},{25,17},{2,10},{10... | collective-permute-start | bytes 147464 | tf_op jit(solution)/shard_map/ppermute | solution.py:365
  11.7 12.4 %collective-permute-start.3 = (f32[3,32,128]{2,1,0:T(8,128)S(1)}, f32[3,32,128]{2,1,0:T(8,128)S(1)}, u32[]{:S(2)}, u32[]{:S(2)}) collective-permute-start(f32[3,32,128]{2,1,0:T(8,128)S(1)} %pad_maximum_fusion.1), channel_id=1, source_target_pairs={{0,24},{8,16},{16,8},{24,0},{1,25},{9,17},{17,9},{25,1},{2,26},{10... | collective-permute-start | bytes 147464 | tf_op jit(solution)/shard_map/ppermute | solution.py:364
  14.5 0.9 copy-start
  15.4 0.9 copy-start.1
  16.3 0.7 copy-start.5
  17.0 0.7 copy-start.6
  24.1 0.7 copy-start.3
  24.8 13.5 %copy-start.4 = (f32[1,640]{1,0:T(1,128)S(1)}, f32[1,640]{1,0:T(1,128)}, u32[]{:S(2)}) copy-start(f32[1,640]{1,0:T(1,128)} %speed_ref.5) | copy-start | bytes 7684
  25.8 3.0 %collective-permute-start.4 = (f32[3,32,128]{2,1,0:T(8,128)S(1)}, f32[3,32,128]{2,1,0:T(8,128)S(1)}, u32[]{:S(2)}, u32[]{:S(2)}) collective-permute-start(f32[3,32,128]{2,1,0:T(8,128)S(1)} %get-tuple-element.50), channel_id=1, source_target_pairs={{0,1},{1,0},{2,3},{3,2},{4,5},{5,4},{6,7},{7,6},{8,9},{9,8},{10,11... | collective-permute-start | bytes 147464 | tf_op jit(solution)/shard_map/ppermute | solution.py:361
  25.8 5.9 %collective-permute-start.5 = (f32[3,32,128]{2,1,0:T(8,128)S(1)}, f32[3,32,128]{2,1,0:T(8,128)S(1)}, u32[]{:S(2)}, u32[]{:S(2)}) collective-permute-start(f32[3,32,128]{2,1,0:T(8,128)S(1)} %get-tuple-element.51), channel_id=1, source_target_pairs={{0,7},{1,2},{2,1},{3,4},{4,3},{5,6},{6,5},{7,0},{8,15},{9,10},{10,... | collective-permute-start | bytes 147464 | tf_op jit(solution)/shard_map/ppermute | solution.py:360
  31.7 4.2 %collective-permute-start.6 = (f32[3,32,128]{2,1,0:T(8,128)S(1)}, f32[3,32,128]{2,1,0:T(8,128)S(1)}, u32[]{:S(2)}, u32[]{:S(2)}) collective-permute-start(f32[3,32,128]{2,1,0:T(8,128)S(1)} %pad_maximum_fusion.2), channel_id=1, source_target_pairs={{0,8},{8,0},{16,24},{24,16},{1,9},{9,1},{17,25},{25,17},{2,10},{10... | collective-permute-start | bytes 147464 | tf_op jit(solution)/shard_map/ppermute | solution.py:365
  33.3 5.0 %collective-permute-start.7 = (f32[3,32,128]{2,1,0:T(8,128)S(1)}, f32[3,32,128]{2,1,0:T(8,128)S(1)}, u32[]{:S(2)}, u32[]{:S(2)}) collective-permute-start(f32[3,32,128]{2,1,0:T(8,128)S(1)} %pad_maximum_fusion.3), channel_id=1, source_target_pairs={{0,24},{8,16},{16,8},{24,0},{1,25},{9,17},{17,9},{25,1},{2,26},{10... | collective-permute-start | bytes 147464 | tf_op jit(solution)/shard_map/ppermute | solution.py:364
  40.1 1.2 %collective-permute-start.8 = (f32[3,32,128]{2,1,0:T(8,128)S(1)}, f32[3,32,128]{2,1,0:T(8,128)S(1)}, u32[]{:S(2)}, u32[]{:S(2)}) collective-permute-start(f32[3,32,128]{2,1,0:T(8,128)S(1)} %get-tuple-element.61), channel_id=1, source_target_pairs={{0,1},{1,0},{2,3},{3,2},{4,5},{5,4},{6,7},{7,6},{8,9},{9,8},{10,11... | collective-permute-start | bytes 147464 | tf_op jit(solution)/shard_map/ppermute | solution.py:361
  40.1 5.4 %collective-permute-start.9 = (f32[3,32,128]{2,1,0:T(8,128)S(1)}, f32[3,32,128]{2,1,0:T(8,128)S(1)}, u32[]{:S(2)}, u32[]{:S(2)}) collective-permute-start(f32[3,32,128]{2,1,0:T(8,128)S(1)} %get-tuple-element.62), channel_id=1, source_target_pairs={{0,7},{1,2},{2,1},{3,4},{4,3},{5,6},{6,5},{7,0},{8,15},{9,10},{10,... | collective-permute-start | bytes 147464 | tf_op jit(solution)/shard_map/ppermute | solution.py:360
  45.5 4.2 %collective-permute-start.10 = (f32[3,32,128]{2,1,0:T(8,128)S(1)}, f32[3,32,128]{2,1,0:T(8,128)S(1)}, u32[]{:S(2)}, u32[]{:S(2)}) collective-permute-start(f32[3,32,128]{2,1,0:T(8,128)S(1)} %pad_maximum_fusion.4), channel_id=1, source_target_pairs={{0,8},{8,0},{16,24},{24,16},{1,9},{9,1},{17,25},{25,17},{2,10},{10... | collective-permute-start | bytes 147464 | tf_op jit(solution)/shard_map/ppermute | solution.py:365
  46.1 5.0 %collective-permute-start.11 = (f32[3,32,128]{2,1,0:T(8,128)S(1)}, f32[3,32,128]{2,1,0:T(8,128)S(1)}, u32[]{:S(2)}, u32[]{:S(2)}) collective-permute-start(f32[3,32,128]{2,1,0:T(8,128)S(1)} %pad_maximum_fusion.5), channel_id=1, source_target_pairs={{0,24},{8,16},{16,8},{24,0},{1,25},{9,17},{17,9},{25,1},{2,26},{10... | collective-permute-start | bytes 147464 | tf_op jit(solution)/shard_map/ppermute | solution.py:364
  52.2 1.3 %collective-permute-start.12 = (f32[3,32,128]{2,1,0:T(8,128)S(1)}, f32[3,32,128]{2,1,0:T(8,128)S(1)}, u32[]{:S(2)}, u32[]{:S(2)}) collective-permute-start(f32[3,32,128]{2,1,0:T(8,128)S(1)} %get-tuple-element.66), channel_id=1, source_target_pairs={{0,1},{1,0},{2,3},{3,2},{4,5},{5,4},{6,7},{7,6},{8,9},{9,8},{10,11... | collective-permute-start | bytes 147464 | tf_op jit(solution)/shard_map/ppermute | solution.py:361
  52.2 5.4 %collective-permute-start.13 = (f32[3,32,128]{2,1,0:T(8,128)S(1)}, f32[3,32,128]{2,1,0:T(8,128)S(1)}, u32[]{:S(2)}, u32[]{:S(2)}) collective-permute-start(f32[3,32,128]{2,1,0:T(8,128)S(1)} %get-tuple-element.67), channel_id=1, source_target_pairs={{0,7},{1,2},{2,1},{3,4},{4,3},{5,6},{6,5},{7,0},{8,15},{9,10},{10,... | collective-permute-start | bytes 147464 | tf_op jit(solution)/shard_map/ppermute | solution.py:360
  57.6 4.2 %collective-permute-start.14 = (f32[3,32,128]{2,1,0:T(8,128)S(1)}, f32[3,32,128]{2,1,0:T(8,128)S(1)}, u32[]{:S(2)}, u32[]{:S(2)}) collective-permute-start(f32[3,32,128]{2,1,0:T(8,128)S(1)} %pad_maximum_fusion.6), channel_id=1, source_target_pairs={{0,8},{8,0},{16,24},{24,16},{1,9},{9,1},{17,25},{25,17},{2,10},{10... | collective-permute-start | bytes 147464 | tf_op jit(solution)/shard_map/ppermute | solution.py:365
  59.1 5.0 %collective-permute-start.15 = (f32[3,32,128]{2,1,0:T(8,128)S(1)}, f32[3,32,128]{2,1,0:T(8,128)S(1)}, u32[]{:S(2)}, u32[]{:S(2)}) collective-permute-start(f32[3,32,128]{2,1,0:T(8,128)S(1)} %pad_maximum_fusion.7), channel_id=1, source_target_pairs={{0,24},{8,16},{16,8},{24,0},{1,25},{9,17},{17,9},{25,1},{2,26},{10... | collective-permute-start | bytes 147464 | tf_op jit(solution)/shard_map/ppermute | solution.py:364
  65.9 1.2 %collective-permute-start.16 = (f32[3,32,128]{2,1,0:T(8,128)S(1)}, f32[3,32,128]{2,1,0:T(8,128)S(1)}, u32[]{:S(2)}, u32[]{:S(2)}) collective-permute-start(f32[3,32,128]{2,1,0:T(8,128)S(1)} %get-tuple-element.71), channel_id=1, source_target_pairs={{0,1},{1,0},{2,3},{3,2},{4,5},{5,4},{6,7},{7,6},{8,9},{9,8},{10,11... | collective-permute-start | bytes 147464 | tf_op jit(solution)/shard_map/ppermute | solution.py:361
  65.9 5.4 %collective-permute-start.17 = (f32[3,32,128]{2,1,0:T(8,128)S(1)}, f32[3,32,128]{2,1,0:T(8,128)S(1)}, u32[]{:S(2)}, u32[]{:S(2)}) collective-permute-start(f32[3,32,128]{2,1,0:T(8,128)S(1)} %get-tuple-element.72), channel_id=1, source_target_pairs={{0,7},{1,2},{2,1},{3,4},{4,3},{5,6},{6,5},{7,0},{8,15},{9,10},{10,... | collective-permute-start | bytes 147464 | tf_op jit(solution)/shard_map/ppermute | solution.py:360
  71.3 4.2 %collective-permute-start.18 = (f32[3,32,128]{2,1,0:T(8,128)S(1)}, f32[3,32,128]{2,1,0:T(8,128)S(1)}, u32[]{:S(2)}, u32[]{:S(2)}) collective-permute-start(f32[3,32,128]{2,1,0:T(8,128)S(1)} %pad_maximum_fusion.8), channel_id=1, source_target_pairs={{0,8},{8,0},{16,24},{24,16},{1,9},{9,1},{17,25},{25,17},{2,10},{10... | collective-permute-start | bytes 147464 | tf_op jit(solution)/shard_map/ppermute | solution.py:365
  71.9 5.0 %collective-permute-start.19 = (f32[3,32,128]{2,1,0:T(8,128)S(1)}, f32[3,32,128]{2,1,0:T(8,128)S(1)}, u32[]{:S(2)}, u32[]{:S(2)}) collective-permute-start(f32[3,32,128]{2,1,0:T(8,128)S(1)} %pad_maximum_fusion.9), channel_id=1, source_target_pairs={{0,24},{8,16},{16,8},{24,0},{1,25},{9,17},{17,9},{25,1},{2,26},{10... | collective-permute-start | bytes 147464 | tf_op jit(solution)/shard_map/ppermute | solution.py:364
  78.0 1.3 %collective-permute-start.20 = (f32[3,32,128]{2,1,0:T(8,128)S(1)}, f32[3,32,128]{2,1,0:T(8,128)S(1)}, u32[]{:S(2)}, u32[]{:S(2)}) collective-permute-start(f32[3,32,128]{2,1,0:T(8,128)S(1)} %get-tuple-element.76), channel_id=1, source_target_pairs={{0,1},{1,0},{2,3},{3,2},{4,5},{5,4},{6,7},{7,6},{8,9},{9,8},{10,11... | collective-permute-start | bytes 147464 | tf_op jit(solution)/shard_map/ppermute | solution.py:361
  78.0 5.4 %collective-permute-start.21 = (f32[3,32,128]{2,1,0:T(8,128)S(1)}, f32[3,32,128]{2,1,0:T(8,128)S(1)}, u32[]{:S(2)}, u32[]{:S(2)}) collective-permute-start(f32[3,32,128]{2,1,0:T(8,128)S(1)} %get-tuple-element.77), channel_id=1, source_target_pairs={{0,7},{1,2},{2,1},{3,4},{4,3},{5,6},{6,5},{7,0},{8,15},{9,10},{10,... | collective-permute-start | bytes 147464 | tf_op jit(solution)/shard_map/ppermute | solution.py:360
  83.4 4.2 %collective-permute-start.22 = (f32[3,32,128]{2,1,0:T(8,128)S(1)}, f32[3,32,128]{2,1,0:T(8,128)S(1)}, u32[]{:S(2)}, u32[]{:S(2)}) collective-permute-start(f32[3,32,128]{2,1,0:T(8,128)S(1)} %pad_maximum_fusion.10), channel_id=1, source_target_pairs={{0,8},{8,0},{16,24},{24,16},{1,9},{9,1},{17,25},{25,17},{2,10},{10... | collective-permute-start | bytes 147464 | tf_op jit(solution)/shard_map/ppermute | solution.py:365
  84.9 5.0 %collective-permute-start.23 = (f32[3,32,128]{2,1,0:T(8,128)S(1)}, f32[3,32,128]{2,1,0:T(8,128)S(1)}, u32[]{:S(2)}, u32[]{:S(2)}) collective-permute-start(f32[3,32,128]{2,1,0:T(8,128)S(1)} %pad_maximum_fusion.11), channel_id=1, source_target_pairs={{0,24},{8,16},{16,8},{24,0},{1,25},{9,17},{17,9},{25,1},{2,26},{10... | collective-permute-start | bytes 147464 | tf_op jit(solution)/shard_map/ppermute | solution.py:364

commit v2 on v0

v2 whole, which is shorter than its diff:
```python
import functools

import jax
import jax.numpy as jnp
from jax import lax
from jax.experimental import pallas as pl
from jax.experimental.pallas import tpu as pltpu
from jax.sharding import PartitionSpec as P


NSUB = 3
STEP_SCALE = 0.5
LANES = 128
PARTS = 3

f32 = jnp.float32
bf16 = jnp.bfloat16
i16 = jnp.int16


def round_up(value, step):
    return -(-value // step) * step


def swap_routes(count):
    inner = [(i, i ^ 1) for i in range(count)]
    outer = [(i, (((i + 1) ^ 1) - 1) % count) for i in range(count)]
    return inner, outer


OUTER_SENT = ((0, 2), (1, 2), (2, 2))
REST_SENT = ((0, 1), (1, 1), (2, 1), (1, 0), (2, 0))


def link_signs():
    lat_inner = 1 - 2 * lax.rem(lax.axis_index("lat"), 2)
    lon_inner = 1 - 2 * lax.rem(lax.axis_index("lon"), 2)
    return lat_inner, lon_inner


def sent_row(member):
    lat_inner, lon_inner = link_signs()
    lat_link, lon_link = member
    p = (0, lat_inner, -lat_inner)[lat_link]
    q = (0, lon_inner, -lon_inner)[lon_link]
    flat = (p + 1) * 3 + (q + 1)
    return flat - jnp.where(flat > 4, 1, 0)


def local_positions(index, own, own_padded, halo, lat_count):
    lat_inner, lon_inner = link_signs()
    a = lax.axis_index("lat")
    beyond = index - own
    piece = lax.div(jnp.maximum(beyond, 0), halo)
    slot = beyond - piece * halo
    flat = piece + jnp.where(piece >= 4, 1, 0)
    p = jnp.where(flat >= 6, 1, jnp.where(flat >= 3, 0, -1))
    q = flat - 3 * (p + 1) - 1
    lon_member = jnp.where(q == 0, 2, jnp.where(q == lon_inner, 0, 1))
    member = jnp.where(p == 0, lon_member, jnp.where(p == lat_inner, 2, 5) + lon_member)
    outside = (a + p < 0) | (a + p >= lat_count)
    row = own_padded + member * halo + slot
    return jnp.where(beyond < 0, index, jnp.where(outside, -1, row))


def put_parts(stack_ref, value, start):
    rows, width = value.shape
    rest = value
    for part in range(PARTS):
        piece = rest.astype(bf16)
        stack_ref[part * rows : (part + 1) * rows, start : start + width] = piece
        if part < PARTS - 1:
            rest = rest - piece.astype(f32)


def sum_parts(product, rows):
    total = product[(PARTS - 1) * rows : PARTS * rows]
    for part in range(PARTS - 2, -1, -1):
        total = total + product[part * rows : (part + 1) * rows]
    return total


def gather_matmul(stack_ref, matrices, rows):
    product = None
    for matrix in matrices:
        term = jnp.dot(stack_ref[...], matrix, preferred_element_type=f32)
        product = term if product is None else product + term
    return sum_parts(product, rows)


def fetch(pairs, sems):
    copies = [pltpu.make_async_copy(source, target, sems.at[i]) for i, (source, target) in enumerate(pairs)]
    for copy in copies:
        copy.start()
    for copy in copies:
        copy.wait()


def by_blocks(rows, body):
    block = 64 if rows % 64 == 0 else 16

    def step(i, carry):
        first = pl.multiple_of(i * block, block)
        body(first, block)
        return carry

    lax.fori_loop(0, rows // block, step, 0)


def row_numbers(first, block, width):
    return (lax.broadcasted_iota(jnp.int32, (block, width), 0) + first).astype(i16)


def fill_sent(matrix_ref, list_ref, members):
    rows = matrix_ref.shape[0]
    halo = list_ref.shape[1]
    lanes = [list_ref[pl.ds(sent_row(member), 1), :].astype(i16) for member in members]

    def body(first, block):
        row = row_numbers(first, block, halo)
        for member, index in enumerate(lanes):
            hit = jnp.where(row == index, jnp.ones((), bf16), jnp.zeros((), bf16))
            matrix_ref[pl.ds(first, block), member * halo : (member + 1) * halo] = hit

    by_blocks(rows, body)


def store_outer(pieces, outer_ref):
    halo = outer_ref.shape[2]
    for member in range(3):
        outer_ref[member] = pieces[:, member * halo : (member + 1) * halo]


def store_rest(pieces, inner_ref, lat_inner_ref, lat_outer_ref):
    halo = inner_ref.shape[2]
    for member in range(3):
        inner_ref[member] = pieces[:, member * halo : (member + 1) * halo]
    lat_inner_ref[...] = pieces[:, 3 * halo : 4 * halo]
    lat_outer_ref[...] = pieces[:, 4 * halo : 5 * halo]


def start_kernel(pressure_hbm, list_hbm, cells_ref, stack_ref, outer_ref, matrix_ref, lists_ref, pressure_ref, sems):
    fetch([(list_hbm, lists_ref), (pressure_hbm, pressure_ref)], sems)
    levels = pressure_ref.shape[0]
    rows = cells_ref.shape[0]
    fill_sent(matrix_ref, lists_ref, OUTER_SENT)
    cells_ref[0:levels, :] = pressure_ref[:, 0, :]
    cells_ref[levels:rows, :] = jnp.zeros((rows - levels, cells_ref.shape[1]), f32)
    put_parts(stack_ref, cells_ref[...], 0)
    store_outer(gather_matmul(stack_ref, [matrix_ref[...]], rows), outer_ref)


def first_rest_kernel(stack_ref, list_ref, inner_ref, lat_inner_ref, lat_outer_ref, matrix_ref):
    fill_sent(matrix_ref, list_ref, REST_SENT)
    store_rest(gather_matmul(stack_ref, [matrix_ref[...]], inner_ref.shape[1]), inner_ref, lat_inner_ref, lat_outer_ref)


def rest_kernel(stack_ref, matrix_ref, inner_ref, lat_inner_ref, lat_outer_ref):
    store_rest(gather_matmul(stack_ref, [matrix_ref[...]], inner_ref.shape[1]), inner_ref, lat_inner_ref, lat_outer_ref)


def gradient_kernel(edge_cells_hbm, near_ref, far_ref, ends_ref, sems, *, cells, halo, lat_count):
    fetch([(edge_cells_hbm, ends_ref)], sems)
    edges = ends_ref.shape[1]
    edge_pad = near_ref.shape[1]
    ends = local_positions(ends_ref[...], cells, cells, halo, lat_count)
    near, far = ends[0:1, :], ends[1:2, :]
    same = near == far
    near, far = jnp.where(same, -1, near), jnp.where(same, -1, far)
    if edge_pad > edges:
        fill = jnp.full((1, edge_pad - edges), -1, jnp.int32)
        near, far = jnp.concatenate([near, fill], axis=1), jnp.concatenate([far, fill], axis=1)
    near, far = near.astype(i16), far.astype(i16)

    def fill_rows(matrix_ref, base):
        def body(first, block):
            row = row_numbers(first + base, block, edge_pad)
            one = jnp.ones((), bf16)
            matrix_ref[pl.ds(first, block), :] = jnp.where(row == far, one, jnp.where(row == near, -one, jnp.zeros((), bf16)))

        by_blocks(matrix_ref.shape[0], body)

    fill_rows(near_ref, 0)
    fill_rows(far_ref, near_ref.shape[0])


def edge_setup_kernel(velocity_hbm, list_hbm, dual_hbm, edges_ref, scale_ref, outer_matrix_ref, rest_matrix_ref, velocity_ref, list_ref, dual_ref, sems):
    fetch([(list_hbm, list_ref), (velocity_hbm, velocity_ref), (dual_hbm, dual_ref)], sems)
    levels, _, edges = velocity_ref.shape
    edges_ref[...] = jnp.zeros(edges_ref.shape, f32)
    edges_ref[0:levels, 0:edges] = velocity_ref[:, 0, :]
    scale_ref[...] = jnp.zeros(scale_ref.shape, f32)
    scale_ref[:, 0:edges] = STEP_SCALE * dual_ref[...]
    fill_sent(outer_matrix_ref, list_ref, OUTER_SENT)
    fill_sent(rest_matrix_ref, list_ref, REST_SENT)


def weight_kernel(
    sides_hbm, weight_hbm, near_high_ref, near_low_ref, far_high_ref, far_low_ref, sides_ref, weight_ref, sems, *, edges, edge_pad, halo, lat_count
):
    fetch([(sides_hbm, sides_ref), (weight_hbm, weight_ref)], sems)
    cells = sides_ref.shape[2]
    place = [local_positions(sides_ref[i], edges, edge_pad, halo, lat_count) for i in range(3)]
    weight = [weight_ref[i] for i in range(3)]
    for later in (1, 2):
        for earlier in range(later):
            same = place[later] == place[earlier]
            weight[earlier] = weight[earlier] + jnp.where(same, weight[later], 0.0)
            weight[later] = jnp.where(same, 0.0, weight[later])
            place[later] = jnp.where(same, -1, place[later])
    high = [value.astype(bf16) for value in weight]
    low = [(value - top.astype(f32)).astype(bf16) for value, top in zip(weight, high)]
    place = [value.astype(i16) for value in place]
    zero = jnp.zeros((), bf16)

    def fill_rows(high_ref, low_ref, base):
        def body(first, block):
            row = row_numbers(first + base, block, cells)
            hits = [row == value for value in place]
            for target, values in ((high_ref, high), (low_ref, low)):
                entry = jnp.where(hits[0], values[0], jnp.where(hits[1], values[1], jnp.where(hits[2], values[2], zero)))
                target[pl.ds(first, block), :] = entry

        by_blocks(high_ref.shape[0], body)

    fill_rows(near_high_ref, near_low_ref, 0)
    fill_rows(far_high_ref, far_low_ref, near_high_ref.shape[0])


def cell_setup_kernel(
    coupling_hbm, list_ref, speed_hbm, speed_ref, inverse_ref, forward_ref, back_ref, outer_matrix_ref, rest_matrix_ref, coupling_ref, column_ref, sems
):
    fetch([(coupling_hbm, coupling_ref), (speed_hbm, speed_ref)], sems)
    levels, _, cells = coupling_ref.shape
    for group in range(cells // LANES):
        column_ref[0:levels, group, :] = coupling_ref[:, 0, group * LANES : (group + 1) * LANES]
    above = column_ref[0]
    inverse = 1.0 / (1.0 + above)
    inverse_ref[0] = inverse
    ratio = above * inverse
    back_ref[0] = ratio
    for level in range(1, levels):
        below = above
        above = column_ref[level]
        inverse = 1.0 / (1.0 + below + above - below * ratio)
        inverse_ref[level] = inverse
        forward_ref[level] = below * inverse
        ratio = above * inverse
        back_ref[level] = ratio
    fill_sent(outer_matrix_ref, list_ref, OUTER_SENT)
    fill_sent(rest_matrix_ref, list_ref, REST_SENT)


def part_kernel(own_ref, inner_ref, outer_ref, *rest):
    *matrix_refs, total_ref, stack_ref = rest
    rows, width = own_ref.shape
    halo = inner_ref.shape[2]
    put_parts(stack_ref, own_ref[...], 0)
    put_parts(stack_ref, inner_ref[0], width)
    put_parts(stack_ref, outer_ref[0], width + halo)
    total_ref[...] = gather_matmul(stack_ref, [ref[...] for ref in matrix_refs], rows)


def lat_share(total_ref, lat_inner_ref, lat_outer_ref, matrix_refs, stack_ref):
    rows = total_ref.shape[0]
    halo = lat_inner_ref.shape[2]
    for member in range(3):
        put_parts(stack_ref, lat_inner_ref[member], member * halo)
        put_parts(stack_ref, lat_outer_ref[member], (3 + member) * halo)
    return total_ref[...] + gather_matmul(stack_ref, [ref[...] for ref in matrix_refs], rows)


def edge_kernel(total_ref, lat_inner_ref, lat_outer_ref, far_ref, edges_ref, scale_ref, matrix_ref, new_edges_ref, outer_ref, own_stack_ref, stack_ref):
    rows = edges_ref.shape[0]
    difference = lat_share(total_ref, lat_inner_ref, lat_outer_ref, [far_ref], stack_ref)
    new_edges = edges_ref[...] - scale_ref[...] * difference
    new_edges_ref[...] = new_edges
    put_parts(own_stack_ref, new_edges, 0)
    store_outer(gather_matmul(own_stack_ref, [matrix_ref[...]], rows), outer_ref)


def solve_columns(total_ref, lat_inner_ref, lat_outer_ref, high_ref, low_ref, cells_ref, speed_ref, inverse_ref, forward_ref, back_ref, levels, stack_ref, column_ref):
    rows, cells = cells_ref.shape
    divergence = lat_share(total_ref, lat_inner_ref, lat_outer_ref, [high_ref, low_ref], stack_ref)
    right_side = cells_ref[...] - speed_ref[...] * divergence
    for group in range(cells // LANES):
        column_ref[:, group, :] = right_side[:, group * LANES : (group + 1) * LANES]
    current = column_ref[0] * inverse_ref[0]
    scaled = [current]
    for level in range(1, levels):
        current = column_ref[level] * inverse_ref[level] + forward_ref[level] * current
        scaled.append(current)
    column_ref[levels - 1] = current
    for level in range(levels - 2, -1, -1):
        current = scaled[level] + back_ref[level] * current
        column_ref[level] = current
    for level in range(levels, rows):
        column_ref[level] = jnp.zeros_like(current)


def cell_kernel(
    total_ref,
    lat_inner_ref,
    lat_outer_ref,
    high_ref,
    low_ref,
    cells_ref,
    speed_ref,
    inverse_ref,
    forward_ref,
    back_ref,
    matrix_ref,
    new_cells_ref,
    outer_ref,
    own_stack_ref,
    stack_ref,
    column_ref,
    *,
    levels,
):
    rows, cells = cells_ref.shape
    solve_columns(total_ref, lat_inner_ref, lat_outer_ref, high_ref, low_ref, cells_ref, speed_ref, inverse_ref, forward_ref, back_ref, levels, stack_ref, column_ref)
    for group in range(cells // LANES):
        part = column_ref[:, group, :]
        new_cells_ref[:, group * LANES : (group + 1) * LANES] = part
        put_parts(own_stack_ref, part, group * LANES)
    store_outer(gather_matmul(own_stack_ref, [matrix_ref[...]], rows), outer_ref)


def last_kernel(
    total_ref, lat_inner_ref, lat_outer_ref, high_ref, low_ref, cells_ref, speed_ref, inverse_ref, forward_ref, back_ref, out_ref, stack_ref, column_ref, *, levels
):
    cells = cells_ref.shape[1]
    solve_columns(total_ref, lat_inner_ref, lat_outer_ref, high_ref, low_ref, cells_ref, speed_ref, inverse_ref, forward_ref, back_ref, levels, stack_ref, column_ref)
    for group in range(cells // LANES):
        out_ref[:, 0, group * LANES : (group + 1) * LANES] = column_ref[0:levels, group, :]


def call(body, outs, scratch, *operands, raw=(), copies=0):
    in_vmem = pl.BlockSpec(memory_space=pltpu.VMEM)
    in_hbm = pl.BlockSpec(memory_space=pltpu.HBM)
    scratch_shapes = [pltpu.VMEM(shape, kind) for shape, kind in scratch]
    if copies:
        scratch_shapes.append(pltpu.SemaphoreType.DMA((copies,)))
    return pl.pallas_call(
        body,
        out_shape=tuple(jax.ShapeDtypeStruct(shape, kind) for shape, kind in outs),
        in_specs=[in_hbm if i in raw else in_vmem for i in range(len(operands))],
        out_specs=tuple(in_vmem for _ in outs),
        scratch_shapes=scratch_shapes,
        compiler_params=pltpu.CompilerParams(vmem_limit_bytes=24 * 1024 * 1024),
    )(*operands)


def on_device(lat_count, lon_count, pressure, velocity, edge_cells, cell_edges, send_cells, send_edges, inv_dual, edge_weight, sound_speed, coupling):
    _, levels, cells = pressure.shape
    edges = velocity.shape[2]
    halo = send_cells.shape[2]
    rows = round_up(levels, 16)
    edge_pad = round_up(edges, 2 * LANES)
    bundle = ((3, rows, halo), f32)
    straight = ((rows, halo), f32)
    lon_routes = swap_routes(lon_count)
    lat_routes = swap_routes(lat_count)
    i32 = jnp.int32

    by_level = lambda value: value.transpose(1, 0, 2)
    stack_cells = ((PARTS * rows, cells), bf16)
    stack_edges = ((PARTS * rows, edge_pad), bf16)
    stack_lat = ((PARTS * rows, 6 * halo), bf16)
    column = ((rows, cells // LANES, LANES), f32)
    sent_outer = lambda width: ((width, 3 * halo), bf16)
    sent_rest = lambda width: ((width, 5 * halo), bf16)

    for phase in range(2 * NSUB):
        at_cells = phase % 2 == 0
        if phase == 0:
            values, stack, outer, cell_outer, cell_list = call(
                start_kernel,
                [((rows, cells), f32), stack_cells, bundle, sent_outer(cells), (send_cells.shape[1:], i32)],
                [((levels, 1, cells), f32)],
                by_level(pressure),
                send_cells[0],
                raw=(0, 1),
                copies=2,
            )
        outer_in = lax.ppermute(outer, "lon", lon_routes[1])
        if phase == 0:
            inner, lat_inner, lat_outer = call(first_rest_kernel, [bundle, straight, straight], [sent_rest(cells)], stack, cell_list)
        else:
            inner, lat_inner, lat_outer = call(rest_kernel, [bundle, straight, straight], [], stack, cell_rest if at_cells else edge_rest)
        inner_in = lax.ppermute(inner, "lon", lon_routes[0])
        if phase == 0:
            gradient_near, gradient_far = call(
                functools.partial(gradient_kernel, cells=cells, halo=halo, lat_count=lat_count),
                [((cells + 2 * halo, edge_pad), bf16), ((6 * halo, edge_pad), bf16)],
                [(edge_cells.shape[1:], i32)],
                edge_cells[0],
                raw=(0,),
                copies=1,
            )
        if phase == 1:
            near_high, near_low, far_high, far_low = call(
                functools.partial(weight_kernel, edges=edges, edge_pad=edge_pad, halo=halo, lat_count=lat_count),
                [((edge_pad + 2 * halo, cells), bf16)] * 2 + [((6 * halo, cells), bf16)] * 2,
                [((3, 1, cells), i32), ((3, 1, cells), f32)],
                by_level(cell_edges),
                by_level(edge_weight),
                raw=(0, 1),
                copies=2,
            )
        first = jnp.stack([inner_in[1], outer_in[1], lat_inner])
        second = jnp.stack([inner_in[2], outer_in[2], lat_outer])
        second_in = lax.ppermute(second, "lat", lat_routes[1])
        first_in = lax.ppermute(first, "lat", lat_routes[0])
        if phase == 0:
            normal, scale, edge_outer, edge_rest = call(
                edge_setup_kernel,
                [((rows, edge_pad), f32), ((1, edge_pad), f32), sent_outer(edge_pad), sent_rest(edge_pad)],
                [((levels, 1, edges), f32), (send_edges.shape[1:], i32), ((1, edges), f32)],
                by_level(velocity),
                send_edges[0],
                inv_dual,
                raw=(0, 1, 2),
                copies=3,
            )
        if phase == 1:
            speed, inverse, forward, back, cell_outer, cell_rest = call(
                cell_setup_kernel,
                [((1, cells), f32), column, column, column, sent_outer(cells), sent_rest(cells)],
                [((levels, 1, cells), f32), column],
                by_level(coupling),
                cell_list,
                sound_speed,
                raw=(0, 2),
                copies=2,
            )
        if at_cells:
            (total,) = call(
                part_kernel,
                [((rows, edge_pad), f32)],
                [((PARTS * rows, cells + 2 * halo), bf16)],
                values,
                inner_in,
                outer_in,
                gradient_near,
            )
            normal, outer, stack = call(
                edge_kernel,
                [((rows, edge_pad), f32), bundle, stack_edges],
                [stack_lat],
                total,
                first_in,
                second_in,
                gradient_far,
                normal,
                scale,
                edge_outer,
            )
        else:
            (total,) = call(
                part_kernel,
                [((rows, cells), f32)],
                [((PARTS * rows, edge_pad + 2 * halo), bf16)],
                normal,
                inner_in,
                outer_in,
                near_high,
                near_low,
            )
            operands = (total, first_in, second_in, far_high, far_low, values, speed, inverse, forward, back)
            if phase < 2 * NSUB - 1:
                values, outer, stack = call(
                    functools.partial(cell_kernel, levels=levels),
                    [((rows, cells), f32), bundle, stack_cells],
                    [stack_lat, column],
                    *operands,
                    cell_outer,
                )
            else:
                (values,) = call(functools.partial(last_kernel, levels=levels), [((levels, 1, cells), f32)], [stack_lat, column], *operands)
    return by_level(values), normal[:levels, :edges][None]


def solution(mesh):
    return jax.shard_map(
        functools.partial(on_device, mesh.shape["lat"], mesh.shape["lon"]),
        mesh=mesh,
        in_specs=(
            P("lat", None, "lon"),
            P("lat", None, "lon"),
            P("lat", None, "lon"),
            P("lat", None, "lon"),
            P("lat", None, "lon"),
            P("lat", None, "lon"),
            P("lat", "lon"),
            P("lat", None, "lon"),
            P("lat", "lon"),
            P("lat", None, "lon"),
        ),
        out_specs=(P("lat", None, "lon"), P("lat", None, "lon")),
        check_vma=False,
    )
```

time: 206 us -> 85.3 us (0.41)
  local copies, waits for them, and re-layouts: 92.4 us -> 5.38 us
  starting transfers between devices: 47.8 us -> 24.3 us
  Pallas kernels: 0 us -> 16.1 us
  other arithmetic: 13.8 us -> 0.06 us
  waiting for transfers between devices: 46.5 us -> 38.2 us
  between operations: 4.19 us -> 0.93 us
    gather x96 -> x0, local copies, waits for them, and re-layouts: 70.1 us -> none  [the longest x72 36.5 us: extend(): jnp.take(source, send_list[member], axis=1)]
    ppermute x24, starting transfers between devices: 47.8 us -> 24.3 us  [the longest x6 8.9 us: on_device(): outer_in = lax.ppermute(outer, 'lon', lon_routes[1])]
    pallas_call x0 -> x23, Pallas kernels: none -> 16.1 us  [call(): pl.pallas_call(body, out_shape=tuple((jax.ShapeDtypeStruct(shape, kind) f...]
    unnamed x459 -> x21, local copies, waits for them, and re-layouts: 19.8 us -> 5.33 us
    ppermute x24, waiting for transfers between devices: 46.5 us -> 38.2 us  [the longest x6 21.4 us: on_device(): outer_in = lax.ppermute(outer, 'lon', lon_routes[1])]
    sub x6 -> x0, other arithmetic: 3.21 us -> none  [the longest x3 2.42 us: column_solve(): result.insert(0, scaled[level_index] - ratios[level_index] * result[0])]
    unnamed x4 -> x0, other arithmetic: 3.21 us -> none
    div x3 -> x0, other arithmetic: 3.01 us -> none  [column_solve(): current = (right_side[level_index] - lower_term * scaled[-1]) / divisor]
  transfers between devices with their start and end apart: 24 -> 24, of which waited for: 20 -> 18; matrix products, arithmetic and copies ran while one was open for 7% -> 1% of each run, Pallas kernels for 0% -> 9%
where the time goes in v2:
time: 85.3 us; the launch traced here: 85 us
  waiting for transfers between devices  38.2 us (45%)
  starting transfers between devices  24.3 us (28%)
  Pallas kernels  16.1 us (19%)
  local copies, waits for them, and re-layouts  5.38 us (6%)
  between operations  0.93 us (1%)
    ppermute x6, waiting for transfers between devices, on_device(): outer_in = lax.ppermute(outer, 'lon', lon_routes[1])  21.4 us
    pallas_call x23, Pallas kernels, call(): pl.pallas_call(body, out_shape=tuple((jax.ShapeDtypeStruct(shape, kind) f...  16.1 us
    ppermute x6, waiting for transfers between devices, on_device(): second_in = lax.ppermute(second, 'lat', lat_routes[1])  9.04 us
    ppermute x6, starting transfers between devices, on_device(): outer_in = lax.ppermute(outer, 'lon', lon_routes[1])  8.9 us
    ppermute x6, starting transfers between devices, on_device(): first_in = lax.ppermute(first, 'lat', lat_routes[0])  7.43 us
    ppermute x6, starting transfers between devices, on_device(): second_in = lax.ppermute(second, 'lat', lat_routes[1])  7.02 us
    unnamed x21, local copies, waits for them, and re-layouts  5.33 us
    ppermute x6, waiting for transfers between devices, on_device(): first_in = lax.ppermute(first, 'lat', lat_routes[0])  4.2 us
  transfers between devices with their start and end apart: 24, of which 18 were waited for; matrix products, arithmetic and copies ran while one was open for 1% of the time, Pallas kernels for 9%

profile of v2, /device:TPU:0, one launch (start us, length us, event | category | flops | bytes accessed | tf_op | source)
XLA Modules:
  0.0 85.0 jit_solution(3293772456936699098)
XLA Ops:
  0.6 0.9 %copy-done.1 = f32[1,30,640]{2,0,1:T(1,128)S(1)} copy-done((f32[1,30,640]{2,0,1:T(1,128)S(1)}, f32[1,30,640]{2,0,1:T(1,128)}, u32[]{:S(2)}) %copy-start.1) | copy-done | bytes 76824
  1.5 0.7 copy-done.6
  2.2 1.2 %shard_map.113 = (f32[32,640]{1,0:T(8,128)S(1)}, bf16[96,640]{1,0:T(8,128)(2,1)S(1)}, f32[3,32,128]{2,1,0:T(8,128)S(1)}, bf16[640,384]{1,0:T(8,128)(2,1)}, s32[8,128]{1,0:T(8,128)S(1)}) custom-call(f32[30,1,640]{2,1,0:T(1,128)S(1)} %bitcast.24, s32[8,128]{1,0:T(8,128)S(1)} %bitcast.41), custom_call_target="tpu_custom_call" | custom-call | tf_op jit(solution)/shard_map/pallas_call | solution.py:345
  4.4 4.7 %collective-permute-start.1 = (f32[3,32,128]{2,1,0:T(8,128)S(1)}, f32[3,32,128]{2,1,0:T(8,128)S(1)}, u32[]{:S(2)}, u32[]{:S(2)}) collective-permute-start(f32[3,32,128]{2,1,0:T(8,128)S(1)} %get-tuple-element.59), channel_id=1, source_target_pairs={{0,7},{1,2},{2,1},{3,4},{4,3},{5,6},{6,5},{7,0},{8,15},{9,10},{10,... | collective-permute-start | bytes 147464 | tf_op jit(solution)/shard_map/ppermute | solution.py:387
  9.2 1.9 %collective-permute-done.1.outer_ref = f32[3,32,128]{2,1,0:T(8,128)S(1)} collective-permute-done((f32[3,32,128]{2,1,0:T(8,128)S(1)}, f32[3,32,128]{2,1,0:T(8,128)S(1)}, u32[]{:S(2)}, u32[]{:S(2)}) %collective-permute-start.1) | collective-permute-done | bytes 49184 | tf_op jit(solution)/shard_map/ppermute | solution.py:387
  11.0 1.6 %collective-permute-start.2 = (f32[3,32,128]{2,1,0:T(8,128)S(1)}, f32[3,32,128]{2,1,0:T(8,128)S(1)}, u32[]{:S(2)}, u32[]{:S(2)}) collective-permute-start(f32[3,32,128]{2,1,0:T(8,128)S(1)} %pad_maximum_fusion), channel_id=1, source_target_pairs={{0,8},{8,0},{16,24},{24,16},{1,9},{9,1},{17,25},{25,17},{2,10},{10... | collective-permute-start | bytes 147464 | tf_op jit(solution)/shard_map/ppermute | solution.py:415
  12.6 1.5 %collective-permute-start.3 = (f32[3,32,128]{2,1,0:T(8,128)S(1)}, f32[3,32,128]{2,1,0:T(8,128)S(1)}, u32[]{:S(2)}, u32[]{:S(2)}) collective-permute-start(f32[3,32,128]{2,1,0:T(8,128)S(1)} %pad_maximum_fusion.1), channel_id=1, source_target_pairs={{0,24},{8,16},{16,8},{24,0},{1,25},{9,17},{17,9},{25,1},{2,26},{10... | collective-permute-start | bytes 147464 | tf_op jit(solution)/shard_map/ppermute | solution.py:414
  14.1 0.7 copy-done.3
  14.8 0.8 shard_map.115
  15.6 0.9 %copy-done = f32[1,30,960]{2,0,1:T(1,128)S(1)} copy-done((f32[1,30,960]{2,0,1:T(1,128)S(1)}, f32[1,30,960]{2,0,1:T(1,128)}, u32[]{:S(2)}) %copy-start) | copy-done | bytes 115224
  16.5 0.7 copy-done.7
  17.2 0.7 copy-done.8
  17.9 0.7 shard_map.117
  20.2 2.9 %collective-permute-start.5 = (f32[3,32,128]{2,1,0:T(8,128)S(1)}, f32[3,32,128]{2,1,0:T(8,128)S(1)}, u32[]{:S(2)}, u32[]{:S(2)}) collective-permute-start(f32[3,32,128]{2,1,0:T(8,128)S(1)} %get-tuple-element.71), channel_id=1, source_target_pairs={{0,7},{1,2},{2,1},{3,4},{4,3},{5,6},{6,5},{7,0},{8,15},{9,10},{10,... | collective-permute-start | bytes 147464 | tf_op jit(solution)/shard_map/ppermute | solution.py:387
  23.1 2.9 %collective-permute-done.5.outer_ref = f32[3,32,128]{2,1,0:T(8,128)S(1)} collective-permute-done((f32[3,32,128]{2,1,0:T(8,128)S(1)}, f32[3,32,128]{2,1,0:T(8,128)S(1)}, u32[]{:S(2)}, u32[]{:S(2)}) %collective-permute-start.5) | collective-permute-done | bytes 49184 | tf_op jit(solution)/shard_map/ppermute | solution.py:387
  26.1 1.6 %collective-permute-start.6 = (f32[3,32,128]{2,1,0:T(8,128)S(1)}, f32[3,32,128]{2,1,0:T(8,128)S(1)}, u32[]{:S(2)}, u32[]{:S(2)}) collective-permute-start(f32[3,32,128]{2,1,0:T(8,128)S(1)} %pad_maximum_fusion.2), channel_id=1, source_target_pairs={{0,8},{8,0},{16,24},{24,16},{1,9},{9,1},{17,25},{25,17},{2,10},{10... | collective-permute-start | bytes 147464 | tf_op jit(solution)/shard_map/ppermute | solution.py:415
  28.1 0.7 shard_map.122
  28.9 1.7 %shard_map.120 = (bf16[1280,640]{1,0:T(8,128)(2,1)S(1)}, bf16[1280,640]{1,0:T(8,128)(2,1)S(1)}, bf16[768,640]{1,0:T(8,128)(2,1)S(1)}, bf16[768,640]{1,0:T(8,128)(2,1)S(1)}) custom-call(s32[3,1,640]{2,1,0:T(1,128)S(1)} %bitcast.39, f32[3,1,640]{2,1,0:T(1,128)S(1)} %bitcast.40), custom_call_target="tpu_custom_call" | custom-call | tf_op jit(solution)/shard_map/pallas_call | solution.py:345
  30.5 0.7 shard_map.121.total_ref
  31.2 1.4 %collective-permute-done.7.lat_outer_ref = f32[3,32,128]{2,1,0:T(8,128)S(1)} collective-permute-done((f32[3,32,128]{2,1,0:T(8,128)S(1)}, f32[3,32,128]{2,1,0:T(8,128)S(1)}, u32[]{:S(2)}, u32[]{:S(2)}) %collective-permute-start.7) | collective-permute-done | bytes 49184 | tf_op jit(solution)/shard_map/ppermute | solution.py:414
  32.6 1.2 %shard_map.123 = (f32[32,640]{1,0:T(8,128)S(1)}, f32[3,32,128]{2,1,0:T(8,128)S(1)}, bf16[96,640]{1,0:T(8,128)(2,1)S(1)}) custom-call(f32[32,640]{1,0:T(8,128)S(1)} %shard_map.121.total_ref, f32[3,32,128]{2,1,0:T(8,128)S(1)} %collective-permute-done.6.lat_inner_ref, f32[3,32,128]{2,1,0:T(8,128)S(1)} %collective-permute-done.7.lat_outer_ref, ...), custom_call_target="tpu_custom_call" | custom-call | tf_op jit(solution)/shard_map/pallas_call | solution.py:345
  34.1 1.0 %collective-permute-start.9 = (f32[3,32,128]{2,1,0:T(8,128)S(1)}, f32[3,32,128]{2,1,0:T(8,128)S(1)}, u32[]{:S(2)}, u32[]{:S(2)}) collective-permute-start(f32[3,32,128]{2,1,0:T(8,128)S(1)} %get-tuple-element.87), channel_id=1, source_target_pairs={{0,7},{1,2},{2,1},{3,4},{4,3},{5,6},{6,5},{7,0},{8,15},{9,10},{10,... | collective-permute-start | bytes 147464 | tf_op jit(solution)/shard_map/ppermute | solution.py:387
  35.4 4.2 %collective-permute-done.9.outer_ref = f32[3,32,128]{2,1,0:T(8,128)S(1)} collective-permute-done((f32[3,32,128]{2,1,0:T(8,128)S(1)}, f32[3,32,128]{2,1,0:T(8,128)S(1)}, u32[]{:S(2)}, u32[]{:S(2)}) %collective-permute-start.9) | collective-permute-done | bytes 49184 | tf_op jit(solution)/shard_map/ppermute | solution.py:387
  40.1 1.4 %collective-permute-start.11 = (f32[3,32,128]{2,1,0:T(8,128)S(1)}, f32[3,32,128]{2,1,0:T(8,128)S(1)}, u32[]{:S(2)}, u32[]{:S(2)}) collective-permute-start(f32[3,32,128]{2,1,0:T(8,128)S(1)} %pad_maximum_fusion.5), channel_id=1, source_target_pairs={{0,24},{8,16},{16,8},{24,0},{1,25},{9,17},{17,9},{25,1},{2,26},{10... | collective-permute-start | bytes 147464 | tf_op jit(solution)/shard_map/ppermute | solution.py:414
  42.0 1.7 %collective-permute-done.10.lat_inner_ref = f32[3,32,128]{2,1,0:T(8,128)S(1)} collective-permute-done((f32[3,32,128]{2,1,0:T(8,128)S(1)}, f32[3,32,128]{2,1,0:T(8,128)S(1)}, u32[]{:S(2)}, u32[]{:S(2)}) %collective-permute-start.10) | collective-permute-done | bytes 49184 | tf_op jit(solution)/shard_map/ppermute | solution.py:415
  43.7 1.4 %collective-permute-done.11.lat_outer_ref = f32[3,32,128]{2,1,0:T(8,128)S(1)} collective-permute-done((f32[3,32,128]{2,1,0:T(8,128)S(1)}, f32[3,32,128]{2,1,0:T(8,128)S(1)}, u32[]{:S(2)}, u32[]{:S(2)}) %collective-permute-start.11) | collective-permute-done | bytes 49184 | tf_op jit(solution)/shard_map/ppermute | solution.py:414
  46.3 1.1 %collective-permute-done.12.inner_ref = f32[3,32,128]{2,1,0:T(8,128)S(1)} collective-permute-done((f32[3,32,128]{2,1,0:T(8,128)S(1)}, f32[3,32,128]{2,1,0:T(8,128)S(1)}, u32[]{:S(2)}, u32[]{:S(2)}) %collective-permute-start.12) | collective-permute-done | bytes 49184 | tf_op jit(solution)/shard_map/ppermute | solution.py:392
  47.4 4.2 %collective-permute-done.13.outer_ref = f32[3,32,128]{2,1,0:T(8,128)S(1)} collective-permute-done((f32[3,32,128]{2,1,0:T(8,128)S(1)}, f32[3,32,128]{2,1,0:T(8,128)S(1)}, u32[]{:S(2)}, u32[]{:S(2)}) %collective-permute-start.13) | collective-permute-done | bytes 49184 | tf_op jit(solution)/shard_map/ppermute | solution.py:387
  51.6 1.6 %collective-permute-start.14 = (f32[3,32,128]{2,1,0:T(8,128)S(1)}, f32[3,32,128]{2,1,0:T(8,128)S(1)}, u32[]{:S(2)}, u32[]{:S(2)}) collective-permute-start(f32[3,32,128]{2,1,0:T(8,128)S(1)} %pad_maximum_fusion.6), channel_id=1, source_target_pairs={{0,8},{8,0},{16,24},{24,16},{1,9},{9,1},{17,25},{25,17},{2,10},{10... | collective-permute-start | bytes 147464 | tf_op jit(solution)/shard_map/ppermute | solution.py:415
  53.2 1.1 %collective-permute-start.15 = (f32[3,32,128]{2,1,0:T(8,128)S(1)}, f32[3,32,128]{2,1,0:T(8,128)S(1)}, u32[]{:S(2)}, u32[]{:S(2)}) collective-permute-start(f32[3,32,128]{2,1,0:T(8,128)S(1)} %pad_maximum_fusion.7), channel_id=1, source_target_pairs={{0,24},{8,16},{16,8},{24,0},{1,25},{9,17},{17,9},{25,1},{2,26},{10... | collective-permute-start | bytes 147464 | tf_op jit(solution)/shard_map/ppermute | solution.py:414
  54.3 0.7 shard_map.128.total_ref
  54.9 0.8 collective-permute-done.14.lat_inner_ref
  55.8 2.4 %collective-permute-done.15.lat_outer_ref = f32[3,32,128]{2,1,0:T(8,128)S(1)} collective-permute-done((f32[3,32,128]{2,1,0:T(8,128)S(1)}, f32[3,32,128]{2,1,0:T(8,128)S(1)}, u32[]{:S(2)}, u32[]{:S(2)}) %collective-permute-start.15) | collective-permute-done | bytes 49184 | tf_op jit(solution)/shard_map/ppermute | solution.py:414
  58.2 1.1 %shard_map.129 = (f32[32,640]{1,0:T(8,128)S(1)}, f32[3,32,128]{2,1,0:T(8,128)S(1)}, bf16[96,640]{1,0:T(8,128)(2,1)S(1)}) custom-call(f32[32,640]{1,0:T(8,128)S(1)} %shard_map.128.total_ref, f32[3,32,128]{2,1,0:T(8,128)S(1)} %collective-permute-done.14.lat_inner_ref, f32[3,32,128]{2,1,0:T(8,128)S(1)} %collective-permute-done.15.lat_outer_ref, ...), custom_call_target="tpu_custom_call" | custom-call | tf_op jit(solution)/shard_map/pallas_call | solution.py:345
  59.8 1.1 %collective-permute-done.16.inner_ref = f32[3,32,128]{2,1,0:T(8,128)S(1)} collective-permute-done((f32[3,32,128]{2,1,0:T(8,128)S(1)}, f32[3,32,128]{2,1,0:T(8,128)S(1)}, u32[]{:S(2)}, u32[]{:S(2)}) %collective-permute-start.16) | collective-permute-done | bytes 49184 | tf_op jit(solution)/shard_map/ppermute | solution.py:392
  60.9 4.2 %collective-permute-done.17.outer_ref = f32[3,32,128]{2,1,0:T(8,128)S(1)} collective-permute-done((f32[3,32,128]{2,1,0:T(8,128)S(1)}, f32[3,32,128]{2,1,0:T(8,128)S(1)}, u32[]{:S(2)}, u32[]{:S(2)}) %collective-permute-start.17) | collective-permute-done | bytes 49184 | tf_op jit(solution)/shard_map/ppermute | solution.py:387
  65.7 1.4 %collective-permute-start.19 = (f32[3,32,128]{2,1,0:T(8,128)S(1)}, f32[3,32,128]{2,1,0:T(8,128)S(1)}, u32[]{:S(2)}, u32[]{:S(2)}) collective-permute-start(f32[3,32,128]{2,1,0:T(8,128)S(1)} %pad_maximum_fusion.9), channel_id=1, source_target_pairs={{0,24},{8,16},{16,8},{24,0},{1,25},{9,17},{17,9},{25,1},{2,26},{10... | collective-permute-start | bytes 147464 | tf_op jit(solution)/shard_map/ppermute | solution.py:414
  67.6 1.7 %collective-permute-done.18.lat_inner_ref = f32[3,32,128]{2,1,0:T(8,128)S(1)} collective-permute-done((f32[3,32,128]{2,1,0:T(8,128)S(1)}, f32[3,32,128]{2,1,0:T(8,128)S(1)}, u32[]{:S(2)}, u32[]{:S(2)}) %collective-permute-start.18) | collective-permute-done | bytes 49184 | tf_op jit(solution)/shard_map/ppermute | solution.py:415
  69.2 1.4 %collective-permute-done.19.lat_outer_ref = f32[3,32,128]{2,1,0:T(8,128)S(1)} collective-permute-done((f32[3,32,128]{2,1,0:T(8,128)S(1)}, f32[3,32,128]{2,1,0:T(8,128)S(1)}, u32[]{:S(2)}, u32[]{:S(2)}) %collective-permute-start.19) | collective-permute-done | bytes 49184 | tf_op jit(solution)/shard_map/ppermute | solution.py:414
  70.7 0.7 shard_map.132
  71.8 1.1 %collective-permute-done.20.inner_ref = f32[3,32,128]{2,1,0:T(8,128)S(1)} collective-permute-done((f32[3,32,128]{2,1,0:T(8,128)S(1)}, f32[3,32,128]{2,1,0:T(8,128)S(1)}, u32[]{:S(2)}, u32[]{:S(2)}) %collective-permute-start.20) | collective-permute-done | bytes 49184 | tf_op jit(solution)/shard_map/ppermute | solution.py:392
  73.0 4.2 %collective-permute-done.21.outer_ref = f32[3,32,128]{2,1,0:T(8,128)S(1)} collective-permute-done((f32[3,32,128]{2,1,0:T(8,128)S(1)}, f32[3,32,128]{2,1,0:T(8,128)S(1)}, u32[]{:S(2)}, u32[]{:S(2)}) %collective-permute-start.21) | collective-permute-done | bytes 49184 | tf_op jit(solution)/shard_map/ppermute | solution.py:387
  77.2 1.6 %collective-permute-start.22 = (f32[3,32,128]{2,1,0:T(8,128)S(1)}, f32[3,32,128]{2,1,0:T(8,128)S(1)}, u32[]{:S(2)}, u32[]{:S(2)}) collective-permute-start(f32[3,32,128]{2,1,0:T(8,128)S(1)} %pad_maximum_fusion.10), channel_id=1, source_target_pairs={{0,8},{8,0},{16,24},{24,16},{1,9},{9,1},{17,25},{25,17},{2,10},{10... | collective-permute-start | bytes 147464 | tf_op jit(solution)/shard_map/ppermute | solution.py:415
  78.7 1.1 %collective-permute-start.23 = (f32[3,32,128]{2,1,0:T(8,128)S(1)}, f32[3,32,128]{2,1,0:T(8,128)S(1)}, u32[]{:S(2)}, u32[]{:S(2)}) collective-permute-start(f32[3,32,128]{2,1,0:T(8,128)S(1)} %pad_maximum_fusion.11), channel_id=1, source_target_pairs={{0,24},{8,16},{16,8},{24,0},{1,25},{9,17},{17,9},{25,1},{2,26},{10... | collective-permute-start | bytes 147464 | tf_op jit(solution)/shard_map/ppermute | solution.py:414
  79.8 0.8 copy.12
  80.6 0.7 shard_map.134.total_ref
  81.3 2.4 %collective-permute-done.23.lat_outer_ref = f32[3,32,128]{2,1,0:T(8,128)S(1)} collective-permute-done((f32[3,32,128]{2,1,0:T(8,128)S(1)}, f32[3,32,128]{2,1,0:T(8,128)S(1)}, u32[]{:S(2)}, u32[]{:S(2)}) %collective-permute-start.23) | collective-permute-done | bytes 49184 | tf_op jit(solution)/shard_map/ppermute | solution.py:414
  83.7 1.3 %shard_map.135 = f32[30,1,640]{2,1,0:T(1,128)} custom-call(f32[32,640]{1,0:T(8,128)S(1)} %shard_map.134.total_ref, f32[3,32,128]{2,1,0:T(8,128)S(1)} %collective-permute-done.22.lat_inner_ref, f32[3,32,128]{2,1,0:T(8,128)S(1)} %collective-permute-done.23.lat_outer_ref, bf16[768,640]{1,0:T(8,128)(2,1)S(1)} %get-tuple-element.76.high_ref, ...), custom_call_target="tpu_custom_call" | custom-call | tf_op jit(solution)/shard_map/pallas_call | solution.py:345
  (69 shorter events, 7.9 us)
Async XLA Ops:
  0.6 0.9 %copy-start.1 = (f32[1,30,640]{2,0,1:T(1,128)S(1)}, f32[1,30,640]{2,0,1:T(1,128)}, u32[]{:S(2)}) copy-start(f32[1,30,640]{2,0,1:T(1,128)} %param.10) | copy-start | bytes 230404
  1.5 0.7 copy-start.6
  3.9 5.3 %collective-permute-start = (f32[3,32,128]{2,1,0:T(8,128)S(1)}, f32[3,32,128]{2,1,0:T(8,128)S(1)}, u32[]{:S(2)}, u32[]{:S(2)}) collective-permute-start(f32[3,32,128]{2,1,0:T(8,128)S(1)} %get-tuple-element.58), channel_id=1, source_target_pairs={{0,1},{1,0},{2,3},{3,2},{4,5},{5,4},{6,7},{7,6},{8,9},{9,8},{10,11... | collective-permute-start | bytes 147464 | tf_op jit(solution)/shard_map/ppermute | solution.py:392
  4.4 6.6 %collective-permute-start.1 = (f32[3,32,128]{2,1,0:T(8,128)S(1)}, f32[3,32,128]{2,1,0:T(8,128)S(1)}, u32[]{:S(2)}, u32[]{:S(2)}) collective-permute-start(f32[3,32,128]{2,1,0:T(8,128)S(1)} %get-tuple-element.59), channel_id=1, source_target_pairs={{0,7},{1,2},{2,1},{3,4},{4,3},{5,6},{6,5},{7,0},{8,15},{9,10},{10,... | collective-permute-start | bytes 147464 | tf_op jit(solution)/shard_map/ppermute | solution.py:387
  11.0 8.0 %collective-permute-start.2 = (f32[3,32,128]{2,1,0:T(8,128)S(1)}, f32[3,32,128]{2,1,0:T(8,128)S(1)}, u32[]{:S(2)}, u32[]{:S(2)}) collective-permute-start(f32[3,32,128]{2,1,0:T(8,128)S(1)} %pad_maximum_fusion), channel_id=1, source_target_pairs={{0,8},{8,0},{16,24},{24,16},{1,9},{9,1},{17,25},{25,17},{2,10},{10... | collective-permute-start | bytes 147464 | tf_op jit(solution)/shard_map/ppermute | solution.py:415
  12.6 6.5 %collective-permute-start.3 = (f32[3,32,128]{2,1,0:T(8,128)S(1)}, f32[3,32,128]{2,1,0:T(8,128)S(1)}, u32[]{:S(2)}, u32[]{:S(2)}) collective-permute-start(f32[3,32,128]{2,1,0:T(8,128)S(1)} %pad_maximum_fusion.1), channel_id=1, source_target_pairs={{0,24},{8,16},{16,8},{24,0},{1,25},{9,17},{17,9},{25,1},{2,26},{10... | collective-permute-start | bytes 147464 | tf_op jit(solution)/shard_map/ppermute | solution.py:414
  14.1 0.7 copy-start.3
  15.6 0.9 %copy-start = (f32[1,30,960]{2,0,1:T(1,128)S(1)}, f32[1,30,960]{2,0,1:T(1,128)}, u32[]{:S(2)}) copy-start(f32[1,30,960]{2,0,1:T(1,128)} %param.11) | copy-start | bytes 345604
  16.5 0.7 copy-start.7
  17.2 0.7 copy-start.8
  19.1 9.1 %copy-start.2 = (f32[1,30,640]{2,0,1:T(1,128)S(1)}, f32[1,30,640]{2,0,1:T(1,128)}, u32[]{:S(2)}) copy-start(f32[1,30,640]{2,0,1:T(1,128)} %param.19) | copy-start | bytes 230404
  19.1 9.1 %copy-start.9 = (f32[1,640]{1,0:T(1,128)S(1)}, f32[1,640]{1,0:T(1,128)}, u32[]{:S(2)}) copy-start(f32[1,640]{1,0:T(1,128)} %speed_hbm.1) | copy-start | bytes 7684
  19.7 9.1 %copy-start.4 = (s32[1,3,640]{2,0,1:T(1,128)S(1)}, s32[1,3,640]{2,0,1:T(1,128)}, u32[]{:S(2)}) copy-start(s32[1,3,640]{2,0,1:T(1,128)} %param.13) | copy-start | bytes 23044
  19.7 9.1 %copy-start.5 = (f32[1,3,640]{2,0,1:T(1,128)S(1)}, f32[1,3,640]{2,0,1:T(1,128)}, u32[]{:S(2)}) copy-start(f32[1,3,640]{2,0,1:T(1,128)} %param.17) | copy-start | bytes 23044
  20.1 3.0 %collective-permute-start.4 = (f32[3,32,128]{2,1,0:T(8,128)S(1)}, f32[3,32,128]{2,1,0:T(8,128)S(1)}, u32[]{:S(2)}, u32[]{:S(2)}) collective-permute-start(f32[3,32,128]{2,1,0:T(8,128)S(1)} %get-tuple-element.70), channel_id=1, source_target_pairs={{0,1},{1,0},{2,3},{3,2},{4,5},{5,4},{6,7},{7,6},{8,9},{9,8},{10,11... | collective-permute-start | bytes 147464 | tf_op jit(solution)/shard_map/ppermute | solution.py:392
  20.2 5.9 %collective-permute-start.5 = (f32[3,32,128]{2,1,0:T(8,128)S(1)}, f32[3,32,128]{2,1,0:T(8,128)S(1)}, u32[]{:S(2)}, u32[]{:S(2)}) collective-permute-start(f32[3,32,128]{2,1,0:T(8,128)S(1)} %get-tuple-element.71), channel_id=1, source_target_pairs={{0,7},{1,2},{2,1},{3,4},{4,3},{5,6},{6,5},{7,0},{8,15},{9,10},{10,... | collective-permute-start | bytes 147464 | tf_op jit(solution)/shard_map/ppermute | solution.py:387
  26.1 5.2 %collective-permute-start.6 = (f32[3,32,128]{2,1,0:T(8,128)S(1)}, f32[3,32,128]{2,1,0:T(8,128)S(1)}, u32[]{:S(2)}, u32[]{:S(2)}) collective-permute-start(f32[3,32,128]{2,1,0:T(8,128)S(1)} %pad_maximum_fusion.2), channel_id=1, source_target_pairs={{0,8},{8,0},{16,24},{24,16},{1,9},{9,1},{17,25},{25,17},{2,10},{10... | collective-permute-start | bytes 147464 | tf_op jit(solution)/shard_map/ppermute | solution.py:415
  27.6 5.0 %collective-permute-start.7 = (f32[3,32,128]{2,1,0:T(8,128)S(1)}, f32[3,32,128]{2,1,0:T(8,128)S(1)}, u32[]{:S(2)}, u32[]{:S(2)}) collective-permute-start(f32[3,32,128]{2,1,0:T(8,128)S(1)} %pad_maximum_fusion.3), channel_id=1, source_target_pairs={{0,24},{8,16},{16,8},{24,0},{1,25},{9,17},{17,9},{25,1},{2,26},{10... | collective-permute-start | bytes 147464 | tf_op jit(solution)/shard_map/ppermute | solution.py:414
  34.1 1.3 %collective-permute-start.8 = (f32[3,32,128]{2,1,0:T(8,128)S(1)}, f32[3,32,128]{2,1,0:T(8,128)S(1)}, u32[]{:S(2)}, u32[]{:S(2)}) collective-permute-start(f32[3,32,128]{2,1,0:T(8,128)S(1)} %get-tuple-element.86), channel_id=1, source_target_pairs={{0,1},{1,0},{2,3},{3,2},{4,5},{5,4},{6,7},{7,6},{8,9},{9,8},{10,11... | collective-permute-start | bytes 147464 | tf_op jit(solution)/shard_map/ppermute | solution.py:392
  34.1 5.4 %collective-permute-start.9 = (f32[3,32,128]{2,1,0:T(8,128)S(1)}, f32[3,32,128]{2,1,0:T(8,128)S(1)}, u32[]{:S(2)}, u32[]{:S(2)}) collective-permute-start(f32[3,32,128]{2,1,0:T(8,128)S(1)} %get-tuple-element.87), channel_id=1, source_target_pairs={{0,7},{1,2},{2,1},{3,4},{4,3},{5,6},{6,5},{7,0},{8,15},{9,10},{10,... | collective-permute-start | bytes 147464 | tf_op jit(solution)/shard_map/ppermute | solution.py:387
  39.5 4.2 %collective-permute-start.10 = (f32[3,32,128]{2,1,0:T(8,128)S(1)}, f32[3,32,128]{2,1,0:T(8,128)S(1)}, u32[]{:S(2)}, u32[]{:S(2)}) collective-permute-start(f32[3,32,128]{2,1,0:T(8,128)S(1)} %pad_maximum_fusion.4), channel_id=1, source_target_pairs={{0,8},{8,0},{16,24},{24,16},{1,9},{9,1},{17,25},{25,17},{2,10},{10... | collective-permute-start | bytes 147464 | tf_op jit(solution)/shard_map/ppermute | solution.py:415
  40.1 5.0 %collective-permute-start.11 = (f32[3,32,128]{2,1,0:T(8,128)S(1)}, f32[3,32,128]{2,1,0:T(8,128)S(1)}, u32[]{:S(2)}, u32[]{:S(2)}) collective-permute-start(f32[3,32,128]{2,1,0:T(8,128)S(1)} %pad_maximum_fusion.5), channel_id=1, source_target_pairs={{0,24},{8,16},{16,8},{24,0},{1,25},{9,17},{17,9},{25,1},{2,26},{10... | collective-permute-start | bytes 147464 | tf_op jit(solution)/shard_map/ppermute | solution.py:414
  46.1 1.3 %collective-permute-start.12 = (f32[3,32,128]{2,1,0:T(8,128)S(1)}, f32[3,32,128]{2,1,0:T(8,128)S(1)}, u32[]{:S(2)}, u32[]{:S(2)}) collective-permute-start(f32[3,32,128]{2,1,0:T(8,128)S(1)} %get-tuple-element.92), channel_id=1, source_target_pairs={{0,1},{1,0},{2,3},{3,2},{4,5},{5,4},{6,7},{7,6},{8,9},{9,8},{10,11... | collective-permute-start | bytes 147464 | tf_op jit(solution)/shard_map/ppermute | solution.py:392
  46.2 5.4 %collective-permute-start.13 = (f32[3,32,128]{2,1,0:T(8,128)S(1)}, f32[3,32,128]{2,1,0:T(8,128)S(1)}, u32[]{:S(2)}, u32[]{:S(2)}) collective-permute-start(f32[3,32,128]{2,1,0:T(8,128)S(1)} %get-tuple-element.93), channel_id=1, source_target_pairs={{0,7},{1,2},{2,1},{3,4},{4,3},{5,6},{6,5},{7,0},{8,15},{9,10},{10,... | collective-permute-start | bytes 147464 | tf_op jit(solution)/shard_map/ppermute | solution.py:387
  51.6 4.2 %collective-permute-start.14 = (f32[3,32,128]{2,1,0:T(8,128)S(1)}, f32[3,32,128]{2,1,0:T(8,128)S(1)}, u32[]{:S(2)}, u32[]{:S(2)}) collective-permute-start(f32[3,32,128]{2,1,0:T(8,128)S(1)} %pad_maximum_fusion.6), channel_id=1, source_target_pairs={{0,8},{8,0},{16,24},{24,16},{1,9},{9,1},{17,25},{25,17},{2,10},{10... | collective-permute-start | bytes 147464 | tf_op jit(solution)/shard_map/ppermute | solution.py:415
  53.2 5.0 %collective-permute-start.15 = (f32[3,32,128]{2,1,0:T(8,128)S(1)}, f32[3,32,128]{2,1,0:T(8,128)S(1)}, u32[]{:S(2)}, u32[]{:S(2)}) collective-permute-start(f32[3,32,128]{2,1,0:T(8,128)S(1)} %pad_maximum_fusion.7), channel_id=1, source_target_pairs={{0,24},{8,16},{16,8},{24,0},{1,25},{9,17},{17,9},{25,1},{2,26},{10... | collective-permute-start | bytes 147464 | tf_op jit(solution)/shard_map/ppermute | solution.py:414
  59.6 1.3 %collective-permute-start.16 = (f32[3,32,128]{2,1,0:T(8,128)S(1)}, f32[3,32,128]{2,1,0:T(8,128)S(1)}, u32[]{:S(2)}, u32[]{:S(2)}) collective-permute-start(f32[3,32,128]{2,1,0:T(8,128)S(1)} %get-tuple-element.98), channel_id=1, source_target_pairs={{0,1},{1,0},{2,3},{3,2},{4,5},{5,4},{6,7},{7,6},{8,9},{9,8},{10,11... | collective-permute-start | bytes 147464 | tf_op jit(solution)/shard_map/ppermute | solution.py:392
  59.7 5.4 %collective-permute-start.17 = (f32[3,32,128]{2,1,0:T(8,128)S(1)}, f32[3,32,128]{2,1,0:T(8,128)S(1)}, u32[]{:S(2)}, u32[]{:S(2)}) collective-permute-start(f32[3,32,128]{2,1,0:T(8,128)S(1)} %get-tuple-element.99), channel_id=1, source_target_pairs={{0,7},{1,2},{2,1},{3,4},{4,3},{5,6},{6,5},{7,0},{8,15},{9,10},{10,... | collective-permute-start | bytes 147464 | tf_op jit(solution)/shard_map/ppermute | solution.py:387
  65.1 4.2 %collective-permute-start.18 = (f32[3,32,128]{2,1,0:T(8,128)S(1)}, f32[3,32,128]{2,1,0:T(8,128)S(1)}, u32[]{:S(2)}, u32[]{:S(2)}) collective-permute-start(f32[3,32,128]{2,1,0:T(8,128)S(1)} %pad_maximum_fusion.8), channel_id=1, source_target_pairs={{0,8},{8,0},{16,24},{24,16},{1,9},{9,1},{17,25},{25,17},{2,10},{10... | collective-permute-start | bytes 147464 | tf_op jit(solution)/shard_map/ppermute | solution.py:415
  65.7 5.0 %collective-permute-start.19 = (f32[3,32,128]{2,1,0:T(8,128)S(1)}, f32[3,32,128]{2,1,0:T(8,128)S(1)}, u32[]{:S(2)}, u32[]{:S(2)}) collective-permute-start(f32[3,32,128]{2,1,0:T(8,128)S(1)} %pad_maximum_fusion.9), channel_id=1, source_target_pairs={{0,24},{8,16},{16,8},{24,0},{1,25},{9,17},{17,9},{25,1},{2,26},{10... | collective-permute-start | bytes 147464 | tf_op jit(solution)/shard_map/ppermute | solution.py:414
  71.7 1.3 %collective-permute-start.20 = (f32[3,32,128]{2,1,0:T(8,128)S(1)}, f32[3,32,128]{2,1,0:T(8,128)S(1)}, u32[]{:S(2)}, u32[]{:S(2)}) collective-permute-start(f32[3,32,128]{2,1,0:T(8,128)S(1)} %get-tuple-element.104), channel_id=1, source_target_pairs={{0,1},{1,0},{2,3},{3,2},{4,5},{5,4},{6,7},{7,6},{8,9},{9,8},{10,11... | collective-permute-start | bytes 147464 | tf_op jit(solution)/shard_map/ppermute | solution.py:392
  71.8 5.4 %collective-permute-start.21 = (f32[3,32,128]{2,1,0:T(8,128)S(1)}, f32[3,32,128]{2,1,0:T(8,128)S(1)}, u32[]{:S(2)}, u32[]{:S(2)}) collective-permute-start(f32[3,32,128]{2,1,0:T(8,128)S(1)} %get-tuple-element.105), channel_id=1, source_target_pairs={{0,7},{1,2},{2,1},{3,4},{4,3},{5,6},{6,5},{7,0},{8,15},{9,10},{10,... | collective-permute-start | bytes 147464 | tf_op jit(solution)/shard_map/ppermute | solution.py:387
  77.2 4.2 %collective-permute-start.22 = (f32[3,32,128]{2,1,0:T(8,128)S(1)}, f32[3,32,128]{2,1,0:T(8,128)S(1)}, u32[]{:S(2)}, u32[]{:S(2)}) collective-permute-start(f32[3,32,128]{2,1,0:T(8,128)S(1)} %pad_maximum_fusion.10), channel_id=1, source_target_pairs={{0,8},{8,0},{16,24},{24,16},{1,9},{9,1},{17,25},{25,17},{2,10},{10... | collective-permute-start | bytes 147464 | tf_op jit(solution)/shard_map/ppermute | solution.py:415
  78.7 5.0 %collective-permute-start.23 = (f32[3,32,128]{2,1,0:T(8,128)S(1)}, f32[3,32,128]{2,1,0:T(8,128)S(1)}, u32[]{:S(2)}, u32[]{:S(2)}) collective-permute-start(f32[3,32,128]{2,1,0:T(8,128)S(1)} %pad_maximum_fusion.11), channel_id=1, source_target_pairs={{0,24},{8,16},{16,8},{24,0},{1,25},{9,17},{17,9},{25,1},{2,26},{10... | collective-permute-start | bytes 147464 | tf_op jit(solution)/shard_map/ppermute | solution.py:414

commit v3 on v2

--- a/solution.py
+++ b/solution.py
@@ -88,11 +88,15 @@
     return sum_parts(product, rows)
 
 
-def fetch(pairs, sems):
+def start_fetch(pairs, sems):
     copies = [pltpu.make_async_copy(source, target, sems.at[i]) for i, (source, target) in enumerate(pairs)]
     for copy in copies:
         copy.start()
-    for copy in copies:
+    return copies
+
+
+def fetch(pairs, sems):
+    for copy in start_fetch(pairs, sems):
         copy.wait()
 
 
@@ -139,11 +143,13 @@
     lat_outer_ref[...] = pieces[:, 4 * halo : 5 * halo]
 
 
-def start_kernel(pressure_hbm, list_hbm, cells_ref, stack_ref, outer_ref, matrix_ref, lists_ref, pressure_ref, sems):
-    fetch([(list_hbm, lists_ref), (pressure_hbm, pressure_ref)], sems)
+def start_kernel(pressure_hbm, list_hbm, cells_ref, stack_ref, outer_ref, lists_ref, pressure_ref, matrix_ref, sems):
+    lists, pressure = start_fetch([(list_hbm, lists_ref), (pressure_hbm, pressure_ref)], sems)
     levels = pressure_ref.shape[0]
     rows = cells_ref.shape[0]
+    lists.wait()
     fill_sent(matrix_ref, lists_ref, OUTER_SENT)
+    pressure.wait()
     cells_ref[0:levels, :] = pressure_ref[:, 0, :]
     cells_ref[levels:rows, :] = jnp.zeros((rows - levels, cells_ref.shape[1]), f32)
     put_parts(stack_ref, cells_ref[...], 0)
@@ -185,14 +191,17 @@
 
 
 def edge_setup_kernel(velocity_hbm, list_hbm, dual_hbm, edges_ref, scale_ref, outer_matrix_ref, rest_matrix_ref, velocity_ref, list_ref, dual_ref, sems):
-    fetch([(list_hbm, list_ref), (velocity_hbm, velocity_ref), (dual_hbm, dual_ref)], sems)
+    lists, velocity, dual = start_fetch([(list_hbm, list_ref), (velocity_hbm, velocity_ref), (dual_hbm, dual_ref)], sems)
     levels, _, edges = velocity_ref.shape
     edges_ref[...] = jnp.zeros(edges_ref.shape, f32)
-    edges_ref[0:levels, 0:edges] = velocity_ref[:, 0, :]
     scale_ref[...] = jnp.zeros(scale_ref.shape, f32)
-    scale_ref[:, 0:edges] = STEP_SCALE * dual_ref[...]
+    lists.wait()
     fill_sent(outer_matrix_ref, list_ref, OUTER_SENT)
     fill_sent(rest_matrix_ref, list_ref, REST_SENT)
+    velocity.wait()
+    dual.wait()
+    edges_ref[0:levels, 0:edges] = velocity_ref[:, 0, :]
+    scale_ref[:, 0:edges] = STEP_SCALE * dual_ref[...]
 
 
 def weight_kernel(
@@ -230,8 +239,12 @@
 def cell_setup_kernel(
     coupling_hbm, list_ref, speed_hbm, speed_ref, inverse_ref, forward_ref, back_ref, outer_matrix_ref, rest_matrix_ref, coupling_ref, column_ref, sems
 ):
-    fetch([(coupling_hbm, coupling_ref), (speed_hbm, speed_ref)], sems)
+    coupling, speed = start_fetch([(coupling_hbm, coupling_ref), (speed_hbm, speed_ref)], sems)
     levels, _, cells = coupling_ref.shape
+    fill_sent(outer_matrix_ref, list_ref, OUTER_SENT)
+    fill_sent(rest_matrix_ref, list_ref, REST_SENT)
+    coupling.wait()
+    speed.wait()
     for group in range(cells // LANES):
         column_ref[0:levels, group, :] = coupling_ref[:, 0, group * LANES : (group + 1) * LANES]
     above = column_ref[0]
@@ -247,8 +260,6 @@
         forward_ref[level] = below * inverse
         ratio = above * inverse
         back_ref[level] = ratio
-    fill_sent(outer_matrix_ref, list_ref, OUTER_SENT)
-    fill_sent(rest_matrix_ref, list_ref, REST_SENT)
 
 
 def part_kernel(own_ref, inner_ref, outer_ref, *rest):
@@ -342,6 +353,7 @@
     scratch_shapes = [pltpu.VMEM(shape, kind) for shape, kind in scratch]
     if copies:
         scratch_shapes.append(pltpu.SemaphoreType.DMA((copies,)))
+    operands = [pltpu.with_memory_space_constraint(x, pltpu.HBM) if i in raw else x for i, x in enumerate(operands)]
     return pl.pallas_call(
         body,
         out_shape=tuple(jax.ShapeDtypeStruct(shape, kind) for shape, kind in outs),
@@ -375,10 +387,10 @@
     for phase in range(2 * NSUB):
         at_cells = phase % 2 == 0
         if phase == 0:
-            values, stack, outer, cell_outer, cell_list = call(
+            values, stack, outer, cell_list = call(
                 start_kernel,
-                [((rows, cells), f32), stack_cells, bundle, sent_outer(cells), (send_cells.shape[1:], i32)],
-                [((levels, 1, cells), f32)],
+                [((rows, cells), f32), stack_cells, bundle, (send_cells.shape[1:], i32)],
+                [((levels, 1, cells), f32), sent_outer(cells)],
                 by_level(pressure),
                 send_cells[0],
                 raw=(0, 1),

time: 85.3 us -> 82.6 us (0.968)
  local copies, waits for them, and re-layouts: 5.38 us -> 0.82 us
  waiting for transfers between devices: 38.2 us -> 35 us
  starting transfers between devices: 24.3 us -> 26.9 us
  Pallas kernels: 16.1 us -> 18.6 us
    unnamed x21 -> x1, local copies, waits for them, and re-layouts: 5.33 us -> 0.78 us
    pallas_call x23, Pallas kernels: 16.1 us -> 18.6 us  [call(): pl.pallas_call(body, out_shape=tuple((jax.ShapeDtypeStruct(shape, kind) f...]
    ppermute x6, starting transfers between devices: 7.02 us -> 9.06 us  [on_device(): second_in = lax.ppermute(second, 'lat', lat_routes[1])]
    ppermute x6, waiting for transfers between devices: 9.04 us -> 7.53 us  [on_device(): second_in = lax.ppermute(second, 'lat', lat_routes[1])]
    ppermute x6, waiting for transfers between devices: 4.2 us -> 3.33 us  [on_device(): first_in = lax.ppermute(first, 'lat', lat_routes[0])]
  transfers between devices with their start and end apart: 24 -> 24, of which waited for: 18 -> 17; matrix products, arithmetic and copies ran while one was open for 1% -> 1% of each run, Pallas kernels for 9% -> 12%
where the time goes in v3:
time: 82.6 us; the launch traced here: 82.2 us
  waiting for transfers between devices  35 us (42%)
  starting transfers between devices  26.9 us (33%)
  Pallas kernels  18.6 us (23%)
  between operations  0.86 us (1%)
    ppermute x6, waiting for transfers between devices, on_device(): outer_in = lax.ppermute(outer, 'lon', lon_routes[1])  21.1 us
    pallas_call x23, Pallas kernels, call(): pl.pallas_call(body, out_shape=tuple((jax.ShapeDtypeStruct(shape, kind) f...  18.6 us
    ppermute x6, starting transfers between devices, on_device(): outer_in = lax.ppermute(outer, 'lon', lon_routes[1])  9.52 us
    ppermute x6, starting transfers between devices, on_device(): second_in = lax.ppermute(second, 'lat', lat_routes[1])  9.06 us
    ppermute x6, waiting for transfers between devices, on_device(): second_in = lax.ppermute(second, 'lat', lat_routes[1])  7.53 us
    ppermute x6, starting transfers between devices, on_device(): first_in = lax.ppermute(first, 'lat', lat_routes[0])  7.41 us
    ppermute x6, waiting for transfers between devices, on_device(): first_in = lax.ppermute(first, 'lat', lat_routes[0])  3.33 us
    ppermute x6, waiting for transfers between devices, on_device(): inner_in = lax.ppermute(inner, 'lon', lon_routes[0])  3.03 us
  transfers between devices with their start and end apart: 24, of which 17 were waited for; matrix products, arithmetic and copies ran while one was open for 1% of the time, Pallas kernels for 12%

profile of v3, /device:TPU:0, one launch (start us, length us, event | category | flops | bytes accessed | tf_op | source)
XLA Modules:
  0.0 82.2 jit_solution(12175466990249484066)
XLA Ops:
  0.6 1.2 %shard_map.113 = (f32[32,640]{1,0:T(8,128)S(1)}, bf16[96,640]{1,0:T(8,128)(2,1)S(1)}, f32[3,32,128]{2,1,0:T(8,128)S(1)}, s32[8,128]{1,0:T(8,128)S(1)}) custom-call(f32[30,1,640]{2,1,0:T(1,128)} %bitcast.36, s32[8,128]{1,0:T(8,128)} %bitcast.42), custom_call_target="tpu_custom_call" | custom-call | tf_op jit(solution)/shard_map/pallas_call | solution.py:357
  1.8 0.5 shard_map.114
  2.3 0.6 collective-permute-start
  2.9 4.7 %collective-permute-start.1 = (f32[3,32,128]{2,1,0:T(8,128)S(1)}, f32[3,32,128]{2,1,0:T(8,128)S(1)}, u32[]{:S(2)}, u32[]{:S(2)}) collective-permute-start(f32[3,32,128]{2,1,0:T(8,128)S(1)} %get-tuple-element.59), channel_id=1, source_target_pairs={{0,7},{1,2},{2,1},{3,4},{4,3},{5,6},{6,5},{7,0},{8,15},{9,10},{10,... | collective-permute-start | bytes 147464 | tf_op jit(solution)/shard_map/ppermute | solution.py:399
  7.6 1.9 %collective-permute-done.1.outer_ref = f32[3,32,128]{2,1,0:T(8,128)S(1)} collective-permute-done((f32[3,32,128]{2,1,0:T(8,128)S(1)}, f32[3,32,128]{2,1,0:T(8,128)S(1)}, u32[]{:S(2)}, u32[]{:S(2)}) %collective-permute-start.1) | collective-permute-done | bytes 49184 | tf_op jit(solution)/shard_map/ppermute | solution.py:399
  9.4 1.6 %collective-permute-start.2 = (f32[3,32,128]{2,1,0:T(8,128)S(1)}, f32[3,32,128]{2,1,0:T(8,128)S(1)}, u32[]{:S(2)}, u32[]{:S(2)}) collective-permute-start(f32[3,32,128]{2,1,0:T(8,128)S(1)} %pad_maximum_fusion), channel_id=1, source_target_pairs={{0,8},{8,0},{16,24},{24,16},{1,9},{9,1},{17,25},{25,17},{2,10},{10... | collective-permute-start | bytes 147464 | tf_op jit(solution)/shard_map/ppermute | solution.py:427
  11.0 1.5 %collective-permute-start.3 = (f32[3,32,128]{2,1,0:T(8,128)S(1)}, f32[3,32,128]{2,1,0:T(8,128)S(1)}, u32[]{:S(2)}, u32[]{:S(2)}) collective-permute-start(f32[3,32,128]{2,1,0:T(8,128)S(1)} %pad_maximum_fusion.1), channel_id=1, source_target_pairs={{0,24},{8,16},{16,8},{24,0},{1,25},{9,17},{17,9},{25,1},{2,26},{10... | collective-permute-start | bytes 147464 | tf_op jit(solution)/shard_map/ppermute | solution.py:426
  12.5 1.5 %shard_map.115 = (bf16[896,1024]{1,0:T(8,128)(2,1)S(1)}, bf16[768,1024]{1,0:T(8,128)(2,1)S(1)}) custom-call(s32[2,960]{1,0:T(2,128)} %bitcast.39), custom_call_target="tpu_custom_call" | custom-call | tf_op jit(solution)/shard_map/pallas_call | solution.py:357
  14.0 1.3 %shard_map.117 = (f32[32,1024]{1,0:T(8,128)S(1)}, f32[1,1024]{1,0:T(1,128)S(1)}, bf16[1024,384]{1,0:T(8,128)(2,1)S(1)}, bf16[1024,640]{1,0:T(8,128)(2,1)S(1)}) custom-call(f32[30,1,960]{2,1,0:T(1,128)} %bitcast.35, s32[8,128]{1,0:T(8,128)} %bitcast.43, f32[1,960]{1,0:T(1,128)} %dual_hbm.1), custom_call_target="tpu_custom_call" | custom-call | tf_op jit(solution)/shard_map/pallas_call | solution.py:357
  16.0 0.6 shard_map.118
  17.1 2.7 %collective-permute-start.5 = (f32[3,32,128]{2,1,0:T(8,128)S(1)}, f32[3,32,128]{2,1,0:T(8,128)S(1)}, u32[]{:S(2)}, u32[]{:S(2)}) collective-permute-start(f32[3,32,128]{2,1,0:T(8,128)S(1)} %get-tuple-element.71), channel_id=1, source_target_pairs={{0,7},{1,2},{2,1},{3,4},{4,3},{5,6},{6,5},{7,0},{8,15},{9,10},{10,... | collective-permute-start | bytes 147464 | tf_op jit(solution)/shard_map/ppermute | solution.py:399
  19.8 2.9 %collective-permute-done.5.outer_ref = f32[3,32,128]{2,1,0:T(8,128)S(1)} collective-permute-done((f32[3,32,128]{2,1,0:T(8,128)S(1)}, f32[3,32,128]{2,1,0:T(8,128)S(1)}, u32[]{:S(2)}, u32[]{:S(2)}) %collective-permute-start.5) | collective-permute-done | bytes 49184 | tf_op jit(solution)/shard_map/ppermute | solution.py:399
  22.7 1.6 %collective-permute-start.6 = (f32[3,32,128]{2,1,0:T(8,128)S(1)}, f32[3,32,128]{2,1,0:T(8,128)S(1)}, u32[]{:S(2)}, u32[]{:S(2)}) collective-permute-start(f32[3,32,128]{2,1,0:T(8,128)S(1)} %pad_maximum_fusion.2), channel_id=1, source_target_pairs={{0,8},{8,0},{16,24},{24,16},{1,9},{9,1},{17,25},{25,17},{2,10},{10... | collective-permute-start | bytes 147464 | tf_op jit(solution)/shard_map/ppermute | solution.py:427
  24.3 1.3 %collective-permute-start.7 = (f32[3,32,128]{2,1,0:T(8,128)S(1)}, f32[3,32,128]{2,1,0:T(8,128)S(1)}, u32[]{:S(2)}, u32[]{:S(2)}) collective-permute-start(f32[3,32,128]{2,1,0:T(8,128)S(1)} %pad_maximum_fusion.3), channel_id=1, source_target_pairs={{0,24},{8,16},{16,8},{24,0},{1,25},{9,17},{17,9},{25,1},{2,26},{10... | collective-permute-start | bytes 147464 | tf_op jit(solution)/shard_map/ppermute | solution.py:426
  25.5 1.2 %shard_map.122 = (f32[1,640]{1,0:T(1,128)S(1)}, f32[32,5,128]{2,1,0:T(8,128)S(1)}, f32[32,5,128]{2,1,0:T(8,128)S(1)}, f32[32,5,128]{2,1,0:T(8,128)S(1)}, bf16[64...) custom-call(f32[30,1,640]{2,1,0:T(1,128)} %bitcast.37, s32[8,128]{1,0:T(8,128)S(1)} %get-tuple-element.57.list_ref, ...), custom_call_target="tpu_custom_call" | custom-call | tf_op jit(solution)/shard_map/pallas_call | solution.py:357
  26.7 2.4 %shard_map.120 = (bf16[1280,640]{1,0:T(8,128)(2,1)S(1)}, bf16[1280,640]{1,0:T(8,128)(2,1)S(1)}, bf16[768,640]{1,0:T(8,128)(2,1)S(1)}, bf16[768,640]{1,0:T(8,128)(2,1)S(1)}) custom-call(s32[3,1,640]{2,1,0:T(1,128)} %bitcast.40, f32[3,1,640]{2,1,0:T(1,128)} %bitcast.41), custom_call_target="tpu_custom_call" | custom-call | tf_op jit(solution)/shard_map/pallas_call | solution.py:357
  29.1 0.7 shard_map.121.total_ref
  29.8 1.2 %shard_map.123 = (f32[32,640]{1,0:T(8,128)S(1)}, f32[3,32,128]{2,1,0:T(8,128)S(1)}, bf16[96,640]{1,0:T(8,128)(2,1)S(1)}) custom-call(f32[32,640]{1,0:T(8,128)S(1)} %shard_map.121.total_ref, f32[3,32,128]{2,1,0:T(8,128)S(1)} %collective-permute-done.6.lat_inner_ref, f32[3,32,128]{2,1,0:T(8,128)S(1)} %collective-permute-done.7.lat_outer_ref, ...), custom_call_target="tpu_custom_call" | custom-call | tf_op jit(solution)/shard_map/pallas_call | solution.py:357
  31.4 1.5 %collective-permute-start.9 = (f32[3,32,128]{2,1,0:T(8,128)S(1)}, f32[3,32,128]{2,1,0:T(8,128)S(1)}, u32[]{:S(2)}, u32[]{:S(2)}) collective-permute-start(f32[3,32,128]{2,1,0:T(8,128)S(1)} %get-tuple-element.87), channel_id=1, source_target_pairs={{0,7},{1,2},{2,1},{3,4},{4,3},{5,6},{6,5},{7,0},{8,15},{9,10},{10,... | collective-permute-start | bytes 147464 | tf_op jit(solution)/shard_map/ppermute | solution.py:399
  32.9 3.9 %collective-permute-done.9.outer_ref = f32[3,32,128]{2,1,0:T(8,128)S(1)} collective-permute-done((f32[3,32,128]{2,1,0:T(8,128)S(1)}, f32[3,32,128]{2,1,0:T(8,128)S(1)}, u32[]{:S(2)}, u32[]{:S(2)}) %collective-permute-start.9) | collective-permute-done | bytes 49184 | tf_op jit(solution)/shard_map/ppermute | solution.py:399
  36.8 0.8 collective-permute-start.10
  37.5 1.5 %collective-permute-start.11 = (f32[3,32,128]{2,1,0:T(8,128)S(1)}, f32[3,32,128]{2,1,0:T(8,128)S(1)}, u32[]{:S(2)}, u32[]{:S(2)}) collective-permute-start(f32[3,32,128]{2,1,0:T(8,128)S(1)} %pad_maximum_fusion.5), channel_id=1, source_target_pairs={{0,24},{8,16},{16,8},{24,0},{1,25},{9,17},{17,9},{25,1},{2,26},{10... | collective-permute-start | bytes 147464 | tf_op jit(solution)/shard_map/ppermute | solution.py:426
  39.5 1.5 %collective-permute-done.10.lat_inner_ref = f32[3,32,128]{2,1,0:T(8,128)S(1)} collective-permute-done((f32[3,32,128]{2,1,0:T(8,128)S(1)}, f32[3,32,128]{2,1,0:T(8,128)S(1)}, u32[]{:S(2)}, u32[]{:S(2)}) %collective-permute-start.10) | collective-permute-done | bytes 49184 | tf_op jit(solution)/shard_map/ppermute | solution.py:427
  40.9 1.6 %collective-permute-done.11.lat_outer_ref = f32[3,32,128]{2,1,0:T(8,128)S(1)} collective-permute-done((f32[3,32,128]{2,1,0:T(8,128)S(1)}, f32[3,32,128]{2,1,0:T(8,128)S(1)}, u32[]{:S(2)}, u32[]{:S(2)}) %collective-permute-start.11) | collective-permute-done | bytes 49184 | tf_op jit(solution)/shard_map/ppermute | solution.py:426
  42.5 0.6 shard_map.126
  43.6 0.5 collective-permute-start.13
  44.1 0.7 collective-permute-done.12.inner_ref
  44.8 4.2 %collective-permute-done.13.outer_ref = f32[3,32,128]{2,1,0:T(8,128)S(1)} collective-permute-done((f32[3,32,128]{2,1,0:T(8,128)S(1)}, f32[3,32,128]{2,1,0:T(8,128)S(1)}, u32[]{:S(2)}, u32[]{:S(2)}) %collective-permute-start.13) | collective-permute-done | bytes 49184 | tf_op jit(solution)/shard_map/ppermute | solution.py:399
  49.0 1.4 %collective-permute-start.14 = (f32[3,32,128]{2,1,0:T(8,128)S(1)}, f32[3,32,128]{2,1,0:T(8,128)S(1)}, u32[]{:S(2)}, u32[]{:S(2)}) collective-permute-start(f32[3,32,128]{2,1,0:T(8,128)S(1)} %pad_maximum_fusion.6), channel_id=1, source_target_pairs={{0,8},{8,0},{16,24},{24,16},{1,9},{9,1},{17,25},{25,17},{2,10},{10... | collective-permute-start | bytes 147464 | tf_op jit(solution)/shard_map/ppermute | solution.py:427
  50.4 1.7 %collective-permute-start.15 = (f32[3,32,128]{2,1,0:T(8,128)S(1)}, f32[3,32,128]{2,1,0:T(8,128)S(1)}, u32[]{:S(2)}, u32[]{:S(2)}) collective-permute-start(f32[3,32,128]{2,1,0:T(8,128)S(1)} %pad_maximum_fusion.7), channel_id=1, source_target_pairs={{0,24},{8,16},{16,8},{24,0},{1,25},{9,17},{17,9},{25,1},{2,26},{10... | collective-permute-start | bytes 147464 | tf_op jit(solution)/shard_map/ppermute | solution.py:426
  52.1 0.7 shard_map.128.total_ref
  53.2 2.2 %collective-permute-done.15.lat_outer_ref = f32[3,32,128]{2,1,0:T(8,128)S(1)} collective-permute-done((f32[3,32,128]{2,1,0:T(8,128)S(1)}, f32[3,32,128]{2,1,0:T(8,128)S(1)}, u32[]{:S(2)}, u32[]{:S(2)}) %collective-permute-start.15) | collective-permute-done | bytes 49184 | tf_op jit(solution)/shard_map/ppermute | solution.py:426
  55.4 1.1 %shard_map.129 = (f32[32,640]{1,0:T(8,128)S(1)}, f32[3,32,128]{2,1,0:T(8,128)S(1)}, bf16[96,640]{1,0:T(8,128)(2,1)S(1)}) custom-call(f32[32,640]{1,0:T(8,128)S(1)} %shard_map.128.total_ref, f32[3,32,128]{2,1,0:T(8,128)S(1)} %collective-permute-done.14.lat_inner_ref, f32[3,32,128]{2,1,0:T(8,128)S(1)} %collective-permute-done.15.lat_outer_ref, ...), custom_call_target="tpu_custom_call" | custom-call | tf_op jit(solution)/shard_map/pallas_call | solution.py:357
  57.0 1.1 %collective-permute-done.16.inner_ref = f32[3,32,128]{2,1,0:T(8,128)S(1)} collective-permute-done((f32[3,32,128]{2,1,0:T(8,128)S(1)}, f32[3,32,128]{2,1,0:T(8,128)S(1)}, u32[]{:S(2)}, u32[]{:S(2)}) %collective-permute-start.16) | collective-permute-done | bytes 49184 | tf_op jit(solution)/shard_map/ppermute | solution.py:404
  58.1 4.2 %collective-permute-done.17.outer_ref = f32[3,32,128]{2,1,0:T(8,128)S(1)} collective-permute-done((f32[3,32,128]{2,1,0:T(8,128)S(1)}, f32[3,32,128]{2,1,0:T(8,128)S(1)}, u32[]{:S(2)}, u32[]{:S(2)}) %collective-permute-start.17) | collective-permute-done | bytes 49184 | tf_op jit(solution)/shard_map/ppermute | solution.py:399
  62.3 0.8 collective-permute-start.18
  63.1 1.5 %collective-permute-start.19 = (f32[3,32,128]{2,1,0:T(8,128)S(1)}, f32[3,32,128]{2,1,0:T(8,128)S(1)}, u32[]{:S(2)}, u32[]{:S(2)}) collective-permute-start(f32[3,32,128]{2,1,0:T(8,128)S(1)} %pad_maximum_fusion.9), channel_id=1, source_target_pairs={{0,24},{8,16},{16,8},{24,0},{1,25},{9,17},{17,9},{25,1},{2,26},{10... | collective-permute-start | bytes 147464 | tf_op jit(solution)/shard_map/ppermute | solution.py:426
  65.0 1.5 %collective-permute-done.18.lat_inner_ref = f32[3,32,128]{2,1,0:T(8,128)S(1)} collective-permute-done((f32[3,32,128]{2,1,0:T(8,128)S(1)}, f32[3,32,128]{2,1,0:T(8,128)S(1)}, u32[]{:S(2)}, u32[]{:S(2)}) %collective-permute-start.18) | collective-permute-done | bytes 49184 | tf_op jit(solution)/shard_map/ppermute | solution.py:427
  66.5 1.6 %collective-permute-done.19.lat_outer_ref = f32[3,32,128]{2,1,0:T(8,128)S(1)} collective-permute-done((f32[3,32,128]{2,1,0:T(8,128)S(1)}, f32[3,32,128]{2,1,0:T(8,128)S(1)}, u32[]{:S(2)}, u32[]{:S(2)}) %collective-permute-start.19) | collective-permute-done | bytes 49184 | tf_op jit(solution)/shard_map/ppermute | solution.py:426
  68.1 0.7 shard_map.132
  69.3 1.1 %collective-permute-done.20.inner_ref = f32[3,32,128]{2,1,0:T(8,128)S(1)} collective-permute-done((f32[3,32,128]{2,1,0:T(8,128)S(1)}, f32[3,32,128]{2,1,0:T(8,128)S(1)}, u32[]{:S(2)}, u32[]{:S(2)}) %collective-permute-start.20) | collective-permute-done | bytes 49184 | tf_op jit(solution)/shard_map/ppermute | solution.py:404
  70.4 4.2 %collective-permute-done.21.outer_ref = f32[3,32,128]{2,1,0:T(8,128)S(1)} collective-permute-done((f32[3,32,128]{2,1,0:T(8,128)S(1)}, f32[3,32,128]{2,1,0:T(8,128)S(1)}, u32[]{:S(2)}, u32[]{:S(2)}) %collective-permute-start.21) | collective-permute-done | bytes 49184 | tf_op jit(solution)/shard_map/ppermute | solution.py:399
  74.6 1.4 %collective-permute-start.22 = (f32[3,32,128]{2,1,0:T(8,128)S(1)}, f32[3,32,128]{2,1,0:T(8,128)S(1)}, u32[]{:S(2)}, u32[]{:S(2)}) collective-permute-start(f32[3,32,128]{2,1,0:T(8,128)S(1)} %pad_maximum_fusion.10), channel_id=1, source_target_pairs={{0,8},{8,0},{16,24},{24,16},{1,9},{9,1},{17,25},{25,17},{2,10},{10... | collective-permute-start | bytes 147464 | tf_op jit(solution)/shard_map/ppermute | solution.py:427
  75.9 1.7 %collective-permute-start.23 = (f32[3,32,128]{2,1,0:T(8,128)S(1)}, f32[3,32,128]{2,1,0:T(8,128)S(1)}, u32[]{:S(2)}, u32[]{:S(2)}) collective-permute-start(f32[3,32,128]{2,1,0:T(8,128)S(1)} %pad_maximum_fusion.11), channel_id=1, source_target_pairs={{0,24},{8,16},{16,8},{24,0},{1,25},{9,17},{17,9},{25,1},{2,26},{10... | collective-permute-start | bytes 147464 | tf_op jit(solution)/shard_map/ppermute | solution.py:426
  77.6 0.8 copy.12
  78.4 0.7 shard_map.134.total_ref
  79.1 1.8 %collective-permute-done.23.lat_outer_ref = f32[3,32,128]{2,1,0:T(8,128)S(1)} collective-permute-done((f32[3,32,128]{2,1,0:T(8,128)S(1)}, f32[3,32,128]{2,1,0:T(8,128)S(1)}, u32[]{:S(2)}, u32[]{:S(2)}) %collective-permute-start.23) | collective-permute-done | bytes 49184 | tf_op jit(solution)/shard_map/ppermute | solution.py:426
  80.9 1.3 %shard_map.135 = f32[30,1,640]{2,1,0:T(1,128)} custom-call(f32[32,640]{1,0:T(8,128)S(1)} %shard_map.134.total_ref, f32[3,32,128]{2,1,0:T(8,128)S(1)} %collective-permute-done.22.lat_inner_ref, f32[3,32,128]{2,1,0:T(8,128)S(1)} %collective-permute-done.23.lat_outer_ref, bf16[768,640]{1,0:T(8,128)(2,1)S(1)} %get-tuple-element.76.high_ref, ...), custom_call_target="tpu_custom_call" | custom-call | tf_op jit(solution)/shard_map/pallas_call | solution.py:357
  (49 shorter events, 4.3 us)
Async XLA Ops:
  2.3 5.3 %collective-permute-start = (f32[3,32,128]{2,1,0:T(8,128)S(1)}, f32[3,32,128]{2,1,0:T(8,128)S(1)}, u32[]{:S(2)}, u32[]{:S(2)}) collective-permute-start(f32[3,32,128]{2,1,0:T(8,128)S(1)} %get-tuple-element.58), channel_id=1, source_target_pairs={{0,1},{1,0},{2,3},{3,2},{4,5},{5,4},{6,7},{7,6},{8,9},{9,8},{10,11... | collective-permute-start | bytes 147464 | tf_op jit(solution)/shard_map/ppermute | solution.py:404
  2.9 6.6 %collective-permute-start.1 = (f32[3,32,128]{2,1,0:T(8,128)S(1)}, f32[3,32,128]{2,1,0:T(8,128)S(1)}, u32[]{:S(2)}, u32[]{:S(2)}) collective-permute-start(f32[3,32,128]{2,1,0:T(8,128)S(1)} %get-tuple-element.59), channel_id=1, source_target_pairs={{0,7},{1,2},{2,1},{3,4},{4,3},{5,6},{6,5},{7,0},{8,15},{9,10},{10,... | collective-permute-start | bytes 147464 | tf_op jit(solution)/shard_map/ppermute | solution.py:399
  9.4 6.3 %collective-permute-start.2 = (f32[3,32,128]{2,1,0:T(8,128)S(1)}, f32[3,32,128]{2,1,0:T(8,128)S(1)}, u32[]{:S(2)}, u32[]{:S(2)}) collective-permute-start(f32[3,32,128]{2,1,0:T(8,128)S(1)} %pad_maximum_fusion), channel_id=1, source_target_pairs={{0,8},{8,0},{16,24},{24,16},{1,9},{9,1},{17,25},{25,17},{2,10},{10... | collective-permute-start | bytes 147464 | tf_op jit(solution)/shard_map/ppermute | solution.py:427
  11.0 5.0 %collective-permute-start.3 = (f32[3,32,128]{2,1,0:T(8,128)S(1)}, f32[3,32,128]{2,1,0:T(8,128)S(1)}, u32[]{:S(2)}, u32[]{:S(2)}) collective-permute-start(f32[3,32,128]{2,1,0:T(8,128)S(1)} %pad_maximum_fusion.1), channel_id=1, source_target_pairs={{0,24},{8,16},{16,8},{24,0},{1,25},{9,17},{17,9},{25,1},{2,26},{10... | collective-permute-start | bytes 147464 | tf_op jit(solution)/shard_map/ppermute | solution.py:426
  17.0 2.8 %collective-permute-start.4 = (f32[3,32,128]{2,1,0:T(8,128)S(1)}, f32[3,32,128]{2,1,0:T(8,128)S(1)}, u32[]{:S(2)}, u32[]{:S(2)}) collective-permute-start(f32[3,32,128]{2,1,0:T(8,128)S(1)} %get-tuple-element.70), channel_id=1, source_target_pairs={{0,1},{1,0},{2,3},{3,2},{4,5},{5,4},{6,7},{7,6},{8,9},{9,8},{10,11... | collective-permute-start | bytes 147464 | tf_op jit(solution)/shard_map/ppermute | solution.py:404
  17.1 5.6 %collective-permute-start.5 = (f32[3,32,128]{2,1,0:T(8,128)S(1)}, f32[3,32,128]{2,1,0:T(8,128)S(1)}, u32[]{:S(2)}, u32[]{:S(2)}) collective-permute-start(f32[3,32,128]{2,1,0:T(8,128)S(1)} %get-tuple-element.71), channel_id=1, source_target_pairs={{0,7},{1,2},{2,1},{3,4},{4,3},{5,6},{6,5},{7,0},{8,15},{9,10},{10,... | collective-permute-start | bytes 147464 | tf_op jit(solution)/shard_map/ppermute | solution.py:399
  22.7 7.1 %collective-permute-start.6 = (f32[3,32,128]{2,1,0:T(8,128)S(1)}, f32[3,32,128]{2,1,0:T(8,128)S(1)}, u32[]{:S(2)}, u32[]{:S(2)}) collective-permute-start(f32[3,32,128]{2,1,0:T(8,128)S(1)} %pad_maximum_fusion.2), channel_id=1, source_target_pairs={{0,8},{8,0},{16,24},{24,16},{1,9},{9,1},{17,25},{25,17},{2,10},{10... | collective-permute-start | bytes 147464 | tf_op jit(solution)/shard_map/ppermute | solution.py:427
  24.3 5.6 %collective-permute-start.7 = (f32[3,32,128]{2,1,0:T(8,128)S(1)}, f32[3,32,128]{2,1,0:T(8,128)S(1)}, u32[]{:S(2)}, u32[]{:S(2)}) collective-permute-start(f32[3,32,128]{2,1,0:T(8,128)S(1)} %pad_maximum_fusion.3), channel_id=1, source_target_pairs={{0,24},{8,16},{16,8},{24,0},{1,25},{9,17},{17,9},{25,1},{2,26},{10... | collective-permute-start | bytes 147464 | tf_op jit(solution)/shard_map/ppermute | solution.py:426
  31.3 1.6 %collective-permute-start.8 = (f32[3,32,128]{2,1,0:T(8,128)S(1)}, f32[3,32,128]{2,1,0:T(8,128)S(1)}, u32[]{:S(2)}, u32[]{:S(2)}) collective-permute-start(f32[3,32,128]{2,1,0:T(8,128)S(1)} %get-tuple-element.86), channel_id=1, source_target_pairs={{0,1},{1,0},{2,3},{3,2},{4,5},{5,4},{6,7},{7,6},{8,9},{9,8},{10,11... | collective-permute-start | bytes 147464 | tf_op jit(solution)/shard_map/ppermute | solution.py:404
  31.4 5.4 %collective-permute-start.9 = (f32[3,32,128]{2,1,0:T(8,128)S(1)}, f32[3,32,128]{2,1,0:T(8,128)S(1)}, u32[]{:S(2)}, u32[]{:S(2)}) collective-permute-start(f32[3,32,128]{2,1,0:T(8,128)S(1)} %get-tuple-element.87), channel_id=1, source_target_pairs={{0,7},{1,2},{2,1},{3,4},{4,3},{5,6},{6,5},{7,0},{8,15},{9,10},{10,... | collective-permute-start | bytes 147464 | tf_op jit(solution)/shard_map/ppermute | solution.py:399
  36.8 4.2 %collective-permute-start.10 = (f32[3,32,128]{2,1,0:T(8,128)S(1)}, f32[3,32,128]{2,1,0:T(8,128)S(1)}, u32[]{:S(2)}, u32[]{:S(2)}) collective-permute-start(f32[3,32,128]{2,1,0:T(8,128)S(1)} %pad_maximum_fusion.4), channel_id=1, source_target_pairs={{0,8},{8,0},{16,24},{24,16},{1,9},{9,1},{17,25},{25,17},{2,10},{10... | collective-permute-start | bytes 147464 | tf_op jit(solution)/shard_map/ppermute | solution.py:427
  37.5 5.0 %collective-permute-start.11 = (f32[3,32,128]{2,1,0:T(8,128)S(1)}, f32[3,32,128]{2,1,0:T(8,128)S(1)}, u32[]{:S(2)}, u32[]{:S(2)}) collective-permute-start(f32[3,32,128]{2,1,0:T(8,128)S(1)} %pad_maximum_fusion.5), channel_id=1, source_target_pairs={{0,24},{8,16},{16,8},{24,0},{1,25},{9,17},{17,9},{25,1},{2,26},{10... | collective-permute-start | bytes 147464 | tf_op jit(solution)/shard_map/ppermute | solution.py:426
  43.5 1.3 %collective-permute-start.12 = (f32[3,32,128]{2,1,0:T(8,128)S(1)}, f32[3,32,128]{2,1,0:T(8,128)S(1)}, u32[]{:S(2)}, u32[]{:S(2)}) collective-permute-start(f32[3,32,128]{2,1,0:T(8,128)S(1)} %get-tuple-element.92), channel_id=1, source_target_pairs={{0,1},{1,0},{2,3},{3,2},{4,5},{5,4},{6,7},{7,6},{8,9},{9,8},{10,11... | collective-permute-start | bytes 147464 | tf_op jit(solution)/shard_map/ppermute | solution.py:404
  43.6 5.4 %collective-permute-start.13 = (f32[3,32,128]{2,1,0:T(8,128)S(1)}, f32[3,32,128]{2,1,0:T(8,128)S(1)}, u32[]{:S(2)}, u32[]{:S(2)}) collective-permute-start(f32[3,32,128]{2,1,0:T(8,128)S(1)} %get-tuple-element.93), channel_id=1, source_target_pairs={{0,7},{1,2},{2,1},{3,4},{4,3},{5,6},{6,5},{7,0},{8,15},{9,10},{10,... | collective-permute-start | bytes 147464 | tf_op jit(solution)/shard_map/ppermute | solution.py:399
  49.0 4.2 %collective-permute-start.14 = (f32[3,32,128]{2,1,0:T(8,128)S(1)}, f32[3,32,128]{2,1,0:T(8,128)S(1)}, u32[]{:S(2)}, u32[]{:S(2)}) collective-permute-start(f32[3,32,128]{2,1,0:T(8,128)S(1)} %pad_maximum_fusion.6), channel_id=1, source_target_pairs={{0,8},{8,0},{16,24},{24,16},{1,9},{9,1},{17,25},{25,17},{2,10},{10... | collective-permute-start | bytes 147464 | tf_op jit(solution)/shard_map/ppermute | solution.py:427
  50.4 5.0 %collective-permute-start.15 = (f32[3,32,128]{2,1,0:T(8,128)S(1)}, f32[3,32,128]{2,1,0:T(8,128)S(1)}, u32[]{:S(2)}, u32[]{:S(2)}) collective-permute-start(f32[3,32,128]{2,1,0:T(8,128)S(1)} %pad_maximum_fusion.7), channel_id=1, source_target_pairs={{0,24},{8,16},{16,8},{24,0},{1,25},{9,17},{17,9},{25,1},{2,26},{10... | collective-permute-start | bytes 147464 | tf_op jit(solution)/shard_map/ppermute | solution.py:426
  56.8 1.3 %collective-permute-start.16 = (f32[3,32,128]{2,1,0:T(8,128)S(1)}, f32[3,32,128]{2,1,0:T(8,128)S(1)}, u32[]{:S(2)}, u32[]{:S(2)}) collective-permute-start(f32[3,32,128]{2,1,0:T(8,128)S(1)} %get-tuple-element.98), channel_id=1, source_target_pairs={{0,1},{1,0},{2,3},{3,2},{4,5},{5,4},{6,7},{7,6},{8,9},{9,8},{10,11... | collective-permute-start | bytes 147464 | tf_op jit(solution)/shard_map/ppermute | solution.py:404
  56.9 5.4 %collective-permute-start.17 = (f32[3,32,128]{2,1,0:T(8,128)S(1)}, f32[3,32,128]{2,1,0:T(8,128)S(1)}, u32[]{:S(2)}, u32[]{:S(2)}) collective-permute-start(f32[3,32,128]{2,1,0:T(8,128)S(1)} %get-tuple-element.99), channel_id=1, source_target_pairs={{0,7},{1,2},{2,1},{3,4},{4,3},{5,6},{6,5},{7,0},{8,15},{9,10},{10,... | collective-permute-start | bytes 147464 | tf_op jit(solution)/shard_map/ppermute | solution.py:399
  62.3 4.2 %collective-permute-start.18 = (f32[3,32,128]{2,1,0:T(8,128)S(1)}, f32[3,32,128]{2,1,0:T(8,128)S(1)}, u32[]{:S(2)}, u32[]{:S(2)}) collective-permute-start(f32[3,32,128]{2,1,0:T(8,128)S(1)} %pad_maximum_fusion.8), channel_id=1, source_target_pairs={{0,8},{8,0},{16,24},{24,16},{1,9},{9,1},{17,25},{25,17},{2,10},{10... | collective-permute-start | bytes 147464 | tf_op jit(solution)/shard_map/ppermute | solution.py:427
  63.1 5.0 %collective-permute-start.19 = (f32[3,32,128]{2,1,0:T(8,128)S(1)}, f32[3,32,128]{2,1,0:T(8,128)S(1)}, u32[]{:S(2)}, u32[]{:S(2)}) collective-permute-start(f32[3,32,128]{2,1,0:T(8,128)S(1)} %pad_maximum_fusion.9), channel_id=1, source_target_pairs={{0,24},{8,16},{16,8},{24,0},{1,25},{9,17},{17,9},{25,1},{2,26},{10... | collective-permute-start | bytes 147464 | tf_op jit(solution)/shard_map/ppermute | solution.py:426
  69.1 1.3 %collective-permute-start.20 = (f32[3,32,128]{2,1,0:T(8,128)S(1)}, f32[3,32,128]{2,1,0:T(8,128)S(1)}, u32[]{:S(2)}, u32[]{:S(2)}) collective-permute-start(f32[3,32,128]{2,1,0:T(8,128)S(1)} %get-tuple-element.104), channel_id=1, source_target_pairs={{0,1},{1,0},{2,3},{3,2},{4,5},{5,4},{6,7},{7,6},{8,9},{9,8},{10,11... | collective-permute-start | bytes 147464 | tf_op jit(solution)/shard_map/ppermute | solution.py:404
  69.2 5.4 %collective-permute-start.21 = (f32[3,32,128]{2,1,0:T(8,128)S(1)}, f32[3,32,128]{2,1,0:T(8,128)S(1)}, u32[]{:S(2)}, u32[]{:S(2)}) collective-permute-start(f32[3,32,128]{2,1,0:T(8,128)S(1)} %get-tuple-element.105), channel_id=1, source_target_pairs={{0,7},{1,2},{2,1},{3,4},{4,3},{5,6},{6,5},{7,0},{8,15},{9,10},{10,... | collective-permute-start | bytes 147464 | tf_op jit(solution)/shard_map/ppermute | solution.py:399
  74.6 4.5 %collective-permute-start.22 = (f32[3,32,128]{2,1,0:T(8,128)S(1)}, f32[3,32,128]{2,1,0:T(8,128)S(1)}, u32[]{:S(2)}, u32[]{:S(2)}) collective-permute-start(f32[3,32,128]{2,1,0:T(8,128)S(1)} %pad_maximum_fusion.10), channel_id=1, source_target_pairs={{0,8},{8,0},{16,24},{24,16},{1,9},{9,1},{17,25},{25,17},{2,10},{10... | collective-permute-start | bytes 147464 | tf_op jit(solution)/shard_map/ppermute | solution.py:427
  75.9 5.0 %collective-permute-start.23 = (f32[3,32,128]{2,1,0:T(8,128)S(1)}, f32[3,32,128]{2,1,0:T(8,128)S(1)}, u32[]{:S(2)}, u32[]{:S(2)}) collective-permute-start(f32[3,32,128]{2,1,0:T(8,128)S(1)} %pad_maximum_fusion.11), channel_id=1, source_target_pairs={{0,24},{8,16},{16,8},{24,0},{1,25},{9,17},{17,9},{25,1},{2,26},{10... | collective-permute-start | bytes 147464 | tf_op jit(solution)/shard_map/ppermute | solution.py:426

commit v4 on v3

--- a/solution.py
+++ b/solution.py
@@ -26,6 +26,15 @@
     inner = [(i, i ^ 1) for i in range(count)]
     outer = [(i, (((i + 1) ^ 1) - 1) % count) for i in range(count)]
     return inner, outer
+
+
+def lat_outer_routes(lat_count, lon_count):
+    routes = []
+    for a, target in swap_routes(lat_count)[1]:
+        for b in range(lon_count):
+            alone = a in (0, lat_count - 1)
+            routes.append((a * lon_count + b, a * lon_count + (b ^ 1) if alone else target * lon_count + b))
+    return routes
 
 
 OUTER_SENT = ((0, 2), (1, 2), (2, 2))
@@ -373,7 +382,8 @@
     bundle = ((3, rows, halo), f32)
     straight = ((rows, halo), f32)
     lon_routes = swap_routes(lon_count)
-    lat_routes = swap_routes(lat_count)
+    lat_inner_route = swap_routes(lat_count)[0]
+    lat_outer_route = lat_outer_routes(lat_count, lon_count)
     i32 = jnp.int32
 
     by_level = lambda value: value.transpose(1, 0, 2)
@@ -423,8 +433,8 @@
             )
         first = jnp.stack([inner_in[1], outer_in[1], lat_inner])
         second = jnp.stack([inner_in[2], outer_in[2], lat_outer])
-        second_in = lax.ppermute(second, "lat", lat_routes[1])
-        first_in = lax.ppermute(first, "lat", lat_routes[0])
+        first_in = lax.ppermute(first, "lat", lat_inner_route)
+        second_in = lax.ppermute(second, ("lat", "lon"), lat_outer_route)
         if phase == 0:
             normal, scale, edge_outer, edge_rest = call(
                 edge_setup_kernel,

time: 82.6 us -> 77 us (0.932)
  waiting for transfers between devices: 35 us -> 28.3 us
  starting transfers between devices: 26.9 us -> 28 us
    ppermute x12, waiting for transfers between devices: 10.9 us -> 6.33 us  [the longest x6 6.31 us: on_device(): first_in = lax.ppermute(first, 'lat', lat_inner_route)]
    ppermute x6, starting transfers between devices: 9.52 us -> 11.7 us  [on_device(): outer_in = lax.ppermute(outer, 'lon', lon_routes[1])]
    ppermute x12, starting transfers between devices: 16.5 us -> 14.4 us  [the longest x6 14.4 us: on_device(): first_in = lax.ppermute(first, 'lat', lat_inner_route)]
    ppermute x6, waiting for transfers between devices: 21.1 us -> 20 us  [on_device(): outer_in = lax.ppermute(outer, 'lon', lon_routes[1])]
    ppermute x6, waiting for transfers between devices: 3.03 us -> 1.98 us  [on_device(): inner_in = lax.ppermute(inner, 'lon', lon_routes[0])]
    ppermute x6, starting transfers between devices: 0.91 us -> 1.92 us  [on_device(): inner_in = lax.ppermute(inner, 'lon', lon_routes[0])]
  transfers between devices with their start and end apart: 24 -> 24, of which waited for: 17 -> 12; matrix products, arithmetic and copies ran while one was open for 1% -> 1% of each run, Pallas kernels for 12% -> 13%
where the time goes in v4:
time: 77 us; the launch traced here: 76.6 us
  waiting for transfers between devices  28.3 us (37%)
  starting transfers between devices  28 us (36%)
  Pallas kernels  18.6 us (24%)
  between operations  0.84 us (1%)
  local copies, waits for them, and re-layouts  0.82 us (1%)
    ppermute x6, waiting for transfers between devices, on_device(): outer_in = lax.ppermute(outer, 'lon', lon_routes[1])  20 us
    pallas_call x23, Pallas kernels, call(): pl.pallas_call(body, out_shape=tuple((jax.ShapeDtypeStruct(shape, kind) f...  18.6 us
    ppermute x6, starting transfers between devices, on_device(): first_in = lax.ppermute(first, 'lat', lat_inner_route)  14.4 us
    ppermute x6, starting transfers between devices, on_device(): outer_in = lax.ppermute(outer, 'lon', lon_routes[1])  11.7 us
    ppermute x6, waiting for transfers between devices, on_device(): first_in = lax.ppermute(first, 'lat', lat_inner_route)  6.31 us
    ppermute x6, waiting for transfers between devices, on_device(): inner_in = lax.ppermute(inner, 'lon', lon_routes[0])  1.98 us
    ppermute x6, starting transfers between devices, on_device(): inner_in = lax.ppermute(inner, 'lon', lon_routes[0])  1.92 us
  transfers between devices with their start and end apart: 24, of which 12 were waited for; matrix products, arithmetic and copies ran while one was open for 1% of the time, Pallas kernels for 13%

profile of v4, /device:TPU:0, one launch (start us, length us, event | category | flops | bytes accessed | tf_op | source)
XLA Modules:
  0.0 76.6 jit_solution(7869969376101322971)
XLA Ops:
  0.6 1.2 %shard_map.113 = (f32[32,640]{1,0:T(8,128)S(1)}, bf16[96,640]{1,0:T(8,128)(2,1)S(1)}, f32[3,32,128]{2,1,0:T(8,128)S(1)}, s32[8,128]{1,0:T(8,128)S(1)}) custom-call(f32[30,1,640]{2,1,0:T(1,128)} %bitcast.36, s32[8,128]{1,0:T(8,128)} %bitcast.42), custom_call_target="tpu_custom_call" | custom-call | tf_op jit(solution)/shard_map/pallas_call | solution.py:366
  1.8 0.5 shard_map.114
  2.3 0.6 collective-permute-start
  2.9 4.7 %collective-permute-start.1 = (f32[3,32,128]{2,1,0:T(8,128)S(1)}, f32[3,32,128]{2,1,0:T(8,128)S(1)}, u32[]{:S(2)}, u32[]{:S(2)}) collective-permute-start(f32[3,32,128]{2,1,0:T(8,128)S(1)} %get-tuple-element.59), channel_id=1, source_target_pairs={{0,7},{1,2},{2,1},{3,4},{4,3},{5,6},{6,5},{7,0},{8,15},{9,10},{10,... | collective-permute-start | bytes 147464 | tf_op jit(solution)/shard_map/ppermute | solution.py:409
  7.6 1.9 %collective-permute-done.1.outer_ref = f32[3,32,128]{2,1,0:T(8,128)S(1)} collective-permute-done((f32[3,32,128]{2,1,0:T(8,128)S(1)}, f32[3,32,128]{2,1,0:T(8,128)S(1)}, u32[]{:S(2)}, u32[]{:S(2)}) %collective-permute-start.1) | collective-permute-done | bytes 49184 | tf_op jit(solution)/shard_map/ppermute | solution.py:409
  9.4 1.6 %collective-permute-start.2 = (f32[3,32,128]{2,1,0:T(8,128)S(1)}, f32[3,32,128]{2,1,0:T(8,128)S(1)}, u32[]{:S(2)}, u32[]{:S(2)}) collective-permute-start(f32[3,32,128]{2,1,0:T(8,128)S(1)} %pad_maximum_fusion), channel_id=1, source_target_pairs={{0,8},{8,0},{16,24},{24,16},{1,9},{9,1},{17,25},{25,17},{2,10},{10... | collective-permute-start | bytes 147464 | tf_op jit(solution)/shard_map/ppermute | solution.py:436
  11.0 1.5 %shard_map.115 = (bf16[896,1024]{1,0:T(8,128)(2,1)S(1)}, bf16[768,1024]{1,0:T(8,128)(2,1)S(1)}) custom-call(s32[2,960]{1,0:T(2,128)} %bitcast.39), custom_call_target="tpu_custom_call" | custom-call | tf_op jit(solution)/shard_map/pallas_call | solution.py:366
  12.5 1.3 %shard_map.117 = (f32[32,1024]{1,0:T(8,128)S(1)}, f32[1,1024]{1,0:T(1,128)S(1)}, bf16[1024,384]{1,0:T(8,128)(2,1)S(1)}, bf16[1024,640]{1,0:T(8,128)(2,1)S(1)}) custom-call(f32[30,1,960]{2,1,0:T(1,128)} %bitcast.35, s32[8,128]{1,0:T(8,128)} %bitcast.43, f32[1,960]{1,0:T(1,128)} %dual_hbm.1), custom_call_target="tpu_custom_call" | custom-call | tf_op jit(solution)/shard_map/pallas_call | solution.py:366
  13.8 0.4 shard_map.116.total_ref
  14.3 0.7 shard_map.118
  14.9 0.4 shard_map.119
  15.3 0.6 collective-permute-start.4
  15.9 3.2 %collective-permute-start.5 = (f32[3,32,128]{2,1,0:T(8,128)S(1)}, f32[3,32,128]{2,1,0:T(8,128)S(1)}, u32[]{:S(2)}, u32[]{:S(2)}) collective-permute-start(f32[3,32,128]{2,1,0:T(8,128)S(1)} %get-tuple-element.71), channel_id=1, source_target_pairs={{0,7},{1,2},{2,1},{3,4},{4,3},{5,6},{6,5},{7,0},{8,15},{9,10},{10,... | collective-permute-start | bytes 147464 | tf_op jit(solution)/shard_map/ppermute | solution.py:409
  19.0 2.6 %collective-permute-done.5.outer_ref = f32[3,32,128]{2,1,0:T(8,128)S(1)} collective-permute-done((f32[3,32,128]{2,1,0:T(8,128)S(1)}, f32[3,32,128]{2,1,0:T(8,128)S(1)}, u32[]{:S(2)}, u32[]{:S(2)}) %collective-permute-start.5) | collective-permute-done | bytes 49184 | tf_op jit(solution)/shard_map/ppermute | solution.py:409
  21.6 2.7 %collective-permute-start.6 = (f32[3,32,128]{2,1,0:T(8,128)S(1)}, f32[3,32,128]{2,1,0:T(8,128)S(1)}, u32[]{:S(2)}, u32[]{:S(2)}) collective-permute-start(f32[3,32,128]{2,1,0:T(8,128)S(1)} %pad_maximum_fusion.2), channel_id=1, source_target_pairs={{0,8},{8,0},{16,24},{24,16},{1,9},{9,1},{17,25},{25,17},{2,10},{10... | collective-permute-start | bytes 147464 | tf_op jit(solution)/shard_map/ppermute | solution.py:436
  24.3 1.2 %shard_map.122 = (f32[1,640]{1,0:T(1,128)S(1)}, f32[32,5,128]{2,1,0:T(8,128)S(1)}, f32[32,5,128]{2,1,0:T(8,128)S(1)}, f32[32,5,128]{2,1,0:T(8,128)S(1)}, bf16[64...) custom-call(f32[30,1,640]{2,1,0:T(1,128)} %bitcast.37, s32[8,128]{1,0:T(8,128)S(1)} %get-tuple-element.57.list_ref, ...), custom_call_target="tpu_custom_call" | custom-call | tf_op jit(solution)/shard_map/pallas_call | solution.py:366
  25.5 2.4 %shard_map.120 = (bf16[1280,640]{1,0:T(8,128)(2,1)S(1)}, bf16[1280,640]{1,0:T(8,128)(2,1)S(1)}, bf16[768,640]{1,0:T(8,128)(2,1)S(1)}, bf16[768,640]{1,0:T(8,128)(2,1)S(1)}) custom-call(s32[3,1,640]{2,1,0:T(1,128)} %bitcast.40, f32[3,1,640]{2,1,0:T(1,128)} %bitcast.41), custom_call_target="tpu_custom_call" | custom-call | tf_op jit(solution)/shard_map/pallas_call | solution.py:366
  27.9 0.7 shard_map.121.total_ref
  28.6 1.2 %shard_map.123 = (f32[32,640]{1,0:T(8,128)S(1)}, f32[3,32,128]{2,1,0:T(8,128)S(1)}, bf16[96,640]{1,0:T(8,128)(2,1)S(1)}) custom-call(f32[32,640]{1,0:T(8,128)S(1)} %shard_map.121.total_ref, f32[3,32,128]{2,1,0:T(8,128)S(1)} %collective-permute-done.6.lat_inner_ref, f32[3,32,128]{2,1,0:T(8,128)S(1)} %collective-permute-done.7.lat_outer_ref, ...), custom_call_target="tpu_custom_call" | custom-call | tf_op jit(solution)/shard_map/pallas_call | solution.py:366
  30.0 0.6 collective-permute-start.8
  30.6 2.1 %collective-permute-start.9 = (f32[3,32,128]{2,1,0:T(8,128)S(1)}, f32[3,32,128]{2,1,0:T(8,128)S(1)}, u32[]{:S(2)}, u32[]{:S(2)}) collective-permute-start(f32[3,32,128]{2,1,0:T(8,128)S(1)} %get-tuple-element.87), channel_id=1, source_target_pairs={{0,7},{1,2},{2,1},{3,4},{4,3},{5,6},{6,5},{7,0},{8,15},{9,10},{10,... | collective-permute-start | bytes 147464 | tf_op jit(solution)/shard_map/ppermute | solution.py:409
  32.7 3.2 %collective-permute-done.9.outer_ref = f32[3,32,128]{2,1,0:T(8,128)S(1)} collective-permute-done((f32[3,32,128]{2,1,0:T(8,128)S(1)}, f32[3,32,128]{2,1,0:T(8,128)S(1)}, u32[]{:S(2)}, u32[]{:S(2)}) %collective-permute-start.9) | collective-permute-done | bytes 49184 | tf_op jit(solution)/shard_map/ppermute | solution.py:409
  35.9 1.0 %collective-permute-start.10 = (f32[3,32,128]{2,1,0:T(8,128)S(1)}, f32[3,32,128]{2,1,0:T(8,128)S(1)}, u32[]{:S(2)}, u32[]{:S(2)}) collective-permute-start(f32[3,32,128]{2,1,0:T(8,128)S(1)} %pad_maximum_fusion.4), channel_id=1, source_target_pairs={{0,8},{8,0},{16,24},{24,16},{1,9},{9,1},{17,25},{25,17},{2,10},{10... | collective-permute-start | bytes 147464 | tf_op jit(solution)/shard_map/ppermute | solution.py:436
  36.9 0.4 shard_map.125.total_ref
  37.4 2.7 %collective-permute-done.10.lat_inner_ref = f32[3,32,128]{2,1,0:T(8,128)S(1)} collective-permute-done((f32[3,32,128]{2,1,0:T(8,128)S(1)}, f32[3,32,128]{2,1,0:T(8,128)S(1)}, u32[]{:S(2)}, u32[]{:S(2)}) %collective-permute-start.10) | collective-permute-done | bytes 49184 | tf_op jit(solution)/shard_map/ppermute | solution.py:436
  40.1 0.6 shard_map.126
  40.7 0.4 shard_map.127
  41.2 1.3 %collective-permute-start.13 = (f32[3,32,128]{2,1,0:T(8,128)S(1)}, f32[3,32,128]{2,1,0:T(8,128)S(1)}, u32[]{:S(2)}, u32[]{:S(2)}) collective-permute-start(f32[3,32,128]{2,1,0:T(8,128)S(1)} %get-tuple-element.93), channel_id=1, source_target_pairs={{0,7},{1,2},{2,1},{3,4},{4,3},{5,6},{6,5},{7,0},{8,15},{9,10},{10,... | collective-permute-start | bytes 147464 | tf_op jit(solution)/shard_map/ppermute | solution.py:409
  42.5 4.1 %collective-permute-done.13.outer_ref = f32[3,32,128]{2,1,0:T(8,128)S(1)} collective-permute-done((f32[3,32,128]{2,1,0:T(8,128)S(1)}, f32[3,32,128]{2,1,0:T(8,128)S(1)}, u32[]{:S(2)}, u32[]{:S(2)}) %collective-permute-start.13) | collective-permute-done | bytes 49184 | tf_op jit(solution)/shard_map/ppermute | solution.py:409
  46.6 3.0 %collective-permute-start.14 = (f32[3,32,128]{2,1,0:T(8,128)S(1)}, f32[3,32,128]{2,1,0:T(8,128)S(1)}, u32[]{:S(2)}, u32[]{:S(2)}) collective-permute-start(f32[3,32,128]{2,1,0:T(8,128)S(1)} %pad_maximum_fusion.6), channel_id=1, source_target_pairs={{0,8},{8,0},{16,24},{24,16},{1,9},{9,1},{17,25},{25,17},{2,10},{10... | collective-permute-start | bytes 147464 | tf_op jit(solution)/shard_map/ppermute | solution.py:436
  49.6 0.7 shard_map.128.total_ref
  50.3 1.4 %collective-permute-done.14.lat_inner_ref = f32[3,32,128]{2,1,0:T(8,128)S(1)} collective-permute-done((f32[3,32,128]{2,1,0:T(8,128)S(1)}, f32[3,32,128]{2,1,0:T(8,128)S(1)}, u32[]{:S(2)}, u32[]{:S(2)}) %collective-permute-start.14) | collective-permute-done | bytes 49184 | tf_op jit(solution)/shard_map/ppermute | solution.py:436
  51.6 1.1 %shard_map.129 = (f32[32,640]{1,0:T(8,128)S(1)}, f32[3,32,128]{2,1,0:T(8,128)S(1)}, bf16[96,640]{1,0:T(8,128)(2,1)S(1)}) custom-call(f32[32,640]{1,0:T(8,128)S(1)} %shard_map.128.total_ref, f32[3,32,128]{2,1,0:T(8,128)S(1)} %collective-permute-done.14.lat_inner_ref, f32[3,32,128]{2,1,0:T(8,128)S(1)} %collective-permute-done.15.lat_outer_ref, ...), custom_call_target="tpu_custom_call" | custom-call | tf_op jit(solution)/shard_map/pallas_call | solution.py:366
  53.2 0.4 collective-permute-start.17
  53.5 0.8 %collective-permute-done.16.inner_ref = f32[3,32,128]{2,1,0:T(8,128)S(1)} collective-permute-done((f32[3,32,128]{2,1,0:T(8,128)S(1)}, f32[3,32,128]{2,1,0:T(8,128)S(1)}, u32[]{:S(2)}, u32[]{:S(2)}) %collective-permute-start.16) | collective-permute-done | bytes 49184 | tf_op jit(solution)/shard_map/ppermute | solution.py:414
  54.4 4.2 %collective-permute-done.17.outer_ref = f32[3,32,128]{2,1,0:T(8,128)S(1)} collective-permute-done((f32[3,32,128]{2,1,0:T(8,128)S(1)}, f32[3,32,128]{2,1,0:T(8,128)S(1)}, u32[]{:S(2)}, u32[]{:S(2)}) %collective-permute-start.17) | collective-permute-done | bytes 49184 | tf_op jit(solution)/shard_map/ppermute | solution.py:409
  58.6 3.1 %collective-permute-start.18 = (f32[3,32,128]{2,1,0:T(8,128)S(1)}, f32[3,32,128]{2,1,0:T(8,128)S(1)}, u32[]{:S(2)}, u32[]{:S(2)}) collective-permute-start(f32[3,32,128]{2,1,0:T(8,128)S(1)} %pad_maximum_fusion.8), channel_id=1, source_target_pairs={{0,8},{8,0},{16,24},{24,16},{1,9},{9,1},{17,25},{25,17},{2,10},{10... | collective-permute-start | bytes 147464 | tf_op jit(solution)/shard_map/ppermute | solution.py:436
  61.6 0.4 shard_map.131.total_ref
  62.1 1.6 %collective-permute-done.18.lat_inner_ref = f32[3,32,128]{2,1,0:T(8,128)S(1)} collective-permute-done((f32[3,32,128]{2,1,0:T(8,128)S(1)}, f32[3,32,128]{2,1,0:T(8,128)S(1)}, u32[]{:S(2)}, u32[]{:S(2)}) %collective-permute-start.18) | collective-permute-done | bytes 49184 | tf_op jit(solution)/shard_map/ppermute | solution.py:436
  63.7 0.6 shard_map.132
  64.4 0.4 shard_map.133
  64.9 1.1 %collective-permute-done.20.inner_ref = f32[3,32,128]{2,1,0:T(8,128)S(1)} collective-permute-done((f32[3,32,128]{2,1,0:T(8,128)S(1)}, f32[3,32,128]{2,1,0:T(8,128)S(1)}, u32[]{:S(2)}, u32[]{:S(2)}) %collective-permute-start.20) | collective-permute-done | bytes 49184 | tf_op jit(solution)/shard_map/ppermute | solution.py:414
  66.0 4.2 %collective-permute-done.21.outer_ref = f32[3,32,128]{2,1,0:T(8,128)S(1)} collective-permute-done((f32[3,32,128]{2,1,0:T(8,128)S(1)}, f32[3,32,128]{2,1,0:T(8,128)S(1)}, u32[]{:S(2)}, u32[]{:S(2)}) %collective-permute-start.21) | collective-permute-done | bytes 49184 | tf_op jit(solution)/shard_map/ppermute | solution.py:409
  70.2 3.1 %collective-permute-start.22 = (f32[3,32,128]{2,1,0:T(8,128)S(1)}, f32[3,32,128]{2,1,0:T(8,128)S(1)}, u32[]{:S(2)}, u32[]{:S(2)}) collective-permute-start(f32[3,32,128]{2,1,0:T(8,128)S(1)} %pad_maximum_fusion.10), channel_id=1, source_target_pairs={{0,8},{8,0},{16,24},{24,16},{1,9},{9,1},{17,25},{25,17},{2,10},{10... | collective-permute-start | bytes 147464 | tf_op jit(solution)/shard_map/ppermute | solution.py:436
  73.3 0.8 %copy.12 = f32[1,30,960]{2,0,1:T(1,128)} copy(f32[1,30,960]{2,1,0:T(8,128)S(1)} %slice_bitcast_fusion) | data formatting | bytes 230400
  74.1 0.7 shard_map.134.total_ref
  74.8 0.6 collective-permute-done.22.lat_inner_ref
  75.3 1.3 %shard_map.135 = f32[30,1,640]{2,1,0:T(1,128)} custom-call(f32[32,640]{1,0:T(8,128)S(1)} %shard_map.134.total_ref, f32[3,32,128]{2,1,0:T(8,128)S(1)} %collective-permute-done.22.lat_inner_ref, f32[3,32,128]{2,1,0:T(8,128)S(1)} %collective-permute-done.23.lat_outer_ref, bf16[768,640]{1,0:T(8,128)(2,1)S(1)} %get-tuple-element.76.high_ref, ...), custom_call_target="tpu_custom_call" | custom-call | tf_op jit(solution)/shard_map/pallas_call | solution.py:366
  (49 shorter events, 1.0 us)
Async XLA Ops:
  2.3 5.3 %collective-permute-start = (f32[3,32,128]{2,1,0:T(8,128)S(1)}, f32[3,32,128]{2,1,0:T(8,128)S(1)}, u32[]{:S(2)}, u32[]{:S(2)}) collective-permute-start(f32[3,32,128]{2,1,0:T(8,128)S(1)} %get-tuple-element.58), channel_id=1, source_target_pairs={{0,1},{1,0},{2,3},{3,2},{4,5},{5,4},{6,7},{7,6},{8,9},{9,8},{10,11... | collective-permute-start | bytes 147464 | tf_op jit(solution)/shard_map/ppermute | solution.py:414
  2.9 6.6 %collective-permute-start.1 = (f32[3,32,128]{2,1,0:T(8,128)S(1)}, f32[3,32,128]{2,1,0:T(8,128)S(1)}, u32[]{:S(2)}, u32[]{:S(2)}) collective-permute-start(f32[3,32,128]{2,1,0:T(8,128)S(1)} %get-tuple-element.59), channel_id=1, source_target_pairs={{0,7},{1,2},{2,1},{3,4},{4,3},{5,6},{6,5},{7,0},{8,15},{9,10},{10,... | collective-permute-start | bytes 147464 | tf_op jit(solution)/shard_map/ppermute | solution.py:409
  9.4 4.8 %collective-permute-start.2 = (f32[3,32,128]{2,1,0:T(8,128)S(1)}, f32[3,32,128]{2,1,0:T(8,128)S(1)}, u32[]{:S(2)}, u32[]{:S(2)}) collective-permute-start(f32[3,32,128]{2,1,0:T(8,128)S(1)} %pad_maximum_fusion), channel_id=1, source_target_pairs={{0,8},{8,0},{16,24},{24,16},{1,9},{9,1},{17,25},{25,17},{2,10},{10... | collective-permute-start | bytes 147464 | tf_op jit(solution)/shard_map/ppermute | solution.py:436
  11.0 3.2 %collective-permute-start.3 = (f32[3,32,128]{2,1,0:T(8,128)S(1)}, f32[3,32,128]{2,1,0:T(8,128)S(1)}, u32[]{:S(2)}, u32[]{:S(2)}) collective-permute-start(f32[3,32,128]{2,1,0:T(8,128)S(1)} %pad_maximum_fusion.1), channel_id=1, source_target_pairs={{0,1},{1,0},{2,3},{3,2},{4,5},{5,4},{6,7},{7,6},{8,16},{9,17},{10,... | collective-permute-start | bytes 147464 | tf_op jit(solution)/shard_map/ppermute | solution.py:437
  15.3 3.7 %collective-permute-start.4 = (f32[3,32,128]{2,1,0:T(8,128)S(1)}, f32[3,32,128]{2,1,0:T(8,128)S(1)}, u32[]{:S(2)}, u32[]{:S(2)}) collective-permute-start(f32[3,32,128]{2,1,0:T(8,128)S(1)} %get-tuple-element.70), channel_id=1, source_target_pairs={{0,1},{1,0},{2,3},{3,2},{4,5},{5,4},{6,7},{7,6},{8,9},{9,8},{10,11... | collective-permute-start | bytes 147464 | tf_op jit(solution)/shard_map/ppermute | solution.py:414
  15.9 5.7 %collective-permute-start.5 = (f32[3,32,128]{2,1,0:T(8,128)S(1)}, f32[3,32,128]{2,1,0:T(8,128)S(1)}, u32[]{:S(2)}, u32[]{:S(2)}) collective-permute-start(f32[3,32,128]{2,1,0:T(8,128)S(1)} %get-tuple-element.71), channel_id=1, source_target_pairs={{0,7},{1,2},{2,1},{3,4},{4,3},{5,6},{6,5},{7,0},{8,15},{9,10},{10,... | collective-permute-start | bytes 147464 | tf_op jit(solution)/shard_map/ppermute | solution.py:409
  21.6 7.0 %collective-permute-start.6 = (f32[3,32,128]{2,1,0:T(8,128)S(1)}, f32[3,32,128]{2,1,0:T(8,128)S(1)}, u32[]{:S(2)}, u32[]{:S(2)}) collective-permute-start(f32[3,32,128]{2,1,0:T(8,128)S(1)} %pad_maximum_fusion.2), channel_id=1, source_target_pairs={{0,8},{8,0},{16,24},{24,16},{1,9},{9,1},{17,25},{25,17},{2,10},{10... | collective-permute-start | bytes 147464 | tf_op jit(solution)/shard_map/ppermute | solution.py:436
  24.3 4.3 %collective-permute-start.7 = (f32[3,32,128]{2,1,0:T(8,128)S(1)}, f32[3,32,128]{2,1,0:T(8,128)S(1)}, u32[]{:S(2)}, u32[]{:S(2)}) collective-permute-start(f32[3,32,128]{2,1,0:T(8,128)S(1)} %pad_maximum_fusion.3), channel_id=1, source_target_pairs={{0,1},{1,0},{2,3},{3,2},{4,5},{5,4},{6,7},{7,6},{8,16},{9,17},{10,... | collective-permute-start | bytes 147464 | tf_op jit(solution)/shard_map/ppermute | solution.py:437
  30.0 2.7 %collective-permute-start.8 = (f32[3,32,128]{2,1,0:T(8,128)S(1)}, f32[3,32,128]{2,1,0:T(8,128)S(1)}, u32[]{:S(2)}, u32[]{:S(2)}) collective-permute-start(f32[3,32,128]{2,1,0:T(8,128)S(1)} %get-tuple-element.86), channel_id=1, source_target_pairs={{0,1},{1,0},{2,3},{3,2},{4,5},{5,4},{6,7},{7,6},{8,9},{9,8},{10,11... | collective-permute-start | bytes 147464 | tf_op jit(solution)/shard_map/ppermute | solution.py:414
  30.6 5.3 %collective-permute-start.9 = (f32[3,32,128]{2,1,0:T(8,128)S(1)}, f32[3,32,128]{2,1,0:T(8,128)S(1)}, u32[]{:S(2)}, u32[]{:S(2)}) collective-permute-start(f32[3,32,128]{2,1,0:T(8,128)S(1)} %get-tuple-element.87), channel_id=1, source_target_pairs={{0,7},{1,2},{2,1},{3,4},{4,3},{5,6},{6,5},{7,0},{8,15},{9,10},{10,... | collective-permute-start | bytes 147464 | tf_op jit(solution)/shard_map/ppermute | solution.py:409
  35.9 4.2 %collective-permute-start.10 = (f32[3,32,128]{2,1,0:T(8,128)S(1)}, f32[3,32,128]{2,1,0:T(8,128)S(1)}, u32[]{:S(2)}, u32[]{:S(2)}) collective-permute-start(f32[3,32,128]{2,1,0:T(8,128)S(1)} %pad_maximum_fusion.4), channel_id=1, source_target_pairs={{0,8},{8,0},{16,24},{24,16},{1,9},{9,1},{17,25},{25,17},{2,10},{10... | collective-permute-start | bytes 147464 | tf_op jit(solution)/shard_map/ppermute | solution.py:436
  36.9 3.2 %collective-permute-start.11 = (f32[3,32,128]{2,1,0:T(8,128)S(1)}, f32[3,32,128]{2,1,0:T(8,128)S(1)}, u32[]{:S(2)}, u32[]{:S(2)}) collective-permute-start(f32[3,32,128]{2,1,0:T(8,128)S(1)} %pad_maximum_fusion.5), channel_id=1, source_target_pairs={{0,1},{1,0},{2,3},{3,2},{4,5},{5,4},{6,7},{7,6},{8,16},{9,17},{10,... | collective-permute-start | bytes 147464 | tf_op jit(solution)/shard_map/ppermute | solution.py:437
  41.1 1.4 %collective-permute-start.12 = (f32[3,32,128]{2,1,0:T(8,128)S(1)}, f32[3,32,128]{2,1,0:T(8,128)S(1)}, u32[]{:S(2)}, u32[]{:S(2)}) collective-permute-start(f32[3,32,128]{2,1,0:T(8,128)S(1)} %get-tuple-element.92), channel_id=1, source_target_pairs={{0,1},{1,0},{2,3},{3,2},{4,5},{5,4},{6,7},{7,6},{8,9},{9,8},{10,11... | collective-permute-start | bytes 147464 | tf_op jit(solution)/shard_map/ppermute | solution.py:414
  41.2 5.4 %collective-permute-start.13 = (f32[3,32,128]{2,1,0:T(8,128)S(1)}, f32[3,32,128]{2,1,0:T(8,128)S(1)}, u32[]{:S(2)}, u32[]{:S(2)}) collective-permute-start(f32[3,32,128]{2,1,0:T(8,128)S(1)} %get-tuple-element.93), channel_id=1, source_target_pairs={{0,7},{1,2},{2,1},{3,4},{4,3},{5,6},{6,5},{7,0},{8,15},{9,10},{10,... | collective-permute-start | bytes 147464 | tf_op jit(solution)/shard_map/ppermute | solution.py:409
  46.6 5.1 %collective-permute-start.14 = (f32[3,32,128]{2,1,0:T(8,128)S(1)}, f32[3,32,128]{2,1,0:T(8,128)S(1)}, u32[]{:S(2)}, u32[]{:S(2)}) collective-permute-start(f32[3,32,128]{2,1,0:T(8,128)S(1)} %pad_maximum_fusion.6), channel_id=1, source_target_pairs={{0,8},{8,0},{16,24},{24,16},{1,9},{9,1},{17,25},{25,17},{2,10},{10... | collective-permute-start | bytes 147464 | tf_op jit(solution)/shard_map/ppermute | solution.py:436
  49.6 2.1 %collective-permute-start.15 = (f32[3,32,128]{2,1,0:T(8,128)S(1)}, f32[3,32,128]{2,1,0:T(8,128)S(1)}, u32[]{:S(2)}, u32[]{:S(2)}) collective-permute-start(f32[3,32,128]{2,1,0:T(8,128)S(1)} %pad_maximum_fusion.7), channel_id=1, source_target_pairs={{0,1},{1,0},{2,3},{3,2},{4,5},{5,4},{6,7},{7,6},{8,16},{9,17},{10,... | collective-permute-start | bytes 147464 | tf_op jit(solution)/shard_map/ppermute | solution.py:437
  53.1 1.3 %collective-permute-start.16 = (f32[3,32,128]{2,1,0:T(8,128)S(1)}, f32[3,32,128]{2,1,0:T(8,128)S(1)}, u32[]{:S(2)}, u32[]{:S(2)}) collective-permute-start(f32[3,32,128]{2,1,0:T(8,128)S(1)} %get-tuple-element.98), channel_id=1, source_target_pairs={{0,1},{1,0},{2,3},{3,2},{4,5},{5,4},{6,7},{7,6},{8,9},{9,8},{10,11... | collective-permute-start | bytes 147464 | tf_op jit(solution)/shard_map/ppermute | solution.py:414
  53.2 5.4 %collective-permute-start.17 = (f32[3,32,128]{2,1,0:T(8,128)S(1)}, f32[3,32,128]{2,1,0:T(8,128)S(1)}, u32[]{:S(2)}, u32[]{:S(2)}) collective-permute-start(f32[3,32,128]{2,1,0:T(8,128)S(1)} %get-tuple-element.99), channel_id=1, source_target_pairs={{0,7},{1,2},{2,1},{3,4},{4,3},{5,6},{6,5},{7,0},{8,15},{9,10},{10,... | collective-permute-start | bytes 147464 | tf_op jit(solution)/shard_map/ppermute | solution.py:409
  58.6 5.1 %collective-permute-start.18 = (f32[3,32,128]{2,1,0:T(8,128)S(1)}, f32[3,32,128]{2,1,0:T(8,128)S(1)}, u32[]{:S(2)}, u32[]{:S(2)}) collective-permute-start(f32[3,32,128]{2,1,0:T(8,128)S(1)} %pad_maximum_fusion.8), channel_id=1, source_target_pairs={{0,8},{8,0},{16,24},{24,16},{1,9},{9,1},{17,25},{25,17},{2,10},{10... | collective-permute-start | bytes 147464 | tf_op jit(solution)/shard_map/ppermute | solution.py:436
  61.6 2.1 %collective-permute-start.19 = (f32[3,32,128]{2,1,0:T(8,128)S(1)}, f32[3,32,128]{2,1,0:T(8,128)S(1)}, u32[]{:S(2)}, u32[]{:S(2)}) collective-permute-start(f32[3,32,128]{2,1,0:T(8,128)S(1)} %pad_maximum_fusion.9), channel_id=1, source_target_pairs={{0,1},{1,0},{2,3},{3,2},{4,5},{5,4},{6,7},{7,6},{8,16},{9,17},{10,... | collective-permute-start | bytes 147464 | tf_op jit(solution)/shard_map/ppermute | solution.py:437
  64.7 1.3 %collective-permute-start.20 = (f32[3,32,128]{2,1,0:T(8,128)S(1)}, f32[3,32,128]{2,1,0:T(8,128)S(1)}, u32[]{:S(2)}, u32[]{:S(2)}) collective-permute-start(f32[3,32,128]{2,1,0:T(8,128)S(1)} %get-tuple-element.104), channel_id=1, source_target_pairs={{0,1},{1,0},{2,3},{3,2},{4,5},{5,4},{6,7},{7,6},{8,9},{9,8},{10,11... | collective-permute-start | bytes 147464 | tf_op jit(solution)/shard_map/ppermute | solution.py:414
  64.8 5.4 %collective-permute-start.21 = (f32[3,32,128]{2,1,0:T(8,128)S(1)}, f32[3,32,128]{2,1,0:T(8,128)S(1)}, u32[]{:S(2)}, u32[]{:S(2)}) collective-permute-start(f32[3,32,128]{2,1,0:T(8,128)S(1)} %get-tuple-element.105), channel_id=1, source_target_pairs={{0,7},{1,2},{2,1},{3,4},{4,3},{5,6},{6,5},{7,0},{8,15},{9,10},{10,... | collective-permute-start | bytes 147464 | tf_op jit(solution)/shard_map/ppermute | solution.py:409
  70.2 5.1 %collective-permute-start.22 = (f32[3,32,128]{2,1,0:T(8,128)S(1)}, f32[3,32,128]{2,1,0:T(8,128)S(1)}, u32[]{:S(2)}, u32[]{:S(2)}) collective-permute-start(f32[3,32,128]{2,1,0:T(8,128)S(1)} %pad_maximum_fusion.10), channel_id=1, source_target_pairs={{0,8},{8,0},{16,24},{24,16},{1,9},{9,1},{17,25},{25,17},{2,10},{10... | collective-permute-start | bytes 147464 | tf_op jit(solution)/shard_map/ppermute | solution.py:436
  73.3 2.1 %collective-permute-start.23 = (f32[3,32,128]{2,1,0:T(8,128)S(1)}, f32[3,32,128]{2,1,0:T(8,128)S(1)}, u32[]{:S(2)}, u32[]{:S(2)}) collective-permute-start(f32[3,32,128]{2,1,0:T(8,128)S(1)} %pad_maximum_fusion.11), channel_id=1, source_target_pairs={{0,1},{1,0},{2,3},{3,2},{4,5},{5,4},{6,7},{7,6},{8,16},{9,17},{10,... | collective-permute-start | bytes 147464 | tf_op jit(solution)/shard_map/ppermute | solution.py:437

commit v5 on v4

--- a/solution.py
+++ b/solution.py
@@ -254,21 +254,24 @@
     fill_sent(rest_matrix_ref, list_ref, REST_SENT)
     coupling.wait()
     speed.wait()
+    step = column_ref.shape[0] // round_up(levels, 16)
+    column_ref[...] = jnp.zeros(column_ref.shape, f32)
     for group in range(cells // LANES):
-        column_ref[0:levels, group, :] = coupling_ref[:, 0, group * LANES : (group + 1) * LANES]
-    above = column_ref[0]
+        column_ref[pl.ds(group, levels, stride=step), :] = coupling_ref[:, 0, group * LANES : (group + 1) * LANES]
+    at = lambda level: slice(level * step, (level + 1) * step)
+    above = column_ref[at(0), :]
     inverse = 1.0 / (1.0 + above)
-    inverse_ref[0] = inverse
+    inverse_ref[at(0), :] = inverse
     ratio = above * inverse
-    back_ref[0] = ratio
+    back_ref[at(0), :] = ratio
     for level in range(1, levels):
         below = above
-        above = column_ref[level]
+        above = column_ref[at(level), :]
         inverse = 1.0 / (1.0 + below + above - below * ratio)
-        inverse_ref[level] = inverse
-        forward_ref[level] = below * inverse
+        inverse_ref[at(level), :] = inverse
+        forward_ref[at(level), :] = below * inverse
         ratio = above * inverse
-        back_ref[level] = ratio
+        back_ref[at(level), :] = ratio
 
 
 def part_kernel(own_ref, inner_ref, outer_ref, *rest):
@@ -303,19 +306,27 @@
     rows, cells = cells_ref.shape
     divergence = lat_share(total_ref, lat_inner_ref, lat_outer_ref, [high_ref, low_ref], stack_ref)
     right_side = cells_ref[...] - speed_ref[...] * divergence
+    step = column_ref.shape[0] // rows
     for group in range(cells // LANES):
-        column_ref[:, group, :] = right_side[:, group * LANES : (group + 1) * LANES]
-    current = column_ref[0] * inverse_ref[0]
+        column_ref[pl.ds(group, rows, stride=step), :] = right_side[:, group * LANES : (group + 1) * LANES]
+    for group in range(cells // LANES, step):
+        column_ref[pl.ds(group, rows, stride=step), :] = jnp.zeros((rows, LANES), f32)
+    at = lambda level: slice(level * step, (level + 1) * step)
+    current = column_ref[at(0), :] * inverse_ref[at(0), :]
     scaled = [current]
     for level in range(1, levels):
-        current = column_ref[level] * inverse_ref[level] + forward_ref[level] * current
+        current = column_ref[at(level), :] * inverse_ref[at(level), :] + forward_ref[at(level), :] * current
         scaled.append(current)
-    column_ref[levels - 1] = current
+    column_ref[at(levels - 1), :] = current
     for level in range(levels - 2, -1, -1):
-        current = scaled[level] + back_ref[level] * current
-        column_ref[level] = current
+        current = scaled[level] + back_ref[at(level), :] * current
+        column_ref[at(level), :] = current
     for level in range(levels, rows):
-        column_ref[level] = jnp.zeros_like(current)
+        column_ref[at(level), :] = jnp.zeros_like(current)
+
+
+def solved(column_ref, group, rows):
+    return column_ref[pl.ds(group, rows, stride=column_ref.shape[0] // rows), :]
 
 
 def cell_kernel(
@@ -341,7 +352,7 @@
     rows, cells = cells_ref.shape
     solve_columns(total_ref, lat_inner_ref, lat_outer_ref, high_ref, low_ref, cells_ref, speed_ref, inverse_ref, forward_ref, back_ref, levels, stack_ref, column_ref)
     for group in range(cells // LANES):
-        part = column_ref[:, group, :]
+        part = solved(column_ref, group, rows)
         new_cells_ref[:, group * LANES : (group + 1) * LANES] = part
         put_parts(own_stack_ref, part, group * LANES)
     store_outer(gather_matmul(own_stack_ref, [matrix_ref[...]], rows), outer_ref)
@@ -350,10 +361,10 @@
 def last_kernel(
     total_ref, lat_inner_ref, lat_outer_ref, high_ref, low_ref, cells_ref, speed_ref, inverse_ref, forward_ref, back_ref, out_ref, stack_ref, column_ref, *, levels
 ):
-    cells = cells_ref.shape[1]
+    rows, cells = cells_ref.shape
     solve_columns(total_ref, lat_inner_ref, lat_outer_ref, high_ref, low_ref, cells_ref, speed_ref, inverse_ref, forward_ref, back_ref, levels, stack_ref, column_ref)
     for group in range(cells // LANES):
-        out_ref[:, 0, group * LANES : (group + 1) * LANES] = column_ref[0:levels, group, :]
+        out_ref[:, 0, group * LANES : (group + 1) * LANES] = solved(column_ref, group, rows)[0:levels]
 
 
 def call(body, outs, scratch, *operands, raw=(), copies=0):
@@ -390,7 +401,7 @@
     stack_cells = ((PARTS * rows, cells), bf16)
     stack_edges = ((PARTS * rows, edge_pad), bf16)
     stack_lat = ((PARTS * rows, 6 * halo), bf16)
-    column = ((rows, cells // LANES, LANES), f32)
+    column = ((rows * round_up(cells // LANES, 8), LANES), f32)
     sent_outer = lambda width: ((width, 3 * halo), bf16)
     sent_rest = lambda width: ((width, 5 * halo), bf16)
 

time: 77 us -> 76.5 us (level)
  no operation moved by 1% of the time
where the time goes in v5:
time: 76.5 us; the launch traced here: 76.1 us
  waiting for transfers between devices  28.3 us (37%)
  starting transfers between devices  28 us (37%)
  Pallas kernels  18 us (24%)
  between operations  0.84 us (1%)
  local copies, waits for them, and re-layouts  0.82 us (1%)
    ppermute x6, waiting for transfers between devices, on_device(): outer_in = lax.ppermute(outer, 'lon', lon_routes[1])  20 us
    pallas_call x23, Pallas kernels, call(): pl.pallas_call(body, out_shape=tuple((jax.ShapeDtypeStruct(shape, kind) f...  18 us
    ppermute x6, starting transfers between devices, on_device(): first_in = lax.ppermute(first, 'lat', lat_inner_route)  14.4 us
    ppermute x6, starting transfers between devices, on_device(): outer_in = lax.ppermute(outer, 'lon', lon_routes[1])  11.7 us
    ppermute x6, waiting for transfers between devices, on_device(): first_in = lax.ppermute(first, 'lat', lat_inner_route)  6.32 us
    ppermute x6, waiting for transfers between devices, on_device(): inner_in = lax.ppermute(inner, 'lon', lon_routes[0])  1.98 us
    ppermute x6, starting transfers between devices, on_device(): inner_in = lax.ppermute(inner, 'lon', lon_routes[0])  1.92 us
  transfers between devices with their start and end apart: 24, of which 12 were waited for; matrix products, arithmetic and copies ran while one was open for 1% of the time, Pallas kernels for 13%

profile of v5, /device:TPU:0, one launch (start us, length us, event | category | flops | bytes accessed | tf_op | source)
XLA Modules:
  0.0 76.1 jit_solution(16462320703363382580)
XLA Ops:
  0.6 1.2 %shard_map.113 = (f32[32,640]{1,0:T(8,128)S(1)}, bf16[96,640]{1,0:T(8,128)(2,1)S(1)}, f32[3,32,128]{2,1,0:T(8,128)S(1)}, s32[8,128]{1,0:T(8,128)S(1)}) custom-call(f32[30,1,640]{2,1,0:T(1,128)} %bitcast.36, s32[8,128]{1,0:T(8,128)} %bitcast.42), custom_call_target="tpu_custom_call" | custom-call | tf_op jit(solution)/shard_map/pallas_call | solution.py:377
  1.8 0.5 shard_map.114
  2.3 0.6 collective-permute-start
  2.9 4.7 %collective-permute-start.1 = (f32[3,32,128]{2,1,0:T(8,128)S(1)}, f32[3,32,128]{2,1,0:T(8,128)S(1)}, u32[]{:S(2)}, u32[]{:S(2)}) collective-permute-start(f32[3,32,128]{2,1,0:T(8,128)S(1)} %get-tuple-element.59), channel_id=1, source_target_pairs={{0,7},{1,2},{2,1},{3,4},{4,3},{5,6},{6,5},{7,0},{8,15},{9,10},{10,... | collective-permute-start | bytes 147464 | tf_op jit(solution)/shard_map/ppermute | solution.py:420
  7.6 1.9 %collective-permute-done.1.outer_ref = f32[3,32,128]{2,1,0:T(8,128)S(1)} collective-permute-done((f32[3,32,128]{2,1,0:T(8,128)S(1)}, f32[3,32,128]{2,1,0:T(8,128)S(1)}, u32[]{:S(2)}, u32[]{:S(2)}) %collective-permute-start.1) | collective-permute-done | bytes 49184 | tf_op jit(solution)/shard_map/ppermute | solution.py:420
  9.4 1.6 %collective-permute-start.2 = (f32[3,32,128]{2,1,0:T(8,128)S(1)}, f32[3,32,128]{2,1,0:T(8,128)S(1)}, u32[]{:S(2)}, u32[]{:S(2)}) collective-permute-start(f32[3,32,128]{2,1,0:T(8,128)S(1)} %pad_maximum_fusion), channel_id=1, source_target_pairs={{0,8},{8,0},{16,24},{24,16},{1,9},{9,1},{17,25},{25,17},{2,10},{10... | collective-permute-start | bytes 147464 | tf_op jit(solution)/shard_map/ppermute | solution.py:447
  11.0 1.5 %shard_map.115 = (bf16[896,1024]{1,0:T(8,128)(2,1)S(1)}, bf16[768,1024]{1,0:T(8,128)(2,1)S(1)}) custom-call(s32[2,960]{1,0:T(2,128)} %bitcast.39), custom_call_target="tpu_custom_call" | custom-call | tf_op jit(solution)/shard_map/pallas_call | solution.py:377
  12.5 1.3 %shard_map.117 = (f32[32,1024]{1,0:T(8,128)S(1)}, f32[1,1024]{1,0:T(1,128)S(1)}, bf16[1024,384]{1,0:T(8,128)(2,1)S(1)}, bf16[1024,640]{1,0:T(8,128)(2,1)S(1)}) custom-call(f32[30,1,960]{2,1,0:T(1,128)} %bitcast.35, s32[8,128]{1,0:T(8,128)} %bitcast.43, f32[1,960]{1,0:T(1,128)} %dual_hbm.1), custom_call_target="tpu_custom_call" | custom-call | tf_op jit(solution)/shard_map/pallas_call | solution.py:377
  13.8 0.4 shard_map.116.total_ref
  14.3 0.7 shard_map.118
  14.9 0.4 shard_map.119
  15.3 0.6 collective-permute-start.4
  15.9 3.2 %collective-permute-start.5 = (f32[3,32,128]{2,1,0:T(8,128)S(1)}, f32[3,32,128]{2,1,0:T(8,128)S(1)}, u32[]{:S(2)}, u32[]{:S(2)}) collective-permute-start(f32[3,32,128]{2,1,0:T(8,128)S(1)} %get-tuple-element.71), channel_id=1, source_target_pairs={{0,7},{1,2},{2,1},{3,4},{4,3},{5,6},{6,5},{7,0},{8,15},{9,10},{10,... | collective-permute-start | bytes 147464 | tf_op jit(solution)/shard_map/ppermute | solution.py:420
  19.0 2.6 %collective-permute-done.5.outer_ref = f32[3,32,128]{2,1,0:T(8,128)S(1)} collective-permute-done((f32[3,32,128]{2,1,0:T(8,128)S(1)}, f32[3,32,128]{2,1,0:T(8,128)S(1)}, u32[]{:S(2)}, u32[]{:S(2)}) %collective-permute-start.5) | collective-permute-done | bytes 49184 | tf_op jit(solution)/shard_map/ppermute | solution.py:420
  21.6 2.7 %collective-permute-start.6 = (f32[3,32,128]{2,1,0:T(8,128)S(1)}, f32[3,32,128]{2,1,0:T(8,128)S(1)}, u32[]{:S(2)}, u32[]{:S(2)}) collective-permute-start(f32[3,32,128]{2,1,0:T(8,128)S(1)} %pad_maximum_fusion.2), channel_id=1, source_target_pairs={{0,8},{8,0},{16,24},{24,16},{1,9},{9,1},{17,25},{25,17},{2,10},{10... | collective-permute-start | bytes 147464 | tf_op jit(solution)/shard_map/ppermute | solution.py:447
  24.3 1.2 %shard_map.122 = (f32[1,640]{1,0:T(1,128)S(1)}, f32[256,128]{1,0:T(8,128)S(1)}, f32[256,128]{1,0:T(8,128)S(1)}, f32[256,128]{1,0:T(8,128)S(1)}, bf16[640,384]{1,...) custom-call(f32[30,1,640]{2,1,0:T(1,128)} %bitcast.37, s32[8,128]{1,0:T(8,128)S(1)} %get-tuple-element.57.list_ref, ...), custom_call_target="tpu_custom_call" | custom-call | tf_op jit(solution)/shard_map/pallas_call | solution.py:377
  25.5 2.4 %shard_map.120 = (bf16[1280,640]{1,0:T(8,128)(2,1)S(1)}, bf16[1280,640]{1,0:T(8,128)(2,1)S(1)}, bf16[768,640]{1,0:T(8,128)(2,1)S(1)}, bf16[768,640]{1,0:T(8,128)(2,1)S(1)}) custom-call(s32[3,1,640]{2,1,0:T(1,128)} %bitcast.40, f32[3,1,640]{2,1,0:T(1,128)} %bitcast.41), custom_call_target="tpu_custom_call" | custom-call | tf_op jit(solution)/shard_map/pallas_call | solution.py:377
  27.9 0.7 shard_map.121.total_ref
  28.6 0.9 %shard_map.123 = (f32[32,640]{1,0:T(8,128)S(1)}, f32[3,32,128]{2,1,0:T(8,128)S(1)}, bf16[96,640]{1,0:T(8,128)(2,1)S(1)}) custom-call(f32[32,640]{1,0:T(8,128)S(1)} %shard_map.121.total_ref, f32[3,32,128]{2,1,0:T(8,128)S(1)} %collective-permute-done.6.lat_inner_ref, f32[3,32,128]{2,1,0:T(8,128)S(1)} %collective-permute-done.7.lat_outer_ref, ...), custom_call_target="tpu_custom_call" | custom-call | tf_op jit(solution)/shard_map/pallas_call | solution.py:377
  29.8 0.6 collective-permute-start.8
  30.4 2.1 %collective-permute-start.9 = (f32[3,32,128]{2,1,0:T(8,128)S(1)}, f32[3,32,128]{2,1,0:T(8,128)S(1)}, u32[]{:S(2)}, u32[]{:S(2)}) collective-permute-start(f32[3,32,128]{2,1,0:T(8,128)S(1)} %get-tuple-element.87), channel_id=1, source_target_pairs={{0,7},{1,2},{2,1},{3,4},{4,3},{5,6},{6,5},{7,0},{8,15},{9,10},{10,... | collective-permute-start | bytes 147464 | tf_op jit(solution)/shard_map/ppermute | solution.py:420
  32.5 3.2 %collective-permute-done.9.outer_ref = f32[3,32,128]{2,1,0:T(8,128)S(1)} collective-permute-done((f32[3,32,128]{2,1,0:T(8,128)S(1)}, f32[3,32,128]{2,1,0:T(8,128)S(1)}, u32[]{:S(2)}, u32[]{:S(2)}) %collective-permute-start.9) | collective-permute-done | bytes 49184 | tf_op jit(solution)/shard_map/ppermute | solution.py:420
  35.7 1.0 %collective-permute-start.10 = (f32[3,32,128]{2,1,0:T(8,128)S(1)}, f32[3,32,128]{2,1,0:T(8,128)S(1)}, u32[]{:S(2)}, u32[]{:S(2)}) collective-permute-start(f32[3,32,128]{2,1,0:T(8,128)S(1)} %pad_maximum_fusion.4), channel_id=1, source_target_pairs={{0,8},{8,0},{16,24},{24,16},{1,9},{9,1},{17,25},{25,17},{2,10},{10... | collective-permute-start | bytes 147464 | tf_op jit(solution)/shard_map/ppermute | solution.py:447
  36.7 0.4 shard_map.125.total_ref
  37.1 2.7 %collective-permute-done.10.lat_inner_ref = f32[3,32,128]{2,1,0:T(8,128)S(1)} collective-permute-done((f32[3,32,128]{2,1,0:T(8,128)S(1)}, f32[3,32,128]{2,1,0:T(8,128)S(1)}, u32[]{:S(2)}, u32[]{:S(2)}) %collective-permute-start.10) | collective-permute-done | bytes 49184 | tf_op jit(solution)/shard_map/ppermute | solution.py:447
  39.8 0.6 shard_map.126
  40.5 0.4 shard_map.127
  40.9 1.3 %collective-permute-start.13 = (f32[3,32,128]{2,1,0:T(8,128)S(1)}, f32[3,32,128]{2,1,0:T(8,128)S(1)}, u32[]{:S(2)}, u32[]{:S(2)}) collective-permute-start(f32[3,32,128]{2,1,0:T(8,128)S(1)} %get-tuple-element.93), channel_id=1, source_target_pairs={{0,7},{1,2},{2,1},{3,4},{4,3},{5,6},{6,5},{7,0},{8,15},{9,10},{10,... | collective-permute-start | bytes 147464 | tf_op jit(solution)/shard_map/ppermute | solution.py:420
  42.2 4.1 %collective-permute-done.13.outer_ref = f32[3,32,128]{2,1,0:T(8,128)S(1)} collective-permute-done((f32[3,32,128]{2,1,0:T(8,128)S(1)}, f32[3,32,128]{2,1,0:T(8,128)S(1)}, u32[]{:S(2)}, u32[]{:S(2)}) %collective-permute-start.13) | collective-permute-done | bytes 49184 | tf_op jit(solution)/shard_map/ppermute | solution.py:420
  46.3 3.0 %collective-permute-start.14 = (f32[3,32,128]{2,1,0:T(8,128)S(1)}, f32[3,32,128]{2,1,0:T(8,128)S(1)}, u32[]{:S(2)}, u32[]{:S(2)}) collective-permute-start(f32[3,32,128]{2,1,0:T(8,128)S(1)} %pad_maximum_fusion.6), channel_id=1, source_target_pairs={{0,8},{8,0},{16,24},{24,16},{1,9},{9,1},{17,25},{25,17},{2,10},{10... | collective-permute-start | bytes 147464 | tf_op jit(solution)/shard_map/ppermute | solution.py:447
  49.3 0.7 shard_map.128.total_ref
  50.0 1.4 %collective-permute-done.14.lat_inner_ref = f32[3,32,128]{2,1,0:T(8,128)S(1)} collective-permute-done((f32[3,32,128]{2,1,0:T(8,128)S(1)}, f32[3,32,128]{2,1,0:T(8,128)S(1)}, u32[]{:S(2)}, u32[]{:S(2)}) %collective-permute-start.14) | collective-permute-done | bytes 49184 | tf_op jit(solution)/shard_map/ppermute | solution.py:447
  51.4 0.9 %shard_map.129 = (f32[32,640]{1,0:T(8,128)S(1)}, f32[3,32,128]{2,1,0:T(8,128)S(1)}, bf16[96,640]{1,0:T(8,128)(2,1)S(1)}) custom-call(f32[32,640]{1,0:T(8,128)S(1)} %shard_map.128.total_ref, f32[3,32,128]{2,1,0:T(8,128)S(1)} %collective-permute-done.14.lat_inner_ref, f32[3,32,128]{2,1,0:T(8,128)S(1)} %collective-permute-done.15.lat_outer_ref, ...), custom_call_target="tpu_custom_call" | custom-call | tf_op jit(solution)/shard_map/pallas_call | solution.py:377
  52.6 0.4 collective-permute-start.17
  53.0 0.8 %collective-permute-done.16.inner_ref = f32[3,32,128]{2,1,0:T(8,128)S(1)} collective-permute-done((f32[3,32,128]{2,1,0:T(8,128)S(1)}, f32[3,32,128]{2,1,0:T(8,128)S(1)}, u32[]{:S(2)}, u32[]{:S(2)}) %collective-permute-start.16) | collective-permute-done | bytes 49184 | tf_op jit(solution)/shard_map/ppermute | solution.py:425
  53.9 4.2 %collective-permute-done.17.outer_ref = f32[3,32,128]{2,1,0:T(8,128)S(1)} collective-permute-done((f32[3,32,128]{2,1,0:T(8,128)S(1)}, f32[3,32,128]{2,1,0:T(8,128)S(1)}, u32[]{:S(2)}, u32[]{:S(2)}) %collective-permute-start.17) | collective-permute-done | bytes 49184 | tf_op jit(solution)/shard_map/ppermute | solution.py:420
  58.0 3.1 %collective-permute-start.18 = (f32[3,32,128]{2,1,0:T(8,128)S(1)}, f32[3,32,128]{2,1,0:T(8,128)S(1)}, u32[]{:S(2)}, u32[]{:S(2)}) collective-permute-start(f32[3,32,128]{2,1,0:T(8,128)S(1)} %pad_maximum_fusion.8), channel_id=1, source_target_pairs={{0,8},{8,0},{16,24},{24,16},{1,9},{9,1},{17,25},{25,17},{2,10},{10... | collective-permute-start | bytes 147464 | tf_op jit(solution)/shard_map/ppermute | solution.py:447
  61.1 0.4 shard_map.131.total_ref
  61.6 1.6 %collective-permute-done.18.lat_inner_ref = f32[3,32,128]{2,1,0:T(8,128)S(1)} collective-permute-done((f32[3,32,128]{2,1,0:T(8,128)S(1)}, f32[3,32,128]{2,1,0:T(8,128)S(1)}, u32[]{:S(2)}, u32[]{:S(2)}) %collective-permute-start.18) | collective-permute-done | bytes 49184 | tf_op jit(solution)/shard_map/ppermute | solution.py:447
  63.2 0.6 shard_map.132
  63.8 0.4 shard_map.133
  64.4 1.1 %collective-permute-done.20.inner_ref = f32[3,32,128]{2,1,0:T(8,128)S(1)} collective-permute-done((f32[3,32,128]{2,1,0:T(8,128)S(1)}, f32[3,32,128]{2,1,0:T(8,128)S(1)}, u32[]{:S(2)}, u32[]{:S(2)}) %collective-permute-start.20) | collective-permute-done | bytes 49184 | tf_op jit(solution)/shard_map/ppermute | solution.py:425
  65.5 4.2 %collective-permute-done.21.outer_ref = f32[3,32,128]{2,1,0:T(8,128)S(1)} collective-permute-done((f32[3,32,128]{2,1,0:T(8,128)S(1)}, f32[3,32,128]{2,1,0:T(8,128)S(1)}, u32[]{:S(2)}, u32[]{:S(2)}) %collective-permute-start.21) | collective-permute-done | bytes 49184 | tf_op jit(solution)/shard_map/ppermute | solution.py:420
  69.7 3.1 %collective-permute-start.22 = (f32[3,32,128]{2,1,0:T(8,128)S(1)}, f32[3,32,128]{2,1,0:T(8,128)S(1)}, u32[]{:S(2)}, u32[]{:S(2)}) collective-permute-start(f32[3,32,128]{2,1,0:T(8,128)S(1)} %pad_maximum_fusion.10), channel_id=1, source_target_pairs={{0,8},{8,0},{16,24},{24,16},{1,9},{9,1},{17,25},{25,17},{2,10},{10... | collective-permute-start | bytes 147464 | tf_op jit(solution)/shard_map/ppermute | solution.py:447
  72.8 0.8 %copy.12 = f32[1,30,960]{2,0,1:T(1,128)} copy(f32[1,30,960]{2,1,0:T(8,128)S(1)} %slice_bitcast_fusion) | data formatting | bytes 230400
  73.5 0.7 shard_map.134.total_ref
  74.2 0.6 collective-permute-done.22.lat_inner_ref
  74.8 1.3 %shard_map.135 = f32[30,1,640]{2,1,0:T(1,128)} custom-call(f32[32,640]{1,0:T(8,128)S(1)} %shard_map.134.total_ref, f32[3,32,128]{2,1,0:T(8,128)S(1)} %collective-permute-done.22.lat_inner_ref, f32[3,32,128]{2,1,0:T(8,128)S(1)} %collective-permute-done.23.lat_outer_ref, bf16[768,640]{1,0:T(8,128)(2,1)S(1)} %get-tuple-element.76.high_ref, ...), custom_call_target="tpu_custom_call" | custom-call | tf_op jit(solution)/shard_map/pallas_call | solution.py:377
  (49 shorter events, 1.0 us)
Async XLA Ops:
  2.3 5.3 %collective-permute-start = (f32[3,32,128]{2,1,0:T(8,128)S(1)}, f32[3,32,128]{2,1,0:T(8,128)S(1)}, u32[]{:S(2)}, u32[]{:S(2)}) collective-permute-start(f32[3,32,128]{2,1,0:T(8,128)S(1)} %get-tuple-element.58), channel_id=1, source_target_pairs={{0,1},{1,0},{2,3},{3,2},{4,5},{5,4},{6,7},{7,6},{8,9},{9,8},{10,11... | collective-permute-start | bytes 147464 | tf_op jit(solution)/shard_map/ppermute | solution.py:425
  2.9 6.6 %collective-permute-start.1 = (f32[3,32,128]{2,1,0:T(8,128)S(1)}, f32[3,32,128]{2,1,0:T(8,128)S(1)}, u32[]{:S(2)}, u32[]{:S(2)}) collective-permute-start(f32[3,32,128]{2,1,0:T(8,128)S(1)} %get-tuple-element.59), channel_id=1, source_target_pairs={{0,7},{1,2},{2,1},{3,4},{4,3},{5,6},{6,5},{7,0},{8,15},{9,10},{10,... | collective-permute-start | bytes 147464 | tf_op jit(solution)/shard_map/ppermute | solution.py:420
  9.4 4.8 %collective-permute-start.2 = (f32[3,32,128]{2,1,0:T(8,128)S(1)}, f32[3,32,128]{2,1,0:T(8,128)S(1)}, u32[]{:S(2)}, u32[]{:S(2)}) collective-permute-start(f32[3,32,128]{2,1,0:T(8,128)S(1)} %pad_maximum_fusion), channel_id=1, source_target_pairs={{0,8},{8,0},{16,24},{24,16},{1,9},{9,1},{17,25},{25,17},{2,10},{10... | collective-permute-start | bytes 147464 | tf_op jit(solution)/shard_map/ppermute | solution.py:447
  11.0 3.2 %collective-permute-start.3 = (f32[3,32,128]{2,1,0:T(8,128)S(1)}, f32[3,32,128]{2,1,0:T(8,128)S(1)}, u32[]{:S(2)}, u32[]{:S(2)}) collective-permute-start(f32[3,32,128]{2,1,0:T(8,128)S(1)} %pad_maximum_fusion.1), channel_id=1, source_target_pairs={{0,1},{1,0},{2,3},{3,2},{4,5},{5,4},{6,7},{7,6},{8,16},{9,17},{10,... | collective-permute-start | bytes 147464 | tf_op jit(solution)/shard_map/ppermute | solution.py:448
  15.3 3.7 %collective-permute-start.4 = (f32[3,32,128]{2,1,0:T(8,128)S(1)}, f32[3,32,128]{2,1,0:T(8,128)S(1)}, u32[]{:S(2)}, u32[]{:S(2)}) collective-permute-start(f32[3,32,128]{2,1,0:T(8,128)S(1)} %get-tuple-element.70), channel_id=1, source_target_pairs={{0,1},{1,0},{2,3},{3,2},{4,5},{5,4},{6,7},{7,6},{8,9},{9,8},{10,11... | collective-permute-start | bytes 147464 | tf_op jit(solution)/shard_map/ppermute | solution.py:425
  15.9 5.7 %collective-permute-start.5 = (f32[3,32,128]{2,1,0:T(8,128)S(1)}, f32[3,32,128]{2,1,0:T(8,128)S(1)}, u32[]{:S(2)}, u32[]{:S(2)}) collective-permute-start(f32[3,32,128]{2,1,0:T(8,128)S(1)} %get-tuple-element.71), channel_id=1, source_target_pairs={{0,7},{1,2},{2,1},{3,4},{4,3},{5,6},{6,5},{7,0},{8,15},{9,10},{10,... | collective-permute-start | bytes 147464 | tf_op jit(solution)/shard_map/ppermute | solution.py:420
  21.6 7.0 %collective-permute-start.6 = (f32[3,32,128]{2,1,0:T(8,128)S(1)}, f32[3,32,128]{2,1,0:T(8,128)S(1)}, u32[]{:S(2)}, u32[]{:S(2)}) collective-permute-start(f32[3,32,128]{2,1,0:T(8,128)S(1)} %pad_maximum_fusion.2), channel_id=1, source_target_pairs={{0,8},{8,0},{16,24},{24,16},{1,9},{9,1},{17,25},{25,17},{2,10},{10... | collective-permute-start | bytes 147464 | tf_op jit(solution)/shard_map/ppermute | solution.py:447
  24.3 4.3 %collective-permute-start.7 = (f32[3,32,128]{2,1,0:T(8,128)S(1)}, f32[3,32,128]{2,1,0:T(8,128)S(1)}, u32[]{:S(2)}, u32[]{:S(2)}) collective-permute-start(f32[3,32,128]{2,1,0:T(8,128)S(1)} %pad_maximum_fusion.3), channel_id=1, source_target_pairs={{0,1},{1,0},{2,3},{3,2},{4,5},{5,4},{6,7},{7,6},{8,16},{9,17},{10,... | collective-permute-start | bytes 147464 | tf_op jit(solution)/shard_map/ppermute | solution.py:448
  29.8 2.7 %collective-permute-start.8 = (f32[3,32,128]{2,1,0:T(8,128)S(1)}, f32[3,32,128]{2,1,0:T(8,128)S(1)}, u32[]{:S(2)}, u32[]{:S(2)}) collective-permute-start(f32[3,32,128]{2,1,0:T(8,128)S(1)} %get-tuple-element.86), channel_id=1, source_target_pairs={{0,1},{1,0},{2,3},{3,2},{4,5},{5,4},{6,7},{7,6},{8,9},{9,8},{10,11... | collective-permute-start | bytes 147464 | tf_op jit(solution)/shard_map/ppermute | solution.py:425
  30.4 5.3 %collective-permute-start.9 = (f32[3,32,128]{2,1,0:T(8,128)S(1)}, f32[3,32,128]{2,1,0:T(8,128)S(1)}, u32[]{:S(2)}, u32[]{:S(2)}) collective-permute-start(f32[3,32,128]{2,1,0:T(8,128)S(1)} %get-tuple-element.87), channel_id=1, source_target_pairs={{0,7},{1,2},{2,1},{3,4},{4,3},{5,6},{6,5},{7,0},{8,15},{9,10},{10,... | collective-permute-start | bytes 147464 | tf_op jit(solution)/shard_map/ppermute | solution.py:420
  35.7 4.2 %collective-permute-start.10 = (f32[3,32,128]{2,1,0:T(8,128)S(1)}, f32[3,32,128]{2,1,0:T(8,128)S(1)}, u32[]{:S(2)}, u32[]{:S(2)}) collective-permute-start(f32[3,32,128]{2,1,0:T(8,128)S(1)} %pad_maximum_fusion.4), channel_id=1, source_target_pairs={{0,8},{8,0},{16,24},{24,16},{1,9},{9,1},{17,25},{25,17},{2,10},{10... | collective-permute-start | bytes 147464 | tf_op jit(solution)/shard_map/ppermute | solution.py:447
  36.7 3.2 %collective-permute-start.11 = (f32[3,32,128]{2,1,0:T(8,128)S(1)}, f32[3,32,128]{2,1,0:T(8,128)S(1)}, u32[]{:S(2)}, u32[]{:S(2)}) collective-permute-start(f32[3,32,128]{2,1,0:T(8,128)S(1)} %pad_maximum_fusion.5), channel_id=1, source_target_pairs={{0,1},{1,0},{2,3},{3,2},{4,5},{5,4},{6,7},{7,6},{8,16},{9,17},{10,... | collective-permute-start | bytes 147464 | tf_op jit(solution)/shard_map/ppermute | solution.py:448
  40.9 1.4 %collective-permute-start.12 = (f32[3,32,128]{2,1,0:T(8,128)S(1)}, f32[3,32,128]{2,1,0:T(8,128)S(1)}, u32[]{:S(2)}, u32[]{:S(2)}) collective-permute-start(f32[3,32,128]{2,1,0:T(8,128)S(1)} %get-tuple-element.92), channel_id=1, source_target_pairs={{0,1},{1,0},{2,3},{3,2},{4,5},{5,4},{6,7},{7,6},{8,9},{9,8},{10,11... | collective-permute-start | bytes 147464 | tf_op jit(solution)/shard_map/ppermute | solution.py:425
  40.9 5.4 %collective-permute-start.13 = (f32[3,32,128]{2,1,0:T(8,128)S(1)}, f32[3,32,128]{2,1,0:T(8,128)S(1)}, u32[]{:S(2)}, u32[]{:S(2)}) collective-permute-start(f32[3,32,128]{2,1,0:T(8,128)S(1)} %get-tuple-element.93), channel_id=1, source_target_pairs={{0,7},{1,2},{2,1},{3,4},{4,3},{5,6},{6,5},{7,0},{8,15},{9,10},{10,... | collective-permute-start | bytes 147464 | tf_op jit(solution)/shard_map/ppermute | solution.py:420
  46.3 5.1 %collective-permute-start.14 = (f32[3,32,128]{2,1,0:T(8,128)S(1)}, f32[3,32,128]{2,1,0:T(8,128)S(1)}, u32[]{:S(2)}, u32[]{:S(2)}) collective-permute-start(f32[3,32,128]{2,1,0:T(8,128)S(1)} %pad_maximum_fusion.6), channel_id=1, source_target_pairs={{0,8},{8,0},{16,24},{24,16},{1,9},{9,1},{17,25},{25,17},{2,10},{10... | collective-permute-start | bytes 147464 | tf_op jit(solution)/shard_map/ppermute | solution.py:447
  49.3 2.1 %collective-permute-start.15 = (f32[3,32,128]{2,1,0:T(8,128)S(1)}, f32[3,32,128]{2,1,0:T(8,128)S(1)}, u32[]{:S(2)}, u32[]{:S(2)}) collective-permute-start(f32[3,32,128]{2,1,0:T(8,128)S(1)} %pad_maximum_fusion.7), channel_id=1, source_target_pairs={{0,1},{1,0},{2,3},{3,2},{4,5},{5,4},{6,7},{7,6},{8,16},{9,17},{10,... | collective-permute-start | bytes 147464 | tf_op jit(solution)/shard_map/ppermute | solution.py:448
  52.6 1.3 %collective-permute-start.16 = (f32[3,32,128]{2,1,0:T(8,128)S(1)}, f32[3,32,128]{2,1,0:T(8,128)S(1)}, u32[]{:S(2)}, u32[]{:S(2)}) collective-permute-start(f32[3,32,128]{2,1,0:T(8,128)S(1)} %get-tuple-element.98), channel_id=1, source_target_pairs={{0,1},{1,0},{2,3},{3,2},{4,5},{5,4},{6,7},{7,6},{8,9},{9,8},{10,11... | collective-permute-start | bytes 147464 | tf_op jit(solution)/shard_map/ppermute | solution.py:425
  52.6 5.4 %collective-permute-start.17 = (f32[3,32,128]{2,1,0:T(8,128)S(1)}, f32[3,32,128]{2,1,0:T(8,128)S(1)}, u32[]{:S(2)}, u32[]{:S(2)}) collective-permute-start(f32[3,32,128]{2,1,0:T(8,128)S(1)} %get-tuple-element.99), channel_id=1, source_target_pairs={{0,7},{1,2},{2,1},{3,4},{4,3},{5,6},{6,5},{7,0},{8,15},{9,10},{10,... | collective-permute-start | bytes 147464 | tf_op jit(solution)/shard_map/ppermute | solution.py:420
  58.0 5.1 %collective-permute-start.18 = (f32[3,32,128]{2,1,0:T(8,128)S(1)}, f32[3,32,128]{2,1,0:T(8,128)S(1)}, u32[]{:S(2)}, u32[]{:S(2)}) collective-permute-start(f32[3,32,128]{2,1,0:T(8,128)S(1)} %pad_maximum_fusion.8), channel_id=1, source_target_pairs={{0,8},{8,0},{16,24},{24,16},{1,9},{9,1},{17,25},{25,17},{2,10},{10... | collective-permute-start | bytes 147464 | tf_op jit(solution)/shard_map/ppermute | solution.py:447
  61.1 2.1 %collective-permute-start.19 = (f32[3,32,128]{2,1,0:T(8,128)S(1)}, f32[3,32,128]{2,1,0:T(8,128)S(1)}, u32[]{:S(2)}, u32[]{:S(2)}) collective-permute-start(f32[3,32,128]{2,1,0:T(8,128)S(1)} %pad_maximum_fusion.9), channel_id=1, source_target_pairs={{0,1},{1,0},{2,3},{3,2},{4,5},{5,4},{6,7},{7,6},{8,16},{9,17},{10,... | collective-permute-start | bytes 147464 | tf_op jit(solution)/shard_map/ppermute | solution.py:448
  64.2 1.3 %collective-permute-start.20 = (f32[3,32,128]{2,1,0:T(8,128)S(1)}, f32[3,32,128]{2,1,0:T(8,128)S(1)}, u32[]{:S(2)}, u32[]{:S(2)}) collective-permute-start(f32[3,32,128]{2,1,0:T(8,128)S(1)} %get-tuple-element.104), channel_id=1, source_target_pairs={{0,1},{1,0},{2,3},{3,2},{4,5},{5,4},{6,7},{7,6},{8,9},{9,8},{10,11... | collective-permute-start | bytes 147464 | tf_op jit(solution)/shard_map/ppermute | solution.py:425
  64.3 5.4 %collective-permute-start.21 = (f32[3,32,128]{2,1,0:T(8,128)S(1)}, f32[3,32,128]{2,1,0:T(8,128)S(1)}, u32[]{:S(2)}, u32[]{:S(2)}) collective-permute-start(f32[3,32,128]{2,1,0:T(8,128)S(1)} %get-tuple-element.105), channel_id=1, source_target_pairs={{0,7},{1,2},{2,1},{3,4},{4,3},{5,6},{6,5},{7,0},{8,15},{9,10},{10,... | collective-permute-start | bytes 147464 | tf_op jit(solution)/shard_map/ppermute | solution.py:420
  69.7 5.1 %collective-permute-start.22 = (f32[3,32,128]{2,1,0:T(8,128)S(1)}, f32[3,32,128]{2,1,0:T(8,128)S(1)}, u32[]{:S(2)}, u32[]{:S(2)}) collective-permute-start(f32[3,32,128]{2,1,0:T(8,128)S(1)} %pad_maximum_fusion.10), channel_id=1, source_target_pairs={{0,8},{8,0},{16,24},{24,16},{1,9},{9,1},{17,25},{25,17},{2,10},{10... | collective-permute-start | bytes 147464 | tf_op jit(solution)/shard_map/ppermute | solution.py:447
  72.8 2.1 %collective-permute-start.23 = (f32[3,32,128]{2,1,0:T(8,128)S(1)}, f32[3,32,128]{2,1,0:T(8,128)S(1)}, u32[]{:S(2)}, u32[]{:S(2)}) collective-permute-start(f32[3,32,128]{2,1,0:T(8,128)S(1)} %pad_maximum_fusion.11), channel_id=1, source_target_pairs={{0,1},{1,0},{2,3},{3,2},{4,5},{5,4},{6,7},{7,6},{8,16},{9,17},{10,... | collective-permute-start | bytes 147464 | tf_op jit(solution)/shard_map/ppermute | solution.py:448

commit v6 on v5

--- a/solution.py
+++ b/solution.py
@@ -284,27 +284,32 @@
     total_ref[...] = gather_matmul(stack_ref, [ref[...] for ref in matrix_refs], rows)
 
 
-def lat_share(total_ref, lat_inner_ref, lat_outer_ref, matrix_refs, stack_ref):
+def lat_share(total_ref, lat_ref, matrix_refs, stack_ref, half):
     rows = total_ref.shape[0]
-    halo = lat_inner_ref.shape[2]
+    halo = lat_ref.shape[2]
     for member in range(3):
-        put_parts(stack_ref, lat_inner_ref[member], member * halo)
-        put_parts(stack_ref, lat_outer_ref[member], (3 + member) * halo)
-    return total_ref[...] + gather_matmul(stack_ref, [ref[...] for ref in matrix_refs], rows)
-
-
-def edge_kernel(total_ref, lat_inner_ref, lat_outer_ref, far_ref, edges_ref, scale_ref, matrix_ref, new_edges_ref, outer_ref, own_stack_ref, stack_ref):
+        put_parts(stack_ref, lat_ref[member], member * halo)
+    matrices = [ref[half * 3 * halo : (half + 1) * 3 * halo, :] for ref in matrix_refs]
+    return total_ref[...] + gather_matmul(stack_ref, matrices, rows)
+
+
+def inner_share_kernel(total_ref, lat_inner_ref, *rest):
+    *matrix_refs, new_total_ref, stack_ref = rest
+    new_total_ref[...] = lat_share(total_ref, lat_inner_ref, matrix_refs, stack_ref, 0)
+
+
+def edge_kernel(total_ref, lat_outer_ref, far_ref, edges_ref, scale_ref, matrix_ref, new_edges_ref, outer_ref, own_stack_ref, stack_ref):
     rows = edges_ref.shape[0]
-    difference = lat_share(total_ref, lat_inner_ref, lat_outer_ref, [far_ref], stack_ref)
+    difference = lat_share(total_ref, lat_outer_ref, [far_ref], stack_ref, 1)
     new_edges = edges_ref[...] - scale_ref[...] * difference
     new_edges_ref[...] = new_edges
     put_parts(own_stack_ref, new_edges, 0)
     store_outer(gather_matmul(own_stack_ref, [matrix_ref[...]], rows), outer_ref)
 
 
-def solve_columns(total_ref, lat_inner_ref, lat_outer_ref, high_ref, low_ref, cells_ref, speed_ref, inverse_ref, forward_ref, back_ref, levels, stack_ref, column_ref):
+def solve_columns(total_ref, lat_outer_ref, high_ref, low_ref, cells_ref, speed_ref, inverse_ref, forward_ref, back_ref, levels, stack_ref, column_ref):
     rows, cells = cells_ref.shape
-    divergence = lat_share(total_ref, lat_inner_ref, lat_outer_ref, [high_ref, low_ref], stack_ref)
+    divergence = lat_share(total_ref, lat_outer_ref, [high_ref, low_ref], stack_ref, 1)
     right_side = cells_ref[...] - speed_ref[...] * divergence
     step = column_ref.shape[0] // rows
     for group in range(cells // LANES):
@@ -331,7 +336,6 @@
 
 def cell_kernel(
     total_ref,
-    lat_inner_ref,
     lat_outer_ref,
     high_ref,
     low_ref,
@@ -350,7 +354,7 @@
     levels,
 ):
     rows, cells = cells_ref.shape
-    solve_columns(total_ref, lat_inner_ref, lat_outer_ref, high_ref, low_ref, cells_ref, speed_ref, inverse_ref, forward_ref, back_ref, levels, stack_ref, column_ref)
+    solve_columns(total_ref, lat_outer_ref, high_ref, low_ref, cells_ref, speed_ref, inverse_ref, forward_ref, back_ref, levels, stack_ref, column_ref)
     for group in range(cells // LANES):
         part = solved(column_ref, group, rows)
         new_cells_ref[:, group * LANES : (group + 1) * LANES] = part
@@ -359,10 +363,10 @@
 
 
 def last_kernel(
-    total_ref, lat_inner_ref, lat_outer_ref, high_ref, low_ref, cells_ref, speed_ref, inverse_ref, forward_ref, back_ref, out_ref, stack_ref, column_ref, *, levels
+    total_ref, lat_outer_ref, high_ref, low_ref, cells_ref, speed_ref, inverse_ref, forward_ref, back_ref, out_ref, stack_ref, column_ref, *, levels
 ):
     rows, cells = cells_ref.shape
-    solve_columns(total_ref, lat_inner_ref, lat_outer_ref, high_ref, low_ref, cells_ref, speed_ref, inverse_ref, forward_ref, back_ref, levels, stack_ref, column_ref)
+    solve_columns(total_ref, lat_outer_ref, high_ref, low_ref, cells_ref, speed_ref, inverse_ref, forward_ref, back_ref, levels, stack_ref, column_ref)
     for group in range(cells // LANES):
         out_ref[:, 0, group * LANES : (group + 1) * LANES] = solved(column_ref, group, rows)[0:levels]
 
@@ -400,7 +404,7 @@
     by_level = lambda value: value.transpose(1, 0, 2)
     stack_cells = ((PARTS * rows, cells), bf16)
     stack_edges = ((PARTS * rows, edge_pad), bf16)
-    stack_lat = ((PARTS * rows, 6 * halo), bf16)
+    stack_lat = ((PARTS * rows, 3 * halo), bf16)
     column = ((rows * round_up(cells // LANES, 8), LANES), f32)
     sent_outer = lambda width: ((width, 3 * halo), bf16)
     sent_rest = lambda width: ((width, 5 * halo), bf16)
@@ -478,12 +482,12 @@
                 outer_in,
                 gradient_near,
             )
+            (total,) = call(inner_share_kernel, [((rows, edge_pad), f32)], [stack_lat], total, first_in, gradient_far)
             normal, outer, stack = call(
                 edge_kernel,
                 [((rows, edge_pad), f32), bundle, stack_edges],
                 [stack_lat],
                 total,
-                first_in,
                 second_in,
                 gradient_far,
                 normal,
@@ -501,7 +505,8 @@
                 near_high,
                 near_low,
             )
-            operands = (total, first_in, second_in, far_high, far_low, values, speed, inverse, forward, back)
+            (total,) = call(inner_share_kernel, [((rows, cells), f32)], [stack_lat], total, first_in, far_high, far_low)
+            operands = (total, second_in, far_high, far_low, values, speed, inverse, forward, back)
             if phase < 2 * NSUB - 1:
                 values, outer, stack = call(
                     functools.partial(cell_kernel, levels=levels),

time: 76.5 us -> 76.4 us (level)
  starting transfers between devices: 28 us -> 26.8 us
  Pallas kernels: 18 us -> 18.8 us
    ppermute x6, starting transfers between devices: 14.4 us -> 13.1 us  [on_device(): first_in = lax.ppermute(first, 'lat', lat_inner_route)]
    pallas_call x23 -> x29, Pallas kernels: 18 us -> 18.8 us  [call(): pl.pallas_call(body, out_shape=tuple((jax.ShapeDtypeStruct(shape, kind) f...]
  transfers between devices with their start and end apart: 24 -> 24, of which waited for: 12 -> 12; matrix products, arithmetic and copies ran while one was open for 1% -> 1% of each run, Pallas kernels for 13% -> 15%
where the time goes in v6:
time: 76.4 us; the launch traced here: 76.1 us
  waiting for transfers between devices  28.7 us (38%)
  starting transfers between devices  26.8 us (35%)
  Pallas kernels  18.8 us (25%)
  between operations  0.89 us (1%)
  local copies, waits for them, and re-layouts  0.82 us (1%)
    ppermute x6, waiting for transfers between devices, on_device(): outer_in = lax.ppermute(outer, 'lon', lon_routes[1])  20 us
    pallas_call x29, Pallas kernels, call(): pl.pallas_call(body, out_shape=tuple((jax.ShapeDtypeStruct(shape, kind) f...  18.8 us
    ppermute x6, starting transfers between devices, on_device(): first_in = lax.ppermute(first, 'lat', lat_inner_route)  13.1 us
    ppermute x6, starting transfers between devices, on_device(): outer_in = lax.ppermute(outer, 'lon', lon_routes[1])  11.7 us
    ppermute x6, waiting for transfers between devices, on_device(): first_in = lax.ppermute(first, 'lat', lat_inner_route)  6.6 us
    ppermute x6, waiting for transfers between devices, on_device(): inner_in = lax.ppermute(inner, 'lon', lon_routes[0])  1.99 us
    ppermute x6, starting transfers between devices, on_device(): inner_in = lax.ppermute(inner, 'lon', lon_routes[0])  1.91 us
  transfers between devices with their start and end apart: 24, of which 12 were waited for; matrix products, arithmetic and copies ran while one was open for 1% of the time, Pallas kernels for 15%

profile of v6, /device:TPU:0, one launch (start us, length us, event | category | flops | bytes accessed | tf_op | source)
XLA Modules:
  0.0 76.1 jit_solution(9007266354769773319)
XLA Ops:
  0.6 1.2 %shard_map.113 = (f32[32,640]{1,0:T(8,128)S(1)}, bf16[96,640]{1,0:T(8,128)(2,1)S(1)}, f32[3,32,128]{2,1,0:T(8,128)S(1)}, s32[8,128]{1,0:T(8,128)S(1)}) custom-call(f32[30,1,640]{2,1,0:T(1,128)} %bitcast.36, s32[8,128]{1,0:T(8,128)} %bitcast.42), custom_call_target="tpu_custom_call" | custom-call | tf_op jit(solution)/shard_map/pallas_call | solution.py:381
  1.8 0.5 shard_map.114
  2.3 0.6 collective-permute-start
  2.9 4.7 %collective-permute-start.1 = (f32[3,32,128]{2,1,0:T(8,128)S(1)}, f32[3,32,128]{2,1,0:T(8,128)S(1)}, u32[]{:S(2)}, u32[]{:S(2)}) collective-permute-start(f32[3,32,128]{2,1,0:T(8,128)S(1)} %get-tuple-element.59), channel_id=1, source_target_pairs={{0,7},{1,2},{2,1},{3,4},{4,3},{5,6},{6,5},{7,0},{8,15},{9,10},{10,... | collective-permute-start | bytes 147464 | tf_op jit(solution)/shard_map/ppermute | solution.py:424
  7.6 1.9 %collective-permute-done.1.outer_ref = f32[3,32,128]{2,1,0:T(8,128)S(1)} collective-permute-done((f32[3,32,128]{2,1,0:T(8,128)S(1)}, f32[3,32,128]{2,1,0:T(8,128)S(1)}, u32[]{:S(2)}, u32[]{:S(2)}) %collective-permute-start.1) | collective-permute-done | bytes 49184 | tf_op jit(solution)/shard_map/ppermute | solution.py:424
  9.4 1.6 %collective-permute-start.2 = (f32[3,32,128]{2,1,0:T(8,128)S(1)}, f32[3,32,128]{2,1,0:T(8,128)S(1)}, u32[]{:S(2)}, u32[]{:S(2)}) collective-permute-start(f32[3,32,128]{2,1,0:T(8,128)S(1)} %pad_maximum_fusion), channel_id=1, source_target_pairs={{0,8},{8,0},{16,24},{24,16},{1,9},{9,1},{17,25},{25,17},{2,10},{10... | collective-permute-start | bytes 147464 | tf_op jit(solution)/shard_map/ppermute | solution.py:451
  11.0 1.5 %shard_map.115 = (bf16[896,1024]{1,0:T(8,128)(2,1)S(1)}, bf16[768,1024]{1,0:T(8,128)(2,1)S(1)}) custom-call(s32[2,960]{1,0:T(2,128)} %bitcast.39), custom_call_target="tpu_custom_call" | custom-call | tf_op jit(solution)/shard_map/pallas_call | solution.py:381
  12.5 1.3 %shard_map.118 = (f32[32,1024]{1,0:T(8,128)S(1)}, f32[1,1024]{1,0:T(1,128)S(1)}, bf16[1024,384]{1,0:T(8,128)(2,1)S(1)}, bf16[1024,640]{1,0:T(8,128)(2,1)S(1)}) custom-call(f32[30,1,960]{2,1,0:T(1,128)} %bitcast.35, s32[8,128]{1,0:T(8,128)} %bitcast.43, f32[1,960]{1,0:T(1,128)} %dual_hbm.1), custom_call_target="tpu_custom_call" | custom-call | tf_op jit(solution)/shard_map/pallas_call | solution.py:381
  13.8 0.4 shard_map.116.total_ref
  14.6 0.5 shard_map.119
  15.0 0.4 shard_map.120
  15.4 0.6 collective-permute-start.4
  16.0 3.2 %collective-permute-start.5 = (f32[3,32,128]{2,1,0:T(8,128)S(1)}, f32[3,32,128]{2,1,0:T(8,128)S(1)}, u32[]{:S(2)}, u32[]{:S(2)}) collective-permute-start(f32[3,32,128]{2,1,0:T(8,128)S(1)} %get-tuple-element.71), channel_id=1, source_target_pairs={{0,7},{1,2},{2,1},{3,4},{4,3},{5,6},{6,5},{7,0},{8,15},{9,10},{10,... | collective-permute-start | bytes 147464 | tf_op jit(solution)/shard_map/ppermute | solution.py:424
  19.1 2.6 %collective-permute-done.5.outer_ref = f32[3,32,128]{2,1,0:T(8,128)S(1)} collective-permute-done((f32[3,32,128]{2,1,0:T(8,128)S(1)}, f32[3,32,128]{2,1,0:T(8,128)S(1)}, u32[]{:S(2)}, u32[]{:S(2)}) %collective-permute-start.5) | collective-permute-done | bytes 49184 | tf_op jit(solution)/shard_map/ppermute | solution.py:424
  21.7 2.7 %collective-permute-start.6 = (f32[3,32,128]{2,1,0:T(8,128)S(1)}, f32[3,32,128]{2,1,0:T(8,128)S(1)}, u32[]{:S(2)}, u32[]{:S(2)}) collective-permute-start(f32[3,32,128]{2,1,0:T(8,128)S(1)} %pad_maximum_fusion.2), channel_id=1, source_target_pairs={{0,8},{8,0},{16,24},{24,16},{1,9},{9,1},{17,25},{25,17},{2,10},{10... | collective-permute-start | bytes 147464 | tf_op jit(solution)/shard_map/ppermute | solution.py:451
  24.4 1.2 %shard_map.124 = (f32[1,640]{1,0:T(1,128)S(1)}, f32[256,128]{1,0:T(8,128)S(1)}, f32[256,128]{1,0:T(8,128)S(1)}, f32[256,128]{1,0:T(8,128)S(1)}, bf16[640,384]{1,...) custom-call(f32[30,1,640]{2,1,0:T(1,128)} %bitcast.37, s32[8,128]{1,0:T(8,128)S(1)} %get-tuple-element.57.list_ref, ...), custom_call_target="tpu_custom_call" | custom-call | tf_op jit(solution)/shard_map/pallas_call | solution.py:381
  25.6 2.4 %shard_map.121 = (bf16[1280,640]{1,0:T(8,128)(2,1)S(1)}, bf16[1280,640]{1,0:T(8,128)(2,1)S(1)}, bf16[768,640]{1,0:T(8,128)(2,1)S(1)}, bf16[768,640]{1,0:T(8,128)(2,1)S(1)}) custom-call(s32[3,1,640]{2,1,0:T(1,128)} %bitcast.40, f32[3,1,640]{2,1,0:T(1,128)} %bitcast.41), custom_call_target="tpu_custom_call" | custom-call | tf_op jit(solution)/shard_map/pallas_call | solution.py:381
  28.0 0.7 shard_map.122.total_ref
  29.0 0.7 shard_map.125
  30.1 0.6 collective-permute-start.8
  30.6 2.1 %collective-permute-start.9 = (f32[3,32,128]{2,1,0:T(8,128)S(1)}, f32[3,32,128]{2,1,0:T(8,128)S(1)}, u32[]{:S(2)}, u32[]{:S(2)}) collective-permute-start(f32[3,32,128]{2,1,0:T(8,128)S(1)} %get-tuple-element.87), channel_id=1, source_target_pairs={{0,7},{1,2},{2,1},{3,4},{4,3},{5,6},{6,5},{7,0},{8,15},{9,10},{10,... | collective-permute-start | bytes 147464 | tf_op jit(solution)/shard_map/ppermute | solution.py:424
  32.8 3.2 %collective-permute-done.9.outer_ref = f32[3,32,128]{2,1,0:T(8,128)S(1)} collective-permute-done((f32[3,32,128]{2,1,0:T(8,128)S(1)}, f32[3,32,128]{2,1,0:T(8,128)S(1)}, u32[]{:S(2)}, u32[]{:S(2)}) %collective-permute-start.9) | collective-permute-done | bytes 49184 | tf_op jit(solution)/shard_map/ppermute | solution.py:424
  36.0 0.7 collective-permute-start.10
  36.7 0.4 shard_map.127.total_ref
  37.1 3.0 %collective-permute-done.10.lat_inner_ref = f32[3,32,128]{2,1,0:T(8,128)S(1)} collective-permute-done((f32[3,32,128]{2,1,0:T(8,128)S(1)}, f32[3,32,128]{2,1,0:T(8,128)S(1)}, u32[]{:S(2)}, u32[]{:S(2)}) %collective-permute-start.10) | collective-permute-done | bytes 49184 | tf_op jit(solution)/shard_map/ppermute | solution.py:451
  40.4 0.5 shard_map.129
  40.9 0.4 shard_map.130
  41.3 1.3 %collective-permute-start.13 = (f32[3,32,128]{2,1,0:T(8,128)S(1)}, f32[3,32,128]{2,1,0:T(8,128)S(1)}, u32[]{:S(2)}, u32[]{:S(2)}) collective-permute-start(f32[3,32,128]{2,1,0:T(8,128)S(1)} %get-tuple-element.93), channel_id=1, source_target_pairs={{0,7},{1,2},{2,1},{3,4},{4,3},{5,6},{6,5},{7,0},{8,15},{9,10},{10,... | collective-permute-start | bytes 147464 | tf_op jit(solution)/shard_map/ppermute | solution.py:424
  42.7 4.1 %collective-permute-done.13.outer_ref = f32[3,32,128]{2,1,0:T(8,128)S(1)} collective-permute-done((f32[3,32,128]{2,1,0:T(8,128)S(1)}, f32[3,32,128]{2,1,0:T(8,128)S(1)}, u32[]{:S(2)}, u32[]{:S(2)}) %collective-permute-start.13) | collective-permute-done | bytes 49184 | tf_op jit(solution)/shard_map/ppermute | solution.py:424
  46.7 2.7 %collective-permute-start.14 = (f32[3,32,128]{2,1,0:T(8,128)S(1)}, f32[3,32,128]{2,1,0:T(8,128)S(1)}, u32[]{:S(2)}, u32[]{:S(2)}) collective-permute-start(f32[3,32,128]{2,1,0:T(8,128)S(1)} %pad_maximum_fusion.6), channel_id=1, source_target_pairs={{0,8},{8,0},{16,24},{24,16},{1,9},{9,1},{17,25},{25,17},{2,10},{10... | collective-permute-start | bytes 147464 | tf_op jit(solution)/shard_map/ppermute | solution.py:451
  49.4 0.7 shard_map.131.total_ref
  50.1 1.4 %collective-permute-done.14.lat_inner_ref = f32[3,32,128]{2,1,0:T(8,128)S(1)} collective-permute-done((f32[3,32,128]{2,1,0:T(8,128)S(1)}, f32[3,32,128]{2,1,0:T(8,128)S(1)}, u32[]{:S(2)}, u32[]{:S(2)}) %collective-permute-start.14) | collective-permute-done | bytes 49184 | tf_op jit(solution)/shard_map/ppermute | solution.py:451
  51.8 0.7 shard_map.133
  52.9 0.4 collective-permute-start.17
  53.3 0.8 %collective-permute-done.16.inner_ref = f32[3,32,128]{2,1,0:T(8,128)S(1)} collective-permute-done((f32[3,32,128]{2,1,0:T(8,128)S(1)}, f32[3,32,128]{2,1,0:T(8,128)S(1)}, u32[]{:S(2)}, u32[]{:S(2)}) %collective-permute-start.16) | collective-permute-done | bytes 49184 | tf_op jit(solution)/shard_map/ppermute | solution.py:429
  54.2 4.2 %collective-permute-done.17.outer_ref = f32[3,32,128]{2,1,0:T(8,128)S(1)} collective-permute-done((f32[3,32,128]{2,1,0:T(8,128)S(1)}, f32[3,32,128]{2,1,0:T(8,128)S(1)}, u32[]{:S(2)}, u32[]{:S(2)}) %collective-permute-start.17) | collective-permute-done | bytes 49184 | tf_op jit(solution)/shard_map/ppermute | solution.py:424
  58.3 2.7 %collective-permute-start.18 = (f32[3,32,128]{2,1,0:T(8,128)S(1)}, f32[3,32,128]{2,1,0:T(8,128)S(1)}, u32[]{:S(2)}, u32[]{:S(2)}) collective-permute-start(f32[3,32,128]{2,1,0:T(8,128)S(1)} %pad_maximum_fusion.8), channel_id=1, source_target_pairs={{0,8},{8,0},{16,24},{24,16},{1,9},{9,1},{17,25},{25,17},{2,10},{10... | collective-permute-start | bytes 147464 | tf_op jit(solution)/shard_map/ppermute | solution.py:451
  61.1 0.4 shard_map.135.total_ref
  61.5 1.6 %collective-permute-done.18.lat_inner_ref = f32[3,32,128]{2,1,0:T(8,128)S(1)} collective-permute-done((f32[3,32,128]{2,1,0:T(8,128)S(1)}, f32[3,32,128]{2,1,0:T(8,128)S(1)}, u32[]{:S(2)}, u32[]{:S(2)}) %collective-permute-start.18) | collective-permute-done | bytes 49184 | tf_op jit(solution)/shard_map/ppermute | solution.py:451
  63.4 0.5 shard_map.137
  63.9 0.4 shard_map.138
  64.4 1.1 %collective-permute-done.20.inner_ref = f32[3,32,128]{2,1,0:T(8,128)S(1)} collective-permute-done((f32[3,32,128]{2,1,0:T(8,128)S(1)}, f32[3,32,128]{2,1,0:T(8,128)S(1)}, u32[]{:S(2)}, u32[]{:S(2)}) %collective-permute-start.20) | collective-permute-done | bytes 49184 | tf_op jit(solution)/shard_map/ppermute | solution.py:429
  65.6 4.2 %collective-permute-done.21.outer_ref = f32[3,32,128]{2,1,0:T(8,128)S(1)} collective-permute-done((f32[3,32,128]{2,1,0:T(8,128)S(1)}, f32[3,32,128]{2,1,0:T(8,128)S(1)}, u32[]{:S(2)}, u32[]{:S(2)}) %collective-permute-start.21) | collective-permute-done | bytes 49184 | tf_op jit(solution)/shard_map/ppermute | solution.py:424
  69.7 2.8 %collective-permute-start.22 = (f32[3,32,128]{2,1,0:T(8,128)S(1)}, f32[3,32,128]{2,1,0:T(8,128)S(1)}, u32[]{:S(2)}, u32[]{:S(2)}) collective-permute-start(f32[3,32,128]{2,1,0:T(8,128)S(1)} %pad_maximum_fusion.10), channel_id=1, source_target_pairs={{0,8},{8,0},{16,24},{24,16},{1,9},{9,1},{17,25},{25,17},{2,10},{10... | collective-permute-start | bytes 147464 | tf_op jit(solution)/shard_map/ppermute | solution.py:451
  72.5 0.8 %copy.12 = f32[1,30,960]{2,0,1:T(1,128)} copy(f32[1,30,960]{2,1,0:T(8,128)S(1)} %slice_bitcast_fusion) | data formatting | bytes 230400
  73.3 0.7 shard_map.139.total_ref
  74.0 0.6 collective-permute-done.22.lat_inner_ref
  74.9 1.1 %shard_map.141 = f32[30,1,640]{2,1,0:T(1,128)} custom-call(f32[32,640]{1,0:T(8,128)S(1)} %shard_map.140.total_ref, f32[3,32,128]{2,1,0:T(8,128)S(1)} %collective-permute-done.23.lat_outer_ref, bf16[768,640]{1,0:T(8,128)(2,1)S(1)} %get-tuple-element.75.rest_0_.high_ref, bf16[768,640]{1,0:T(8,128)(2,1)S(1)} %get-tuple-element.76.rest_1_.low_ref, ...), custom_call_target="tpu_custom_call" | custom-call | tf_op jit(solution)/shard_map/pallas_call | solution.py:381
  (55 shorter events, 2.9 us)
Async XLA Ops:
  2.3 5.3 %collective-permute-start = (f32[3,32,128]{2,1,0:T(8,128)S(1)}, f32[3,32,128]{2,1,0:T(8,128)S(1)}, u32[]{:S(2)}, u32[]{:S(2)}) collective-permute-start(f32[3,32,128]{2,1,0:T(8,128)S(1)} %get-tuple-element.58), channel_id=1, source_target_pairs={{0,1},{1,0},{2,3},{3,2},{4,5},{5,4},{6,7},{7,6},{8,9},{9,8},{10,11... | collective-permute-start | bytes 147464 | tf_op jit(solution)/shard_map/ppermute | solution.py:429
  2.9 6.6 %collective-permute-start.1 = (f32[3,32,128]{2,1,0:T(8,128)S(1)}, f32[3,32,128]{2,1,0:T(8,128)S(1)}, u32[]{:S(2)}, u32[]{:S(2)}) collective-permute-start(f32[3,32,128]{2,1,0:T(8,128)S(1)} %get-tuple-element.59), channel_id=1, source_target_pairs={{0,7},{1,2},{2,1},{3,4},{4,3},{5,6},{6,5},{7,0},{8,15},{9,10},{10,... | collective-permute-start | bytes 147464 | tf_op jit(solution)/shard_map/ppermute | solution.py:424
  9.4 4.8 %collective-permute-start.2 = (f32[3,32,128]{2,1,0:T(8,128)S(1)}, f32[3,32,128]{2,1,0:T(8,128)S(1)}, u32[]{:S(2)}, u32[]{:S(2)}) collective-permute-start(f32[3,32,128]{2,1,0:T(8,128)S(1)} %pad_maximum_fusion), channel_id=1, source_target_pairs={{0,8},{8,0},{16,24},{24,16},{1,9},{9,1},{17,25},{25,17},{2,10},{10... | collective-permute-start | bytes 147464 | tf_op jit(solution)/shard_map/ppermute | solution.py:451
  11.0 3.5 %collective-permute-start.3 = (f32[3,32,128]{2,1,0:T(8,128)S(1)}, f32[3,32,128]{2,1,0:T(8,128)S(1)}, u32[]{:S(2)}, u32[]{:S(2)}) collective-permute-start(f32[3,32,128]{2,1,0:T(8,128)S(1)} %pad_maximum_fusion.1), channel_id=1, source_target_pairs={{0,1},{1,0},{2,3},{3,2},{4,5},{5,4},{6,7},{7,6},{8,16},{9,17},{10,... | collective-permute-start | bytes 147464 | tf_op jit(solution)/shard_map/ppermute | solution.py:452
  15.4 3.7 %collective-permute-start.4 = (f32[3,32,128]{2,1,0:T(8,128)S(1)}, f32[3,32,128]{2,1,0:T(8,128)S(1)}, u32[]{:S(2)}, u32[]{:S(2)}) collective-permute-start(f32[3,32,128]{2,1,0:T(8,128)S(1)} %get-tuple-element.70), channel_id=1, source_target_pairs={{0,1},{1,0},{2,3},{3,2},{4,5},{5,4},{6,7},{7,6},{8,9},{9,8},{10,11... | collective-permute-start | bytes 147464 | tf_op jit(solution)/shard_map/ppermute | solution.py:429
  16.0 5.7 %collective-permute-start.5 = (f32[3,32,128]{2,1,0:T(8,128)S(1)}, f32[3,32,128]{2,1,0:T(8,128)S(1)}, u32[]{:S(2)}, u32[]{:S(2)}) collective-permute-start(f32[3,32,128]{2,1,0:T(8,128)S(1)} %get-tuple-element.71), channel_id=1, source_target_pairs={{0,7},{1,2},{2,1},{3,4},{4,3},{5,6},{6,5},{7,0},{8,15},{9,10},{10,... | collective-permute-start | bytes 147464 | tf_op jit(solution)/shard_map/ppermute | solution.py:424
  21.7 7.0 %collective-permute-start.6 = (f32[3,32,128]{2,1,0:T(8,128)S(1)}, f32[3,32,128]{2,1,0:T(8,128)S(1)}, u32[]{:S(2)}, u32[]{:S(2)}) collective-permute-start(f32[3,32,128]{2,1,0:T(8,128)S(1)} %pad_maximum_fusion.2), channel_id=1, source_target_pairs={{0,8},{8,0},{16,24},{24,16},{1,9},{9,1},{17,25},{25,17},{2,10},{10... | collective-permute-start | bytes 147464 | tf_op jit(solution)/shard_map/ppermute | solution.py:451
  24.4 4.6 %collective-permute-start.7 = (f32[3,32,128]{2,1,0:T(8,128)S(1)}, f32[3,32,128]{2,1,0:T(8,128)S(1)}, u32[]{:S(2)}, u32[]{:S(2)}) collective-permute-start(f32[3,32,128]{2,1,0:T(8,128)S(1)} %pad_maximum_fusion.3), channel_id=1, source_target_pairs={{0,1},{1,0},{2,3},{3,2},{4,5},{5,4},{6,7},{7,6},{8,16},{9,17},{10,... | collective-permute-start | bytes 147464 | tf_op jit(solution)/shard_map/ppermute | solution.py:452
  30.1 2.7 %collective-permute-start.8 = (f32[3,32,128]{2,1,0:T(8,128)S(1)}, f32[3,32,128]{2,1,0:T(8,128)S(1)}, u32[]{:S(2)}, u32[]{:S(2)}) collective-permute-start(f32[3,32,128]{2,1,0:T(8,128)S(1)} %get-tuple-element.86), channel_id=1, source_target_pairs={{0,1},{1,0},{2,3},{3,2},{4,5},{5,4},{6,7},{7,6},{8,9},{9,8},{10,11... | collective-permute-start | bytes 147464 | tf_op jit(solution)/shard_map/ppermute | solution.py:429
  30.6 5.3 %collective-permute-start.9 = (f32[3,32,128]{2,1,0:T(8,128)S(1)}, f32[3,32,128]{2,1,0:T(8,128)S(1)}, u32[]{:S(2)}, u32[]{:S(2)}) collective-permute-start(f32[3,32,128]{2,1,0:T(8,128)S(1)} %get-tuple-element.87), channel_id=1, source_target_pairs={{0,7},{1,2},{2,1},{3,4},{4,3},{5,6},{6,5},{7,0},{8,15},{9,10},{10,... | collective-permute-start | bytes 147464 | tf_op jit(solution)/shard_map/ppermute | solution.py:424
  36.0 4.2 %collective-permute-start.10 = (f32[3,32,128]{2,1,0:T(8,128)S(1)}, f32[3,32,128]{2,1,0:T(8,128)S(1)}, u32[]{:S(2)}, u32[]{:S(2)}) collective-permute-start(f32[3,32,128]{2,1,0:T(8,128)S(1)} %pad_maximum_fusion.4), channel_id=1, source_target_pairs={{0,8},{8,0},{16,24},{24,16},{1,9},{9,1},{17,25},{25,17},{2,10},{10... | collective-permute-start | bytes 147464 | tf_op jit(solution)/shard_map/ppermute | solution.py:451
  36.7 3.7 %collective-permute-start.11 = (f32[3,32,128]{2,1,0:T(8,128)S(1)}, f32[3,32,128]{2,1,0:T(8,128)S(1)}, u32[]{:S(2)}, u32[]{:S(2)}) collective-permute-start(f32[3,32,128]{2,1,0:T(8,128)S(1)} %pad_maximum_fusion.5), channel_id=1, source_target_pairs={{0,1},{1,0},{2,3},{3,2},{4,5},{5,4},{6,7},{7,6},{8,16},{9,17},{10,... | collective-permute-start | bytes 147464 | tf_op jit(solution)/shard_map/ppermute | solution.py:452
  41.3 1.4 %collective-permute-start.12 = (f32[3,32,128]{2,1,0:T(8,128)S(1)}, f32[3,32,128]{2,1,0:T(8,128)S(1)}, u32[]{:S(2)}, u32[]{:S(2)}) collective-permute-start(f32[3,32,128]{2,1,0:T(8,128)S(1)} %get-tuple-element.92), channel_id=1, source_target_pairs={{0,1},{1,0},{2,3},{3,2},{4,5},{5,4},{6,7},{7,6},{8,9},{9,8},{10,11... | collective-permute-start | bytes 147464 | tf_op jit(solution)/shard_map/ppermute | solution.py:429
  41.3 5.4 %collective-permute-start.13 = (f32[3,32,128]{2,1,0:T(8,128)S(1)}, f32[3,32,128]{2,1,0:T(8,128)S(1)}, u32[]{:S(2)}, u32[]{:S(2)}) collective-permute-start(f32[3,32,128]{2,1,0:T(8,128)S(1)} %get-tuple-element.93), channel_id=1, source_target_pairs={{0,7},{1,2},{2,1},{3,4},{4,3},{5,6},{6,5},{7,0},{8,15},{9,10},{10,... | collective-permute-start | bytes 147464 | tf_op jit(solution)/shard_map/ppermute | solution.py:424
  46.7 4.8 %collective-permute-start.14 = (f32[3,32,128]{2,1,0:T(8,128)S(1)}, f32[3,32,128]{2,1,0:T(8,128)S(1)}, u32[]{:S(2)}, u32[]{:S(2)}) collective-permute-start(f32[3,32,128]{2,1,0:T(8,128)S(1)} %pad_maximum_fusion.6), channel_id=1, source_target_pairs={{0,8},{8,0},{16,24},{24,16},{1,9},{9,1},{17,25},{25,17},{2,10},{10... | collective-permute-start | bytes 147464 | tf_op jit(solution)/shard_map/ppermute | solution.py:451
  49.4 2.4 %collective-permute-start.15 = (f32[3,32,128]{2,1,0:T(8,128)S(1)}, f32[3,32,128]{2,1,0:T(8,128)S(1)}, u32[]{:S(2)}, u32[]{:S(2)}) collective-permute-start(f32[3,32,128]{2,1,0:T(8,128)S(1)} %pad_maximum_fusion.7), channel_id=1, source_target_pairs={{0,1},{1,0},{2,3},{3,2},{4,5},{5,4},{6,7},{7,6},{8,16},{9,17},{10,... | collective-permute-start | bytes 147464 | tf_op jit(solution)/shard_map/ppermute | solution.py:452
  52.9 1.3 %collective-permute-start.16 = (f32[3,32,128]{2,1,0:T(8,128)S(1)}, f32[3,32,128]{2,1,0:T(8,128)S(1)}, u32[]{:S(2)}, u32[]{:S(2)}) collective-permute-start(f32[3,32,128]{2,1,0:T(8,128)S(1)} %get-tuple-element.98), channel_id=1, source_target_pairs={{0,1},{1,0},{2,3},{3,2},{4,5},{5,4},{6,7},{7,6},{8,9},{9,8},{10,11... | collective-permute-start | bytes 147464 | tf_op jit(solution)/shard_map/ppermute | solution.py:429
  52.9 5.4 %collective-permute-start.17 = (f32[3,32,128]{2,1,0:T(8,128)S(1)}, f32[3,32,128]{2,1,0:T(8,128)S(1)}, u32[]{:S(2)}, u32[]{:S(2)}) collective-permute-start(f32[3,32,128]{2,1,0:T(8,128)S(1)} %get-tuple-element.99), channel_id=1, source_target_pairs={{0,7},{1,2},{2,1},{3,4},{4,3},{5,6},{6,5},{7,0},{8,15},{9,10},{10,... | collective-permute-start | bytes 147464 | tf_op jit(solution)/shard_map/ppermute | solution.py:424
  58.3 4.8 %collective-permute-start.18 = (f32[3,32,128]{2,1,0:T(8,128)S(1)}, f32[3,32,128]{2,1,0:T(8,128)S(1)}, u32[]{:S(2)}, u32[]{:S(2)}) collective-permute-start(f32[3,32,128]{2,1,0:T(8,128)S(1)} %pad_maximum_fusion.8), channel_id=1, source_target_pairs={{0,8},{8,0},{16,24},{24,16},{1,9},{9,1},{17,25},{25,17},{2,10},{10... | collective-permute-start | bytes 147464 | tf_op jit(solution)/shard_map/ppermute | solution.py:451
  61.1 2.4 %collective-permute-start.19 = (f32[3,32,128]{2,1,0:T(8,128)S(1)}, f32[3,32,128]{2,1,0:T(8,128)S(1)}, u32[]{:S(2)}, u32[]{:S(2)}) collective-permute-start(f32[3,32,128]{2,1,0:T(8,128)S(1)} %pad_maximum_fusion.9), channel_id=1, source_target_pairs={{0,1},{1,0},{2,3},{3,2},{4,5},{5,4},{6,7},{7,6},{8,16},{9,17},{10,... | collective-permute-start | bytes 147464 | tf_op jit(solution)/shard_map/ppermute | solution.py:452
  64.3 1.3 %collective-permute-start.20 = (f32[3,32,128]{2,1,0:T(8,128)S(1)}, f32[3,32,128]{2,1,0:T(8,128)S(1)}, u32[]{:S(2)}, u32[]{:S(2)}) collective-permute-start(f32[3,32,128]{2,1,0:T(8,128)S(1)} %get-tuple-element.104), channel_id=1, source_target_pairs={{0,1},{1,0},{2,3},{3,2},{4,5},{5,4},{6,7},{7,6},{8,9},{9,8},{10,11... | collective-permute-start | bytes 147464 | tf_op jit(solution)/shard_map/ppermute | solution.py:429
  64.3 5.4 %collective-permute-start.21 = (f32[3,32,128]{2,1,0:T(8,128)S(1)}, f32[3,32,128]{2,1,0:T(8,128)S(1)}, u32[]{:S(2)}, u32[]{:S(2)}) collective-permute-start(f32[3,32,128]{2,1,0:T(8,128)S(1)} %get-tuple-element.105), channel_id=1, source_target_pairs={{0,7},{1,2},{2,1},{3,4},{4,3},{5,6},{6,5},{7,0},{8,15},{9,10},{10,... | collective-permute-start | bytes 147464 | tf_op jit(solution)/shard_map/ppermute | solution.py:424
  69.7 4.8 %collective-permute-start.22 = (f32[3,32,128]{2,1,0:T(8,128)S(1)}, f32[3,32,128]{2,1,0:T(8,128)S(1)}, u32[]{:S(2)}, u32[]{:S(2)}) collective-permute-start(f32[3,32,128]{2,1,0:T(8,128)S(1)} %pad_maximum_fusion.10), channel_id=1, source_target_pairs={{0,8},{8,0},{16,24},{24,16},{1,9},{9,1},{17,25},{25,17},{2,10},{10... | collective-permute-start | bytes 147464 | tf_op jit(solution)/shard_map/ppermute | solution.py:451
  72.5 2.4 %collective-permute-start.23 = (f32[3,32,128]{2,1,0:T(8,128)S(1)}, f32[3,32,128]{2,1,0:T(8,128)S(1)}, u32[]{:S(2)}, u32[]{:S(2)}) collective-permute-start(f32[3,32,128]{2,1,0:T(8,128)S(1)} %pad_maximum_fusion.11), channel_id=1, source_target_pairs={{0,1},{1,0},{2,3},{3,2},{4,5},{5,4},{6,7},{7,6},{8,16},{9,17},{10,... | collective-permute-start | bytes 147464 | tf_op jit(solution)/shard_map/ppermute | solution.py:452

commit v7 on v6

--- a/solution.py
+++ b/solution.py
@@ -65,8 +65,8 @@
     flat = piece + jnp.where(piece >= 4, 1, 0)
     p = jnp.where(flat >= 6, 1, jnp.where(flat >= 3, 0, -1))
     q = flat - 3 * (p + 1) - 1
-    lon_member = jnp.where(q == 0, 2, jnp.where(q == lon_inner, 0, 1))
-    member = jnp.where(p == 0, lon_member, jnp.where(p == lat_inner, 2, 5) + lon_member)
+    lon_member = jnp.where(q == 0, 1, jnp.where(q == lon_inner, 0, 2))
+    member = jnp.where(p == 0, jnp.minimum(lon_member, 1), jnp.where(p == lat_inner, 2, 5) + lon_member)
     outside = (a + p < 0) | (a + p >= lat_count)
     row = own_padded + member * halo + slot
     return jnp.where(beyond < 0, index, jnp.where(outside, -1, row))
@@ -284,12 +284,19 @@
     total_ref[...] = gather_matmul(stack_ref, [ref[...] for ref in matrix_refs], rows)
 
 
-def lat_share(total_ref, lat_ref, matrix_refs, stack_ref, half):
+def early_part_kernel(own_ref, inner_ref, outer_ref, early_ref, *rest):
+    *matrix_refs, total_ref, stack_ref, early_stack_ref = rest
+    near_refs, far_refs = matrix_refs[: len(matrix_refs) // 2], matrix_refs[len(matrix_refs) // 2 :]
+    part_kernel(own_ref, inner_ref, outer_ref, *near_refs, total_ref, stack_ref)
+    total_ref[...] = lat_share(total_ref, early_ref, far_refs, early_stack_ref, 3)
+
+
+def lat_share(total_ref, lat_ref, matrix_refs, stack_ref, first):
     rows = total_ref.shape[0]
-    halo = lat_ref.shape[2]
-    for member in range(3):
+    count, _, halo = lat_ref.shape
+    for member in range(count):
         put_parts(stack_ref, lat_ref[member], member * halo)
-    matrices = [ref[half * 3 * halo : (half + 1) * 3 * halo, :] for ref in matrix_refs]
+    matrices = [ref[first * halo : (first + count) * halo, :] for ref in matrix_refs]
     return total_ref[...] + gather_matmul(stack_ref, matrices, rows)
 
 
@@ -300,7 +307,7 @@
 
 def edge_kernel(total_ref, lat_outer_ref, far_ref, edges_ref, scale_ref, matrix_ref, new_edges_ref, outer_ref, own_stack_ref, stack_ref):
     rows = edges_ref.shape[0]
-    difference = lat_share(total_ref, lat_outer_ref, [far_ref], stack_ref, 1)
+    difference = lat_share(total_ref, lat_outer_ref, [far_ref], stack_ref, 6 - lat_outer_ref.shape[0])
     new_edges = edges_ref[...] - scale_ref[...] * difference
     new_edges_ref[...] = new_edges
     put_parts(own_stack_ref, new_edges, 0)
@@ -309,7 +316,7 @@
 
 def solve_columns(total_ref, lat_outer_ref, high_ref, low_ref, cells_ref, speed_ref, inverse_ref, forward_ref, back_ref, levels, stack_ref, column_ref):
     rows, cells = cells_ref.shape
-    divergence = lat_share(total_ref, lat_outer_ref, [high_ref, low_ref], stack_ref, 1)
+    divergence = lat_share(total_ref, lat_outer_ref, [high_ref, low_ref], stack_ref, 6 - lat_outer_ref.shape[0])
     right_side = cells_ref[...] - speed_ref[...] * divergence
     step = column_ref.shape[0] // rows
     for group in range(cells // LANES):
@@ -404,7 +411,7 @@
     by_level = lambda value: value.transpose(1, 0, 2)
     stack_cells = ((PARTS * rows, cells), bf16)
     stack_edges = ((PARTS * rows, edge_pad), bf16)
-    stack_lat = ((PARTS * rows, 3 * halo), bf16)
+    stack_lat = lambda count: ((PARTS * rows, count * halo), bf16)
     column = ((rows * round_up(cells // LANES, 8), LANES), f32)
     sent_outer = lambda width: ((width, 3 * halo), bf16)
     sent_rest = lambda width: ((width, 5 * halo), bf16)
@@ -446,10 +453,16 @@
                 raw=(0, 1),
                 copies=2,
             )
-        first = jnp.stack([inner_in[1], outer_in[1], lat_inner])
-        second = jnp.stack([inner_in[2], outer_in[2], lat_outer])
+        early = phase >= 2
+        first = jnp.stack([inner_in[1], lat_inner, outer_in[1]])
+        if early:
+            early_in = lax.ppermute(jnp.stack([inner_in[2], lat_outer]), ("lat", "lon"), lat_outer_route)
+            second = outer_in[2:3]
+        else:
+            second = jnp.stack([inner_in[2], lat_outer, outer_in[2]])
         first_in = lax.ppermute(first, "lat", lat_inner_route)
         second_in = lax.ppermute(second, ("lat", "lon"), lat_outer_route)
+        count = second.shape[0]
         if phase == 0:
             normal, scale, edge_outer, edge_rest = call(
                 edge_setup_kernel,
@@ -474,19 +487,19 @@
             )
         if at_cells:
             (total,) = call(
-                part_kernel,
+                early_part_kernel if early else part_kernel,
                 [((rows, edge_pad), f32)],
-                [((PARTS * rows, cells + 2 * halo), bf16)],
+                [((PARTS * rows, cells + 2 * halo), bf16)] + ([stack_lat(2)] if early else []),
                 values,
                 inner_in,
                 outer_in,
-                gradient_near,
-            )
-            (total,) = call(inner_share_kernel, [((rows, edge_pad), f32)], [stack_lat], total, first_in, gradient_far)
+                *([early_in, gradient_near, gradient_far] if early else [gradient_near]),
+            )
+            (total,) = call(inner_share_kernel, [((rows, edge_pad), f32)], [stack_lat(3)], total, first_in, gradient_far)
             normal, outer, stack = call(
                 edge_kernel,
                 [((rows, edge_pad), f32), bundle, stack_edges],
-                [stack_lat],
+                [stack_lat(count)],
                 total,
                 second_in,
                 gradient_far,
@@ -496,27 +509,26 @@
             )
         else:
             (total,) = call(
-                part_kernel,
+                early_part_kernel if early else part_kernel,
                 [((rows, cells), f32)],
-                [((PARTS * rows, edge_pad + 2 * halo), bf16)],
+                [((PARTS * rows, edge_pad + 2 * halo), bf16)] + ([stack_lat(2)] if early else []),
                 normal,
                 inner_in,
                 outer_in,
-                near_high,
-                near_low,
-            )
-            (total,) = call(inner_share_kernel, [((rows, cells), f32)], [stack_lat], total, first_in, far_high, far_low)
+                *([early_in, near_high, near_low, far_high, far_low] if early else [near_high, near_low]),
+            )
+            (total,) = call(inner_share_kernel, [((rows, cells), f32)], [stack_lat(3)], total, first_in, far_high, far_low)
             operands = (total, second_in, far_high, far_low, values, speed, inverse, forward, back)
             if phase < 2 * NSUB - 1:
                 values, outer, stack = call(
                     functools.partial(cell_kernel, levels=levels),
                     [((rows, cells), f32), bundle, stack_cells],
-                    [stack_lat, column],
+                    [stack_lat(count), column],
                     *operands,
                     cell_outer,
                 )
             else:
-                (values,) = call(functools.partial(last_kernel, levels=levels), [((levels, 1, cells), f32)], [stack_lat, column], *operands)
+                (values,) = call(functools.partial(last_kernel, levels=levels), [((levels, 1, cells), f32)], [stack_lat(count), column], *operands)
     return by_level(values), normal[:levels, :edges][None]
 
 

time: 76.4 us -> 81 us (1.060)
  starting transfers between devices: 26.8 us -> 33 us
  waiting for transfers between devices: 28.7 us -> 27 us
    ppermute x6, starting transfers between devices: 13.1 us -> 17.5 us  [on_device(): first_in = lax.ppermute(first, 'lat', lat_inner_route)]
    ppermute x6, waiting for transfers between devices: 6.6 us -> 3.1 us  [on_device(): first_in = lax.ppermute(first, 'lat', lat_inner_route)]
    ppermute x0 -> x4, waiting for transfers between devices: none -> 2.09 us  [on_device(): lax.ppermute(jnp.stack([inner_in[2], lat_outer]), ('lat', 'lon'), lat_out...]
    ppermute x6, starting transfers between devices: 0.02 us -> 1.53 us  [on_device(): second_in = lax.ppermute(second, ('lat', 'lon'), lat_outer_route)]
  transfers between devices with their start and end apart: 24 -> 28, of which waited for: 12 -> 16; matrix products, arithmetic and copies ran while one was open for 1% -> 1% of each run, Pallas kernels for 15% -> 15%
where the time goes in v7:
time: 81 us; the launch traced here: 80.7 us
  starting transfers between devices  33 us (41%)
  waiting for transfers between devices  27 us (33%)
  Pallas kernels  18.9 us (23%)
  between operations  0.89 us (1%)
  local copies, waits for them, and re-layouts  0.82 us (1%)
    ppermute x6, waiting for transfers between devices, on_device(): outer_in = lax.ppermute(outer, 'lon', lon_routes[1])  19.9 us
    pallas_call x29, Pallas kernels, call(): pl.pallas_call(body, out_shape=tuple((jax.ShapeDtypeStruct(shape, kind) f...  18.9 us
    ppermute x6, starting transfers between devices, on_device(): first_in = lax.ppermute(first, 'lat', lat_inner_route)  17.5 us
    ppermute x6, starting transfers between devices, on_device(): outer_in = lax.ppermute(outer, 'lon', lon_routes[1])  11.8 us
    ppermute x6, waiting for transfers between devices, on_device(): first_in = lax.ppermute(first, 'lat', lat_inner_route)  3.1 us
    ppermute x4, waiting for transfers between devices, on_device(): lax.ppermute(jnp.stack([inner_in[2], lat_outer]), ('lat', 'lon'), lat_out...  2.09 us
    ppermute x6, starting transfers between devices, on_device(): inner_in = lax.ppermute(inner, 'lon', lon_routes[0])  1.9 us
    ppermute x6, waiting for transfers between devices, on_device(): inner_in = lax.ppermute(inner, 'lon', lon_routes[0])  1.81 us
  transfers between devices with their start and end apart: 28, of which 16 were waited for; matrix products, arithmetic and copies ran while one was open for 1% of the time, Pallas kernels for 15%

profile of v7, /device:TPU:0, one launch (start us, length us, event | category | flops | bytes accessed | tf_op | source)
XLA Modules:
  0.0 80.7 jit_solution(16279499958137174073)
XLA Ops:
  0.6 1.2 %shard_map.113 = (f32[32,640]{1,0:T(8,128)S(1)}, bf16[96,640]{1,0:T(8,128)(2,1)S(1)}, f32[3,32,128]{2,1,0:T(8,128)S(1)}, s32[8,128]{1,0:T(8,128)S(1)}) custom-call(f32[30,1,640]{2,1,0:T(1,128)} %bitcast.36, s32[8,128]{1,0:T(8,128)} %bitcast.42), custom_call_target="tpu_custom_call" | custom-call | tf_op jit(solution)/shard_map/pallas_call | solution.py:388
  1.8 0.5 shard_map.114
  2.3 0.6 collective-permute-start
  2.9 4.7 %collective-permute-start.1 = (f32[3,32,128]{2,1,0:T(8,128)S(1)}, f32[3,32,128]{2,1,0:T(8,128)S(1)}, u32[]{:S(2)}, u32[]{:S(2)}) collective-permute-start(f32[3,32,128]{2,1,0:T(8,128)S(1)} %get-tuple-element.59), channel_id=1, source_target_pairs={{0,7},{1,2},{2,1},{3,4},{4,3},{5,6},{6,5},{7,0},{8,15},{9,10},{10,... | collective-permute-start | bytes 147464 | tf_op jit(solution)/shard_map/ppermute | solution.py:431
  7.6 1.9 %collective-permute-done.1.outer_ref = f32[3,32,128]{2,1,0:T(8,128)S(1)} collective-permute-done((f32[3,32,128]{2,1,0:T(8,128)S(1)}, f32[3,32,128]{2,1,0:T(8,128)S(1)}, u32[]{:S(2)}, u32[]{:S(2)}) %collective-permute-start.1) | collective-permute-done | bytes 49184 | tf_op jit(solution)/shard_map/ppermute | solution.py:431
  9.4 1.6 %collective-permute-start.2 = (f32[3,32,128]{2,1,0:T(8,128)S(1)}, f32[3,32,128]{2,1,0:T(8,128)S(1)}, u32[]{:S(2)}, u32[]{:S(2)}) collective-permute-start(f32[3,32,128]{2,1,0:T(8,128)S(1)} %pad_maximum_fusion), channel_id=1, source_target_pairs={{0,8},{8,0},{16,24},{24,16},{1,9},{9,1},{17,25},{25,17},{2,10},{10... | collective-permute-start | bytes 147464 | tf_op jit(solution)/shard_map/ppermute | solution.py:463
  11.0 1.5 %shard_map.115 = (bf16[896,1024]{1,0:T(8,128)(2,1)S(1)}, bf16[768,1024]{1,0:T(8,128)(2,1)S(1)}) custom-call(s32[2,960]{1,0:T(2,128)} %bitcast.39), custom_call_target="tpu_custom_call" | custom-call | tf_op jit(solution)/shard_map/pallas_call | solution.py:388
  12.5 1.3 %shard_map.118 = (f32[32,1024]{1,0:T(8,128)S(1)}, f32[1,1024]{1,0:T(1,128)S(1)}, bf16[1024,384]{1,0:T(8,128)(2,1)S(1)}, bf16[1024,640]{1,0:T(8,128)(2,1)S(1)}) custom-call(f32[30,1,960]{2,1,0:T(1,128)} %bitcast.35, s32[8,128]{1,0:T(8,128)} %bitcast.43, f32[1,960]{1,0:T(1,128)} %dual_hbm.1), custom_call_target="tpu_custom_call" | custom-call | tf_op jit(solution)/shard_map/pallas_call | solution.py:388
  13.8 0.4 shard_map.116.total_ref
  14.6 0.5 shard_map.119
  15.4 0.6 collective-permute-start.4
  16.0 3.2 %collective-permute-start.5 = (f32[3,32,128]{2,1,0:T(8,128)S(1)}, f32[3,32,128]{2,1,0:T(8,128)S(1)}, u32[]{:S(2)}, u32[]{:S(2)}) collective-permute-start(f32[3,32,128]{2,1,0:T(8,128)S(1)} %get-tuple-element.71), channel_id=1, source_target_pairs={{0,7},{1,2},{2,1},{3,4},{4,3},{5,6},{6,5},{7,0},{8,15},{9,10},{10,... | collective-permute-start | bytes 147464 | tf_op jit(solution)/shard_map/ppermute | solution.py:431
  19.1 2.6 %collective-permute-done.5.outer_ref = f32[3,32,128]{2,1,0:T(8,128)S(1)} collective-permute-done((f32[3,32,128]{2,1,0:T(8,128)S(1)}, f32[3,32,128]{2,1,0:T(8,128)S(1)}, u32[]{:S(2)}, u32[]{:S(2)}) %collective-permute-start.5) | collective-permute-done | bytes 49184 | tf_op jit(solution)/shard_map/ppermute | solution.py:431
  21.7 2.7 %collective-permute-start.6 = (f32[3,32,128]{2,1,0:T(8,128)S(1)}, f32[3,32,128]{2,1,0:T(8,128)S(1)}, u32[]{:S(2)}, u32[]{:S(2)}) collective-permute-start(f32[3,32,128]{2,1,0:T(8,128)S(1)} %pad_maximum_fusion.2), channel_id=1, source_target_pairs={{0,8},{8,0},{16,24},{24,16},{1,9},{9,1},{17,25},{25,17},{2,10},{10... | collective-permute-start | bytes 147464 | tf_op jit(solution)/shard_map/ppermute | solution.py:463
  24.4 1.2 %shard_map.124 = (f32[1,640]{1,0:T(1,128)S(1)}, f32[256,128]{1,0:T(8,128)S(1)}, f32[256,128]{1,0:T(8,128)S(1)}, f32[256,128]{1,0:T(8,128)S(1)}, bf16[640,384]{1,...) custom-call(f32[30,1,640]{2,1,0:T(1,128)} %bitcast.37, s32[8,128]{1,0:T(8,128)S(1)} %get-tuple-element.57.list_ref, ...), custom_call_target="tpu_custom_call" | custom-call | tf_op jit(solution)/shard_map/pallas_call | solution.py:388
  25.6 2.4 %shard_map.121 = (bf16[1280,640]{1,0:T(8,128)(2,1)S(1)}, bf16[1280,640]{1,0:T(8,128)(2,1)S(1)}, bf16[768,640]{1,0:T(8,128)(2,1)S(1)}, bf16[768,640]{1,0:T(8,128)(2,1)S(1)}) custom-call(s32[3,1,640]{2,1,0:T(1,128)} %bitcast.40, f32[3,1,640]{2,1,0:T(1,128)} %bitcast.41), custom_call_target="tpu_custom_call" | custom-call | tf_op jit(solution)/shard_map/pallas_call | solution.py:388
  28.0 0.7 shard_map.122.total_ref
  29.1 0.7 shard_map.125
  30.1 0.6 collective-permute-start.8
  30.6 2.1 %collective-permute-start.9 = (f32[3,32,128]{2,1,0:T(8,128)S(1)}, f32[3,32,128]{2,1,0:T(8,128)S(1)}, u32[]{:S(2)}, u32[]{:S(2)}) collective-permute-start(f32[3,32,128]{2,1,0:T(8,128)S(1)} %get-tuple-element.87), channel_id=1, source_target_pairs={{0,7},{1,2},{2,1},{3,4},{4,3},{5,6},{6,5},{7,0},{8,15},{9,10},{10,... | collective-permute-start | bytes 147464 | tf_op jit(solution)/shard_map/ppermute | solution.py:431
  32.8 3.2 %collective-permute-done.9.outer_ref = f32[3,32,128]{2,1,0:T(8,128)S(1)} collective-permute-done((f32[3,32,128]{2,1,0:T(8,128)S(1)}, f32[3,32,128]{2,1,0:T(8,128)S(1)}, u32[]{:S(2)}, u32[]{:S(2)}) %collective-permute-start.9) | collective-permute-done | bytes 49184 | tf_op jit(solution)/shard_map/ppermute | solution.py:431
  36.0 0.7 collective-permute-start.11
  36.7 0.5 collective-permute-start.12
  37.2 0.7 collective-permute-done.10.early_ref
  37.9 0.5 shard_map.127.total_ref
  38.4 1.7 %collective-permute-done.11.lat_inner_ref = f32[3,32,128]{2,1,0:T(8,128)S(1)} collective-permute-done((f32[3,32,128]{2,1,0:T(8,128)S(1)}, f32[3,32,128]{2,1,0:T(8,128)S(1)}, u32[]{:S(2)}, u32[]{:S(2)}) %collective-permute-start.11) | collective-permute-done | bytes 49184 | tf_op jit(solution)/shard_map/ppermute | solution.py:463
  41.3 1.1 %collective-permute-start.14 = (f32[3,32,128]{2,1,0:T(8,128)S(1)}, f32[3,32,128]{2,1,0:T(8,128)S(1)}, u32[]{:S(2)}, u32[]{:S(2)}) collective-permute-start(f32[3,32,128]{2,1,0:T(8,128)S(1)} %get-tuple-element.93), channel_id=1, source_target_pairs={{0,7},{1,2},{2,1},{3,4},{4,3},{5,6},{6,5},{7,0},{8,15},{9,10},{10,... | collective-permute-start | bytes 147464 | tf_op jit(solution)/shard_map/ppermute | solution.py:431
  42.5 4.2 %collective-permute-done.14.outer_ref = f32[3,32,128]{2,1,0:T(8,128)S(1)} collective-permute-done((f32[3,32,128]{2,1,0:T(8,128)S(1)}, f32[3,32,128]{2,1,0:T(8,128)S(1)}, u32[]{:S(2)}, u32[]{:S(2)}) %collective-permute-start.14) | collective-permute-done | bytes 49184 | tf_op jit(solution)/shard_map/ppermute | solution.py:431
  46.7 3.4 %collective-permute-start.16 = (f32[3,32,128]{2,1,0:T(8,128)S(1)}, f32[3,32,128]{2,1,0:T(8,128)S(1)}, u32[]{:S(2)}, u32[]{:S(2)}) collective-permute-start(f32[3,32,128]{2,1,0:T(8,128)S(1)} %pad_maximum_fusion.5), channel_id=1, source_target_pairs={{0,8},{8,0},{16,24},{24,16},{1,9},{9,1},{17,25},{25,17},{2,10},{10... | collective-permute-start | bytes 147464 | tf_op jit(solution)/shard_map/ppermute | solution.py:463
  50.1 0.5 collective-permute-start.17
  50.6 0.7 collective-permute-done.15.early_ref
  51.3 0.8 shard_map.131.total_ref
  52.7 0.6 shard_map.133
  53.6 0.6 collective-permute-start.19
  54.3 0.6 collective-permute-done.18.inner_ref
  54.9 4.2 %collective-permute-done.19.outer_ref = f32[3,32,128]{2,1,0:T(8,128)S(1)} collective-permute-done((f32[3,32,128]{2,1,0:T(8,128)S(1)}, f32[3,32,128]{2,1,0:T(8,128)S(1)}, u32[]{:S(2)}, u32[]{:S(2)}) %collective-permute-start.19) | collective-permute-done | bytes 49184 | tf_op jit(solution)/shard_map/ppermute | solution.py:431
  59.0 4.1 %collective-permute-start.21 = (f32[3,32,128]{2,1,0:T(8,128)S(1)}, f32[3,32,128]{2,1,0:T(8,128)S(1)}, u32[]{:S(2)}, u32[]{:S(2)}) collective-permute-start(f32[3,32,128]{2,1,0:T(8,128)S(1)} %pad_maximum_fusion.6), channel_id=1, source_target_pairs={{0,8},{8,0},{16,24},{24,16},{1,9},{9,1},{17,25},{25,17},{2,10},{10... | collective-permute-start | bytes 147464 | tf_op jit(solution)/shard_map/ppermute | solution.py:463
  63.2 0.5 collective-permute-start.22
  63.7 0.7 collective-permute-done.20.early_ref
  64.4 0.5 shard_map.135.total_ref
  64.9 0.5 collective-permute-done.21.lat_inner_ref
  66.6 1.1 %collective-permute-done.23.inner_ref = f32[3,32,128]{2,1,0:T(8,128)S(1)} collective-permute-done((f32[3,32,128]{2,1,0:T(8,128)S(1)}, f32[3,32,128]{2,1,0:T(8,128)S(1)}, u32[]{:S(2)}, u32[]{:S(2)}) %collective-permute-start.23) | collective-permute-done | bytes 49184 | tf_op jit(solution)/shard_map/ppermute | solution.py:436
  67.9 4.0 %collective-permute-done.24.outer_ref = f32[3,32,128]{2,1,0:T(8,128)S(1)} collective-permute-done((f32[3,32,128]{2,1,0:T(8,128)S(1)}, f32[3,32,128]{2,1,0:T(8,128)S(1)}, u32[]{:S(2)}, u32[]{:S(2)}) %collective-permute-start.24) | collective-permute-done | bytes 49184 | tf_op jit(solution)/shard_map/ppermute | solution.py:431
  72.0 5.1 %collective-permute-start.26 = (f32[3,32,128]{2,1,0:T(8,128)S(1)}, f32[3,32,128]{2,1,0:T(8,128)S(1)}, u32[]{:S(2)}, u32[]{:S(2)}) collective-permute-start(f32[3,32,128]{2,1,0:T(8,128)S(1)} %pad_maximum_fusion.7), channel_id=1, source_target_pairs={{0,8},{8,0},{16,24},{24,16},{1,9},{9,1},{17,25},{25,17},{2,10},{10... | collective-permute-start | bytes 147464 | tf_op jit(solution)/shard_map/ppermute | solution.py:463
  77.1 0.8 copy.12
  77.9 0.8 shard_map.139.total_ref
  78.7 0.6 collective-permute-done.26.lat_inner_ref
  79.7 1.0 %shard_map.141 = f32[30,1,640]{2,1,0:T(1,128)} custom-call(f32[32,640]{1,0:T(8,128)S(1)} %shard_map.140.total_ref, f32[1,32,128]{2,1,0:T(8,128)S(1)} %collective-permute-done.27.lat_outer_ref, bf16[768,640]{1,0:T(8,128)(2,1)S(1)} %get-tuple-element.75.rest_0_.high_ref.rest_2_, bf16[768,640]{1,0:T(8,128)(2,1)S(1)} %get-tuple-element.76.rest_1_.low_ref.rest_3_, ...), custom_call_target="tpu_custom_call" | custom-call | tf_op jit(solution)/shard_map/pallas_call | solution.py:388
  (63 shorter events, 5.4 us)
Async XLA Ops:
  2.3 5.3 %collective-permute-start = (f32[3,32,128]{2,1,0:T(8,128)S(1)}, f32[3,32,128]{2,1,0:T(8,128)S(1)}, u32[]{:S(2)}, u32[]{:S(2)}) collective-permute-start(f32[3,32,128]{2,1,0:T(8,128)S(1)} %get-tuple-element.58), channel_id=1, source_target_pairs={{0,1},{1,0},{2,3},{3,2},{4,5},{5,4},{6,7},{7,6},{8,9},{9,8},{10,11... | collective-permute-start | bytes 147464 | tf_op jit(solution)/shard_map/ppermute | solution.py:436
  2.9 6.6 %collective-permute-start.1 = (f32[3,32,128]{2,1,0:T(8,128)S(1)}, f32[3,32,128]{2,1,0:T(8,128)S(1)}, u32[]{:S(2)}, u32[]{:S(2)}) collective-permute-start(f32[3,32,128]{2,1,0:T(8,128)S(1)} %get-tuple-element.59), channel_id=1, source_target_pairs={{0,7},{1,2},{2,1},{3,4},{4,3},{5,6},{6,5},{7,0},{8,15},{9,10},{10,... | collective-permute-start | bytes 147464 | tf_op jit(solution)/shard_map/ppermute | solution.py:431
  9.4 4.8 %collective-permute-start.2 = (f32[3,32,128]{2,1,0:T(8,128)S(1)}, f32[3,32,128]{2,1,0:T(8,128)S(1)}, u32[]{:S(2)}, u32[]{:S(2)}) collective-permute-start(f32[3,32,128]{2,1,0:T(8,128)S(1)} %pad_maximum_fusion), channel_id=1, source_target_pairs={{0,8},{8,0},{16,24},{24,16},{1,9},{9,1},{17,25},{25,17},{2,10},{10... | collective-permute-start | bytes 147464 | tf_op jit(solution)/shard_map/ppermute | solution.py:463
  11.0 3.5 %collective-permute-start.3 = (f32[3,32,128]{2,1,0:T(8,128)S(1)}, f32[3,32,128]{2,1,0:T(8,128)S(1)}, u32[]{:S(2)}, u32[]{:S(2)}) collective-permute-start(f32[3,32,128]{2,1,0:T(8,128)S(1)} %pad_maximum_fusion.1), channel_id=1, source_target_pairs={{0,1},{1,0},{2,3},{3,2},{4,5},{5,4},{6,7},{7,6},{8,16},{9,17},{10,... | collective-permute-start | bytes 147464 | tf_op jit(solution)/shard_map/ppermute | solution.py:464
  15.4 3.7 %collective-permute-start.4 = (f32[3,32,128]{2,1,0:T(8,128)S(1)}, f32[3,32,128]{2,1,0:T(8,128)S(1)}, u32[]{:S(2)}, u32[]{:S(2)}) collective-permute-start(f32[3,32,128]{2,1,0:T(8,128)S(1)} %get-tuple-element.70), channel_id=1, source_target_pairs={{0,1},{1,0},{2,3},{3,2},{4,5},{5,4},{6,7},{7,6},{8,9},{9,8},{10,11... | collective-permute-start | bytes 147464 | tf_op jit(solution)/shard_map/ppermute | solution.py:436
  16.0 5.7 %collective-permute-start.5 = (f32[3,32,128]{2,1,0:T(8,128)S(1)}, f32[3,32,128]{2,1,0:T(8,128)S(1)}, u32[]{:S(2)}, u32[]{:S(2)}) collective-permute-start(f32[3,32,128]{2,1,0:T(8,128)S(1)} %get-tuple-element.71), channel_id=1, source_target_pairs={{0,7},{1,2},{2,1},{3,4},{4,3},{5,6},{6,5},{7,0},{8,15},{9,10},{10,... | collective-permute-start | bytes 147464 | tf_op jit(solution)/shard_map/ppermute | solution.py:431
  21.7 7.0 %collective-permute-start.6 = (f32[3,32,128]{2,1,0:T(8,128)S(1)}, f32[3,32,128]{2,1,0:T(8,128)S(1)}, u32[]{:S(2)}, u32[]{:S(2)}) collective-permute-start(f32[3,32,128]{2,1,0:T(8,128)S(1)} %pad_maximum_fusion.2), channel_id=1, source_target_pairs={{0,8},{8,0},{16,24},{24,16},{1,9},{9,1},{17,25},{25,17},{2,10},{10... | collective-permute-start | bytes 147464 | tf_op jit(solution)/shard_map/ppermute | solution.py:463
  24.4 4.7 %collective-permute-start.7 = (f32[3,32,128]{2,1,0:T(8,128)S(1)}, f32[3,32,128]{2,1,0:T(8,128)S(1)}, u32[]{:S(2)}, u32[]{:S(2)}) collective-permute-start(f32[3,32,128]{2,1,0:T(8,128)S(1)} %pad_maximum_fusion.3), channel_id=1, source_target_pairs={{0,1},{1,0},{2,3},{3,2},{4,5},{5,4},{6,7},{7,6},{8,16},{9,17},{10,... | collective-permute-start | bytes 147464 | tf_op jit(solution)/shard_map/ppermute | solution.py:464
  30.1 2.7 %collective-permute-start.8 = (f32[3,32,128]{2,1,0:T(8,128)S(1)}, f32[3,32,128]{2,1,0:T(8,128)S(1)}, u32[]{:S(2)}, u32[]{:S(2)}) collective-permute-start(f32[3,32,128]{2,1,0:T(8,128)S(1)} %get-tuple-element.86), channel_id=1, source_target_pairs={{0,1},{1,0},{2,3},{3,2},{4,5},{5,4},{6,7},{7,6},{8,9},{9,8},{10,11... | collective-permute-start | bytes 147464 | tf_op jit(solution)/shard_map/ppermute | solution.py:436
  30.6 5.3 %collective-permute-start.9 = (f32[3,32,128]{2,1,0:T(8,128)S(1)}, f32[3,32,128]{2,1,0:T(8,128)S(1)}, u32[]{:S(2)}, u32[]{:S(2)}) collective-permute-start(f32[3,32,128]{2,1,0:T(8,128)S(1)} %get-tuple-element.87), channel_id=1, source_target_pairs={{0,7},{1,2},{2,1},{3,4},{4,3},{5,6},{6,5},{7,0},{8,15},{9,10},{10,... | collective-permute-start | bytes 147464 | tf_op jit(solution)/shard_map/ppermute | solution.py:431
  36.0 4.2 %collective-permute-start.11 = (f32[3,32,128]{2,1,0:T(8,128)S(1)}, f32[3,32,128]{2,1,0:T(8,128)S(1)}, u32[]{:S(2)}, u32[]{:S(2)}) collective-permute-start(f32[3,32,128]{2,1,0:T(8,128)S(1)} %pad_maximum_fusion.4), channel_id=1, source_target_pairs={{0,8},{8,0},{16,24},{24,16},{1,9},{9,1},{17,25},{25,17},{2,10},{10... | collective-permute-start | bytes 147464 | tf_op jit(solution)/shard_map/ppermute | solution.py:463
  36.7 1.2 %collective-permute-start.10 = (f32[2,32,128]{2,1,0:T(8,128)S(1)}, f32[2,32,128]{2,1,0:T(8,128)S(1)}, u32[]{:S(2)}, u32[]{:S(2)}) collective-permute-start(f32[2,32,128]{2,1,0:T(8,128)S(1)} %pad_maximum_fusion.8), channel_id=1, source_target_pairs={{0,1},{1,0},{2,3},{3,2},{4,5},{5,4},{6,7},{7,6},{8,16},{9,17},{10,... | collective-permute-start | bytes 98312 | tf_op jit(solution)/shard_map/ppermute | solution.py:459
  36.7 3.8 %collective-permute-start.12 = (f32[1,32,128]{2,1,0:T(8,128)S(1)}, f32[1,32,128]{2,1,0:T(8,128)S(1)}, u32[]{:S(2)}, u32[]{:S(2)}) collective-permute-start(f32[1,32,128]{2,1,0:T(8,128)S(1)} %get-tuple-element.122), channel_id=1, source_target_pairs={{0,1},{1,0},{2,3},{3,2},{4,5},{5,4},{6,7},{7,6},{8,16},{9,17},{10,... | collective-permute-start | bytes 49160 | tf_op jit(solution)/shard_map/ppermute | solution.py:464
  41.2 1.3 %collective-permute-start.13 = (f32[3,32,128]{2,1,0:T(8,128)S(1)}, f32[3,32,128]{2,1,0:T(8,128)S(1)}, u32[]{:S(2)}, u32[]{:S(2)}) collective-permute-start(f32[3,32,128]{2,1,0:T(8,128)S(1)} %get-tuple-element.92), channel_id=1, source_target_pairs={{0,1},{1,0},{2,3},{3,2},{4,5},{5,4},{6,7},{7,6},{8,9},{9,8},{10,11... | collective-permute-start | bytes 147464 | tf_op jit(solution)/shard_map/ppermute | solution.py:436
  41.3 5.4 %collective-permute-start.14 = (f32[3,32,128]{2,1,0:T(8,128)S(1)}, f32[3,32,128]{2,1,0:T(8,128)S(1)}, u32[]{:S(2)}, u32[]{:S(2)}) collective-permute-start(f32[3,32,128]{2,1,0:T(8,128)S(1)} %get-tuple-element.93), channel_id=1, source_target_pairs={{0,7},{1,2},{2,1},{3,4},{4,3},{5,6},{6,5},{7,0},{8,15},{9,10},{10,... | collective-permute-start | bytes 147464 | tf_op jit(solution)/shard_map/ppermute | solution.py:431
  46.7 5.6 %collective-permute-start.16 = (f32[3,32,128]{2,1,0:T(8,128)S(1)}, f32[3,32,128]{2,1,0:T(8,128)S(1)}, u32[]{:S(2)}, u32[]{:S(2)}) collective-permute-start(f32[3,32,128]{2,1,0:T(8,128)S(1)} %pad_maximum_fusion.5), channel_id=1, source_target_pairs={{0,8},{8,0},{16,24},{24,16},{1,9},{9,1},{17,25},{25,17},{2,10},{10... | collective-permute-start | bytes 147464 | tf_op jit(solution)/shard_map/ppermute | solution.py:463
  50.1 1.2 %collective-permute-start.15 = (f32[2,32,128]{2,1,0:T(8,128)S(1)}, f32[2,32,128]{2,1,0:T(8,128)S(1)}, u32[]{:S(2)}, u32[]{:S(2)}) collective-permute-start(f32[2,32,128]{2,1,0:T(8,128)S(1)} %pad_maximum_fusion.9), channel_id=1, source_target_pairs={{0,1},{1,0},{2,3},{3,2},{4,5},{5,4},{6,7},{7,6},{8,16},{9,17},{10,... | collective-permute-start | bytes 98312 | tf_op jit(solution)/shard_map/ppermute | solution.py:459
  50.1 2.6 %collective-permute-start.17 = (f32[1,32,128]{2,1,0:T(8,128)S(1)}, f32[1,32,128]{2,1,0:T(8,128)S(1)}, u32[]{:S(2)}, u32[]{:S(2)}) collective-permute-start(f32[1,32,128]{2,1,0:T(8,128)S(1)} %get-tuple-element.118), channel_id=1, source_target_pairs={{0,1},{1,0},{2,3},{3,2},{4,5},{5,4},{6,7},{7,6},{8,16},{9,17},{10,... | collective-permute-start | bytes 49160 | tf_op jit(solution)/shard_map/ppermute | solution.py:464
  53.6 1.3 %collective-permute-start.18 = (f32[3,32,128]{2,1,0:T(8,128)S(1)}, f32[3,32,128]{2,1,0:T(8,128)S(1)}, u32[]{:S(2)}, u32[]{:S(2)}) collective-permute-start(f32[3,32,128]{2,1,0:T(8,128)S(1)} %get-tuple-element.98), channel_id=1, source_target_pairs={{0,1},{1,0},{2,3},{3,2},{4,5},{5,4},{6,7},{7,6},{8,9},{9,8},{10,11... | collective-permute-start | bytes 147464 | tf_op jit(solution)/shard_map/ppermute | solution.py:436
  53.6 5.4 %collective-permute-start.19 = (f32[3,32,128]{2,1,0:T(8,128)S(1)}, f32[3,32,128]{2,1,0:T(8,128)S(1)}, u32[]{:S(2)}, u32[]{:S(2)}) collective-permute-start(f32[3,32,128]{2,1,0:T(8,128)S(1)} %get-tuple-element.99), channel_id=1, source_target_pairs={{0,7},{1,2},{2,1},{3,4},{4,3},{5,6},{6,5},{7,0},{8,15},{9,10},{10,... | collective-permute-start | bytes 147464 | tf_op jit(solution)/shard_map/ppermute | solution.py:431
  59.0 6.3 %collective-permute-start.21 = (f32[3,32,128]{2,1,0:T(8,128)S(1)}, f32[3,32,128]{2,1,0:T(8,128)S(1)}, u32[]{:S(2)}, u32[]{:S(2)}) collective-permute-start(f32[3,32,128]{2,1,0:T(8,128)S(1)} %pad_maximum_fusion.6), channel_id=1, source_target_pairs={{0,8},{8,0},{16,24},{24,16},{1,9},{9,1},{17,25},{25,17},{2,10},{10... | collective-permute-start | bytes 147464 | tf_op jit(solution)/shard_map/ppermute | solution.py:463
  63.2 1.2 %collective-permute-start.20 = (f32[2,32,128]{2,1,0:T(8,128)S(1)}, f32[2,32,128]{2,1,0:T(8,128)S(1)}, u32[]{:S(2)}, u32[]{:S(2)}) collective-permute-start(f32[2,32,128]{2,1,0:T(8,128)S(1)} %pad_maximum_fusion.10), channel_id=1, source_target_pairs={{0,1},{1,0},{2,3},{3,2},{4,5},{5,4},{6,7},{7,6},{8,16},{9,17},{10,... | collective-permute-start | bytes 98312 | tf_op jit(solution)/shard_map/ppermute | solution.py:459
  63.2 2.5 %collective-permute-start.22 = (f32[1,32,128]{2,1,0:T(8,128)S(1)}, f32[1,32,128]{2,1,0:T(8,128)S(1)}, u32[]{:S(2)}, u32[]{:S(2)}) collective-permute-start(f32[1,32,128]{2,1,0:T(8,128)S(1)} %get-tuple-element.114), channel_id=1, source_target_pairs={{0,1},{1,0},{2,3},{3,2},{4,5},{5,4},{6,7},{7,6},{8,16},{9,17},{10,... | collective-permute-start | bytes 49160 | tf_op jit(solution)/shard_map/ppermute | solution.py:464
  66.5 1.3 %collective-permute-start.23 = (f32[3,32,128]{2,1,0:T(8,128)S(1)}, f32[3,32,128]{2,1,0:T(8,128)S(1)}, u32[]{:S(2)}, u32[]{:S(2)}) collective-permute-start(f32[3,32,128]{2,1,0:T(8,128)S(1)} %get-tuple-element.104), channel_id=1, source_target_pairs={{0,1},{1,0},{2,3},{3,2},{4,5},{5,4},{6,7},{7,6},{8,9},{9,8},{10,11... | collective-permute-start | bytes 147464 | tf_op jit(solution)/shard_map/ppermute | solution.py:436
  66.6 5.4 %collective-permute-start.24 = (f32[3,32,128]{2,1,0:T(8,128)S(1)}, f32[3,32,128]{2,1,0:T(8,128)S(1)}, u32[]{:S(2)}, u32[]{:S(2)}) collective-permute-start(f32[3,32,128]{2,1,0:T(8,128)S(1)} %get-tuple-element.105), channel_id=1, source_target_pairs={{0,7},{1,2},{2,1},{3,4},{4,3},{5,6},{6,5},{7,0},{8,15},{9,10},{10,... | collective-permute-start | bytes 147464 | tf_op jit(solution)/shard_map/ppermute | solution.py:431
  67.8 10.1 %collective-permute-start.25 = (f32[2,32,128]{2,1,0:T(8,128)S(1)}, f32[2,32,128]{2,1,0:T(8,128)S(1)}, u32[]{:S(2)}, u32[]{:S(2)}) collective-permute-start(f32[2,32,128]{2,1,0:T(8,128)S(1)} %pad_maximum_fusion.11), channel_id=1, source_target_pairs={{0,1},{1,0},{2,3},{3,2},{4,5},{5,4},{6,7},{7,6},{8,16},{9,17},{10,... | collective-permute-start | bytes 98312 | tf_op jit(solution)/shard_map/ppermute | solution.py:459
  71.9 7.7 %collective-permute-start.27 = (f32[1,32,128]{2,1,0:T(8,128)S(1)}, f32[1,32,128]{2,1,0:T(8,128)S(1)}, u32[]{:S(2)}, u32[]{:S(2)}) collective-permute-start(f32[1,32,128]{2,1,0:T(8,128)S(1)} %get-tuple-element.110), channel_id=1, source_target_pairs={{0,1},{1,0},{2,3},{3,2},{4,5},{5,4},{6,7},{7,6},{8,16},{9,17},{10,... | collective-permute-start | bytes 49160 | tf_op jit(solution)/shard_map/ppermute | solution.py:464
  72.0 7.4 %collective-permute-start.26 = (f32[3,32,128]{2,1,0:T(8,128)S(1)}, f32[3,32,128]{2,1,0:T(8,128)S(1)}, u32[]{:S(2)}, u32[]{:S(2)}) collective-permute-start(f32[3,32,128]{2,1,0:T(8,128)S(1)} %pad_maximum_fusion.7), channel_id=1, source_target_pairs={{0,8},{8,0},{16,24},{24,16},{1,9},{9,1},{17,25},{25,17},{2,10},{10... | collective-permute-start | bytes 147464 | tf_op jit(solution)/shard_map/ppermute | solution.py:463

commit v8 on v7

--- a/solution.py
+++ b/solution.py
@@ -453,16 +453,9 @@
                 raw=(0, 1),
                 copies=2,
             )
-        early = phase >= 2
-        first = jnp.stack([inner_in[1], lat_inner, outer_in[1]])
-        if early:
-            early_in = lax.ppermute(jnp.stack([inner_in[2], lat_outer]), ("lat", "lon"), lat_outer_route)
-            second = outer_in[2:3]
-        else:
-            second = jnp.stack([inner_in[2], lat_outer, outer_in[2]])
-        first_in = lax.ppermute(first, "lat", lat_inner_route)
-        second_in = lax.ppermute(second, ("lat", "lon"), lat_outer_route)
-        count = second.shape[0]
+        early_in = lax.ppermute(jnp.stack([inner_in[2], lat_outer]), ("lat", "lon"), lat_outer_route)
+        first_in = lax.ppermute(jnp.stack([inner_in[1], lat_inner, outer_in[1]]), "lat", lat_inner_route)
+        second_in = lax.ppermute(outer_in[2:3], ("lat", "lon"), lat_outer_route)
         if phase == 0:
             normal, scale, edge_outer, edge_rest = call(
                 edge_setup_kernel,
@@ -487,19 +480,21 @@
             )
         if at_cells:
             (total,) = call(
-                early_part_kernel if early else part_kernel,
+                early_part_kernel,
                 [((rows, edge_pad), f32)],
-                [((PARTS * rows, cells + 2 * halo), bf16)] + ([stack_lat(2)] if early else []),
+                [((PARTS * rows, cells + 2 * halo), bf16)] + [stack_lat(2)],
                 values,
                 inner_in,
                 outer_in,
-                *([early_in, gradient_near, gradient_far] if early else [gradient_near]),
+                early_in,
+                gradient_near,
+                gradient_far,
             )
             (total,) = call(inner_share_kernel, [((rows, edge_pad), f32)], [stack_lat(3)], total, first_in, gradient_far)
             normal, outer, stack = call(
                 edge_kernel,
                 [((rows, edge_pad), f32), bundle, stack_edges],
-                [stack_lat(count)],
+                [stack_lat(1)],
                 total,
                 second_in,
                 gradient_far,
@@ -509,13 +504,17 @@
             )
         else:
             (total,) = call(
-                early_part_kernel if early else part_kernel,
+                early_part_kernel,
                 [((rows, cells), f32)],
-                [((PARTS * rows, edge_pad + 2 * halo), bf16)] + ([stack_lat(2)] if early else []),
+                [((PARTS * rows, edge_pad + 2 * halo), bf16)] + [stack_lat(2)],
                 normal,
                 inner_in,
                 outer_in,
-                *([early_in, near_high, near_low, far_high, far_low] if early else [near_high, near_low]),
+                early_in,
+                near_high,
+                near_low,
+                far_high,
+                far_low,
             )
             (total,) = call(inner_share_kernel, [((rows, cells), f32)], [stack_lat(3)], total, first_in, far_high, far_low)
             operands = (total, second_in, far_high, far_low, values, speed, inverse, forward, back)
@@ -523,12 +522,12 @@
                 values, outer, stack = call(
                     functools.partial(cell_kernel, levels=levels),
                     [((rows, cells), f32), bundle, stack_cells],
-                    [stack_lat(count), column],
+                    [stack_lat(1), column],
                     *operands,
                     cell_outer,
                 )
             else:
-                (values,) = call(functools.partial(last_kernel, levels=levels), [((levels, 1, cells), f32)], [stack_lat(count), column], *operands)
+                (values,) = call(functools.partial(last_kernel, levels=levels), [((levels, 1, cells), f32)], [stack_lat(1), column], *operands)
     return by_level(values), normal[:levels, :edges][None]
 
 

time: 81 us -> 82.8 us (1.022)
  starting transfers between devices: 33 us -> 34.5 us
    ppermute x12, starting transfers between devices: 19.1 us -> 22.8 us  [the longest x6 20.3 us: on_device(): lax.ppermute(jnp.stack([inner_in[1], lat_inner, outer_in[1]]), 'lat', lat...]
    ppermute x6, starting transfers between devices: 11.8 us -> 10.6 us  [on_device(): outer_in = lax.ppermute(outer, 'lon', lon_routes[1])]
    ppermute x12, waiting for transfers between devices: 3.22 us -> 2.18 us  [the longest x6 2.06 us: on_device(): lax.ppermute(jnp.stack([inner_in[1], lat_inner, outer_in[1]]), 'lat', lat...]
    ppermute x6, waiting for transfers between devices: 1.81 us -> 2.79 us  [on_device(): inner_in = lax.ppermute(inner, 'lon', lon_routes[0])]
    ppermute x6, starting transfers between devices: 1.9 us -> 0.91 us  [on_device(): inner_in = lax.ppermute(inner, 'lon', lon_routes[0])]
    ppermute x4 -> x6, waiting for transfers between devices: 2.09 us -> 2.1 us  [on_device(): lax.ppermute(jnp.stack([inner_in[2], lat_outer]), ('lat', 'lon'), lat_out...]
  transfers between devices with their start and end apart: 28 -> 30, of which waited for: 16 -> 16; matrix products, arithmetic and copies ran while one was open for 1% -> 1% of each run, Pallas kernels for 15% -> 15%
where the time goes in v8:
time: 82.8 us; the launch traced here: 82.5 us
  starting transfers between devices  34.5 us (42%)
  waiting for transfers between devices  27.2 us (33%)
  Pallas kernels  18.9 us (23%)
  between operations  0.93 us (1%)
    ppermute x6, starting transfers between devices, on_device(): lax.ppermute(jnp.stack([inner_in[1], lat_inner, outer_in[1]]), 'lat', lat...  20.3 us
    ppermute x6, waiting for transfers between devices, on_device(): outer_in = lax.ppermute(outer, 'lon', lon_routes[1])  20.1 us
    pallas_call x29, Pallas kernels, call(): pl.pallas_call(body, out_shape=tuple((jax.ShapeDtypeStruct(shape, kind) f...  18.9 us
    ppermute x6, starting transfers between devices, on_device(): outer_in = lax.ppermute(outer, 'lon', lon_routes[1])  10.6 us
    ppermute x6, waiting for transfers between devices, on_device(): inner_in = lax.ppermute(inner, 'lon', lon_routes[0])  2.79 us
    ppermute x6, starting transfers between devices, on_device(): second_in = lax.ppermute(outer_in[2:3], ('lat', 'lon'), lat_outer_route)  2.54 us
    ppermute x6, waiting for transfers between devices, on_device(): lax.ppermute(jnp.stack([inner_in[2], lat_outer]), ('lat', 'lon'), lat_out...  2.1 us
    ppermute x6, waiting for transfers between devices, on_device(): lax.ppermute(jnp.stack([inner_in[1], lat_inner, outer_in[1]]), 'lat', lat...  2.06 us
  transfers between devices with their start and end apart: 30, of which 16 were waited for; matrix products, arithmetic and copies ran while one was open for 1% of the time, Pallas kernels for 15%

profile of v8, /device:TPU:0, one launch (start us, length us, event | category | flops | bytes accessed | tf_op | source)
XLA Modules:
  0.0 82.5 jit_solution(6741552153458784956)
XLA Ops:
  0.6 1.2 %shard_map.113 = (f32[32,640]{1,0:T(8,128)S(1)}, bf16[96,640]{1,0:T(8,128)(2,1)S(1)}, f32[3,32,128]{2,1,0:T(8,128)S(1)}, s32[8,128]{1,0:T(8,128)S(1)}) custom-call(f32[30,1,640]{2,1,0:T(1,128)} %bitcast.36, s32[8,128]{1,0:T(8,128)} %bitcast.42), custom_call_target="tpu_custom_call" | custom-call | tf_op jit(solution)/shard_map/pallas_call | solution.py:388
  1.8 0.5 shard_map.114
  2.3 0.6 collective-permute-start
  2.9 4.7 %collective-permute-start.1 = (f32[3,32,128]{2,1,0:T(8,128)S(1)}, f32[3,32,128]{2,1,0:T(8,128)S(1)}, u32[]{:S(2)}, u32[]{:S(2)}) collective-permute-start(f32[3,32,128]{2,1,0:T(8,128)S(1)} %get-tuple-element.59), channel_id=1, source_target_pairs={{0,7},{1,2},{2,1},{3,4},{4,3},{5,6},{6,5},{7,0},{8,15},{9,10},{10,... | collective-permute-start | bytes 147464 | tf_op jit(solution)/shard_map/ppermute | solution.py:431
  7.6 1.9 %collective-permute-done.1.outer_ref = f32[3,32,128]{2,1,0:T(8,128)S(1)} collective-permute-done((f32[3,32,128]{2,1,0:T(8,128)S(1)}, f32[3,32,128]{2,1,0:T(8,128)S(1)}, u32[]{:S(2)}, u32[]{:S(2)}) %collective-permute-start.1) | collective-permute-done | bytes 49184 | tf_op jit(solution)/shard_map/ppermute | solution.py:431
  9.4 1.6 %collective-permute-start.3 = (f32[3,32,128]{2,1,0:T(8,128)S(1)}, f32[3,32,128]{2,1,0:T(8,128)S(1)}, u32[]{:S(2)}, u32[]{:S(2)}) collective-permute-start(f32[3,32,128]{2,1,0:T(8,128)S(1)} %pad_maximum_fusion), channel_id=1, source_target_pairs={{0,8},{8,0},{16,24},{24,16},{1,9},{9,1},{17,25},{25,17},{2,10},{10... | collective-permute-start | bytes 147464 | tf_op jit(solution)/shard_map/ppermute | solution.py:457
  11.0 0.5 collective-permute-start.4
  11.5 1.5 %shard_map.115 = (bf16[896,1024]{1,0:T(8,128)(2,1)S(1)}, bf16[768,1024]{1,0:T(8,128)(2,1)S(1)}) custom-call(s32[2,960]{1,0:T(2,128)} %bitcast.39), custom_call_target="tpu_custom_call" | custom-call | tf_op jit(solution)/shard_map/pallas_call | solution.py:388
  13.0 1.3 %shard_map.118 = (f32[32,1024]{1,0:T(8,128)S(1)}, f32[1,1024]{1,0:T(1,128)S(1)}, bf16[1024,384]{1,0:T(8,128)(2,1)S(1)}, bf16[1024,640]{1,0:T(8,128)(2,1)S(1)}) custom-call(f32[30,1,960]{2,1,0:T(1,128)} %bitcast.35, s32[8,128]{1,0:T(8,128)} %bitcast.43, f32[1,960]{1,0:T(1,128)} %dual_hbm.1), custom_call_target="tpu_custom_call" | custom-call | tf_op jit(solution)/shard_map/pallas_call | solution.py:388
  14.3 0.5 shard_map.116.total_ref
  16.0 3.2 %collective-permute-start.6 = (f32[3,32,128]{2,1,0:T(8,128)S(1)}, f32[3,32,128]{2,1,0:T(8,128)S(1)}, u32[]{:S(2)}, u32[]{:S(2)}) collective-permute-start(f32[3,32,128]{2,1,0:T(8,128)S(1)} %get-tuple-element.71), channel_id=1, source_target_pairs={{0,7},{1,2},{2,1},{3,4},{4,3},{5,6},{6,5},{7,0},{8,15},{9,10},{10,... | collective-permute-start | bytes 147464 | tf_op jit(solution)/shard_map/ppermute | solution.py:431
  19.3 2.4 %collective-permute-done.6.outer_ref = f32[3,32,128]{2,1,0:T(8,128)S(1)} collective-permute-done((f32[3,32,128]{2,1,0:T(8,128)S(1)}, f32[3,32,128]{2,1,0:T(8,128)S(1)}, u32[]{:S(2)}, u32[]{:S(2)}) %collective-permute-start.6) | collective-permute-done | bytes 49184 | tf_op jit(solution)/shard_map/ppermute | solution.py:431
  21.7 3.2 %collective-permute-start.8 = (f32[3,32,128]{2,1,0:T(8,128)S(1)}, f32[3,32,128]{2,1,0:T(8,128)S(1)}, u32[]{:S(2)}, u32[]{:S(2)}) collective-permute-start(f32[3,32,128]{2,1,0:T(8,128)S(1)} %pad_maximum_fusion.1), channel_id=1, source_target_pairs={{0,8},{8,0},{16,24},{24,16},{1,9},{9,1},{17,25},{25,17},{2,10},{10... | collective-permute-start | bytes 147464 | tf_op jit(solution)/shard_map/ppermute | solution.py:457
  25.0 0.5 collective-permute-start.9
  25.5 1.2 %shard_map.124 = (f32[1,640]{1,0:T(1,128)S(1)}, f32[256,128]{1,0:T(8,128)S(1)}, f32[256,128]{1,0:T(8,128)S(1)}, f32[256,128]{1,0:T(8,128)S(1)}, bf16[640,384]{1,...) custom-call(f32[30,1,640]{2,1,0:T(1,128)} %bitcast.37, s32[8,128]{1,0:T(8,128)S(1)} %get-tuple-element.57.list_ref, ...), custom_call_target="tpu_custom_call" | custom-call | tf_op jit(solution)/shard_map/pallas_call | solution.py:388
  26.7 2.4 %shard_map.121 = (bf16[1280,640]{1,0:T(8,128)(2,1)S(1)}, bf16[1280,640]{1,0:T(8,128)(2,1)S(1)}, bf16[768,640]{1,0:T(8,128)(2,1)S(1)}, bf16[768,640]{1,0:T(8,128)(2,1)S(1)}) custom-call(s32[3,1,640]{2,1,0:T(1,128)} %bitcast.40, f32[3,1,640]{2,1,0:T(1,128)} %bitcast.41), custom_call_target="tpu_custom_call" | custom-call | tf_op jit(solution)/shard_map/pallas_call | solution.py:388
  29.1 0.8 shard_map.122.total_ref
  30.2 0.6 shard_map.125
  31.2 1.9 %collective-permute-start.11 = (f32[3,32,128]{2,1,0:T(8,128)S(1)}, f32[3,32,128]{2,1,0:T(8,128)S(1)}, u32[]{:S(2)}, u32[]{:S(2)}) collective-permute-start(f32[3,32,128]{2,1,0:T(8,128)S(1)} %get-tuple-element.87), channel_id=1, source_target_pairs={{0,7},{1,2},{2,1},{3,4},{4,3},{5,6},{6,5},{7,0},{8,15},{9,10},{10,... | collective-permute-start | bytes 147464 | tf_op jit(solution)/shard_map/ppermute | solution.py:431
  33.1 3.5 %collective-permute-done.11.outer_ref = f32[3,32,128]{2,1,0:T(8,128)S(1)} collective-permute-done((f32[3,32,128]{2,1,0:T(8,128)S(1)}, f32[3,32,128]{2,1,0:T(8,128)S(1)}, u32[]{:S(2)}, u32[]{:S(2)}) %collective-permute-start.11) | collective-permute-done | bytes 49184 | tf_op jit(solution)/shard_map/ppermute | solution.py:431
  36.6 2.6 %collective-permute-start.13 = (f32[3,32,128]{2,1,0:T(8,128)S(1)}, f32[3,32,128]{2,1,0:T(8,128)S(1)}, u32[]{:S(2)}, u32[]{:S(2)}) collective-permute-start(f32[3,32,128]{2,1,0:T(8,128)S(1)} %pad_maximum_fusion.2), channel_id=1, source_target_pairs={{0,8},{8,0},{16,24},{24,16},{1,9},{9,1},{17,25},{25,17},{2,10},{10... | collective-permute-start | bytes 147464 | tf_op jit(solution)/shard_map/ppermute | solution.py:457
  39.2 0.5 collective-permute-start.14
  39.7 0.7 collective-permute-done.12.early_ref
  40.4 0.5 shard_map.127.total_ref
  40.9 0.7 collective-permute-done.13.lat_inner_ref
  42.9 0.7 collective-permute-start.16
  43.5 0.5 collective-permute-done.15.inner_ref
  44.1 4.2 %collective-permute-done.16.outer_ref = f32[3,32,128]{2,1,0:T(8,128)S(1)} collective-permute-done((f32[3,32,128]{2,1,0:T(8,128)S(1)}, f32[3,32,128]{2,1,0:T(8,128)S(1)}, u32[]{:S(2)}, u32[]{:S(2)}) %collective-permute-start.16) | collective-permute-done | bytes 49184 | tf_op jit(solution)/shard_map/ppermute | solution.py:431
  48.2 4.2 %collective-permute-start.18 = (f32[3,32,128]{2,1,0:T(8,128)S(1)}, f32[3,32,128]{2,1,0:T(8,128)S(1)}, u32[]{:S(2)}, u32[]{:S(2)}) collective-permute-start(f32[3,32,128]{2,1,0:T(8,128)S(1)} %pad_maximum_fusion.3), channel_id=1, source_target_pairs={{0,8},{8,0},{16,24},{24,16},{1,9},{9,1},{17,25},{25,17},{2,10},{10... | collective-permute-start | bytes 147464 | tf_op jit(solution)/shard_map/ppermute | solution.py:457
  52.4 0.5 collective-permute-start.19
  52.9 0.7 collective-permute-done.17.early_ref
  53.6 0.8 shard_map.131.total_ref
  55.0 0.6 shard_map.133
  56.1 1.1 %collective-permute-done.20.inner_ref = f32[3,32,128]{2,1,0:T(8,128)S(1)} collective-permute-done((f32[3,32,128]{2,1,0:T(8,128)S(1)}, f32[3,32,128]{2,1,0:T(8,128)S(1)}, u32[]{:S(2)}, u32[]{:S(2)}) %collective-permute-start.20) | collective-permute-done | bytes 49184 | tf_op jit(solution)/shard_map/ppermute | solution.py:436
  57.2 4.2 %collective-permute-done.21.outer_ref = f32[3,32,128]{2,1,0:T(8,128)S(1)} collective-permute-done((f32[3,32,128]{2,1,0:T(8,128)S(1)}, f32[3,32,128]{2,1,0:T(8,128)S(1)}, u32[]{:S(2)}, u32[]{:S(2)}) %collective-permute-start.21) | collective-permute-done | bytes 49184 | tf_op jit(solution)/shard_map/ppermute | solution.py:431
  61.3 3.6 %collective-permute-start.23 = (f32[3,32,128]{2,1,0:T(8,128)S(1)}, f32[3,32,128]{2,1,0:T(8,128)S(1)}, u32[]{:S(2)}, u32[]{:S(2)}) collective-permute-start(f32[3,32,128]{2,1,0:T(8,128)S(1)} %pad_maximum_fusion.4), channel_id=1, source_target_pairs={{0,8},{8,0},{16,24},{24,16},{1,9},{9,1},{17,25},{25,17},{2,10},{10... | collective-permute-start | bytes 147464 | tf_op jit(solution)/shard_map/ppermute | solution.py:457
  64.9 0.5 collective-permute-start.24
  65.4 0.7 collective-permute-done.22.early_ref
  66.1 0.5 shard_map.135.total_ref
  66.6 0.5 collective-permute-done.23.lat_inner_ref
  67.4 0.4 shard_map.137
  68.4 1.1 %collective-permute-done.25.inner_ref = f32[3,32,128]{2,1,0:T(8,128)S(1)} collective-permute-done((f32[3,32,128]{2,1,0:T(8,128)S(1)}, f32[3,32,128]{2,1,0:T(8,128)S(1)}, u32[]{:S(2)}, u32[]{:S(2)}) %collective-permute-start.25) | collective-permute-done | bytes 49184 | tf_op jit(solution)/shard_map/ppermute | solution.py:436
  69.7 4.0 %collective-permute-done.26.outer_ref = f32[3,32,128]{2,1,0:T(8,128)S(1)} collective-permute-done((f32[3,32,128]{2,1,0:T(8,128)S(1)}, f32[3,32,128]{2,1,0:T(8,128)S(1)}, u32[]{:S(2)}, u32[]{:S(2)}) %collective-permute-start.26) | collective-permute-done | bytes 49184 | tf_op jit(solution)/shard_map/ppermute | solution.py:431
  73.7 5.1 %collective-permute-start.28 = (f32[3,32,128]{2,1,0:T(8,128)S(1)}, f32[3,32,128]{2,1,0:T(8,128)S(1)}, u32[]{:S(2)}, u32[]{:S(2)}) collective-permute-start(f32[3,32,128]{2,1,0:T(8,128)S(1)} %pad_maximum_fusion.5), channel_id=1, source_target_pairs={{0,8},{8,0},{16,24},{24,16},{1,9},{9,1},{17,25},{25,17},{2,10},{10... | collective-permute-start | bytes 147464 | tf_op jit(solution)/shard_map/ppermute | solution.py:457
  78.9 0.8 copy.12
  79.6 0.8 shard_map.139.total_ref
  80.4 0.6 collective-permute-done.28.lat_inner_ref
  81.4 1.0 %shard_map.141 = f32[30,1,640]{2,1,0:T(1,128)} custom-call(f32[32,640]{1,0:T(8,128)S(1)} %shard_map.140.total_ref, f32[1,32,128]{2,1,0:T(8,128)S(1)} %collective-permute-done.29.lat_outer_ref, bf16[768,640]{1,0:T(8,128)(2,1)S(1)} %get-tuple-element.75.rest_2_.rest_0_.high_ref, bf16[768,640]{1,0:T(8,128)(2,1)S(1)} %get-tuple-element.76.rest_3_.rest_1_.low_ref, ...), custom_call_target="tpu_custom_call" | custom-call | tf_op jit(solution)/shard_map/pallas_call | solution.py:388
  (67 shorter events, 5.5 us)
Async XLA Ops:
  2.3 5.3 %collective-permute-start = (f32[3,32,128]{2,1,0:T(8,128)S(1)}, f32[3,32,128]{2,1,0:T(8,128)S(1)}, u32[]{:S(2)}, u32[]{:S(2)}) collective-permute-start(f32[3,32,128]{2,1,0:T(8,128)S(1)} %get-tuple-element.58), channel_id=1, source_target_pairs={{0,1},{1,0},{2,3},{3,2},{4,5},{5,4},{6,7},{7,6},{8,9},{9,8},{10,11... | collective-permute-start | bytes 147464 | tf_op jit(solution)/shard_map/ppermute | solution.py:436
  2.9 6.6 %collective-permute-start.1 = (f32[3,32,128]{2,1,0:T(8,128)S(1)}, f32[3,32,128]{2,1,0:T(8,128)S(1)}, u32[]{:S(2)}, u32[]{:S(2)}) collective-permute-start(f32[3,32,128]{2,1,0:T(8,128)S(1)} %get-tuple-element.59), channel_id=1, source_target_pairs={{0,7},{1,2},{2,1},{3,4},{4,3},{5,6},{6,5},{7,0},{8,15},{9,10},{10,... | collective-permute-start | bytes 147464 | tf_op jit(solution)/shard_map/ppermute | solution.py:431
  9.4 5.4 %collective-permute-start.3 = (f32[3,32,128]{2,1,0:T(8,128)S(1)}, f32[3,32,128]{2,1,0:T(8,128)S(1)}, u32[]{:S(2)}, u32[]{:S(2)}) collective-permute-start(f32[3,32,128]{2,1,0:T(8,128)S(1)} %pad_maximum_fusion), channel_id=1, source_target_pairs={{0,8},{8,0},{16,24},{24,16},{1,9},{9,1},{17,25},{25,17},{2,10},{10... | collective-permute-start | bytes 147464 | tf_op jit(solution)/shard_map/ppermute | solution.py:457
  11.0 3.3 %collective-permute-start.2 = (f32[2,32,128]{2,1,0:T(8,128)S(1)}, f32[2,32,128]{2,1,0:T(8,128)S(1)}, u32[]{:S(2)}, u32[]{:S(2)}) collective-permute-start(f32[2,32,128]{2,1,0:T(8,128)S(1)} %pad_maximum_fusion.6), channel_id=1, source_target_pairs={{0,1},{1,0},{2,3},{3,2},{4,5},{5,4},{6,7},{7,6},{8,16},{9,17},{10,... | collective-permute-start | bytes 98312 | tf_op jit(solution)/shard_map/ppermute | solution.py:456
  11.0 4.1 %collective-permute-start.4 = (f32[1,32,128]{2,1,0:T(8,128)S(1)}, f32[1,32,128]{2,1,0:T(8,128)S(1)}, u32[]{:S(2)}, u32[]{:S(2)}) collective-permute-start(f32[1,32,128]{2,1,0:T(8,128)S(1)} %get-tuple-element.130), channel_id=1, source_target_pairs={{0,1},{1,0},{2,3},{3,2},{4,5},{5,4},{6,7},{7,6},{8,16},{9,17},{10,... | collective-permute-start | bytes 49160 | tf_op jit(solution)/shard_map/ppermute | solution.py:458
  16.0 3.3 %collective-permute-start.5 = (f32[3,32,128]{2,1,0:T(8,128)S(1)}, f32[3,32,128]{2,1,0:T(8,128)S(1)}, u32[]{:S(2)}, u32[]{:S(2)}) collective-permute-start(f32[3,32,128]{2,1,0:T(8,128)S(1)} %get-tuple-element.70), channel_id=1, source_target_pairs={{0,1},{1,0},{2,3},{3,2},{4,5},{5,4},{6,7},{7,6},{8,9},{9,8},{10,11... | collective-permute-start | bytes 147464 | tf_op jit(solution)/shard_map/ppermute | solution.py:436
  16.0 5.7 %collective-permute-start.6 = (f32[3,32,128]{2,1,0:T(8,128)S(1)}, f32[3,32,128]{2,1,0:T(8,128)S(1)}, u32[]{:S(2)}, u32[]{:S(2)}) collective-permute-start(f32[3,32,128]{2,1,0:T(8,128)S(1)} %get-tuple-element.71), channel_id=1, source_target_pairs={{0,7},{1,2},{2,1},{3,4},{4,3},{5,6},{6,5},{7,0},{8,15},{9,10},{10,... | collective-permute-start | bytes 147464 | tf_op jit(solution)/shard_map/ppermute | solution.py:431
  21.7 8.2 %collective-permute-start.8 = (f32[3,32,128]{2,1,0:T(8,128)S(1)}, f32[3,32,128]{2,1,0:T(8,128)S(1)}, u32[]{:S(2)}, u32[]{:S(2)}) collective-permute-start(f32[3,32,128]{2,1,0:T(8,128)S(1)} %pad_maximum_fusion.1), channel_id=1, source_target_pairs={{0,8},{8,0},{16,24},{24,16},{1,9},{9,1},{17,25},{25,17},{2,10},{10... | collective-permute-start | bytes 147464 | tf_op jit(solution)/shard_map/ppermute | solution.py:457
  25.0 4.1 %collective-permute-start.7 = (f32[2,32,128]{2,1,0:T(8,128)S(1)}, f32[2,32,128]{2,1,0:T(8,128)S(1)}, u32[]{:S(2)}, u32[]{:S(2)}) collective-permute-start(f32[2,32,128]{2,1,0:T(8,128)S(1)} %pad_maximum_fusion.7), channel_id=1, source_target_pairs={{0,1},{1,0},{2,3},{3,2},{4,5},{5,4},{6,7},{7,6},{8,16},{9,17},{10,... | collective-permute-start | bytes 98312 | tf_op jit(solution)/shard_map/ppermute | solution.py:456
  25.0 5.3 %collective-permute-start.9 = (f32[1,32,128]{2,1,0:T(8,128)S(1)}, f32[1,32,128]{2,1,0:T(8,128)S(1)}, u32[]{:S(2)}, u32[]{:S(2)}) collective-permute-start(f32[1,32,128]{2,1,0:T(8,128)S(1)} %get-tuple-element.126), channel_id=1, source_target_pairs={{0,1},{1,0},{2,3},{3,2},{4,5},{5,4},{6,7},{7,6},{8,16},{9,17},{10,... | collective-permute-start | bytes 49160 | tf_op jit(solution)/shard_map/ppermute | solution.py:458
  31.2 1.9 %collective-permute-start.10 = (f32[3,32,128]{2,1,0:T(8,128)S(1)}, f32[3,32,128]{2,1,0:T(8,128)S(1)}, u32[]{:S(2)}, u32[]{:S(2)}) collective-permute-start(f32[3,32,128]{2,1,0:T(8,128)S(1)} %get-tuple-element.86), channel_id=1, source_target_pairs={{0,1},{1,0},{2,3},{3,2},{4,5},{5,4},{6,7},{7,6},{8,9},{9,8},{10,11... | collective-permute-start | bytes 147464 | tf_op jit(solution)/shard_map/ppermute | solution.py:436
  31.2 5.4 %collective-permute-start.11 = (f32[3,32,128]{2,1,0:T(8,128)S(1)}, f32[3,32,128]{2,1,0:T(8,128)S(1)}, u32[]{:S(2)}, u32[]{:S(2)}) collective-permute-start(f32[3,32,128]{2,1,0:T(8,128)S(1)} %get-tuple-element.87), channel_id=1, source_target_pairs={{0,7},{1,2},{2,1},{3,4},{4,3},{5,6},{6,5},{7,0},{8,15},{9,10},{10,... | collective-permute-start | bytes 147464 | tf_op jit(solution)/shard_map/ppermute | solution.py:431
  36.6 5.0 %collective-permute-start.13 = (f32[3,32,128]{2,1,0:T(8,128)S(1)}, f32[3,32,128]{2,1,0:T(8,128)S(1)}, u32[]{:S(2)}, u32[]{:S(2)}) collective-permute-start(f32[3,32,128]{2,1,0:T(8,128)S(1)} %pad_maximum_fusion.2), channel_id=1, source_target_pairs={{0,8},{8,0},{16,24},{24,16},{1,9},{9,1},{17,25},{25,17},{2,10},{10... | collective-permute-start | bytes 147464 | tf_op jit(solution)/shard_map/ppermute | solution.py:457
  39.2 1.2 %collective-permute-start.12 = (f32[2,32,128]{2,1,0:T(8,128)S(1)}, f32[2,32,128]{2,1,0:T(8,128)S(1)}, u32[]{:S(2)}, u32[]{:S(2)}) collective-permute-start(f32[2,32,128]{2,1,0:T(8,128)S(1)} %pad_maximum_fusion.8), channel_id=1, source_target_pairs={{0,1},{1,0},{2,3},{3,2},{4,5},{5,4},{6,7},{7,6},{8,16},{9,17},{10,... | collective-permute-start | bytes 98312 | tf_op jit(solution)/shard_map/ppermute | solution.py:456
  39.2 2.7 %collective-permute-start.14 = (f32[1,32,128]{2,1,0:T(8,128)S(1)}, f32[1,32,128]{2,1,0:T(8,128)S(1)}, u32[]{:S(2)}, u32[]{:S(2)}) collective-permute-start(f32[1,32,128]{2,1,0:T(8,128)S(1)} %get-tuple-element.122), channel_id=1, source_target_pairs={{0,1},{1,0},{2,3},{3,2},{4,5},{5,4},{6,7},{7,6},{8,16},{9,17},{10,... | collective-permute-start | bytes 49160 | tf_op jit(solution)/shard_map/ppermute | solution.py:458
  42.8 1.3 %collective-permute-start.15 = (f32[3,32,128]{2,1,0:T(8,128)S(1)}, f32[3,32,128]{2,1,0:T(8,128)S(1)}, u32[]{:S(2)}, u32[]{:S(2)}) collective-permute-start(f32[3,32,128]{2,1,0:T(8,128)S(1)} %get-tuple-element.92), channel_id=1, source_target_pairs={{0,1},{1,0},{2,3},{3,2},{4,5},{5,4},{6,7},{7,6},{8,9},{9,8},{10,11... | collective-permute-start | bytes 147464 | tf_op jit(solution)/shard_map/ppermute | solution.py:436
  42.9 5.4 %collective-permute-start.16 = (f32[3,32,128]{2,1,0:T(8,128)S(1)}, f32[3,32,128]{2,1,0:T(8,128)S(1)}, u32[]{:S(2)}, u32[]{:S(2)}) collective-permute-start(f32[3,32,128]{2,1,0:T(8,128)S(1)} %get-tuple-element.93), channel_id=1, source_target_pairs={{0,7},{1,2},{2,1},{3,4},{4,3},{5,6},{6,5},{7,0},{8,15},{9,10},{10,... | collective-permute-start | bytes 147464 | tf_op jit(solution)/shard_map/ppermute | solution.py:431
  48.2 6.4 %collective-permute-start.18 = (f32[3,32,128]{2,1,0:T(8,128)S(1)}, f32[3,32,128]{2,1,0:T(8,128)S(1)}, u32[]{:S(2)}, u32[]{:S(2)}) collective-permute-start(f32[3,32,128]{2,1,0:T(8,128)S(1)} %pad_maximum_fusion.3), channel_id=1, source_target_pairs={{0,8},{8,0},{16,24},{24,16},{1,9},{9,1},{17,25},{25,17},{2,10},{10... | collective-permute-start | bytes 147464 | tf_op jit(solution)/shard_map/ppermute | solution.py:457
  52.4 1.2 %collective-permute-start.17 = (f32[2,32,128]{2,1,0:T(8,128)S(1)}, f32[2,32,128]{2,1,0:T(8,128)S(1)}, u32[]{:S(2)}, u32[]{:S(2)}) collective-permute-start(f32[2,32,128]{2,1,0:T(8,128)S(1)} %pad_maximum_fusion.9), channel_id=1, source_target_pairs={{0,1},{1,0},{2,3},{3,2},{4,5},{5,4},{6,7},{7,6},{8,16},{9,17},{10,... | collective-permute-start | bytes 98312 | tf_op jit(solution)/shard_map/ppermute | solution.py:456
  52.4 2.5 %collective-permute-start.19 = (f32[1,32,128]{2,1,0:T(8,128)S(1)}, f32[1,32,128]{2,1,0:T(8,128)S(1)}, u32[]{:S(2)}, u32[]{:S(2)}) collective-permute-start(f32[1,32,128]{2,1,0:T(8,128)S(1)} %get-tuple-element.118), channel_id=1, source_target_pairs={{0,1},{1,0},{2,3},{3,2},{4,5},{5,4},{6,7},{7,6},{8,16},{9,17},{10,... | collective-permute-start | bytes 49160 | tf_op jit(solution)/shard_map/ppermute | solution.py:458
  55.9 1.3 %collective-permute-start.20 = (f32[3,32,128]{2,1,0:T(8,128)S(1)}, f32[3,32,128]{2,1,0:T(8,128)S(1)}, u32[]{:S(2)}, u32[]{:S(2)}) collective-permute-start(f32[3,32,128]{2,1,0:T(8,128)S(1)} %get-tuple-element.98), channel_id=1, source_target_pairs={{0,1},{1,0},{2,3},{3,2},{4,5},{5,4},{6,7},{7,6},{8,9},{9,8},{10,11... | collective-permute-start | bytes 147464 | tf_op jit(solution)/shard_map/ppermute | solution.py:436
  55.9 5.4 %collective-permute-start.21 = (f32[3,32,128]{2,1,0:T(8,128)S(1)}, f32[3,32,128]{2,1,0:T(8,128)S(1)}, u32[]{:S(2)}, u32[]{:S(2)}) collective-permute-start(f32[3,32,128]{2,1,0:T(8,128)S(1)} %get-tuple-element.99), channel_id=1, source_target_pairs={{0,7},{1,2},{2,1},{3,4},{4,3},{5,6},{6,5},{7,0},{8,15},{9,10},{10,... | collective-permute-start | bytes 147464 | tf_op jit(solution)/shard_map/ppermute | solution.py:431
  61.3 5.8 %collective-permute-start.23 = (f32[3,32,128]{2,1,0:T(8,128)S(1)}, f32[3,32,128]{2,1,0:T(8,128)S(1)}, u32[]{:S(2)}, u32[]{:S(2)}) collective-permute-start(f32[3,32,128]{2,1,0:T(8,128)S(1)} %pad_maximum_fusion.4), channel_id=1, source_target_pairs={{0,8},{8,0},{16,24},{24,16},{1,9},{9,1},{17,25},{25,17},{2,10},{10... | collective-permute-start | bytes 147464 | tf_op jit(solution)/shard_map/ppermute | solution.py:457
  64.9 1.2 %collective-permute-start.22 = (f32[2,32,128]{2,1,0:T(8,128)S(1)}, f32[2,32,128]{2,1,0:T(8,128)S(1)}, u32[]{:S(2)}, u32[]{:S(2)}) collective-permute-start(f32[2,32,128]{2,1,0:T(8,128)S(1)} %pad_maximum_fusion.10), channel_id=1, source_target_pairs={{0,1},{1,0},{2,3},{3,2},{4,5},{5,4},{6,7},{7,6},{8,16},{9,17},{10,... | collective-permute-start | bytes 98312 | tf_op jit(solution)/shard_map/ppermute | solution.py:456
  64.9 2.5 %collective-permute-start.24 = (f32[1,32,128]{2,1,0:T(8,128)S(1)}, f32[1,32,128]{2,1,0:T(8,128)S(1)}, u32[]{:S(2)}, u32[]{:S(2)}) collective-permute-start(f32[1,32,128]{2,1,0:T(8,128)S(1)} %get-tuple-element.114), channel_id=1, source_target_pairs={{0,1},{1,0},{2,3},{3,2},{4,5},{5,4},{6,7},{7,6},{8,16},{9,17},{10,... | collective-permute-start | bytes 49160 | tf_op jit(solution)/shard_map/ppermute | solution.py:458
  68.2 1.3 %collective-permute-start.25 = (f32[3,32,128]{2,1,0:T(8,128)S(1)}, f32[3,32,128]{2,1,0:T(8,128)S(1)}, u32[]{:S(2)}, u32[]{:S(2)}) collective-permute-start(f32[3,32,128]{2,1,0:T(8,128)S(1)} %get-tuple-element.104), channel_id=1, source_target_pairs={{0,1},{1,0},{2,3},{3,2},{4,5},{5,4},{6,7},{7,6},{8,9},{9,8},{10,11... | collective-permute-start | bytes 147464 | tf_op jit(solution)/shard_map/ppermute | solution.py:436
  68.3 5.4 %collective-permute-start.26 = (f32[3,32,128]{2,1,0:T(8,128)S(1)}, f32[3,32,128]{2,1,0:T(8,128)S(1)}, u32[]{:S(2)}, u32[]{:S(2)}) collective-permute-start(f32[3,32,128]{2,1,0:T(8,128)S(1)} %get-tuple-element.105), channel_id=1, source_target_pairs={{0,7},{1,2},{2,1},{3,4},{4,3},{5,6},{6,5},{7,0},{8,15},{9,10},{10,... | collective-permute-start | bytes 147464 | tf_op jit(solution)/shard_map/ppermute | solution.py:431
  69.5 10.1 %collective-permute-start.27 = (f32[2,32,128]{2,1,0:T(8,128)S(1)}, f32[2,32,128]{2,1,0:T(8,128)S(1)}, u32[]{:S(2)}, u32[]{:S(2)}) collective-permute-start(f32[2,32,128]{2,1,0:T(8,128)S(1)} %pad_maximum_fusion.11), channel_id=1, source_target_pairs={{0,1},{1,0},{2,3},{3,2},{4,5},{5,4},{6,7},{7,6},{8,16},{9,17},{10,... | collective-permute-start | bytes 98312 | tf_op jit(solution)/shard_map/ppermute | solution.py:456
  73.7 7.7 %collective-permute-start.29 = (f32[1,32,128]{2,1,0:T(8,128)S(1)}, f32[1,32,128]{2,1,0:T(8,128)S(1)}, u32[]{:S(2)}, u32[]{:S(2)}) collective-permute-start(f32[1,32,128]{2,1,0:T(8,128)S(1)} %get-tuple-element.110), channel_id=1, source_target_pairs={{0,1},{1,0},{2,3},{3,2},{4,5},{5,4},{6,7},{7,6},{8,16},{9,17},{10,... | collective-permute-start | bytes 49160 | tf_op jit(solution)/shard_map/ppermute | solution.py:458
  73.7 7.4 %collective-permute-start.28 = (f32[3,32,128]{2,1,0:T(8,128)S(1)}, f32[3,32,128]{2,1,0:T(8,128)S(1)}, u32[]{:S(2)}, u32[]{:S(2)}) collective-permute-start(f32[3,32,128]{2,1,0:T(8,128)S(1)} %pad_maximum_fusion.5), channel_id=1, source_target_pairs={{0,8},{8,0},{16,24},{24,16},{1,9},{9,1},{17,25},{25,17},{2,10},{10... | collective-permute-start | bytes 147464 | tf_op jit(solution)/shard_map/ppermute | solution.py:457

commit v9 on v7

--- a/solution.py
+++ b/solution.py
@@ -199,7 +199,9 @@
     fill_rows(far_ref, near_ref.shape[0])
 
 
-def edge_setup_kernel(velocity_hbm, list_hbm, dual_hbm, edges_ref, scale_ref, outer_matrix_ref, rest_matrix_ref, velocity_ref, list_ref, dual_ref, sems):
+def edge_setup_kernel(
+    velocity_hbm, list_hbm, dual_hbm, far_ref, edges_ref, scale_ref, outer_matrix_ref, rest_matrix_ref, late_ref, sent_scale_ref, velocity_ref, list_ref, dual_ref, stack_ref, sems
+):
     lists, velocity, dual = start_fetch([(list_hbm, list_ref), (velocity_hbm, velocity_ref), (dual_hbm, dual_ref)], sems)
     levels, _, edges = velocity_ref.shape
     edges_ref[...] = jnp.zeros(edges_ref.shape, f32)
@@ -211,6 +213,11 @@
     dual.wait()
     edges_ref[0:levels, 0:edges] = velocity_ref[:, 0, :]
     scale_ref[:, 0:edges] = STEP_SCALE * dual_ref[...]
+    late = far_ref[far_ref.shape[0] - late_ref.shape[0] :, :]
+    late_ref[...] = jnp.dot(late, outer_matrix_ref[...], preferred_element_type=f32).astype(bf16)
+    rows = stack_ref.shape[0] // PARTS
+    put_parts(stack_ref, jnp.broadcast_to(scale_ref[...], (rows, scale_ref.shape[1])), 0)
+    sent_scale_ref[...] = gather_matmul(stack_ref, [outer_matrix_ref[...]], rows)[0:1]
 
 
 def weight_kernel(
@@ -305,13 +312,28 @@
     new_total_ref[...] = lat_share(total_ref, lat_inner_ref, matrix_refs, stack_ref, 0)
 
 
-def edge_kernel(total_ref, lat_outer_ref, far_ref, edges_ref, scale_ref, matrix_ref, new_edges_ref, outer_ref, own_stack_ref, stack_ref):
-    rows = edges_ref.shape[0]
+def sent_base_kernel(total_ref, lat_inner_ref, far_ref, edges_ref, scale_ref, matrix_ref, new_total_ref, base_ref, stack_ref, own_stack_ref):
+    total = lat_share(total_ref, lat_inner_ref, [far_ref], stack_ref, 0)
+    new_total_ref[...] = total
+    put_parts(own_stack_ref, edges_ref[...] - scale_ref[...] * total, 0)
+    base_ref[...] = gather_matmul(own_stack_ref, [matrix_ref[...]], total_ref.shape[0])
+
+
+def edge_sent_kernel(base_ref, lat_outer_ref, late_ref, sent_scale_ref, outer_ref, stack_ref):
+    rows = base_ref.shape[0]
+    count, _, halo = lat_outer_ref.shape
+    for member in range(count):
+        put_parts(stack_ref, lat_outer_ref[member], member * halo)
+    late = late_ref[late_ref.shape[0] - count * halo :, :]
+    store_outer(base_ref[...] - sent_scale_ref[...] * gather_matmul(stack_ref, [late], rows), outer_ref)
+
+
+def edge_rest_kernel(total_ref, lat_outer_ref, far_ref, edges_ref, scale_ref, matrix_ref, new_edges_ref, inner_ref, lat_inner_ref, lat_outer_out_ref, stack_ref, own_stack_ref):
     difference = lat_share(total_ref, lat_outer_ref, [far_ref], stack_ref, 6 - lat_outer_ref.shape[0])
     new_edges = edges_ref[...] - scale_ref[...] * difference
     new_edges_ref[...] = new_edges
     put_parts(own_stack_ref, new_edges, 0)
-    store_outer(gather_matmul(own_stack_ref, [matrix_ref[...]], rows), outer_ref)
+    store_rest(gather_matmul(own_stack_ref, [matrix_ref[...]], edges_ref.shape[0]), inner_ref, lat_inner_ref, lat_outer_out_ref)
 
 
 def solve_columns(total_ref, lat_outer_ref, high_ref, low_ref, cells_ref, speed_ref, inverse_ref, forward_ref, back_ref, levels, stack_ref, column_ref):
@@ -431,8 +453,20 @@
         outer_in = lax.ppermute(outer, "lon", lon_routes[1])
         if phase == 0:
             inner, lat_inner, lat_outer = call(first_rest_kernel, [bundle, straight, straight], [sent_rest(cells)], stack, cell_list)
+        elif at_cells:
+            inner, lat_inner, lat_outer = call(rest_kernel, [bundle, straight, straight], [], stack, cell_rest)
         else:
-            inner, lat_inner, lat_outer = call(rest_kernel, [bundle, straight, straight], [], stack, cell_rest if at_cells else edge_rest)
+            normal, inner, lat_inner, lat_outer = call(
+                edge_rest_kernel,
+                [((rows, edge_pad), f32), bundle, straight, straight],
+                [stack_lat(second_in.shape[0]), stack_edges],
+                total,
+                second_in,
+                gradient_far,
+                normal,
+                scale,
+                edge_rest,
+            )
         inner_in = lax.ppermute(inner, "lon", lon_routes[0])
         if phase == 0:
             gradient_near, gradient_far = call(
@@ -464,13 +498,14 @@
         second_in = lax.ppermute(second, ("lat", "lon"), lat_outer_route)
         count = second.shape[0]
         if phase == 0:
-            normal, scale, edge_outer, edge_rest = call(
+            normal, scale, edge_outer, edge_rest, late_sent, sent_scale = call(
                 edge_setup_kernel,
-                [((rows, edge_pad), f32), ((1, edge_pad), f32), sent_outer(edge_pad), sent_rest(edge_pad)],
-                [((levels, 1, edges), f32), (send_edges.shape[1:], i32), ((1, edges), f32)],
+                [((rows, edge_pad), f32), ((1, edge_pad), f32), sent_outer(edge_pad), sent_rest(edge_pad), sent_outer(3 * halo), ((1, 3 * halo), f32)],
+                [((levels, 1, edges), f32), (send_edges.shape[1:], i32), ((1, edges), f32), ((PARTS * 16, edge_pad), bf16)],
                 by_level(velocity),
                 send_edges[0],
                 inv_dual,
+                gradient_far,
                 raw=(0, 1, 2),
                 copies=3,
             )
@@ -495,18 +530,18 @@
                 outer_in,
                 *([early_in, gradient_near, gradient_far] if early else [gradient_near]),
             )
-            (total,) = call(inner_share_kernel, [((rows, edge_pad), f32)], [stack_lat(3)], total, first_in, gradient_far)
-            normal, outer, stack = call(
-                edge_kernel,
-                [((rows, edge_pad), f32), bundle, stack_edges],
-                [stack_lat(count)],
+            total, base = call(
+                sent_base_kernel,
+                [((rows, edge_pad), f32), ((rows, 3 * halo), f32)],
+                [stack_lat(3), stack_edges],
                 total,
-                second_in,
+                first_in,
                 gradient_far,
                 normal,
                 scale,
                 edge_outer,
             )
+            (outer,) = call(edge_sent_kernel, [bundle], [stack_lat(count)], base, second_in, late_sent, sent_scale)
         else:
             (total,) = call(
                 early_part_kernel if early else part_kernel,

time: 81 us -> 81.6 us (level)
  Pallas kernels: 18.9 us -> 19.9 us
    pallas_call x29, Pallas kernels: 18.9 us -> 19.9 us  [call(): pl.pallas_call(body, out_shape=tuple((jax.ShapeDtypeStruct(shape, kind) f...]
  transfers between devices with their start and end apart: 28 -> 28, of which waited for: 16 -> 15; matrix products, arithmetic and copies ran while one was open for 1% -> 1% of each run, Pallas kernels for 15% -> 17%
where the time goes in v9:
time: 81.6 us; the launch traced here: 81.3 us
  starting transfers between devices  32.6 us (40%)
  waiting for transfers between devices  27 us (33%)
  Pallas kernels  19.9 us (24%)
  between operations  0.89 us (1%)
  local copies, waits for them, and re-layouts  0.82 us (1%)
    ppermute x6, waiting for transfers between devices, on_device(): outer_in = lax.ppermute(outer, 'lon', lon_routes[1])  20.2 us
    pallas_call x29, Pallas kernels, call(): pl.pallas_call(body, out_shape=tuple((jax.ShapeDtypeStruct(shape, kind) f...  19.9 us
    ppermute x6, starting transfers between devices, on_device(): first_in = lax.ppermute(first, 'lat', lat_inner_route)  17.1 us
    ppermute x6, starting transfers between devices, on_device(): outer_in = lax.ppermute(outer, 'lon', lon_routes[1])  11.8 us
    ppermute x6, waiting for transfers between devices, on_device(): first_in = lax.ppermute(first, 'lat', lat_inner_route)  3.21 us
    ppermute x4, waiting for transfers between devices, on_device(): lax.ppermute(jnp.stack([inner_in[2], lat_outer]), ('lat', 'lon'), lat_out...  2.09 us
    ppermute x6, starting transfers between devices, on_device(): inner_in = lax.ppermute(inner, 'lon', lon_routes[0])  1.98 us
  transfers between devices with their start and end apart: 28, of which 15 were waited for; matrix products, arithmetic and copies ran while one was open for 1% of the time, Pallas kernels for 17%

profile of v9, /device:TPU:0, one launch (start us, length us, event | category | flops | bytes accessed | tf_op | source)
XLA Modules:
  0.0 81.3 jit_solution(9006968949862021357)
XLA Ops:
  0.6 1.2 %shard_map.113 = (f32[32,640]{1,0:T(8,128)S(1)}, bf16[96,640]{1,0:T(8,128)(2,1)S(1)}, f32[3,32,128]{2,1,0:T(8,128)S(1)}, s32[8,128]{1,0:T(8,128)S(1)}) custom-call(f32[30,1,640]{2,1,0:T(1,128)} %bitcast.36, s32[8,128]{1,0:T(8,128)} %bitcast.42), custom_call_target="tpu_custom_call" | custom-call | tf_op jit(solution)/shard_map/pallas_call | solution.py:410
  1.8 0.5 shard_map.114
  2.3 0.6 collective-permute-start
  2.9 4.7 %collective-permute-start.1 = (f32[3,32,128]{2,1,0:T(8,128)S(1)}, f32[3,32,128]{2,1,0:T(8,128)S(1)}, u32[]{:S(2)}, u32[]{:S(2)}) collective-permute-start(f32[3,32,128]{2,1,0:T(8,128)S(1)} %get-tuple-element.61), channel_id=1, source_target_pairs={{0,7},{1,2},{2,1},{3,4},{4,3},{5,6},{6,5},{7,0},{8,15},{9,10},{10,... | collective-permute-start | bytes 147464 | tf_op jit(solution)/shard_map/ppermute | solution.py:453
  7.6 1.9 %collective-permute-done.1.outer_ref = f32[3,32,128]{2,1,0:T(8,128)S(1)} collective-permute-done((f32[3,32,128]{2,1,0:T(8,128)S(1)}, f32[3,32,128]{2,1,0:T(8,128)S(1)}, u32[]{:S(2)}, u32[]{:S(2)}) %collective-permute-start.1) | collective-permute-done | bytes 49184 | tf_op jit(solution)/shard_map/ppermute | solution.py:453
  9.4 1.6 %collective-permute-start.2 = (f32[3,32,128]{2,1,0:T(8,128)S(1)}, f32[3,32,128]{2,1,0:T(8,128)S(1)}, u32[]{:S(2)}, u32[]{:S(2)}) collective-permute-start(f32[3,32,128]{2,1,0:T(8,128)S(1)} %pad_maximum_fusion), channel_id=1, source_target_pairs={{0,8},{8,0},{16,24},{24,16},{1,9},{9,1},{17,25},{25,17},{2,10},{10... | collective-permute-start | bytes 147464 | tf_op jit(solution)/shard_map/ppermute | solution.py:497
  11.0 1.5 %shard_map.115 = (bf16[896,1024]{1,0:T(8,128)(2,1)S(1)}, bf16[768,1024]{1,0:T(8,128)(2,1)S(1)}) custom-call(s32[2,960]{1,0:T(2,128)} %bitcast.39), custom_call_target="tpu_custom_call" | custom-call | tf_op jit(solution)/shard_map/pallas_call | solution.py:410
  12.5 1.9 %shard_map.117 = (f32[32,1024]{1,0:T(8,128)S(1)}, f32[1,1024]{1,0:T(1,128)S(1)}, bf16[1024,384]{1,0:T(8,128)(2,1)S(1)}, bf16[1024,640]{1,0:T(8,128)(2,1)S(1)}, b...) custom-call(f32[30,1,960]{2,1,0:T(1,128)} %bitcast.35, s32[8,128]{1,0:T(8,128)} %bitcast.43, f32[1,960]{1,0:T(1,128)} %dual_hbm.1, ...), custom_call_target="tpu_custom_call" | custom-call | tf_op jit(solution)/shard_map/pallas_call | solution.py:410
  15.4 0.6 shard_map.119
  15.9 0.6 collective-permute-start.4
  16.7 3.2 %collective-permute-start.5 = (f32[3,32,128]{2,1,0:T(8,128)S(1)}, f32[3,32,128]{2,1,0:T(8,128)S(1)}, u32[]{:S(2)}, u32[]{:S(2)}) collective-permute-start(f32[3,32,128]{2,1,0:T(8,128)S(1)} %shard_map.120), channel_id=1, source_target_pairs={{0,7},{1,2},{2,1},{3,4},{4,3},{5,6},{6,5},{7,0},{8,15},{9,10},{10,... | collective-permute-start | bytes 147464 | tf_op jit(solution)/shard_map/ppermute | solution.py:453
  19.9 2.5 %collective-permute-done.5.outer_ref = f32[3,32,128]{2,1,0:T(8,128)S(1)} collective-permute-done((f32[3,32,128]{2,1,0:T(8,128)S(1)}, f32[3,32,128]{2,1,0:T(8,128)S(1)}, u32[]{:S(2)}, u32[]{:S(2)}) %collective-permute-start.5) | collective-permute-done | bytes 49184 | tf_op jit(solution)/shard_map/ppermute | solution.py:453
  22.4 2.7 %collective-permute-start.6 = (f32[3,32,128]{2,1,0:T(8,128)S(1)}, f32[3,32,128]{2,1,0:T(8,128)S(1)}, u32[]{:S(2)}, u32[]{:S(2)}) collective-permute-start(f32[3,32,128]{2,1,0:T(8,128)S(1)} %pad_maximum_fusion.2), channel_id=1, source_target_pairs={{0,8},{8,0},{16,24},{24,16},{1,9},{9,1},{17,25},{25,17},{2,10},{10... | collective-permute-start | bytes 147464 | tf_op jit(solution)/shard_map/ppermute | solution.py:497
  25.2 1.2 %shard_map.124 = (f32[1,640]{1,0:T(1,128)S(1)}, f32[256,128]{1,0:T(8,128)S(1)}, f32[256,128]{1,0:T(8,128)S(1)}, f32[256,128]{1,0:T(8,128)S(1)}, bf16[640,384]{1,...) custom-call(f32[30,1,640]{2,1,0:T(1,128)} %bitcast.37, s32[8,128]{1,0:T(8,128)S(1)} %get-tuple-element.59.list_ref, ...), custom_call_target="tpu_custom_call" | custom-call | tf_op jit(solution)/shard_map/pallas_call | solution.py:410
  26.4 2.4 %shard_map.121 = (bf16[1280,640]{1,0:T(8,128)(2,1)S(1)}, bf16[1280,640]{1,0:T(8,128)(2,1)S(1)}, bf16[768,640]{1,0:T(8,128)(2,1)S(1)}, bf16[768,640]{1,0:T(8,128)(2,1)S(1)}) custom-call(s32[3,1,640]{2,1,0:T(1,128)} %bitcast.40, f32[3,1,640]{2,1,0:T(1,128)} %bitcast.41), custom_call_target="tpu_custom_call" | custom-call | tf_op jit(solution)/shard_map/pallas_call | solution.py:410
  28.8 0.7 shard_map.122.total_ref
  29.8 0.7 shard_map.125
  30.8 0.6 collective-permute-start.8
  31.4 2.1 %collective-permute-start.9 = (f32[3,32,128]{2,1,0:T(8,128)S(1)}, f32[3,32,128]{2,1,0:T(8,128)S(1)}, u32[]{:S(2)}, u32[]{:S(2)}) collective-permute-start(f32[3,32,128]{2,1,0:T(8,128)S(1)} %get-tuple-element.91), channel_id=1, source_target_pairs={{0,7},{1,2},{2,1},{3,4},{4,3},{5,6},{6,5},{7,0},{8,15},{9,10},{10,... | collective-permute-start | bytes 147464 | tf_op jit(solution)/shard_map/ppermute | solution.py:453
  33.5 3.2 %collective-permute-done.9.outer_ref = f32[3,32,128]{2,1,0:T(8,128)S(1)} collective-permute-done((f32[3,32,128]{2,1,0:T(8,128)S(1)}, f32[3,32,128]{2,1,0:T(8,128)S(1)}, u32[]{:S(2)}, u32[]{:S(2)}) %collective-permute-start.9) | collective-permute-done | bytes 49184 | tf_op jit(solution)/shard_map/ppermute | solution.py:453
  36.8 0.5 collective-permute-start.11
  37.2 0.5 collective-permute-start.12
  37.7 0.7 collective-permute-done.10.early_ref
  38.4 0.5 shard_map.127.total_ref
  39.0 1.9 %collective-permute-done.11.lat_inner_ref = f32[3,32,128]{2,1,0:T(8,128)S(1)} collective-permute-done((f32[3,32,128]{2,1,0:T(8,128)S(1)}, f32[3,32,128]{2,1,0:T(8,128)S(1)}, u32[]{:S(2)}, u32[]{:S(2)}) %collective-permute-start.11) | collective-permute-done | bytes 49184 | tf_op jit(solution)/shard_map/ppermute | solution.py:497
  41.4 0.5 shard_map.129
  42.2 1.1 %collective-permute-start.14 = (f32[3,32,128]{2,1,0:T(8,128)S(1)}, f32[3,32,128]{2,1,0:T(8,128)S(1)}, u32[]{:S(2)}, u32[]{:S(2)}) collective-permute-start(f32[3,32,128]{2,1,0:T(8,128)S(1)} %shard_map.130), channel_id=1, source_target_pairs={{0,7},{1,2},{2,1},{3,4},{4,3},{5,6},{6,5},{7,0},{8,15},{9,10},{10,... | collective-permute-start | bytes 147464 | tf_op jit(solution)/shard_map/ppermute | solution.py:453
  43.2 4.3 %collective-permute-done.14.outer_ref = f32[3,32,128]{2,1,0:T(8,128)S(1)} collective-permute-done((f32[3,32,128]{2,1,0:T(8,128)S(1)}, f32[3,32,128]{2,1,0:T(8,128)S(1)}, u32[]{:S(2)}, u32[]{:S(2)}) %collective-permute-start.14) | collective-permute-done | bytes 49184 | tf_op jit(solution)/shard_map/ppermute | solution.py:453
  47.5 3.4 %collective-permute-start.16 = (f32[3,32,128]{2,1,0:T(8,128)S(1)}, f32[3,32,128]{2,1,0:T(8,128)S(1)}, u32[]{:S(2)}, u32[]{:S(2)}) collective-permute-start(f32[3,32,128]{2,1,0:T(8,128)S(1)} %pad_maximum_fusion.5), channel_id=1, source_target_pairs={{0,8},{8,0},{16,24},{24,16},{1,9},{9,1},{17,25},{25,17},{2,10},{10... | collective-permute-start | bytes 147464 | tf_op jit(solution)/shard_map/ppermute | solution.py:497
  50.9 0.5 collective-permute-start.17
  51.4 0.7 collective-permute-done.15.early_ref
  52.1 0.8 shard_map.131.total_ref
  53.4 0.6 shard_map.133
  54.4 0.7 collective-permute-start.19
  55.1 0.5 collective-permute-done.18.inner_ref
  55.6 4.2 %collective-permute-done.19.outer_ref = f32[3,32,128]{2,1,0:T(8,128)S(1)} collective-permute-done((f32[3,32,128]{2,1,0:T(8,128)S(1)}, f32[3,32,128]{2,1,0:T(8,128)S(1)}, u32[]{:S(2)}, u32[]{:S(2)}) %collective-permute-start.19) | collective-permute-done | bytes 49184 | tf_op jit(solution)/shard_map/ppermute | solution.py:453
  59.8 4.0 %collective-permute-start.21 = (f32[3,32,128]{2,1,0:T(8,128)S(1)}, f32[3,32,128]{2,1,0:T(8,128)S(1)}, u32[]{:S(2)}, u32[]{:S(2)}) collective-permute-start(f32[3,32,128]{2,1,0:T(8,128)S(1)} %pad_maximum_fusion.6), channel_id=1, source_target_pairs={{0,8},{8,0},{16,24},{24,16},{1,9},{9,1},{17,25},{25,17},{2,10},{10... | collective-permute-start | bytes 147464 | tf_op jit(solution)/shard_map/ppermute | solution.py:497
  63.8 0.5 collective-permute-start.22
  64.3 0.7 collective-permute-done.20.early_ref
  65.0 0.5 shard_map.135.total_ref
  66.5 0.5 shard_map.137
  67.3 1.0 %collective-permute-done.23.inner_ref = f32[3,32,128]{2,1,0:T(8,128)S(1)} collective-permute-done((f32[3,32,128]{2,1,0:T(8,128)S(1)}, f32[3,32,128]{2,1,0:T(8,128)S(1)}, u32[]{:S(2)}, u32[]{:S(2)}) %collective-permute-start.23) | collective-permute-done | bytes 49184 | tf_op jit(solution)/shard_map/ppermute | solution.py:470
  68.5 4.2 %collective-permute-done.24.outer_ref = f32[3,32,128]{2,1,0:T(8,128)S(1)} collective-permute-done((f32[3,32,128]{2,1,0:T(8,128)S(1)}, f32[3,32,128]{2,1,0:T(8,128)S(1)}, u32[]{:S(2)}, u32[]{:S(2)}) %collective-permute-start.24) | collective-permute-done | bytes 49184 | tf_op jit(solution)/shard_map/ppermute | solution.py:453
  72.7 5.0 %collective-permute-start.26 = (f32[3,32,128]{2,1,0:T(8,128)S(1)}, f32[3,32,128]{2,1,0:T(8,128)S(1)}, u32[]{:S(2)}, u32[]{:S(2)}) collective-permute-start(f32[3,32,128]{2,1,0:T(8,128)S(1)} %pad_maximum_fusion.7), channel_id=1, source_target_pairs={{0,8},{8,0},{16,24},{24,16},{1,9},{9,1},{17,25},{25,17},{2,10},{10... | collective-permute-start | bytes 147464 | tf_op jit(solution)/shard_map/ppermute | solution.py:497
  77.6 0.8 copy.12
  78.4 0.8 shard_map.139.total_ref
  79.2 0.7 collective-permute-done.26.lat_inner_ref
  80.2 1.0 %shard_map.141 = f32[30,1,640]{2,1,0:T(1,128)} custom-call(f32[32,640]{1,0:T(8,128)S(1)} %shard_map.140.total_ref, f32[1,32,128]{2,1,0:T(8,128)S(1)} %collective-permute-done.27.lat_outer_ref, bf16[768,640]{1,0:T(8,128)(2,1)S(1)} %get-tuple-element.79.rest_0_.high_ref.rest_2_, bf16[768,640]{1,0:T(8,128)(2,1)S(1)} %get-tuple-element.80.rest_1_.low_ref.rest_3_, ...), custom_call_target="tpu_custom_call" | custom-call | tf_op jit(solution)/shard_map/pallas_call | solution.py:410
  (63 shorter events, 5.2 us)
Async XLA Ops:
  2.3 5.3 %collective-permute-start = (f32[3,32,128]{2,1,0:T(8,128)S(1)}, f32[3,32,128]{2,1,0:T(8,128)S(1)}, u32[]{:S(2)}, u32[]{:S(2)}) collective-permute-start(f32[3,32,128]{2,1,0:T(8,128)S(1)} %get-tuple-element.60), channel_id=1, source_target_pairs={{0,1},{1,0},{2,3},{3,2},{4,5},{5,4},{6,7},{7,6},{8,9},{9,8},{10,11... | collective-permute-start | bytes 147464 | tf_op jit(solution)/shard_map/ppermute | solution.py:470
  2.9 6.6 %collective-permute-start.1 = (f32[3,32,128]{2,1,0:T(8,128)S(1)}, f32[3,32,128]{2,1,0:T(8,128)S(1)}, u32[]{:S(2)}, u32[]{:S(2)}) collective-permute-start(f32[3,32,128]{2,1,0:T(8,128)S(1)} %get-tuple-element.61), channel_id=1, source_target_pairs={{0,7},{1,2},{2,1},{3,4},{4,3},{5,6},{6,5},{7,0},{8,15},{9,10},{10,... | collective-permute-start | bytes 147464 | tf_op jit(solution)/shard_map/ppermute | solution.py:453
  9.4 5.4 %collective-permute-start.2 = (f32[3,32,128]{2,1,0:T(8,128)S(1)}, f32[3,32,128]{2,1,0:T(8,128)S(1)}, u32[]{:S(2)}, u32[]{:S(2)}) collective-permute-start(f32[3,32,128]{2,1,0:T(8,128)S(1)} %pad_maximum_fusion), channel_id=1, source_target_pairs={{0,8},{8,0},{16,24},{24,16},{1,9},{9,1},{17,25},{25,17},{2,10},{10... | collective-permute-start | bytes 147464 | tf_op jit(solution)/shard_map/ppermute | solution.py:497
  11.0 4.4 %collective-permute-start.3 = (f32[3,32,128]{2,1,0:T(8,128)S(1)}, f32[3,32,128]{2,1,0:T(8,128)S(1)}, u32[]{:S(2)}, u32[]{:S(2)}) collective-permute-start(f32[3,32,128]{2,1,0:T(8,128)S(1)} %pad_maximum_fusion.1), channel_id=1, source_target_pairs={{0,1},{1,0},{2,3},{3,2},{4,5},{5,4},{6,7},{7,6},{8,16},{9,17},{10,... | collective-permute-start | bytes 147464 | tf_op jit(solution)/shard_map/ppermute | solution.py:498
  15.9 4.0 %collective-permute-start.4 = (f32[3,32,128]{2,1,0:T(8,128)S(1)}, f32[3,32,128]{2,1,0:T(8,128)S(1)}, u32[]{:S(2)}, u32[]{:S(2)}) collective-permute-start(f32[3,32,128]{2,1,0:T(8,128)S(1)} %get-tuple-element.72), channel_id=1, source_target_pairs={{0,1},{1,0},{2,3},{3,2},{4,5},{5,4},{6,7},{7,6},{8,9},{9,8},{10,11... | collective-permute-start | bytes 147464 | tf_op jit(solution)/shard_map/ppermute | solution.py:470
  16.7 5.7 %collective-permute-start.5 = (f32[3,32,128]{2,1,0:T(8,128)S(1)}, f32[3,32,128]{2,1,0:T(8,128)S(1)}, u32[]{:S(2)}, u32[]{:S(2)}) collective-permute-start(f32[3,32,128]{2,1,0:T(8,128)S(1)} %shard_map.120), channel_id=1, source_target_pairs={{0,7},{1,2},{2,1},{3,4},{4,3},{5,6},{6,5},{7,0},{8,15},{9,10},{10,... | collective-permute-start | bytes 147464 | tf_op jit(solution)/shard_map/ppermute | solution.py:453
  22.4 7.0 %collective-permute-start.6 = (f32[3,32,128]{2,1,0:T(8,128)S(1)}, f32[3,32,128]{2,1,0:T(8,128)S(1)}, u32[]{:S(2)}, u32[]{:S(2)}) collective-permute-start(f32[3,32,128]{2,1,0:T(8,128)S(1)} %pad_maximum_fusion.2), channel_id=1, source_target_pairs={{0,8},{8,0},{16,24},{24,16},{1,9},{9,1},{17,25},{25,17},{2,10},{10... | collective-permute-start | bytes 147464 | tf_op jit(solution)/shard_map/ppermute | solution.py:497
  25.2 4.6 %collective-permute-start.7 = (f32[3,32,128]{2,1,0:T(8,128)S(1)}, f32[3,32,128]{2,1,0:T(8,128)S(1)}, u32[]{:S(2)}, u32[]{:S(2)}) collective-permute-start(f32[3,32,128]{2,1,0:T(8,128)S(1)} %pad_maximum_fusion.3), channel_id=1, source_target_pairs={{0,1},{1,0},{2,3},{3,2},{4,5},{5,4},{6,7},{7,6},{8,16},{9,17},{10,... | collective-permute-start | bytes 147464 | tf_op jit(solution)/shard_map/ppermute | solution.py:498
  30.8 2.7 %collective-permute-start.8 = (f32[3,32,128]{2,1,0:T(8,128)S(1)}, f32[3,32,128]{2,1,0:T(8,128)S(1)}, u32[]{:S(2)}, u32[]{:S(2)}) collective-permute-start(f32[3,32,128]{2,1,0:T(8,128)S(1)} %get-tuple-element.90), channel_id=1, source_target_pairs={{0,1},{1,0},{2,3},{3,2},{4,5},{5,4},{6,7},{7,6},{8,9},{9,8},{10,11... | collective-permute-start | bytes 147464 | tf_op jit(solution)/shard_map/ppermute | solution.py:470
  31.4 5.3 %collective-permute-start.9 = (f32[3,32,128]{2,1,0:T(8,128)S(1)}, f32[3,32,128]{2,1,0:T(8,128)S(1)}, u32[]{:S(2)}, u32[]{:S(2)}) collective-permute-start(f32[3,32,128]{2,1,0:T(8,128)S(1)} %get-tuple-element.91), channel_id=1, source_target_pairs={{0,7},{1,2},{2,1},{3,4},{4,3},{5,6},{6,5},{7,0},{8,15},{9,10},{10,... | collective-permute-start | bytes 147464 | tf_op jit(solution)/shard_map/ppermute | solution.py:453
  36.8 4.2 %collective-permute-start.11 = (f32[3,32,128]{2,1,0:T(8,128)S(1)}, f32[3,32,128]{2,1,0:T(8,128)S(1)}, u32[]{:S(2)}, u32[]{:S(2)}) collective-permute-start(f32[3,32,128]{2,1,0:T(8,128)S(1)} %pad_maximum_fusion.4), channel_id=1, source_target_pairs={{0,8},{8,0},{16,24},{24,16},{1,9},{9,1},{17,25},{25,17},{2,10},{10... | collective-permute-start | bytes 147464 | tf_op jit(solution)/shard_map/ppermute | solution.py:497
  37.2 1.2 %collective-permute-start.10 = (f32[2,32,128]{2,1,0:T(8,128)S(1)}, f32[2,32,128]{2,1,0:T(8,128)S(1)}, u32[]{:S(2)}, u32[]{:S(2)}) collective-permute-start(f32[2,32,128]{2,1,0:T(8,128)S(1)} %pad_maximum_fusion.8), channel_id=1, source_target_pairs={{0,1},{1,0},{2,3},{3,2},{4,5},{5,4},{6,7},{7,6},{8,16},{9,17},{10,... | collective-permute-start | bytes 98312 | tf_op jit(solution)/shard_map/ppermute | solution.py:493
  37.2 4.1 %collective-permute-start.12 = (f32[1,32,128]{2,1,0:T(8,128)S(1)}, f32[1,32,128]{2,1,0:T(8,128)S(1)}, u32[]{:S(2)}, u32[]{:S(2)}) collective-permute-start(f32[1,32,128]{2,1,0:T(8,128)S(1)} %get-tuple-element.126), channel_id=1, source_target_pairs={{0,1},{1,0},{2,3},{3,2},{4,5},{5,4},{6,7},{7,6},{8,16},{9,17},{10,... | collective-permute-start | bytes 49160 | tf_op jit(solution)/shard_map/ppermute | solution.py:498
  41.9 1.3 %collective-permute-start.13 = (f32[3,32,128]{2,1,0:T(8,128)S(1)}, f32[3,32,128]{2,1,0:T(8,128)S(1)}, u32[]{:S(2)}, u32[]{:S(2)}) collective-permute-start(f32[3,32,128]{2,1,0:T(8,128)S(1)} %get-tuple-element.96), channel_id=1, source_target_pairs={{0,1},{1,0},{2,3},{3,2},{4,5},{5,4},{6,7},{7,6},{8,9},{9,8},{10,11... | collective-permute-start | bytes 147464 | tf_op jit(solution)/shard_map/ppermute | solution.py:470
  42.2 5.4 %collective-permute-start.14 = (f32[3,32,128]{2,1,0:T(8,128)S(1)}, f32[3,32,128]{2,1,0:T(8,128)S(1)}, u32[]{:S(2)}, u32[]{:S(2)}) collective-permute-start(f32[3,32,128]{2,1,0:T(8,128)S(1)} %shard_map.130), channel_id=1, source_target_pairs={{0,7},{1,2},{2,1},{3,4},{4,3},{5,6},{6,5},{7,0},{8,15},{9,10},{10,... | collective-permute-start | bytes 147464 | tf_op jit(solution)/shard_map/ppermute | solution.py:453
  47.5 5.5 %collective-permute-start.16 = (f32[3,32,128]{2,1,0:T(8,128)S(1)}, f32[3,32,128]{2,1,0:T(8,128)S(1)}, u32[]{:S(2)}, u32[]{:S(2)}) collective-permute-start(f32[3,32,128]{2,1,0:T(8,128)S(1)} %pad_maximum_fusion.5), channel_id=1, source_target_pairs={{0,8},{8,0},{16,24},{24,16},{1,9},{9,1},{17,25},{25,17},{2,10},{10... | collective-permute-start | bytes 147464 | tf_op jit(solution)/shard_map/ppermute | solution.py:497
  50.9 1.2 %collective-permute-start.15 = (f32[2,32,128]{2,1,0:T(8,128)S(1)}, f32[2,32,128]{2,1,0:T(8,128)S(1)}, u32[]{:S(2)}, u32[]{:S(2)}) collective-permute-start(f32[2,32,128]{2,1,0:T(8,128)S(1)} %pad_maximum_fusion.9), channel_id=1, source_target_pairs={{0,1},{1,0},{2,3},{3,2},{4,5},{5,4},{6,7},{7,6},{8,16},{9,17},{10,... | collective-permute-start | bytes 98312 | tf_op jit(solution)/shard_map/ppermute | solution.py:493
  50.9 2.5 %collective-permute-start.17 = (f32[1,32,128]{2,1,0:T(8,128)S(1)}, f32[1,32,128]{2,1,0:T(8,128)S(1)}, u32[]{:S(2)}, u32[]{:S(2)}) collective-permute-start(f32[1,32,128]{2,1,0:T(8,128)S(1)} %get-tuple-element.122), channel_id=1, source_target_pairs={{0,1},{1,0},{2,3},{3,2},{4,5},{5,4},{6,7},{7,6},{8,16},{9,17},{10,... | collective-permute-start | bytes 49160 | tf_op jit(solution)/shard_map/ppermute | solution.py:498
  54.3 1.3 %collective-permute-start.18 = (f32[3,32,128]{2,1,0:T(8,128)S(1)}, f32[3,32,128]{2,1,0:T(8,128)S(1)}, u32[]{:S(2)}, u32[]{:S(2)}) collective-permute-start(f32[3,32,128]{2,1,0:T(8,128)S(1)} %get-tuple-element.102), channel_id=1, source_target_pairs={{0,1},{1,0},{2,3},{3,2},{4,5},{5,4},{6,7},{7,6},{8,9},{9,8},{10,11... | collective-permute-start | bytes 147464 | tf_op jit(solution)/shard_map/ppermute | solution.py:470
  54.4 5.3 %collective-permute-start.19 = (f32[3,32,128]{2,1,0:T(8,128)S(1)}, f32[3,32,128]{2,1,0:T(8,128)S(1)}, u32[]{:S(2)}, u32[]{:S(2)}) collective-permute-start(f32[3,32,128]{2,1,0:T(8,128)S(1)} %get-tuple-element.103), channel_id=1, source_target_pairs={{0,7},{1,2},{2,1},{3,4},{4,3},{5,6},{6,5},{7,0},{8,15},{9,10},{10,... | collective-permute-start | bytes 147464 | tf_op jit(solution)/shard_map/ppermute | solution.py:453
  59.8 6.2 %collective-permute-start.21 = (f32[3,32,128]{2,1,0:T(8,128)S(1)}, f32[3,32,128]{2,1,0:T(8,128)S(1)}, u32[]{:S(2)}, u32[]{:S(2)}) collective-permute-start(f32[3,32,128]{2,1,0:T(8,128)S(1)} %pad_maximum_fusion.6), channel_id=1, source_target_pairs={{0,8},{8,0},{16,24},{24,16},{1,9},{9,1},{17,25},{25,17},{2,10},{10... | collective-permute-start | bytes 147464 | tf_op jit(solution)/shard_map/ppermute | solution.py:497
  63.8 1.2 %collective-permute-start.20 = (f32[2,32,128]{2,1,0:T(8,128)S(1)}, f32[2,32,128]{2,1,0:T(8,128)S(1)}, u32[]{:S(2)}, u32[]{:S(2)}) collective-permute-start(f32[2,32,128]{2,1,0:T(8,128)S(1)} %pad_maximum_fusion.10), channel_id=1, source_target_pairs={{0,1},{1,0},{2,3},{3,2},{4,5},{5,4},{6,7},{7,6},{8,16},{9,17},{10,... | collective-permute-start | bytes 98312 | tf_op jit(solution)/shard_map/ppermute | solution.py:493
  63.8 2.7 %collective-permute-start.22 = (f32[1,32,128]{2,1,0:T(8,128)S(1)}, f32[1,32,128]{2,1,0:T(8,128)S(1)}, u32[]{:S(2)}, u32[]{:S(2)}) collective-permute-start(f32[1,32,128]{2,1,0:T(8,128)S(1)} %get-tuple-element.118), channel_id=1, source_target_pairs={{0,1},{1,0},{2,3},{3,2},{4,5},{5,4},{6,7},{7,6},{8,16},{9,17},{10,... | collective-permute-start | bytes 49160 | tf_op jit(solution)/shard_map/ppermute | solution.py:498
  67.0 1.3 %collective-permute-start.23 = (f32[3,32,128]{2,1,0:T(8,128)S(1)}, f32[3,32,128]{2,1,0:T(8,128)S(1)}, u32[]{:S(2)}, u32[]{:S(2)}) collective-permute-start(f32[3,32,128]{2,1,0:T(8,128)S(1)} %get-tuple-element.108), channel_id=1, source_target_pairs={{0,1},{1,0},{2,3},{3,2},{4,5},{5,4},{6,7},{7,6},{8,9},{9,8},{10,11... | collective-permute-start | bytes 147464 | tf_op jit(solution)/shard_map/ppermute | solution.py:470
  67.3 5.4 %collective-permute-start.24 = (f32[3,32,128]{2,1,0:T(8,128)S(1)}, f32[3,32,128]{2,1,0:T(8,128)S(1)}, u32[]{:S(2)}, u32[]{:S(2)}) collective-permute-start(f32[3,32,128]{2,1,0:T(8,128)S(1)} %shard_map.138), channel_id=1, source_target_pairs={{0,7},{1,2},{2,1},{3,4},{4,3},{5,6},{6,5},{7,0},{8,15},{9,10},{10,... | collective-permute-start | bytes 147464 | tf_op jit(solution)/shard_map/ppermute | solution.py:453
  68.3 10.1 %collective-permute-start.25 = (f32[2,32,128]{2,1,0:T(8,128)S(1)}, f32[2,32,128]{2,1,0:T(8,128)S(1)}, u32[]{:S(2)}, u32[]{:S(2)}) collective-permute-start(f32[2,32,128]{2,1,0:T(8,128)S(1)} %pad_maximum_fusion.11), channel_id=1, source_target_pairs={{0,1},{1,0},{2,3},{3,2},{4,5},{5,4},{6,7},{7,6},{8,16},{9,17},{10,... | collective-permute-start | bytes 98312 | tf_op jit(solution)/shard_map/ppermute | solution.py:493
  72.7 7.6 %collective-permute-start.27 = (f32[1,32,128]{2,1,0:T(8,128)S(1)}, f32[1,32,128]{2,1,0:T(8,128)S(1)}, u32[]{:S(2)}, u32[]{:S(2)}) collective-permute-start(f32[1,32,128]{2,1,0:T(8,128)S(1)} %get-tuple-element.114), channel_id=1, source_target_pairs={{0,1},{1,0},{2,3},{3,2},{4,5},{5,4},{6,7},{7,6},{8,16},{9,17},{10,... | collective-permute-start | bytes 49160 | tf_op jit(solution)/shard_map/ppermute | solution.py:498
  72.7 7.2 %collective-permute-start.26 = (f32[3,32,128]{2,1,0:T(8,128)S(1)}, f32[3,32,128]{2,1,0:T(8,128)S(1)}, u32[]{:S(2)}, u32[]{:S(2)}) collective-permute-start(f32[3,32,128]{2,1,0:T(8,128)S(1)} %pad_maximum_fusion.7), channel_id=1, source_target_pairs={{0,8},{8,0},{16,24},{24,16},{1,9},{9,1},{17,25},{25,17},{2,10},{10... | collective-permute-start | bytes 147464 | tf_op jit(solution)/shard_map/ppermute | solution.py:497

commit v10 on v9

--- a/solution.py
+++ b/solution.py
@@ -220,11 +220,24 @@
     sent_scale_ref[...] = gather_matmul(stack_ref, [outer_matrix_ref[...]], rows)[0:1]
 
 
-def weight_kernel(
-    sides_hbm, weight_hbm, near_high_ref, near_low_ref, far_high_ref, far_low_ref, sides_ref, weight_ref, sems, *, edges, edge_pad, halo, lat_count
-):
+def fill_weights(high_ref, low_ref, place, weight, base):
+    high = [value.astype(bf16) for value in weight]
+    low = [(value - top.astype(f32)).astype(bf16) for value, top in zip(weight, high)]
+    place = [value.astype(i16) for value in place]
+    zero = jnp.zeros((), bf16)
+
+    def body(first, block):
+        row = row_numbers(first + base, block, high_ref.shape[1])
+        hits = [row == value for value in place]
+        for target, values in ((high_ref, high), (low_ref, low)):
+            entry = jnp.where(hits[0], values[0], jnp.where(hits[1], values[1], jnp.where(hits[2], values[2], zero)))
+            target[pl.ds(first, block), :] = entry
+
+    by_blocks(high_ref.shape[0], body)
+
+
+def weight_kernel(sides_hbm, weight_hbm, high_ref, low_ref, place_ref, merged_ref, sides_ref, weight_ref, sems, *, edges, edge_pad, halo, lat_count):
     fetch([(sides_hbm, sides_ref), (weight_hbm, weight_ref)], sems)
-    cells = sides_ref.shape[2]
     place = [local_positions(sides_ref[i], edges, edge_pad, halo, lat_count) for i in range(3)]
     weight = [weight_ref[i] for i in range(3)]
     for later in (1, 2):
@@ -233,23 +246,14 @@
             weight[earlier] = weight[earlier] + jnp.where(same, weight[later], 0.0)
             weight[later] = jnp.where(same, 0.0, weight[later])
             place[later] = jnp.where(same, -1, place[later])
-    high = [value.astype(bf16) for value in weight]
-    low = [(value - top.astype(f32)).astype(bf16) for value, top in zip(weight, high)]
-    place = [value.astype(i16) for value in place]
-    zero = jnp.zeros((), bf16)
-
-    def fill_rows(high_ref, low_ref, base):
-        def body(first, block):
-            row = row_numbers(first + base, block, cells)
-            hits = [row == value for value in place]
-            for target, values in ((high_ref, high), (low_ref, low)):
-                entry = jnp.where(hits[0], values[0], jnp.where(hits[1], values[1], jnp.where(hits[2], values[2], zero)))
-                target[pl.ds(first, block), :] = entry
-
-        by_blocks(high_ref.shape[0], body)
-
-    fill_rows(near_high_ref, near_low_ref, 0)
-    fill_rows(far_high_ref, far_low_ref, near_high_ref.shape[0])
+    for i in range(3):
+        place_ref[i] = place[i]
+        merged_ref[i] = weight[i]
+    fill_weights(high_ref, low_ref, place, weight, 0)
+
+
+def far_weight_kernel(place_ref, merged_ref, high_ref, low_ref, *, base):
+    fill_weights(high_ref, low_ref, [place_ref[i] for i in range(3)], [merged_ref[i] for i in range(3)], base)
 
 
 def cell_setup_kernel(
@@ -478,14 +482,21 @@
                 copies=1,
             )
         if phase == 1:
-            near_high, near_low, far_high, far_low = call(
+            near_high, near_low, place, merged = call(
                 functools.partial(weight_kernel, edges=edges, edge_pad=edge_pad, halo=halo, lat_count=lat_count),
-                [((edge_pad + 2 * halo, cells), bf16)] * 2 + [((6 * halo, cells), bf16)] * 2,
+                [((edge_pad + 2 * halo, cells), bf16)] * 2 + [((3, 1, cells), i32), ((3, 1, cells), f32)],
                 [((3, 1, cells), i32), ((3, 1, cells), f32)],
                 by_level(cell_edges),
                 by_level(edge_weight),
                 raw=(0, 1),
                 copies=2,
+            )
+            far_high, far_low = call(
+                functools.partial(far_weight_kernel, base=edge_pad + 2 * halo),
+                [((6 * halo, cells), bf16)] * 2,
+                [],
+                place,
+                merged,
             )
         early = phase >= 2
         first = jnp.stack([inner_in[1], lat_inner, outer_in[1]])

time: 81.6 us -> 78.4 us (0.961)
  starting transfers between devices: 32.6 us -> 29.9 us
    ppermute x6, starting transfers between devices: 1.98 us -> 0.97 us  [on_device(): inner_in = lax.ppermute(inner, 'lon', lon_routes[0])]
    ppermute x6, starting transfers between devices: 17.1 us -> 16.2 us  [on_device(): first_in = lax.ppermute(first, 'lat', lat_inner_route)]
    pallas_call x29 -> x30, Pallas kernels: 19.9 us -> 20 us  [call(): pl.pallas_call(body, out_shape=tuple((jax.ShapeDtypeStruct(shape, kind) f...]
  transfers between devices with their start and end apart: 28 -> 28, of which waited for: 15 -> 15; matrix products, arithmetic and copies ran while one was open for 1% -> 1% of each run, Pallas kernels for 17% -> 19%
where the time goes in v10:
time: 78.4 us; the launch traced here: 78 us
  starting transfers between devices  29.9 us (38%)
  waiting for transfers between devices  26.3 us (34%)
  Pallas kernels  20 us (26%)
  between operations  0.93 us (1%)
  local copies, waits for them, and re-layouts  0.82 us (1%)
    pallas_call x30, Pallas kernels, call(): pl.pallas_call(body, out_shape=tuple((jax.ShapeDtypeStruct(shape, kind) f...  20 us
    ppermute x6, waiting for transfers between devices, on_device(): outer_in = lax.ppermute(outer, 'lon', lon_routes[1])  19.6 us
    ppermute x6, starting transfers between devices, on_device(): first_in = lax.ppermute(first, 'lat', lat_inner_route)  16.2 us
    ppermute x6, starting transfers between devices, on_device(): outer_in = lax.ppermute(outer, 'lon', lon_routes[1])  11 us
    ppermute x6, waiting for transfers between devices, on_device(): first_in = lax.ppermute(first, 'lat', lat_inner_route)  3.08 us
    ppermute x4, waiting for transfers between devices, on_device(): lax.ppermute(jnp.stack([inner_in[2], lat_outer]), ('lat', 'lon'), lat_out...  2.09 us
  transfers between devices with their start and end apart: 28, of which 15 were waited for; matrix products, arithmetic and copies ran while one was open for 1% of the time, Pallas kernels for 19%

profile of v10, /device:TPU:0, one launch (start us, length us, event | category | flops | bytes accessed | tf_op | source)
XLA Modules:
  0.0 78.0 jit_solution(13285944150519806538)
XLA Ops:
  0.6 1.2 %shard_map.113 = (f32[32,640]{1,0:T(8,128)S(1)}, bf16[96,640]{1,0:T(8,128)(2,1)S(1)}, f32[3,32,128]{2,1,0:T(8,128)S(1)}, s32[8,128]{1,0:T(8,128)S(1)}) custom-call(f32[30,1,640]{2,1,0:T(1,128)} %bitcast.36, s32[8,128]{1,0:T(8,128)} %bitcast.42), custom_call_target="tpu_custom_call" | custom-call | tf_op jit(solution)/shard_map/pallas_call | solution.py:414
  1.8 4.6 %collective-permute-start.1 = (f32[3,32,128]{2,1,0:T(8,128)S(1)}, f32[3,32,128]{2,1,0:T(8,128)S(1)}, u32[]{:S(2)}, u32[]{:S(2)}) collective-permute-start(f32[3,32,128]{2,1,0:T(8,128)S(1)} %get-tuple-element.63), channel_id=1, source_target_pairs={{0,7},{1,2},{2,1},{3,4},{4,3},{5,6},{6,5},{7,0},{8,15},{9,10},{10,... | collective-permute-start | bytes 147464 | tf_op jit(solution)/shard_map/ppermute | solution.py:457
  6.4 0.5 shard_map.114
  6.9 1.3 %collective-permute-done.1.outer_ref = f32[3,32,128]{2,1,0:T(8,128)S(1)} collective-permute-done((f32[3,32,128]{2,1,0:T(8,128)S(1)}, f32[3,32,128]{2,1,0:T(8,128)S(1)}, u32[]{:S(2)}, u32[]{:S(2)}) %collective-permute-start.1) | collective-permute-done | bytes 49184 | tf_op jit(solution)/shard_map/ppermute | solution.py:457
  8.3 2.1 %collective-permute-start.2 = (f32[3,32,128]{2,1,0:T(8,128)S(1)}, f32[3,32,128]{2,1,0:T(8,128)S(1)}, u32[]{:S(2)}, u32[]{:S(2)}) collective-permute-start(f32[3,32,128]{2,1,0:T(8,128)S(1)} %pad_maximum_fusion), channel_id=1, source_target_pairs={{0,8},{8,0},{16,24},{24,16},{1,9},{9,1},{17,25},{25,17},{2,10},{10... | collective-permute-start | bytes 147464 | tf_op jit(solution)/shard_map/ppermute | solution.py:508
  10.4 1.5 %shard_map.115 = (bf16[896,1024]{1,0:T(8,128)(2,1)S(1)}, bf16[768,1024]{1,0:T(8,128)(2,1)S(1)}) custom-call(s32[2,960]{1,0:T(2,128)} %bitcast.39), custom_call_target="tpu_custom_call" | custom-call | tf_op jit(solution)/shard_map/pallas_call | solution.py:414
  11.9 1.9 %shard_map.117 = (f32[32,1024]{1,0:T(8,128)S(1)}, f32[1,1024]{1,0:T(1,128)S(1)}, bf16[1024,384]{1,0:T(8,128)(2,1)S(1)}, bf16[1024,640]{1,0:T(8,128)(2,1)S(1)}, b...) custom-call(f32[30,1,960]{2,1,0:T(1,128)} %bitcast.35, s32[8,128]{1,0:T(8,128)} %bitcast.43, f32[1,960]{1,0:T(1,128)} %dual_hbm.1, ...), custom_call_target="tpu_custom_call" | custom-call | tf_op jit(solution)/shard_map/pallas_call | solution.py:414
  14.3 0.5 shard_map.118
  15.0 2.7 %collective-permute-start.5 = (f32[3,32,128]{2,1,0:T(8,128)S(1)}, f32[3,32,128]{2,1,0:T(8,128)S(1)}, u32[]{:S(2)}, u32[]{:S(2)}) collective-permute-start(f32[3,32,128]{2,1,0:T(8,128)S(1)} %shard_map.120), channel_id=1, source_target_pairs={{0,7},{1,2},{2,1},{3,4},{4,3},{5,6},{6,5},{7,0},{8,15},{9,10},{10,... | collective-permute-start | bytes 147464 | tf_op jit(solution)/shard_map/ppermute | solution.py:457
  17.6 0.6 shard_map.119
  18.3 2.3 %collective-permute-done.5.outer_ref = f32[3,32,128]{2,1,0:T(8,128)S(1)} collective-permute-done((f32[3,32,128]{2,1,0:T(8,128)S(1)}, f32[3,32,128]{2,1,0:T(8,128)S(1)}, u32[]{:S(2)}, u32[]{:S(2)}) %collective-permute-start.5) | collective-permute-done | bytes 49184 | tf_op jit(solution)/shard_map/ppermute | solution.py:457
  20.6 2.8 %collective-permute-start.6 = (f32[3,32,128]{2,1,0:T(8,128)S(1)}, f32[3,32,128]{2,1,0:T(8,128)S(1)}, u32[]{:S(2)}, u32[]{:S(2)}) collective-permute-start(f32[3,32,128]{2,1,0:T(8,128)S(1)} %pad_maximum_fusion.2), channel_id=1, source_target_pairs={{0,8},{8,0},{16,24},{24,16},{1,9},{9,1},{17,25},{25,17},{2,10},{10... | collective-permute-start | bytes 147464 | tf_op jit(solution)/shard_map/ppermute | solution.py:508
  23.4 1.9 %shard_map.121 = (bf16[1280,640]{1,0:T(8,128)(2,1)S(1)}, bf16[1280,640]{1,0:T(8,128)(2,1)S(1)}, s32[3,1,640]{2,1,0:T(1,128)S(1)}, f32[3,1,640]{2,1,0:T(1,128)S(1)}) custom-call(s32[3,1,640]{2,1,0:T(1,128)} %bitcast.40, f32[3,1,640]{2,1,0:T(1,128)} %bitcast.41), custom_call_target="tpu_custom_call" | custom-call | tf_op jit(solution)/shard_map/pallas_call | solution.py:414
  25.3 0.7 shard_map.123
  26.0 1.2 %shard_map.125 = (f32[1,640]{1,0:T(1,128)S(1)}, f32[256,128]{1,0:T(8,128)S(1)}, f32[256,128]{1,0:T(8,128)S(1)}, f32[256,128]{1,0:T(8,128)S(1)}, bf16[640,384]{1,...) custom-call(f32[30,1,640]{2,1,0:T(1,128)} %bitcast.37, s32[8,128]{1,0:T(8,128)S(1)} %get-tuple-element.61.list_ref, ...), custom_call_target="tpu_custom_call" | custom-call | tf_op jit(solution)/shard_map/pallas_call | solution.py:414
  27.2 0.7 shard_map.122.total_ref
  28.2 0.7 shard_map.126
  29.3 0.6 collective-permute-start.8
  29.8 2.0 %collective-permute-start.9 = (f32[3,32,128]{2,1,0:T(8,128)S(1)}, f32[3,32,128]{2,1,0:T(8,128)S(1)}, u32[]{:S(2)}, u32[]{:S(2)}) collective-permute-start(f32[3,32,128]{2,1,0:T(8,128)S(1)} %get-tuple-element.95), channel_id=1, source_target_pairs={{0,7},{1,2},{2,1},{3,4},{4,3},{5,6},{6,5},{7,0},{8,15},{9,10},{10,... | collective-permute-start | bytes 147464 | tf_op jit(solution)/shard_map/ppermute | solution.py:457
  31.9 3.3 %collective-permute-done.9.outer_ref = f32[3,32,128]{2,1,0:T(8,128)S(1)} collective-permute-done((f32[3,32,128]{2,1,0:T(8,128)S(1)}, f32[3,32,128]{2,1,0:T(8,128)S(1)}, u32[]{:S(2)}, u32[]{:S(2)}) %collective-permute-start.9) | collective-permute-done | bytes 49184 | tf_op jit(solution)/shard_map/ppermute | solution.py:457
  35.6 0.5 collective-permute-start.12
  36.1 0.7 collective-permute-done.10.early_ref
  36.8 0.5 shard_map.128.total_ref
  37.3 2.0 %collective-permute-done.11.lat_inner_ref = f32[3,32,128]{2,1,0:T(8,128)S(1)} collective-permute-done((f32[3,32,128]{2,1,0:T(8,128)S(1)}, f32[3,32,128]{2,1,0:T(8,128)S(1)}, u32[]{:S(2)}, u32[]{:S(2)}) %collective-permute-start.11) | collective-permute-done | bytes 49184 | tf_op jit(solution)/shard_map/ppermute | solution.py:508
  39.8 0.5 shard_map.130
  40.6 1.0 %collective-permute-start.14 = (f32[3,32,128]{2,1,0:T(8,128)S(1)}, f32[3,32,128]{2,1,0:T(8,128)S(1)}, u32[]{:S(2)}, u32[]{:S(2)}) collective-permute-start(f32[3,32,128]{2,1,0:T(8,128)S(1)} %shard_map.131), channel_id=1, source_target_pairs={{0,7},{1,2},{2,1},{3,4},{4,3},{5,6},{6,5},{7,0},{8,15},{9,10},{10,... | collective-permute-start | bytes 147464 | tf_op jit(solution)/shard_map/ppermute | solution.py:457
  41.6 4.3 %collective-permute-done.14.outer_ref = f32[3,32,128]{2,1,0:T(8,128)S(1)} collective-permute-done((f32[3,32,128]{2,1,0:T(8,128)S(1)}, f32[3,32,128]{2,1,0:T(8,128)S(1)}, u32[]{:S(2)}, u32[]{:S(2)}) %collective-permute-start.14) | collective-permute-done | bytes 49184 | tf_op jit(solution)/shard_map/ppermute | solution.py:457
  45.9 3.4 %collective-permute-start.16 = (f32[3,32,128]{2,1,0:T(8,128)S(1)}, f32[3,32,128]{2,1,0:T(8,128)S(1)}, u32[]{:S(2)}, u32[]{:S(2)}) collective-permute-start(f32[3,32,128]{2,1,0:T(8,128)S(1)} %pad_maximum_fusion.5), channel_id=1, source_target_pairs={{0,8},{8,0},{16,24},{24,16},{1,9},{9,1},{17,25},{25,17},{2,10},{10... | collective-permute-start | bytes 147464 | tf_op jit(solution)/shard_map/ppermute | solution.py:508
  49.3 0.5 collective-permute-start.17
  49.8 0.7 collective-permute-done.15.early_ref
  50.5 0.8 %shard_map.132.total_ref = f32[32,640]{1,0:T(8,128)S(1)} custom-call(f32[32,1024]{1,0:T(8,128)S(1)} %get-tuple-element.99.own_ref.edges_ref, f32[3,32,128]{2,1,0:T(8,128)S(1)} %collective-permute-done.13.inner_ref, f32[3,32,128]{2,1,0:T(8,128)S(1)} %collective-permute-done.14.outer_ref, f32[2,32,128]{2,1,0:T(8,128)S(1)} %collective-permute-done.15.early_ref, ...), custom_call_target="tpu_custom_call" | custom-call | tf_op jit(solution)/shard_map/pallas_call | solution.py:414
  51.8 0.6 shard_map.134
  52.8 0.6 collective-permute-start.19
  53.5 0.6 collective-permute-done.18.inner_ref
  54.0 4.2 %collective-permute-done.19.outer_ref = f32[3,32,128]{2,1,0:T(8,128)S(1)} collective-permute-done((f32[3,32,128]{2,1,0:T(8,128)S(1)}, f32[3,32,128]{2,1,0:T(8,128)S(1)}, u32[]{:S(2)}, u32[]{:S(2)}) %collective-permute-start.19) | collective-permute-done | bytes 49184 | tf_op jit(solution)/shard_map/ppermute | solution.py:457
  58.2 4.0 %collective-permute-start.21 = (f32[3,32,128]{2,1,0:T(8,128)S(1)}, f32[3,32,128]{2,1,0:T(8,128)S(1)}, u32[]{:S(2)}, u32[]{:S(2)}) collective-permute-start(f32[3,32,128]{2,1,0:T(8,128)S(1)} %pad_maximum_fusion.6), channel_id=1, source_target_pairs={{0,8},{8,0},{16,24},{24,16},{1,9},{9,1},{17,25},{25,17},{2,10},{10... | collective-permute-start | bytes 147464 | tf_op jit(solution)/shard_map/ppermute | solution.py:508
  62.2 0.5 collective-permute-start.22
  62.7 0.7 collective-permute-done.20.early_ref
  63.4 0.5 shard_map.136.total_ref
  64.0 0.5 collective-permute-done.21.lat_inner_ref
  64.9 0.5 shard_map.138
  65.8 1.0 %collective-permute-done.23.inner_ref = f32[3,32,128]{2,1,0:T(8,128)S(1)} collective-permute-done((f32[3,32,128]{2,1,0:T(8,128)S(1)}, f32[3,32,128]{2,1,0:T(8,128)S(1)}, u32[]{:S(2)}, u32[]{:S(2)}) %collective-permute-start.23) | collective-permute-done | bytes 49184 | tf_op jit(solution)/shard_map/ppermute | solution.py:474
  66.9 4.2 %collective-permute-done.24.outer_ref = f32[3,32,128]{2,1,0:T(8,128)S(1)} collective-permute-done((f32[3,32,128]{2,1,0:T(8,128)S(1)}, f32[3,32,128]{2,1,0:T(8,128)S(1)}, u32[]{:S(2)}, u32[]{:S(2)}) %collective-permute-start.24) | collective-permute-done | bytes 49184 | tf_op jit(solution)/shard_map/ppermute | solution.py:457
  71.1 3.4 %collective-permute-start.26 = (f32[3,32,128]{2,1,0:T(8,128)S(1)}, f32[3,32,128]{2,1,0:T(8,128)S(1)}, u32[]{:S(2)}, u32[]{:S(2)}) collective-permute-start(f32[3,32,128]{2,1,0:T(8,128)S(1)} %pad_maximum_fusion.7), channel_id=1, source_target_pairs={{0,8},{8,0},{16,24},{24,16},{1,9},{9,1},{17,25},{25,17},{2,10},{10... | collective-permute-start | bytes 147464 | tf_op jit(solution)/shard_map/ppermute | solution.py:508
  74.5 0.8 copy.12
  75.3 0.8 %shard_map.140.total_ref = f32[32,640]{1,0:T(8,128)S(1)} custom-call(f32[32,1024]{1,0:T(8,128)S(1)} %get-tuple-element.111.own_ref, f32[3,32,128]{2,1,0:T(8,128)S(1)} %collective-permute-done.23.inner_ref, f32[3,32,128]{2,1,0:T(8,128)S(1)} %collective-permute-done.24.outer_ref, f32[2,32,128]{2,1,0:T(8,128)S(1)} %collective-permute-done.25.early_ref, ...), custom_call_target="tpu_custom_call" | custom-call | tf_op jit(solution)/shard_map/pallas_call | solution.py:414
  76.1 0.5 collective-permute-done.26.lat_inner_ref
  76.9 1.0 %shard_map.142 = f32[30,1,640]{2,1,0:T(1,128)} custom-call(f32[32,640]{1,0:T(8,128)S(1)} %shard_map.141.total_ref, f32[1,32,128]{2,1,0:T(8,128)S(1)} %collective-permute-done.27.lat_outer_ref, bf16[768,640]{1,0:T(8,128)(2,1)S(1)} %get-tuple-element.83.rest_0_.high_ref.rest_2_, bf16[768,640]{1,0:T(8,128)(2,1)S(1)} %get-tuple-element.84.rest_1_.low_ref.rest_3_, ...), custom_call_target="tpu_custom_call" | custom-call | tf_op jit(solution)/shard_map/pallas_call | solution.py:414
  (64 shorter events, 4.9 us)
Async XLA Ops:
  1.8 6.5 %collective-permute-start.1 = (f32[3,32,128]{2,1,0:T(8,128)S(1)}, f32[3,32,128]{2,1,0:T(8,128)S(1)}, u32[]{:S(2)}, u32[]{:S(2)}) collective-permute-start(f32[3,32,128]{2,1,0:T(8,128)S(1)} %get-tuple-element.63), channel_id=1, source_target_pairs={{0,7},{1,2},{2,1},{3,4},{4,3},{5,6},{6,5},{7,0},{8,15},{9,10},{10,... | collective-permute-start | bytes 147464 | tf_op jit(solution)/shard_map/ppermute | solution.py:457
  6.9 1.4 %collective-permute-start = (f32[3,32,128]{2,1,0:T(8,128)S(1)}, f32[3,32,128]{2,1,0:T(8,128)S(1)}, u32[]{:S(2)}, u32[]{:S(2)}) collective-permute-start(f32[3,32,128]{2,1,0:T(8,128)S(1)} %get-tuple-element.62), channel_id=1, source_target_pairs={{0,1},{1,0},{2,3},{3,2},{4,5},{5,4},{6,7},{7,6},{8,9},{9,8},{10,11... | collective-permute-start | bytes 147464 | tf_op jit(solution)/shard_map/ppermute | solution.py:474
  8.3 6.0 %collective-permute-start.2 = (f32[3,32,128]{2,1,0:T(8,128)S(1)}, f32[3,32,128]{2,1,0:T(8,128)S(1)}, u32[]{:S(2)}, u32[]{:S(2)}) collective-permute-start(f32[3,32,128]{2,1,0:T(8,128)S(1)} %pad_maximum_fusion), channel_id=1, source_target_pairs={{0,8},{8,0},{16,24},{24,16},{1,9},{9,1},{17,25},{25,17},{2,10},{10... | collective-permute-start | bytes 147464 | tf_op jit(solution)/shard_map/ppermute | solution.py:508
  10.4 4.4 %collective-permute-start.3 = (f32[3,32,128]{2,1,0:T(8,128)S(1)}, f32[3,32,128]{2,1,0:T(8,128)S(1)}, u32[]{:S(2)}, u32[]{:S(2)}) collective-permute-start(f32[3,32,128]{2,1,0:T(8,128)S(1)} %pad_maximum_fusion.1), channel_id=1, source_target_pairs={{0,1},{1,0},{2,3},{3,2},{4,5},{5,4},{6,7},{7,6},{8,16},{9,17},{10,... | collective-permute-start | bytes 147464 | tf_op jit(solution)/shard_map/ppermute | solution.py:509
  15.0 5.6 %collective-permute-start.5 = (f32[3,32,128]{2,1,0:T(8,128)S(1)}, f32[3,32,128]{2,1,0:T(8,128)S(1)}, u32[]{:S(2)}, u32[]{:S(2)}) collective-permute-start(f32[3,32,128]{2,1,0:T(8,128)S(1)} %shard_map.120), channel_id=1, source_target_pairs={{0,7},{1,2},{2,1},{3,4},{4,3},{5,6},{6,5},{7,0},{8,15},{9,10},{10,... | collective-permute-start | bytes 147464 | tf_op jit(solution)/shard_map/ppermute | solution.py:457
  18.2 2.4 %collective-permute-start.4 = (f32[3,32,128]{2,1,0:T(8,128)S(1)}, f32[3,32,128]{2,1,0:T(8,128)S(1)}, u32[]{:S(2)}, u32[]{:S(2)}) collective-permute-start(f32[3,32,128]{2,1,0:T(8,128)S(1)} %get-tuple-element.74), channel_id=1, source_target_pairs={{0,1},{1,0},{2,3},{3,2},{4,5},{5,4},{6,7},{7,6},{8,9},{9,8},{10,11... | collective-permute-start | bytes 147464 | tf_op jit(solution)/shard_map/ppermute | solution.py:474
  20.6 7.2 %collective-permute-start.6 = (f32[3,32,128]{2,1,0:T(8,128)S(1)}, f32[3,32,128]{2,1,0:T(8,128)S(1)}, u32[]{:S(2)}, u32[]{:S(2)}) collective-permute-start(f32[3,32,128]{2,1,0:T(8,128)S(1)} %pad_maximum_fusion.2), channel_id=1, source_target_pairs={{0,8},{8,0},{16,24},{24,16},{1,9},{9,1},{17,25},{25,17},{2,10},{10... | collective-permute-start | bytes 147464 | tf_op jit(solution)/shard_map/ppermute | solution.py:508
  23.4 4.8 %collective-permute-start.7 = (f32[3,32,128]{2,1,0:T(8,128)S(1)}, f32[3,32,128]{2,1,0:T(8,128)S(1)}, u32[]{:S(2)}, u32[]{:S(2)}) collective-permute-start(f32[3,32,128]{2,1,0:T(8,128)S(1)} %pad_maximum_fusion.3), channel_id=1, source_target_pairs={{0,1},{1,0},{2,3},{3,2},{4,5},{5,4},{6,7},{7,6},{8,16},{9,17},{10,... | collective-permute-start | bytes 147464 | tf_op jit(solution)/shard_map/ppermute | solution.py:509
  29.3 2.6 %collective-permute-start.8 = (f32[3,32,128]{2,1,0:T(8,128)S(1)}, f32[3,32,128]{2,1,0:T(8,128)S(1)}, u32[]{:S(2)}, u32[]{:S(2)}) collective-permute-start(f32[3,32,128]{2,1,0:T(8,128)S(1)} %get-tuple-element.94), channel_id=1, source_target_pairs={{0,1},{1,0},{2,3},{3,2},{4,5},{5,4},{6,7},{7,6},{8,9},{9,8},{10,11... | collective-permute-start | bytes 147464 | tf_op jit(solution)/shard_map/ppermute | solution.py:474
  29.8 5.3 %collective-permute-start.9 = (f32[3,32,128]{2,1,0:T(8,128)S(1)}, f32[3,32,128]{2,1,0:T(8,128)S(1)}, u32[]{:S(2)}, u32[]{:S(2)}) collective-permute-start(f32[3,32,128]{2,1,0:T(8,128)S(1)} %get-tuple-element.95), channel_id=1, source_target_pairs={{0,7},{1,2},{2,1},{3,4},{4,3},{5,6},{6,5},{7,0},{8,15},{9,10},{10,... | collective-permute-start | bytes 147464 | tf_op jit(solution)/shard_map/ppermute | solution.py:457
  35.2 4.2 %collective-permute-start.11 = (f32[3,32,128]{2,1,0:T(8,128)S(1)}, f32[3,32,128]{2,1,0:T(8,128)S(1)}, u32[]{:S(2)}, u32[]{:S(2)}) collective-permute-start(f32[3,32,128]{2,1,0:T(8,128)S(1)} %pad_maximum_fusion.4), channel_id=1, source_target_pairs={{0,8},{8,0},{16,24},{24,16},{1,9},{9,1},{17,25},{25,17},{2,10},{10... | collective-permute-start | bytes 147464 | tf_op jit(solution)/shard_map/ppermute | solution.py:508
  35.6 1.2 %collective-permute-start.10 = (f32[2,32,128]{2,1,0:T(8,128)S(1)}, f32[2,32,128]{2,1,0:T(8,128)S(1)}, u32[]{:S(2)}, u32[]{:S(2)}) collective-permute-start(f32[2,32,128]{2,1,0:T(8,128)S(1)} %pad_maximum_fusion.8), channel_id=1, source_target_pairs={{0,1},{1,0},{2,3},{3,2},{4,5},{5,4},{6,7},{7,6},{8,16},{9,17},{10,... | collective-permute-start | bytes 98312 | tf_op jit(solution)/shard_map/ppermute | solution.py:504
  35.6 4.2 %collective-permute-start.12 = (f32[1,32,128]{2,1,0:T(8,128)S(1)}, f32[1,32,128]{2,1,0:T(8,128)S(1)}, u32[]{:S(2)}, u32[]{:S(2)}) collective-permute-start(f32[1,32,128]{2,1,0:T(8,128)S(1)} %get-tuple-element.130), channel_id=1, source_target_pairs={{0,1},{1,0},{2,3},{3,2},{4,5},{5,4},{6,7},{7,6},{8,16},{9,17},{10,... | collective-permute-start | bytes 49160 | tf_op jit(solution)/shard_map/ppermute | solution.py:509
  40.3 1.3 %collective-permute-start.13 = (f32[3,32,128]{2,1,0:T(8,128)S(1)}, f32[3,32,128]{2,1,0:T(8,128)S(1)}, u32[]{:S(2)}, u32[]{:S(2)}) collective-permute-start(f32[3,32,128]{2,1,0:T(8,128)S(1)} %get-tuple-element.100), channel_id=1, source_target_pairs={{0,1},{1,0},{2,3},{3,2},{4,5},{5,4},{6,7},{7,6},{8,9},{9,8},{10,11... | collective-permute-start | bytes 147464 | tf_op jit(solution)/shard_map/ppermute | solution.py:474
  40.6 5.4 %collective-permute-start.14 = (f32[3,32,128]{2,1,0:T(8,128)S(1)}, f32[3,32,128]{2,1,0:T(8,128)S(1)}, u32[]{:S(2)}, u32[]{:S(2)}) collective-permute-start(f32[3,32,128]{2,1,0:T(8,128)S(1)} %shard_map.131), channel_id=1, source_target_pairs={{0,7},{1,2},{2,1},{3,4},{4,3},{5,6},{6,5},{7,0},{8,15},{9,10},{10,... | collective-permute-start | bytes 147464 | tf_op jit(solution)/shard_map/ppermute | solution.py:457
  45.9 5.5 %collective-permute-start.16 = (f32[3,32,128]{2,1,0:T(8,128)S(1)}, f32[3,32,128]{2,1,0:T(8,128)S(1)}, u32[]{:S(2)}, u32[]{:S(2)}) collective-permute-start(f32[3,32,128]{2,1,0:T(8,128)S(1)} %pad_maximum_fusion.5), channel_id=1, source_target_pairs={{0,8},{8,0},{16,24},{24,16},{1,9},{9,1},{17,25},{25,17},{2,10},{10... | collective-permute-start | bytes 147464 | tf_op jit(solution)/shard_map/ppermute | solution.py:508
  49.3 1.2 %collective-permute-start.15 = (f32[2,32,128]{2,1,0:T(8,128)S(1)}, f32[2,32,128]{2,1,0:T(8,128)S(1)}, u32[]{:S(2)}, u32[]{:S(2)}) collective-permute-start(f32[2,32,128]{2,1,0:T(8,128)S(1)} %pad_maximum_fusion.9), channel_id=1, source_target_pairs={{0,1},{1,0},{2,3},{3,2},{4,5},{5,4},{6,7},{7,6},{8,16},{9,17},{10,... | collective-permute-start | bytes 98312 | tf_op jit(solution)/shard_map/ppermute | solution.py:504
  49.3 2.5 %collective-permute-start.17 = (f32[1,32,128]{2,1,0:T(8,128)S(1)}, f32[1,32,128]{2,1,0:T(8,128)S(1)}, u32[]{:S(2)}, u32[]{:S(2)}) collective-permute-start(f32[1,32,128]{2,1,0:T(8,128)S(1)} %get-tuple-element.126), channel_id=1, source_target_pairs={{0,1},{1,0},{2,3},{3,2},{4,5},{5,4},{6,7},{7,6},{8,16},{9,17},{10,... | collective-permute-start | bytes 49160 | tf_op jit(solution)/shard_map/ppermute | solution.py:509
  52.7 1.3 %collective-permute-start.18 = (f32[3,32,128]{2,1,0:T(8,128)S(1)}, f32[3,32,128]{2,1,0:T(8,128)S(1)}, u32[]{:S(2)}, u32[]{:S(2)}) collective-permute-start(f32[3,32,128]{2,1,0:T(8,128)S(1)} %get-tuple-element.106), channel_id=1, source_target_pairs={{0,1},{1,0},{2,3},{3,2},{4,5},{5,4},{6,7},{7,6},{8,9},{9,8},{10,11... | collective-permute-start | bytes 147464 | tf_op jit(solution)/shard_map/ppermute | solution.py:474
  52.8 5.3 %collective-permute-start.19 = (f32[3,32,128]{2,1,0:T(8,128)S(1)}, f32[3,32,128]{2,1,0:T(8,128)S(1)}, u32[]{:S(2)}, u32[]{:S(2)}) collective-permute-start(f32[3,32,128]{2,1,0:T(8,128)S(1)} %get-tuple-element.107), channel_id=1, source_target_pairs={{0,7},{1,2},{2,1},{3,4},{4,3},{5,6},{6,5},{7,0},{8,15},{9,10},{10,... | collective-permute-start | bytes 147464 | tf_op jit(solution)/shard_map/ppermute | solution.py:457
  58.2 6.2 %collective-permute-start.21 = (f32[3,32,128]{2,1,0:T(8,128)S(1)}, f32[3,32,128]{2,1,0:T(8,128)S(1)}, u32[]{:S(2)}, u32[]{:S(2)}) collective-permute-start(f32[3,32,128]{2,1,0:T(8,128)S(1)} %pad_maximum_fusion.6), channel_id=1, source_target_pairs={{0,8},{8,0},{16,24},{24,16},{1,9},{9,1},{17,25},{25,17},{2,10},{10... | collective-permute-start | bytes 147464 | tf_op jit(solution)/shard_map/ppermute | solution.py:508
  62.2 1.2 %collective-permute-start.20 = (f32[2,32,128]{2,1,0:T(8,128)S(1)}, f32[2,32,128]{2,1,0:T(8,128)S(1)}, u32[]{:S(2)}, u32[]{:S(2)}) collective-permute-start(f32[2,32,128]{2,1,0:T(8,128)S(1)} %pad_maximum_fusion.10), channel_id=1, source_target_pairs={{0,1},{1,0},{2,3},{3,2},{4,5},{5,4},{6,7},{7,6},{8,16},{9,17},{10,... | collective-permute-start | bytes 98312 | tf_op jit(solution)/shard_map/ppermute | solution.py:504
  62.2 2.7 %collective-permute-start.22 = (f32[1,32,128]{2,1,0:T(8,128)S(1)}, f32[1,32,128]{2,1,0:T(8,128)S(1)}, u32[]{:S(2)}, u32[]{:S(2)}) collective-permute-start(f32[1,32,128]{2,1,0:T(8,128)S(1)} %get-tuple-element.122), channel_id=1, source_target_pairs={{0,1},{1,0},{2,3},{3,2},{4,5},{5,4},{6,7},{7,6},{8,16},{9,17},{10,... | collective-permute-start | bytes 49160 | tf_op jit(solution)/shard_map/ppermute | solution.py:509
  65.4 1.3 %collective-permute-start.23 = (f32[3,32,128]{2,1,0:T(8,128)S(1)}, f32[3,32,128]{2,1,0:T(8,128)S(1)}, u32[]{:S(2)}, u32[]{:S(2)}) collective-permute-start(f32[3,32,128]{2,1,0:T(8,128)S(1)} %get-tuple-element.112), channel_id=1, source_target_pairs={{0,1},{1,0},{2,3},{3,2},{4,5},{5,4},{6,7},{7,6},{8,9},{9,8},{10,11... | collective-permute-start | bytes 147464 | tf_op jit(solution)/shard_map/ppermute | solution.py:474
  65.7 5.4 %collective-permute-start.24 = (f32[3,32,128]{2,1,0:T(8,128)S(1)}, f32[3,32,128]{2,1,0:T(8,128)S(1)}, u32[]{:S(2)}, u32[]{:S(2)}) collective-permute-start(f32[3,32,128]{2,1,0:T(8,128)S(1)} %shard_map.139), channel_id=1, source_target_pairs={{0,7},{1,2},{2,1},{3,4},{4,3},{5,6},{6,5},{7,0},{8,15},{9,10},{10,... | collective-permute-start | bytes 147464 | tf_op jit(solution)/shard_map/ppermute | solution.py:457
  66.7 8.6 %collective-permute-start.25 = (f32[2,32,128]{2,1,0:T(8,128)S(1)}, f32[2,32,128]{2,1,0:T(8,128)S(1)}, u32[]{:S(2)}, u32[]{:S(2)}) collective-permute-start(f32[2,32,128]{2,1,0:T(8,128)S(1)} %pad_maximum_fusion.11), channel_id=1, source_target_pairs={{0,1},{1,0},{2,3},{3,2},{4,5},{5,4},{6,7},{7,6},{8,16},{9,17},{10,... | collective-permute-start | bytes 98312 | tf_op jit(solution)/shard_map/ppermute | solution.py:504
  71.1 5.5 %collective-permute-start.26 = (f32[3,32,128]{2,1,0:T(8,128)S(1)}, f32[3,32,128]{2,1,0:T(8,128)S(1)}, u32[]{:S(2)}, u32[]{:S(2)}) collective-permute-start(f32[3,32,128]{2,1,0:T(8,128)S(1)} %pad_maximum_fusion.7), channel_id=1, source_target_pairs={{0,8},{8,0},{16,24},{24,16},{1,9},{9,1},{17,25},{25,17},{2,10},{10... | collective-permute-start | bytes 147464 | tf_op jit(solution)/shard_map/ppermute | solution.py:508
  74.5 2.4 %collective-permute-start.27 = (f32[1,32,128]{2,1,0:T(8,128)S(1)}, f32[1,32,128]{2,1,0:T(8,128)S(1)}, u32[]{:S(2)}, u32[]{:S(2)}) collective-permute-start(f32[1,32,128]{2,1,0:T(8,128)S(1)} %get-tuple-element.118), channel_id=1, source_target_pairs={{0,1},{1,0},{2,3},{3,2},{4,5},{5,4},{6,7},{7,6},{8,16},{9,17},{10,... | collective-permute-start | bytes 49160 | tf_op jit(solution)/shard_map/ppermute | solution.py:509

commit v11 on v9

--- a/solution.py
+++ b/solution.py
@@ -291,11 +291,12 @@
     total_ref[...] = gather_matmul(stack_ref, [ref[...] for ref in matrix_refs], rows)
 
 
-def early_part_kernel(own_ref, inner_ref, outer_ref, early_ref, *rest):
+def early_part_kernel(own_ref, inner_ref, outer_ref, early_first_ref, early_second_ref, *rest):
     *matrix_refs, total_ref, stack_ref, early_stack_ref = rest
     near_refs, far_refs = matrix_refs[: len(matrix_refs) // 2], matrix_refs[len(matrix_refs) // 2 :]
     part_kernel(own_ref, inner_ref, outer_ref, *near_refs, total_ref, stack_ref)
-    total_ref[...] = lat_share(total_ref, early_ref, far_refs, early_stack_ref, 3)
+    total_ref[...] = lat_share(total_ref, early_first_ref, far_refs, early_stack_ref, 0)
+    total_ref[...] = lat_share(total_ref, early_second_ref, far_refs, early_stack_ref, 3)
 
 
 def lat_share(total_ref, lat_ref, matrix_refs, stack_ref, first):
@@ -309,11 +310,11 @@
 
 def inner_share_kernel(total_ref, lat_inner_ref, *rest):
     *matrix_refs, new_total_ref, stack_ref = rest
-    new_total_ref[...] = lat_share(total_ref, lat_inner_ref, matrix_refs, stack_ref, 0)
+    new_total_ref[...] = lat_share(total_ref, lat_inner_ref, matrix_refs, stack_ref, 3 - lat_inner_ref.shape[0])
 
 
 def sent_base_kernel(total_ref, lat_inner_ref, far_ref, edges_ref, scale_ref, matrix_ref, new_total_ref, base_ref, stack_ref, own_stack_ref):
-    total = lat_share(total_ref, lat_inner_ref, [far_ref], stack_ref, 0)
+    total = lat_share(total_ref, lat_inner_ref, [far_ref], stack_ref, 3 - lat_inner_ref.shape[0])
     new_total_ref[...] = total
     put_parts(own_stack_ref, edges_ref[...] - scale_ref[...] * total, 0)
     base_ref[...] = gather_matmul(own_stack_ref, [matrix_ref[...]], total_ref.shape[0])
@@ -488,8 +489,9 @@
                 copies=2,
             )
         early = phase >= 2
-        first = jnp.stack([inner_in[1], lat_inner, outer_in[1]])
+        first = outer_in[1:2] if early else jnp.stack([inner_in[1], lat_inner, outer_in[1]])
         if early:
+            early_first = lax.ppermute(jnp.stack([inner_in[1], lat_inner]), "lat", lat_inner_route)
             early_in = lax.ppermute(jnp.stack([inner_in[2], lat_outer]), ("lat", "lon"), lat_outer_route)
             second = outer_in[2:3]
         else:
@@ -528,12 +530,12 @@
                 values,
                 inner_in,
                 outer_in,
-                *([early_in, gradient_near, gradient_far] if early else [gradient_near]),
+                *([early_first, early_in, gradient_near, gradient_far] if early else [gradient_near]),
             )
             total, base = call(
                 sent_base_kernel,
                 [((rows, edge_pad), f32), ((rows, 3 * halo), f32)],
-                [stack_lat(3), stack_edges],
+                [stack_lat(count), stack_edges],
                 total,
                 first_in,
                 gradient_far,
@@ -550,9 +552,9 @@
                 normal,
                 inner_in,
                 outer_in,
-                *([early_in, near_high, near_low, far_high, far_low] if early else [near_high, near_low]),
-            )
-            (total,) = call(inner_share_kernel, [((rows, cells), f32)], [stack_lat(3)], total, first_in, far_high, far_low)
+                *([early_first, early_in, near_high, near_low, far_high, far_low] if early else [near_high, near_low]),
+            )
+            (total,) = call(inner_share_kernel, [((rows, cells), f32)], [stack_lat(count)], total, first_in, far_high, far_low)
             operands = (total, second_in, far_high, far_low, values, speed, inverse, forward, back)
             if phase < 2 * NSUB - 1:
                 values, outer, stack = call(

time: 81.6 us -> 75.4 us (0.924)
  waiting for transfers between devices: 27 us -> 17.7 us
  starting transfers between devices: 32.6 us -> 35.6 us
    ppermute x0 -> x4, starting transfers between devices: none -> 8.45 us  [on_device(): lax.ppermute(jnp.stack([inner_in[1], lat_inner]), 'lat', lat_inner_route)]
    ppermute x6, waiting for transfers between devices: 20.2 us -> 11.9 us  [on_device(): outer_in = lax.ppermute(outer, 'lon', lon_routes[1])]
    ppermute x6, starting transfers between devices: 17.1 us -> 12.9 us  [on_device(): first_in = lax.ppermute(first, 'lat', lat_inner_route)]
    ppermute x4, waiting for transfers between devices: 2.09 us -> 0.01 us  [on_device(): lax.ppermute(jnp.stack([inner_in[2], lat_outer]), ('lat', 'lon'), lat_out...]
    ppermute x6, starting transfers between devices: 1.53 us -> 0.02 us  [on_device(): second_in = lax.ppermute(second, ('lat', 'lon'), lat_outer_route)]
    ppermute x6, waiting for transfers between devices: 3.21 us -> 4.42 us  [on_device(): first_in = lax.ppermute(first, 'lat', lat_inner_route)]
  transfers between devices with their start and end apart: 28 -> 32, of which waited for: 15 -> 13; matrix products, arithmetic and copies ran while one was open for 1% -> 1% of each run, Pallas kernels for 17% -> 18%
where the time goes in v11:
time: 75.4 us; the launch traced here: 75.1 us
  starting transfers between devices  35.6 us (47%)
  Pallas kernels  20 us (27%)
  waiting for transfers between devices  17.7 us (23%)
  between operations  0.92 us (1%)
  local copies, waits for them, and re-layouts  0.82 us (1%)
    pallas_call x29, Pallas kernels, call(): pl.pallas_call(body, out_shape=tuple((jax.ShapeDtypeStruct(shape, kind) f...  20 us
    ppermute x6, starting transfers between devices, on_device(): first_in = lax.ppermute(first, 'lat', lat_inner_route)  12.9 us
    ppermute x6, starting transfers between devices, on_device(): outer_in = lax.ppermute(outer, 'lon', lon_routes[1])  12.3 us
    ppermute x6, waiting for transfers between devices, on_device(): outer_in = lax.ppermute(outer, 'lon', lon_routes[1])  11.9 us
    ppermute x4, starting transfers between devices, on_device(): lax.ppermute(jnp.stack([inner_in[1], lat_inner]), 'lat', lat_inner_route)  8.45 us
    ppermute x6, waiting for transfers between devices, on_device(): first_in = lax.ppermute(first, 'lat', lat_inner_route)  4.42 us
    ppermute x6, starting transfers between devices, on_device(): inner_in = lax.ppermute(inner, 'lon', lon_routes[0])  1.9 us
  transfers between devices with their start and end apart: 32, of which 13 were waited for; matrix products, arithmetic and copies ran while one was open for 1% of the time, Pallas kernels for 18%

profile of v11, /device:TPU:0, one launch (start us, length us, event | category | flops | bytes accessed | tf_op | source)
XLA Modules:
  0.0 75.1 jit_solution(4852244640063634390)
XLA Ops:
  0.6 1.2 %shard_map.113 = (f32[32,640]{1,0:T(8,128)S(1)}, bf16[96,640]{1,0:T(8,128)(2,1)S(1)}, f32[3,32,128]{2,1,0:T(8,128)S(1)}, s32[8,128]{1,0:T(8,128)S(1)}) custom-call(f32[30,1,640]{2,1,0:T(1,128)} %bitcast.36, s32[8,128]{1,0:T(8,128)} %bitcast.42), custom_call_target="tpu_custom_call" | custom-call | tf_op jit(solution)/shard_map/pallas_call | solution.py:411
  1.8 0.5 shard_map.114
  2.3 0.6 collective-permute-start
  2.9 4.7 %collective-permute-start.1 = (f32[3,32,128]{2,1,0:T(8,128)S(1)}, f32[3,32,128]{2,1,0:T(8,128)S(1)}, u32[]{:S(2)}, u32[]{:S(2)}) collective-permute-start(f32[3,32,128]{2,1,0:T(8,128)S(1)} %get-tuple-element.61), channel_id=1, source_target_pairs={{0,7},{1,2},{2,1},{3,4},{4,3},{5,6},{6,5},{7,0},{8,15},{9,10},{10,... | collective-permute-start | bytes 147464 | tf_op jit(solution)/shard_map/ppermute | solution.py:454
  7.6 1.9 %collective-permute-done.1.outer_ref = f32[3,32,128]{2,1,0:T(8,128)S(1)} collective-permute-done((f32[3,32,128]{2,1,0:T(8,128)S(1)}, f32[3,32,128]{2,1,0:T(8,128)S(1)}, u32[]{:S(2)}, u32[]{:S(2)}) %collective-permute-start.1) | collective-permute-done | bytes 49184 | tf_op jit(solution)/shard_map/ppermute | solution.py:454
  9.4 1.6 %collective-permute-start.2 = (f32[3,32,128]{2,1,0:T(8,128)S(1)}, f32[3,32,128]{2,1,0:T(8,128)S(1)}, u32[]{:S(2)}, u32[]{:S(2)}) collective-permute-start(f32[3,32,128]{2,1,0:T(8,128)S(1)} %pad_maximum_fusion), channel_id=1, source_target_pairs={{0,8},{8,0},{16,24},{24,16},{1,9},{9,1},{17,25},{25,17},{2,10},{10... | collective-permute-start | bytes 147464 | tf_op jit(solution)/shard_map/ppermute | solution.py:499
  11.0 1.5 %shard_map.115 = (bf16[896,1024]{1,0:T(8,128)(2,1)S(1)}, bf16[768,1024]{1,0:T(8,128)(2,1)S(1)}) custom-call(s32[2,960]{1,0:T(2,128)} %bitcast.39), custom_call_target="tpu_custom_call" | custom-call | tf_op jit(solution)/shard_map/pallas_call | solution.py:411
  12.5 1.9 %shard_map.117 = (f32[32,1024]{1,0:T(8,128)S(1)}, f32[1,1024]{1,0:T(1,128)S(1)}, bf16[1024,384]{1,0:T(8,128)(2,1)S(1)}, bf16[1024,640]{1,0:T(8,128)(2,1)S(1)}, b...) custom-call(f32[30,1,960]{2,1,0:T(1,128)} %bitcast.35, s32[8,128]{1,0:T(8,128)} %bitcast.43, f32[1,960]{1,0:T(1,128)} %dual_hbm.1, ...), custom_call_target="tpu_custom_call" | custom-call | tf_op jit(solution)/shard_map/pallas_call | solution.py:411
  14.4 0.4 shard_map.116.total_ref
  14.9 0.5 shard_map.118
  15.4 0.6 shard_map.119
  16.0 0.6 collective-permute-start.4
  16.7 3.2 %collective-permute-start.5 = (f32[3,32,128]{2,1,0:T(8,128)S(1)}, f32[3,32,128]{2,1,0:T(8,128)S(1)}, u32[]{:S(2)}, u32[]{:S(2)}) collective-permute-start(f32[3,32,128]{2,1,0:T(8,128)S(1)} %shard_map.120), channel_id=1, source_target_pairs={{0,7},{1,2},{2,1},{3,4},{4,3},{5,6},{6,5},{7,0},{8,15},{9,10},{10,... | collective-permute-start | bytes 147464 | tf_op jit(solution)/shard_map/ppermute | solution.py:454
  20.0 2.5 %collective-permute-done.5.outer_ref = f32[3,32,128]{2,1,0:T(8,128)S(1)} collective-permute-done((f32[3,32,128]{2,1,0:T(8,128)S(1)}, f32[3,32,128]{2,1,0:T(8,128)S(1)}, u32[]{:S(2)}, u32[]{:S(2)}) %collective-permute-start.5) | collective-permute-done | bytes 49184 | tf_op jit(solution)/shard_map/ppermute | solution.py:454
  22.5 2.7 %collective-permute-start.6 = (f32[3,32,128]{2,1,0:T(8,128)S(1)}, f32[3,32,128]{2,1,0:T(8,128)S(1)}, u32[]{:S(2)}, u32[]{:S(2)}) collective-permute-start(f32[3,32,128]{2,1,0:T(8,128)S(1)} %pad_maximum_fusion.2), channel_id=1, source_target_pairs={{0,8},{8,0},{16,24},{24,16},{1,9},{9,1},{17,25},{25,17},{2,10},{10... | collective-permute-start | bytes 147464 | tf_op jit(solution)/shard_map/ppermute | solution.py:499
  25.2 1.2 %shard_map.124 = (f32[1,640]{1,0:T(1,128)S(1)}, f32[256,128]{1,0:T(8,128)S(1)}, f32[256,128]{1,0:T(8,128)S(1)}, f32[256,128]{1,0:T(8,128)S(1)}, bf16[640,384]{1,...) custom-call(f32[30,1,640]{2,1,0:T(1,128)} %bitcast.37, s32[8,128]{1,0:T(8,128)S(1)} %get-tuple-element.59.list_ref, ...), custom_call_target="tpu_custom_call" | custom-call | tf_op jit(solution)/shard_map/pallas_call | solution.py:411
  26.4 2.4 %shard_map.121 = (bf16[1280,640]{1,0:T(8,128)(2,1)S(1)}, bf16[1280,640]{1,0:T(8,128)(2,1)S(1)}, bf16[768,640]{1,0:T(8,128)(2,1)S(1)}, bf16[768,640]{1,0:T(8,128)(2,1)S(1)}) custom-call(s32[3,1,640]{2,1,0:T(1,128)} %bitcast.40, f32[3,1,640]{2,1,0:T(1,128)} %bitcast.41), custom_call_target="tpu_custom_call" | custom-call | tf_op jit(solution)/shard_map/pallas_call | solution.py:411
  28.8 0.7 shard_map.122.total_ref
  29.8 0.7 shard_map.125
  30.9 0.6 collective-permute-start.8
  31.4 2.1 %collective-permute-start.9 = (f32[3,32,128]{2,1,0:T(8,128)S(1)}, f32[3,32,128]{2,1,0:T(8,128)S(1)}, u32[]{:S(2)}, u32[]{:S(2)}) collective-permute-start(f32[3,32,128]{2,1,0:T(8,128)S(1)} %get-tuple-element.91), channel_id=1, source_target_pairs={{0,7},{1,2},{2,1},{3,4},{4,3},{5,6},{6,5},{7,0},{8,15},{9,10},{10,... | collective-permute-start | bytes 147464 | tf_op jit(solution)/shard_map/ppermute | solution.py:454
  33.5 0.7 collective-permute-start.10
  34.2 2.5 %collective-permute-done.9.outer_ref = f32[3,32,128]{2,1,0:T(8,128)S(1)} collective-permute-done((f32[3,32,128]{2,1,0:T(8,128)S(1)}, f32[3,32,128]{2,1,0:T(8,128)S(1)}, u32[]{:S(2)}, u32[]{:S(2)}) %collective-permute-start.9) | collective-permute-done | bytes 49184 | tf_op jit(solution)/shard_map/ppermute | solution.py:454
  37.5 0.6 shard_map.127.total_ref
  38.1 2.4 %collective-permute-done.12.lat_inner_ref = f32[1,32,128]{2,1,0:T(8,128)S(1)} collective-permute-done((f32[1,32,128]{2,1,0:T(8,128)S(1)}, f32[1,32,128]{2,1,0:T(8,128)S(1)}, u32[]{:S(2)}, u32[]{:S(2)}) %collective-permute-start.12) | collective-permute-done | bytes 16416 | tf_op jit(solution)/shard_map/ppermute | solution.py:499
  40.9 0.5 shard_map.129
  41.7 1.0 %collective-permute-start.15 = (f32[3,32,128]{2,1,0:T(8,128)S(1)}, f32[3,32,128]{2,1,0:T(8,128)S(1)}, u32[]{:S(2)}, u32[]{:S(2)}) collective-permute-start(f32[3,32,128]{2,1,0:T(8,128)S(1)} %shard_map.130), channel_id=1, source_target_pairs={{0,7},{1,2},{2,1},{3,4},{4,3},{5,6},{6,5},{7,0},{8,15},{9,10},{10,... | collective-permute-start | bytes 147464 | tf_op jit(solution)/shard_map/ppermute | solution.py:454
  42.8 2.5 %collective-permute-start.16 = (f32[2,32,128]{2,1,0:T(8,128)S(1)}, f32[2,32,128]{2,1,0:T(8,128)S(1)}, u32[]{:S(2)}, u32[]{:S(2)}) collective-permute-start(f32[2,32,128]{2,1,0:T(8,128)S(1)} %pad_maximum_fusion.6), channel_id=1, source_target_pairs={{0,8},{8,0},{16,24},{24,16},{1,9},{9,1},{17,25},{25,17},{2,10},{10... | collective-permute-start | bytes 98312 | tf_op jit(solution)/shard_map/ppermute | solution.py:494
  45.3 1.8 %collective-permute-done.15.outer_ref = f32[3,32,128]{2,1,0:T(8,128)S(1)} collective-permute-done((f32[3,32,128]{2,1,0:T(8,128)S(1)}, f32[3,32,128]{2,1,0:T(8,128)S(1)}, u32[]{:S(2)}, u32[]{:S(2)}) %collective-permute-start.15) | collective-permute-done | bytes 49184 | tf_op jit(solution)/shard_map/ppermute | solution.py:454
  47.1 2.5 %collective-permute-start.18 = (f32[1,32,128]{2,1,0:T(8,128)S(1)}, f32[1,32,128]{2,1,0:T(8,128)S(1)}, u32[]{:S(2)}, u32[]{:S(2)}) collective-permute-start(f32[1,32,128]{2,1,0:T(8,128)S(1)} %get-tuple-element.123), channel_id=1, source_target_pairs={{0,8},{8,0},{16,24},{24,16},{1,9},{9,1},{17,25},{25,17},{2,10},{10... | collective-permute-start | bytes 49160 | tf_op jit(solution)/shard_map/ppermute | solution.py:499
  49.6 0.9 %shard_map.131.total_ref = f32[32,640]{1,0:T(8,128)S(1)} custom-call(f32[32,1024]{1,0:T(8,128)S(1)} %get-tuple-element.95.own_ref.edges_ref, f32[3,32,128]{2,1,0:T(8,128)S(1)} %collective-permute-done.14.inner_ref, f32[3,32,128]{2,1,0:T(8,128)S(1)} %collective-permute-done.15.outer_ref, f32[2,32,128]{2,1,0:T(8,128)S(1)} %collective-permute-done.16.early_first_ref, ...), custom_call_target="tpu_custom_call" | custom-call | tf_op jit(solution)/shard_map/pallas_call | solution.py:411
  50.5 0.8 %collective-permute-done.18.lat_inner_ref = f32[1,32,128]{2,1,0:T(8,128)S(1)} collective-permute-done((f32[1,32,128]{2,1,0:T(8,128)S(1)}, f32[1,32,128]{2,1,0:T(8,128)S(1)}, u32[]{:S(2)}, u32[]{:S(2)}) %collective-permute-start.18) | collective-permute-done | bytes 16416 | tf_op jit(solution)/shard_map/ppermute | solution.py:499
  51.5 0.6 shard_map.133
  52.5 0.6 collective-permute-start.21
  53.2 0.6 collective-permute-done.20.inner_ref
  53.8 2.7 %collective-permute-start.22 = (f32[2,32,128]{2,1,0:T(8,128)S(1)}, f32[2,32,128]{2,1,0:T(8,128)S(1)}, u32[]{:S(2)}, u32[]{:S(2)}) collective-permute-start(f32[2,32,128]{2,1,0:T(8,128)S(1)} %pad_maximum_fusion.8), channel_id=1, source_target_pairs={{0,8},{8,0},{16,24},{24,16},{1,9},{9,1},{17,25},{25,17},{2,10},{10... | collective-permute-start | bytes 98312 | tf_op jit(solution)/shard_map/ppermute | solution.py:494
  56.5 1.4 %collective-permute-done.21.outer_ref = f32[3,32,128]{2,1,0:T(8,128)S(1)} collective-permute-done((f32[3,32,128]{2,1,0:T(8,128)S(1)}, f32[3,32,128]{2,1,0:T(8,128)S(1)}, u32[]{:S(2)}, u32[]{:S(2)}) %collective-permute-start.21) | collective-permute-done | bytes 49184 | tf_op jit(solution)/shard_map/ppermute | solution.py:454
  57.9 2.7 %collective-permute-start.24 = (f32[1,32,128]{2,1,0:T(8,128)S(1)}, f32[1,32,128]{2,1,0:T(8,128)S(1)}, u32[]{:S(2)}, u32[]{:S(2)}) collective-permute-start(f32[1,32,128]{2,1,0:T(8,128)S(1)} %get-tuple-element.119), channel_id=1, source_target_pairs={{0,8},{8,0},{16,24},{24,16},{1,9},{9,1},{17,25},{25,17},{2,10},{10... | collective-permute-start | bytes 49160 | tf_op jit(solution)/shard_map/ppermute | solution.py:499
  60.6 0.6 shard_map.135.total_ref
  61.2 1.1 %collective-permute-done.24.lat_inner_ref = f32[1,32,128]{2,1,0:T(8,128)S(1)} collective-permute-done((f32[1,32,128]{2,1,0:T(8,128)S(1)}, f32[1,32,128]{2,1,0:T(8,128)S(1)}, u32[]{:S(2)}, u32[]{:S(2)}) %collective-permute-start.24) | collective-permute-done | bytes 16416 | tf_op jit(solution)/shard_map/ppermute | solution.py:499
  62.8 0.5 shard_map.137
  63.5 0.6 collective-permute-start.27
  64.6 2.5 %collective-permute-start.28 = (f32[2,32,128]{2,1,0:T(8,128)S(1)}, f32[2,32,128]{2,1,0:T(8,128)S(1)}, u32[]{:S(2)}, u32[]{:S(2)}) collective-permute-start(f32[2,32,128]{2,1,0:T(8,128)S(1)} %pad_maximum_fusion.10), channel_id=1, source_target_pairs={{0,8},{8,0},{16,24},{24,16},{1,9},{9,1},{17,25},{25,17},{2,10},{10... | collective-permute-start | bytes 98312 | tf_op jit(solution)/shard_map/ppermute | solution.py:494
  67.1 1.8 %collective-permute-done.27.outer_ref = f32[3,32,128]{2,1,0:T(8,128)S(1)} collective-permute-done((f32[3,32,128]{2,1,0:T(8,128)S(1)}, f32[3,32,128]{2,1,0:T(8,128)S(1)}, u32[]{:S(2)}, u32[]{:S(2)}) %collective-permute-start.27) | collective-permute-done | bytes 49184 | tf_op jit(solution)/shard_map/ppermute | solution.py:454
  68.9 3.0 %collective-permute-start.30 = (f32[1,32,128]{2,1,0:T(8,128)S(1)}, f32[1,32,128]{2,1,0:T(8,128)S(1)}, u32[]{:S(2)}, u32[]{:S(2)}) collective-permute-start(f32[1,32,128]{2,1,0:T(8,128)S(1)} %get-tuple-element.115), channel_id=1, source_target_pairs={{0,8},{8,0},{16,24},{24,16},{1,9},{9,1},{17,25},{25,17},{2,10},{10... | collective-permute-start | bytes 49160 | tf_op jit(solution)/shard_map/ppermute | solution.py:499
  72.0 0.8 %copy.12 = f32[1,30,960]{2,0,1:T(1,128)} copy(f32[1,30,960]{2,1,0:T(8,128)S(1)} %slice_bitcast_fusion) | data formatting | bytes 230400
  72.7 0.9 %shard_map.139.total_ref = f32[32,640]{1,0:T(8,128)S(1)} custom-call(f32[32,1024]{1,0:T(8,128)S(1)} %get-tuple-element.107.own_ref, f32[3,32,128]{2,1,0:T(8,128)S(1)} %collective-permute-done.26.inner_ref, f32[3,32,128]{2,1,0:T(8,128)S(1)} %collective-permute-done.27.outer_ref, f32[2,32,128]{2,1,0:T(8,128)S(1)} %collective-permute-done.28.early_first_ref, ...), custom_call_target="tpu_custom_call" | custom-call | tf_op jit(solution)/shard_map/pallas_call | solution.py:411
  74.1 1.0 %shard_map.141 = f32[30,1,640]{2,1,0:T(1,128)} custom-call(f32[32,640]{1,0:T(8,128)S(1)} %shard_map.140.total_ref, f32[1,32,128]{2,1,0:T(8,128)S(1)} %collective-permute-done.31.lat_outer_ref, bf16[768,640]{1,0:T(8,128)(2,1)S(1)} %get-tuple-element.79.rest_0_.high_ref.rest_2_, bf16[768,640]{1,0:T(8,128)(2,1)S(1)} %get-tuple-element.80.rest_1_.low_ref.rest_3_, ...), custom_call_target="tpu_custom_call" | custom-call | tf_op jit(solution)/shard_map/pallas_call | solution.py:411
  (71 shorter events, 4.5 us)
Async XLA Ops:
  2.3 5.3 %collective-permute-start = (f32[3,32,128]{2,1,0:T(8,128)S(1)}, f32[3,32,128]{2,1,0:T(8,128)S(1)}, u32[]{:S(2)}, u32[]{:S(2)}) collective-permute-start(f32[3,32,128]{2,1,0:T(8,128)S(1)} %get-tuple-element.60), channel_id=1, source_target_pairs={{0,1},{1,0},{2,3},{3,2},{4,5},{5,4},{6,7},{7,6},{8,9},{9,8},{10,11... | collective-permute-start | bytes 147464 | tf_op jit(solution)/shard_map/ppermute | solution.py:471
  2.9 6.6 %collective-permute-start.1 = (f32[3,32,128]{2,1,0:T(8,128)S(1)}, f32[3,32,128]{2,1,0:T(8,128)S(1)}, u32[]{:S(2)}, u32[]{:S(2)}) collective-permute-start(f32[3,32,128]{2,1,0:T(8,128)S(1)} %get-tuple-element.61), channel_id=1, source_target_pairs={{0,7},{1,2},{2,1},{3,4},{4,3},{5,6},{6,5},{7,0},{8,15},{9,10},{10,... | collective-permute-start | bytes 147464 | tf_op jit(solution)/shard_map/ppermute | solution.py:454
  9.4 5.4 %collective-permute-start.2 = (f32[3,32,128]{2,1,0:T(8,128)S(1)}, f32[3,32,128]{2,1,0:T(8,128)S(1)}, u32[]{:S(2)}, u32[]{:S(2)}) collective-permute-start(f32[3,32,128]{2,1,0:T(8,128)S(1)} %pad_maximum_fusion), channel_id=1, source_target_pairs={{0,8},{8,0},{16,24},{24,16},{1,9},{9,1},{17,25},{25,17},{2,10},{10... | collective-permute-start | bytes 147464 | tf_op jit(solution)/shard_map/ppermute | solution.py:499
  11.0 4.4 %collective-permute-start.3 = (f32[3,32,128]{2,1,0:T(8,128)S(1)}, f32[3,32,128]{2,1,0:T(8,128)S(1)}, u32[]{:S(2)}, u32[]{:S(2)}) collective-permute-start(f32[3,32,128]{2,1,0:T(8,128)S(1)} %pad_maximum_fusion.1), channel_id=1, source_target_pairs={{0,1},{1,0},{2,3},{3,2},{4,5},{5,4},{6,7},{7,6},{8,16},{9,17},{10,... | collective-permute-start | bytes 147464 | tf_op jit(solution)/shard_map/ppermute | solution.py:500
  16.0 4.0 %collective-permute-start.4 = (f32[3,32,128]{2,1,0:T(8,128)S(1)}, f32[3,32,128]{2,1,0:T(8,128)S(1)}, u32[]{:S(2)}, u32[]{:S(2)}) collective-permute-start(f32[3,32,128]{2,1,0:T(8,128)S(1)} %get-tuple-element.72), channel_id=1, source_target_pairs={{0,1},{1,0},{2,3},{3,2},{4,5},{5,4},{6,7},{7,6},{8,9},{9,8},{10,11... | collective-permute-start | bytes 147464 | tf_op jit(solution)/shard_map/ppermute | solution.py:471
  16.7 5.7 %collective-permute-start.5 = (f32[3,32,128]{2,1,0:T(8,128)S(1)}, f32[3,32,128]{2,1,0:T(8,128)S(1)}, u32[]{:S(2)}, u32[]{:S(2)}) collective-permute-start(f32[3,32,128]{2,1,0:T(8,128)S(1)} %shard_map.120), channel_id=1, source_target_pairs={{0,7},{1,2},{2,1},{3,4},{4,3},{5,6},{6,5},{7,0},{8,15},{9,10},{10,... | collective-permute-start | bytes 147464 | tf_op jit(solution)/shard_map/ppermute | solution.py:454
  22.5 7.0 %collective-permute-start.6 = (f32[3,32,128]{2,1,0:T(8,128)S(1)}, f32[3,32,128]{2,1,0:T(8,128)S(1)}, u32[]{:S(2)}, u32[]{:S(2)}) collective-permute-start(f32[3,32,128]{2,1,0:T(8,128)S(1)} %pad_maximum_fusion.2), channel_id=1, source_target_pairs={{0,8},{8,0},{16,24},{24,16},{1,9},{9,1},{17,25},{25,17},{2,10},{10... | collective-permute-start | bytes 147464 | tf_op jit(solution)/shard_map/ppermute | solution.py:499
  25.2 4.6 %collective-permute-start.7 = (f32[3,32,128]{2,1,0:T(8,128)S(1)}, f32[3,32,128]{2,1,0:T(8,128)S(1)}, u32[]{:S(2)}, u32[]{:S(2)}) collective-permute-start(f32[3,32,128]{2,1,0:T(8,128)S(1)} %pad_maximum_fusion.3), channel_id=1, source_target_pairs={{0,1},{1,0},{2,3},{3,2},{4,5},{5,4},{6,7},{7,6},{8,16},{9,17},{10,... | collective-permute-start | bytes 147464 | tf_op jit(solution)/shard_map/ppermute | solution.py:500
  30.9 2.7 %collective-permute-start.8 = (f32[3,32,128]{2,1,0:T(8,128)S(1)}, f32[3,32,128]{2,1,0:T(8,128)S(1)}, u32[]{:S(2)}, u32[]{:S(2)}) collective-permute-start(f32[3,32,128]{2,1,0:T(8,128)S(1)} %get-tuple-element.90), channel_id=1, source_target_pairs={{0,1},{1,0},{2,3},{3,2},{4,5},{5,4},{6,7},{7,6},{8,9},{9,8},{10,11... | collective-permute-start | bytes 147464 | tf_op jit(solution)/shard_map/ppermute | solution.py:471
  31.4 5.3 %collective-permute-start.9 = (f32[3,32,128]{2,1,0:T(8,128)S(1)}, f32[3,32,128]{2,1,0:T(8,128)S(1)}, u32[]{:S(2)}, u32[]{:S(2)}) collective-permute-start(f32[3,32,128]{2,1,0:T(8,128)S(1)} %get-tuple-element.91), channel_id=1, source_target_pairs={{0,7},{1,2},{2,1},{3,4},{4,3},{5,6},{6,5},{7,0},{8,15},{9,10},{10,... | collective-permute-start | bytes 147464 | tf_op jit(solution)/shard_map/ppermute | solution.py:454
  33.5 4.0 %collective-permute-start.10 = (f32[2,32,128]{2,1,0:T(8,128)S(1)}, f32[2,32,128]{2,1,0:T(8,128)S(1)}, u32[]{:S(2)}, u32[]{:S(2)}) collective-permute-start(f32[2,32,128]{2,1,0:T(8,128)S(1)} %pad_maximum_fusion.4), channel_id=1, source_target_pairs={{0,8},{8,0},{16,24},{24,16},{1,9},{9,1},{17,25},{25,17},{2,10},{10... | collective-permute-start | bytes 98312 | tf_op jit(solution)/shard_map/ppermute | solution.py:494
  34.2 3.3 %collective-permute-start.11 = (f32[2,32,128]{2,1,0:T(8,128)S(1)}, f32[2,32,128]{2,1,0:T(8,128)S(1)}, u32[]{:S(2)}, u32[]{:S(2)}) collective-permute-start(f32[2,32,128]{2,1,0:T(8,128)S(1)} %pad_maximum_fusion.5), channel_id=1, source_target_pairs={{0,1},{1,0},{2,3},{3,2},{4,5},{5,4},{6,7},{7,6},{8,16},{9,17},{10,... | collective-permute-start | bytes 98312 | tf_op jit(solution)/shard_map/ppermute | solution.py:495
  36.7 3.7 %collective-permute-start.12 = (f32[1,32,128]{2,1,0:T(8,128)S(1)}, f32[1,32,128]{2,1,0:T(8,128)S(1)}, u32[]{:S(2)}, u32[]{:S(2)}) collective-permute-start(f32[1,32,128]{2,1,0:T(8,128)S(1)} %get-tuple-element.127), channel_id=1, source_target_pairs={{0,8},{8,0},{16,24},{24,16},{1,9},{9,1},{17,25},{25,17},{2,10},{10... | collective-permute-start | bytes 49160 | tf_op jit(solution)/shard_map/ppermute | solution.py:499
  37.2 3.8 %collective-permute-start.13 = (f32[1,32,128]{2,1,0:T(8,128)S(1)}, f32[1,32,128]{2,1,0:T(8,128)S(1)}, u32[]{:S(2)}, u32[]{:S(2)}) collective-permute-start(f32[1,32,128]{2,1,0:T(8,128)S(1)} %get-tuple-element.126), channel_id=1, source_target_pairs={{0,1},{1,0},{2,3},{3,2},{4,5},{5,4},{6,7},{7,6},{8,16},{9,17},{10,... | collective-permute-start | bytes 49160 | tf_op jit(solution)/shard_map/ppermute | solution.py:500
  41.5 1.3 %collective-permute-start.14 = (f32[3,32,128]{2,1,0:T(8,128)S(1)}, f32[3,32,128]{2,1,0:T(8,128)S(1)}, u32[]{:S(2)}, u32[]{:S(2)}) collective-permute-start(f32[3,32,128]{2,1,0:T(8,128)S(1)} %get-tuple-element.96), channel_id=1, source_target_pairs={{0,1},{1,0},{2,3},{3,2},{4,5},{5,4},{6,7},{7,6},{8,9},{9,8},{10,11... | collective-permute-start | bytes 147464 | tf_op jit(solution)/shard_map/ppermute | solution.py:471
  41.7 5.4 %collective-permute-start.15 = (f32[3,32,128]{2,1,0:T(8,128)S(1)}, f32[3,32,128]{2,1,0:T(8,128)S(1)}, u32[]{:S(2)}, u32[]{:S(2)}) collective-permute-start(f32[3,32,128]{2,1,0:T(8,128)S(1)} %shard_map.130), channel_id=1, source_target_pairs={{0,7},{1,2},{2,1},{3,4},{4,3},{5,6},{6,5},{7,0},{8,15},{9,10},{10,... | collective-permute-start | bytes 147464 | tf_op jit(solution)/shard_map/ppermute | solution.py:454
  42.8 6.8 %collective-permute-start.16 = (f32[2,32,128]{2,1,0:T(8,128)S(1)}, f32[2,32,128]{2,1,0:T(8,128)S(1)}, u32[]{:S(2)}, u32[]{:S(2)}) collective-permute-start(f32[2,32,128]{2,1,0:T(8,128)S(1)} %pad_maximum_fusion.6), channel_id=1, source_target_pairs={{0,8},{8,0},{16,24},{24,16},{1,9},{9,1},{17,25},{25,17},{2,10},{10... | collective-permute-start | bytes 98312 | tf_op jit(solution)/shard_map/ppermute | solution.py:494
  45.3 4.3 %collective-permute-start.17 = (f32[2,32,128]{2,1,0:T(8,128)S(1)}, f32[2,32,128]{2,1,0:T(8,128)S(1)}, u32[]{:S(2)}, u32[]{:S(2)}) collective-permute-start(f32[2,32,128]{2,1,0:T(8,128)S(1)} %pad_maximum_fusion.7), channel_id=1, source_target_pairs={{0,1},{1,0},{2,3},{3,2},{4,5},{5,4},{6,7},{7,6},{8,16},{9,17},{10,... | collective-permute-start | bytes 98312 | tf_op jit(solution)/shard_map/ppermute | solution.py:495
  47.1 4.2 %collective-permute-start.18 = (f32[1,32,128]{2,1,0:T(8,128)S(1)}, f32[1,32,128]{2,1,0:T(8,128)S(1)}, u32[]{:S(2)}, u32[]{:S(2)}) collective-permute-start(f32[1,32,128]{2,1,0:T(8,128)S(1)} %get-tuple-element.123), channel_id=1, source_target_pairs={{0,8},{8,0},{16,24},{24,16},{1,9},{9,1},{17,25},{25,17},{2,10},{10... | collective-permute-start | bytes 49160 | tf_op jit(solution)/shard_map/ppermute | solution.py:499
  49.6 1.9 %collective-permute-start.19 = (f32[1,32,128]{2,1,0:T(8,128)S(1)}, f32[1,32,128]{2,1,0:T(8,128)S(1)}, u32[]{:S(2)}, u32[]{:S(2)}) collective-permute-start(f32[1,32,128]{2,1,0:T(8,128)S(1)} %get-tuple-element.122), channel_id=1, source_target_pairs={{0,1},{1,0},{2,3},{3,2},{4,5},{5,4},{6,7},{7,6},{8,16},{9,17},{10,... | collective-permute-start | bytes 49160 | tf_op jit(solution)/shard_map/ppermute | solution.py:500
  52.4 1.3 %collective-permute-start.20 = (f32[3,32,128]{2,1,0:T(8,128)S(1)}, f32[3,32,128]{2,1,0:T(8,128)S(1)}, u32[]{:S(2)}, u32[]{:S(2)}) collective-permute-start(f32[3,32,128]{2,1,0:T(8,128)S(1)} %get-tuple-element.102), channel_id=1, source_target_pairs={{0,1},{1,0},{2,3},{3,2},{4,5},{5,4},{6,7},{7,6},{8,9},{9,8},{10,11... | collective-permute-start | bytes 147464 | tf_op jit(solution)/shard_map/ppermute | solution.py:471
  52.5 5.4 %collective-permute-start.21 = (f32[3,32,128]{2,1,0:T(8,128)S(1)}, f32[3,32,128]{2,1,0:T(8,128)S(1)}, u32[]{:S(2)}, u32[]{:S(2)}) collective-permute-start(f32[3,32,128]{2,1,0:T(8,128)S(1)} %get-tuple-element.103), channel_id=1, source_target_pairs={{0,7},{1,2},{2,1},{3,4},{4,3},{5,6},{6,5},{7,0},{8,15},{9,10},{10,... | collective-permute-start | bytes 147464 | tf_op jit(solution)/shard_map/ppermute | solution.py:454
  53.8 6.9 %collective-permute-start.22 = (f32[2,32,128]{2,1,0:T(8,128)S(1)}, f32[2,32,128]{2,1,0:T(8,128)S(1)}, u32[]{:S(2)}, u32[]{:S(2)}) collective-permute-start(f32[2,32,128]{2,1,0:T(8,128)S(1)} %pad_maximum_fusion.8), channel_id=1, source_target_pairs={{0,8},{8,0},{16,24},{24,16},{1,9},{9,1},{17,25},{25,17},{2,10},{10... | collective-permute-start | bytes 98312 | tf_op jit(solution)/shard_map/ppermute | solution.py:494
  56.5 4.1 %collective-permute-start.23 = (f32[2,32,128]{2,1,0:T(8,128)S(1)}, f32[2,32,128]{2,1,0:T(8,128)S(1)}, u32[]{:S(2)}, u32[]{:S(2)}) collective-permute-start(f32[2,32,128]{2,1,0:T(8,128)S(1)} %pad_maximum_fusion.9), channel_id=1, source_target_pairs={{0,1},{1,0},{2,3},{3,2},{4,5},{5,4},{6,7},{7,6},{8,16},{9,17},{10,... | collective-permute-start | bytes 98312 | tf_op jit(solution)/shard_map/ppermute | solution.py:495
  57.9 4.4 %collective-permute-start.24 = (f32[1,32,128]{2,1,0:T(8,128)S(1)}, f32[1,32,128]{2,1,0:T(8,128)S(1)}, u32[]{:S(2)}, u32[]{:S(2)}) collective-permute-start(f32[1,32,128]{2,1,0:T(8,128)S(1)} %get-tuple-element.119), channel_id=1, source_target_pairs={{0,8},{8,0},{16,24},{24,16},{1,9},{9,1},{17,25},{25,17},{2,10},{10... | collective-permute-start | bytes 49160 | tf_op jit(solution)/shard_map/ppermute | solution.py:499
  60.6 2.2 %collective-permute-start.25 = (f32[1,32,128]{2,1,0:T(8,128)S(1)}, f32[1,32,128]{2,1,0:T(8,128)S(1)}, u32[]{:S(2)}, u32[]{:S(2)}) collective-permute-start(f32[1,32,128]{2,1,0:T(8,128)S(1)} %get-tuple-element.118), channel_id=1, source_target_pairs={{0,1},{1,0},{2,3},{3,2},{4,5},{5,4},{6,7},{7,6},{8,16},{9,17},{10,... | collective-permute-start | bytes 49160 | tf_op jit(solution)/shard_map/ppermute | solution.py:500
  63.3 1.3 %collective-permute-start.26 = (f32[3,32,128]{2,1,0:T(8,128)S(1)}, f32[3,32,128]{2,1,0:T(8,128)S(1)}, u32[]{:S(2)}, u32[]{:S(2)}) collective-permute-start(f32[3,32,128]{2,1,0:T(8,128)S(1)} %get-tuple-element.108), channel_id=1, source_target_pairs={{0,1},{1,0},{2,3},{3,2},{4,5},{5,4},{6,7},{7,6},{8,9},{9,8},{10,11... | collective-permute-start | bytes 147464 | tf_op jit(solution)/shard_map/ppermute | solution.py:471
  63.5 5.4 %collective-permute-start.27 = (f32[3,32,128]{2,1,0:T(8,128)S(1)}, f32[3,32,128]{2,1,0:T(8,128)S(1)}, u32[]{:S(2)}, u32[]{:S(2)}) collective-permute-start(f32[3,32,128]{2,1,0:T(8,128)S(1)} %shard_map.138), channel_id=1, source_target_pairs={{0,7},{1,2},{2,1},{3,4},{4,3},{5,6},{6,5},{7,0},{8,15},{9,10},{10,... | collective-permute-start | bytes 147464 | tf_op jit(solution)/shard_map/ppermute | solution.py:454
  64.6 8.1 %collective-permute-start.28 = (f32[2,32,128]{2,1,0:T(8,128)S(1)}, f32[2,32,128]{2,1,0:T(8,128)S(1)}, u32[]{:S(2)}, u32[]{:S(2)}) collective-permute-start(f32[2,32,128]{2,1,0:T(8,128)S(1)} %pad_maximum_fusion.10), channel_id=1, source_target_pairs={{0,8},{8,0},{16,24},{24,16},{1,9},{9,1},{17,25},{25,17},{2,10},{10... | collective-permute-start | bytes 98312 | tf_op jit(solution)/shard_map/ppermute | solution.py:494
  67.1 5.6 %collective-permute-start.29 = (f32[2,32,128]{2,1,0:T(8,128)S(1)}, f32[2,32,128]{2,1,0:T(8,128)S(1)}, u32[]{:S(2)}, u32[]{:S(2)}) collective-permute-start(f32[2,32,128]{2,1,0:T(8,128)S(1)} %pad_maximum_fusion.11), channel_id=1, source_target_pairs={{0,1},{1,0},{2,3},{3,2},{4,5},{5,4},{6,7},{7,6},{8,16},{9,17},{10,... | collective-permute-start | bytes 98312 | tf_op jit(solution)/shard_map/ppermute | solution.py:495
  68.9 5.1 %collective-permute-start.31 = (f32[1,32,128]{2,1,0:T(8,128)S(1)}, f32[1,32,128]{2,1,0:T(8,128)S(1)}, u32[]{:S(2)}, u32[]{:S(2)}) collective-permute-start(f32[1,32,128]{2,1,0:T(8,128)S(1)} %get-tuple-element.114), channel_id=1, source_target_pairs={{0,1},{1,0},{2,3},{3,2},{4,5},{5,4},{6,7},{7,6},{8,16},{9,17},{10,... | collective-permute-start | bytes 49160 | tf_op jit(solution)/shard_map/ppermute | solution.py:500
  68.9 4.9 %collective-permute-start.30 = (f32[1,32,128]{2,1,0:T(8,128)S(1)}, f32[1,32,128]{2,1,0:T(8,128)S(1)}, u32[]{:S(2)}, u32[]{:S(2)}) collective-permute-start(f32[1,32,128]{2,1,0:T(8,128)S(1)} %get-tuple-element.115), channel_id=1, source_target_pairs={{0,8},{8,0},{16,24},{24,16},{1,9},{9,1},{17,25},{25,17},{2,10},{10... | collective-permute-start | bytes 49160 | tf_op jit(solution)/shard_map/ppermute | solution.py:499
